TPU v7x, 8 devices: a whole 2x2x1 slice. The times are simulated.
8 devices in a mesh: tp: 4 (over z, y, x), ep: 2 (over core).
Axes of the slice: x: 2, y: 2, z: 1, core: 2. Of those that a mesh axis runs over, the one named last changes fastest.
Arguments:
- x: bfloat16 [2048, 2048], P(('ep', 'tp'))
- idx: int32 [2048, 2], P(('ep', 'tp'))
- g: float32 [2048, 2], P(('ep', 'tp'))
- cap: int32 [8], replicated
- w1: bfloat16 [8, 2048, 5632], P('ep', None, 'tp')
- w3: bfloat16 [8, 2048, 5632], P('ep', None, 'tp')
- w2: bfloat16 [8, 5632, 2048], P('ep', 'tp')
Outputs:
- output: bfloat16 [2048, 2048], P(('ep', 'tp'))
All inputs are finite; a program needn't handle non-finite values.
Results may differ from a plain program's by a relative error of at most 0.00147.
Values are sent between devices in bfloat16 or wider.
A program may use at most 1 GiB of HBM per device.

v0:
```python
import jax
import jax.numpy as jnp
from jax import lax
from jax.sharding import PartitionSpec as P


def solution(mesh):
    ep = mesh.shape["ep"]

    def local(x, idx, g, cap, w1, w3, w2):
        t_loc, d = x.shape
        top = idx.shape[1]
        e_all = cap.shape[0]
        e_loc = w1.shape[0]
        c = (5 * top * t_loc // (2 * e_all) + 7) // 8 * 8
        flat = idx.reshape(-1)
        oh = (flat[:, None] == jnp.arange(e_all, dtype=jnp.int32)[None, :]).astype(jnp.int32)
        pos = jnp.sum(jnp.cumsum(oh, axis=0) * oh, axis=1) - 1
        sid = jnp.where(pos < cap[flat], flat * c + pos, e_all * c)
        tok = jnp.arange(t_loc * top) // top
        slots = jnp.zeros((e_all * c + 1, d), x.dtype).at[sid].set(x[tok])[: e_all * c]
        slots = slots.reshape(ep, e_loc, c, d)
        recv = lax.all_to_all(slots, "ep", 0, 0, tiled=True)
        full = lax.all_gather(recv, "tp", axis=0, tiled=True)
        h1 = jnp.einsum("secd,edf->secf", full, w1, preferred_element_type=jnp.float32)
        h3 = jnp.einsum("secd,edf->secf", full, w3, preferred_element_type=jnp.float32)
        h = (jax.nn.silu(h1) * h3).astype(jnp.bfloat16)
        p = jnp.einsum("secf,efd->secd", h, w2, preferred_element_type=jnp.float32)
        mine = lax.psum_scatter(p, "tp", scatter_dimension=0, tiled=True).astype(jnp.bfloat16)
        back = lax.all_to_all(mine, "ep", 0, 0, tiled=True).reshape(e_all * c, d)
        back = jnp.concatenate([back, jnp.zeros((1, d), back.dtype)], axis=0)
        yc = back[sid].astype(jnp.float32) * g.reshape(-1)[:, None]
        return jnp.sum(yc.reshape(t_loc, top, d), axis=1).astype(jnp.bfloat16)

    rows = P(("ep", "tp"), None)
    return jax.shard_map(
        local,
        mesh=mesh,
        in_specs=(rows, rows, rows, P(None), P("ep", None, "tp"), P("ep", None, "tp"), P("ep", "tp", None)),
        out_specs=rows,
        check_vma=False,
    )
```

profile of v0, /device:TPU:0, one launch (start us, length us, event | category | flops | bytes accessed | tf_op | source)
XLA Modules:
  0.0 1793.4 jit_solution(15117715592697321759)
XLA Ops:
  6.5 0.0 copy-start
  6.5 0.0 all-gather.2.cloned.1.call-start
  6.5 0.9 copy.15
  7.4 0.1 reshape.149
  7.6 0.1 eq.29
  7.7 0.1 eq.25
  7.9 1.6 fusion.20
  9.5 1.1 reduce-window.6
  10.7 0.2 slice_reduce_fusion
  11.0 0.1 fusion.18
  11.1 4.3 compare_select_fusion.3
  15.4 0.7 broadcast_select_fusion
  16.1 0.0 copy-done
  16.1 23.2 %scatter_custom_fusion = bf16[1281,2048]{1,0:T(8,128)(2,1)} fusion(s32[512]{0:T(512)S(1)} %bitcast.72, bf16[]{:T(256)} %constant.18.clone.1, bf16[256,2048]{1,0:T(8,128)(2,1)S(1)} %copy-done, s32[1024]{0:T(1024)S(1)} %pad_clamp_fusion.1), kind=kCustom, calls=%fused_computation.19 | custom fusion | bytes 5246978 | tf_op jit(solution)/shard_map/scatter | solution.py:21
  39.3 2.9 slice.26
  42.2 0.0 copy-start.4
  42.2 0.0 copy-start.5
  42.2 8.3 all_to_all.10
  50.6 2.8 copy.18
  53.3 0.0 all-gather.2.cloned.1.call-update
  53.4 0.0 copy-done.4
  53.4 0.8 copy.20
  54.2 0.0 copy-done.5
  54.2 0.6 dynamic-slice
  55.4 0.6 pad_clamp_fusion
  56.0 187.4 %all-gather.2.cloned.1.call-done = bf16[8,4,160,2048]{3,2,0,1:T(8,128)(2,1)} async-done(((bf16[2,4,160,2048]{3,2,0,1:T(8,128)(2,1)}), bf16[8,4,160,2048]{3,2,0,1:T(8,128)(2,1)}) %all-gather.2.cloned.1.call-update) | async-done | bytes 20971536 | tf_op jit(solution)/shard_map/all_gather | solution.py:24
  243.4 40.5 %fusion.6 = f32[4,8,160,1408]{3,2,1,0:T(8,128)} fusion(bf16[8,4,160,2048]{3,2,0,1:T(8,128)(2,1)} %all-gather.2.cloned.1.call-done, bf16[4,2048,1408]{2,1,0:T(8,128)(2,1)} %param.12), kind=kOutput, calls=%fused_computation.12 | convolution fusion | flops 29527900160 | bytes 72876032 | tf_op jit(solution)/shard_map/secd,edf->secf/dot_general | solution.py:26
  283.8 46.7 %fusion = bf16[8,4,160,1408]{3,2,0,1:T(8,128)(2,1)} fusion(f32[4,8,160,1408]{3,2,1,0:T(8,128)} %fusion.6, bf16[8,4,160,2048]{3,2,0,1:T(8,128)(2,1)} %all-gather.2.cloned.1.call-done, bf16[4,2048,1408]{2,1,0:T(8,128)(2,1)} %param.11), kind=kOutput, calls=%fused_computation.4 | convolution fusion | flops 29571153920 | bytes 87293952 | tf_op jit(solution)/shard_map/secd,edf->secf/dot_general | solution.py:25
  330.5 41.1 %fusion.12 = f32[8,4,160,2048]{3,2,0,1:T(8,128)} fusion(bf16[8,4,160,1408]{3,2,0,1:T(8,128)(2,1)} %fusion, bf16[4,1408,2048]{2,1,0:T(8,128)(2,1)} %param.13), kind=kOutput, calls=%fused_computation.16 | convolution fusion | flops 29527900160 | bytes 79429632 | tf_op jit(solution)/shard_map/secf,efd->secd/dot_general | solution.py:28
  371.6 1378.2 %all-reduce.3 = bf16[8,4,160,2048]{3,2,0,1:T(8,128)(2,1)} all-reduce(f32[8,4,160,2048]{3,2,0,1:T(8,128)} %fusion.12), channel_id=2, replica_groups=mesh['tp'=4,'ep'=2] {'tp'}, use_global_device_ids=true, to_apply=%region_4.5.clone | all-reduce | flops 10485760 | bytes 62914560
  1749.8 2.9 dynamic-slice_convert_fusion
  1752.8 0.0 copy-start.3
  1752.8 0.8 copy.19
  1753.6 8.2 all_to_all.11
  1761.9 0.0 copy-start.1
  1761.9 2.8 concatenate.3
  1764.6 0.0 copy-done.3
  1764.6 0.0 copy-start.2
  1764.6 7.6 gather_fusion
  1772.2 4.0 reshape.152
  1776.2 0.0 copy-done.2
  1776.2 9.9 multiply_reduce_fusion
  1786.1 0.0 copy-done.1
  (8 shorter events, 0.1 us)
Async XLA Ops:
  6.5 9.5 copy-start
  6.5 236.8 %all-gather.2.cloned.1.call-start = ((), (), s32[]{:S(2)}) async-start(), calls=%async_computation.2 | async-start | bytes 26214400 | tf_op jit(solution)/shard_map/all_gather | solution.py:24
  42.2 11.2 copy-start.4
  42.2 12.0 copy-start.5
  1752.8 11.8 copy-start.3
  1761.9 24.3 %copy-start.1 = (bf16[256,2048]{1,0:T(8,128)(2,1)S(1)}, bf16[256,2048]{1,0:T(8,128)(2,1)}, u32[]{:S(2)}) copy-start(bf16[256,2048]{1,0:T(8,128)(2,1)} %param.7) | copy-start | bytes 3145732
  1764.6 11.6 copy-start.2
Sparse Core Ops, SparseCore 0:
  53.5 189.8 all-gather.1
where the time goes:
time: 1800 us; the launch traced here: 1790 us
  blocking collectives  1390 us (77%)
  waiting for transfers between devices  187 us (10%)
  matrix products  128 us (7%)
  local copies, waits for them, and re-layouts  51.6 us (3%)
    unnamed x1, blocking collectives  1380 us
    all_gather x1, waiting for transfers between devices, local(): full = lax.all_gather(recv, 'tp', axis=0, tiled=True)  187 us
    dot_general x1, matrix products, local(): jnp.einsum('secd,edf->secf', full, w1, preferred_element_type=jnp.float32)  46.7 us
    dot_general x1, matrix products, local(): p = jnp.einsum('secf,efd->secd', h, w2, preferred_element_type=jnp.float32)  41.1 us
    dot_general x1, matrix products, local(): jnp.einsum('secd,edf->secf', full, w3, preferred_element_type=jnp.float32)  40.5 us
  transfers between devices with their start and end apart: 1, of which 1 were waited for; matrix products, arithmetic and copies ran while one was open for 0% of the time, Pallas kernels for 0%

commit v1 on v0

v1 whole, which is shorter than its diff:
```python
import functools

import jax
import jax.numpy as jnp
from jax import lax
from jax.experimental import pallas as pl
from jax.experimental.pallas import tpu as pltpu
from jax.sharding import PartitionSpec as P


F32 = jnp.float32
BF16 = jnp.bfloat16


def _meta_kernel(chips, idx_ref, cap_ref, pos_ref, off_ref, cnt_ref):
    blocks, _, t = idx_ref.shape
    e_all = cap_ref.shape[0]
    ids = lax.broadcasted_iota(jnp.int32, (e_all, t), 0)
    cap = jnp.broadcast_to(cap_ref[...], (e_all, t))
    before = (
        lax.broadcasted_iota(jnp.int32, (t, t), 0) < lax.broadcasted_iota(jnp.int32, (t, t), 1)
    ).astype(F32).astype(BF16)
    hits, earlier, counts = [], [], []
    for b in range(blocks):
        hit = (idx_ref[b, 0:1, :] == ids) | (idx_ref[b, 1:2, :] == ids)
        one = hit.astype(F32)
        rank = jnp.dot(one.astype(BF16), before, preferred_element_type=F32).astype(jnp.int32)
        total = jnp.sum(one, axis=1, keepdims=True).astype(jnp.int32)
        hits.append(hit)
        earlier.append(rank)
        counts.append(jnp.minimum(jnp.broadcast_to(total, (e_all, t)), cap))
    for c in range(chips):
        both = counts[c] + counts[c + chips]
        first = jnp.zeros_like(both)
        for e in range(e_all - 1):
            first = first + jnp.where(ids > e, jnp.broadcast_to(both[e : e + 1, :], both.shape), 0)
        off_ref[c] = first[:, :128]
        cnt_ref[c] = both[:, :128]
        for b, start in ((c, first), (c + chips, first + counts[c])):
            kept = hits[b] & (earlier[b] < cap)
            pos_ref[b] = jnp.where(kept, start + earlier[b], -1)


def _expert_kernel(turns, small, tile, cut, *refs):
    n = len(turns)
    off_ref, cnt_ref, pos_ref = refs[:3]
    x_hbm = refs[3 : 3 + 2 * n]
    w1_hbm, w3_hbm, w2_hbm = refs[3 + 2 * n : 6 + 2 * n]
    outs = refs[6 + 2 * n : 6 + 6 * n]
    acc, xbuf, xs, hs, w1a, w3a, w1b, w3b, w2s, wsem, osem, xsem = refs[6 + 6 * n :]
    e_loc, d, ff = w1_hbm.shape
    t = xbuf.shape[2]
    quarter, half_d = t, d // 2
    span = xs.shape[0] // n
    core, me = lax.axis_index("ep"), lax.axis_index("tp")
    chips = pos_ref.shape[0] // 2

    def chunk(k, e):
        if k == 0:
            return [
                pltpu.make_async_copy(w1_hbm.at[e, :, pl.ds(0, cut)], w1a, wsem.at[0]),
                pltpu.make_async_copy(w3_hbm.at[e, :, pl.ds(0, cut)], w3a, wsem.at[1]),
            ]
        if k == 1:
            return [
                pltpu.make_async_copy(w1_hbm.at[e, :, pl.ds(cut, ff - cut)], w1b, wsem.at[2]),
                pltpu.make_async_copy(w3_hbm.at[e, :, pl.ds(cut, ff - cut)], w3b, wsem.at[3]),
            ]
        h = k - 2
        return [pltpu.make_async_copy(w2_hbm.at[e, :, pl.ds(h * half_d, half_d)], w2s.at[h], wsem.at[2 + k])]

    def start(k, e):
        for c in chunk(k, e):
            c.start()

    def finish(k, e):
        for c in chunk(k, e):
            c.wait()

    def following(k, e):
        @pl.when(e + 1 < e_loc)
        def _():
            start(k, e + 1)

    def out_copies(h):
        copies = []
        for s in range(n):
            for q in range(4):
                side = core if q < 2 else 1 - core
                first = pl.multiple_of(side * (2 * quarter) + (q % 2) * quarter, quarter)
                copies.append(
                    pltpu.make_async_copy(
                        acc.at[s, pl.ds(first, quarter), pl.ds(h * half_d, half_d)],
                        outs[4 * s + q].at[:, pl.ds(h * half_d, half_d)],
                        osem.at[h, 4 * s + q],
                    )
                )
        return copies

    tokens = [pltpu.make_async_copy(x_hbm[i], xbuf.at[i // 2, i % 2], xsem.at[i]) for i in range(2 * n)]
    for c in tokens:
        c.start()
    for k in range(4):
        start(k, 0)
    acc[...] = jnp.zeros_like(acc)
    for c in tokens:
        c.wait()

    def step(e, carry):
        expert = core * e_loc + e

        def each(body):
            def source(s, carry):
                turn = turns[0] if n == 1 else jnp.where(s == 0, turns[0], turns[1])
                chip = jnp.bitwise_xor(me, turn)
                off, cnt = off_ref[chip, expert, 0], cnt_ref[chip, expert, 0]
                base = off // 8 * 8
                need = jnp.where(cnt > 0, off - base + cnt, 0)

                @pl.when((need > 0) & (need <= small))
                def _():
                    body(s, chip, small, base, 0)

                @pl.when(need > small)
                def _():
                    def one(i, carry):
                        body(s, chip, tile, base, pl.multiple_of(i * tile, 16))
                        return carry

                    lax.fori_loop(0, (need + tile - 1) // tile, one, 0)

                return carry

            if n == 1:
                source(0, 0)
            else:
                lax.fori_loop(0, n, source, 0)

        def dispatch(s, chip, m, base, first):
            row = lax.broadcasted_iota(jnp.int32, (m, t), 0) + (base + first)
            pa = pos_ref[chip + core * chips, pl.ds(expert, 1), :]
            pb = pos_ref[chip + (1 - core) * chips, pl.ds(expert, 1), :]
            ha = (row == pa).astype(F32).astype(BF16)
            hb = (row == pb).astype(F32).astype(BF16)
            part = jnp.dot(ha, xbuf[s, 0], preferred_element_type=F32)
            part = part + jnp.dot(hb, xbuf[s, 1], preferred_element_type=F32)
            xs[pl.ds(pl.multiple_of(s * span + first, 16), m), :] = part.astype(BF16)

        def hidden(wa, wb, lo, width):
            def body(s, chip, m, base, first):
                at = pl.ds(pl.multiple_of(s * span + first, 16), m)
                h1 = jnp.dot(xs[at, :], wa[...], preferred_element_type=F32)
                h3 = jnp.dot(xs[at, :], wb[...], preferred_element_type=F32)
                hs[at, lo : lo + width] = (jax.nn.silu(h1) * h3).astype(BF16)

            return body

        def project(k):
            def body(s, chip, m, base, first):
                at = pl.ds(pl.multiple_of(s * span + first, 16), m)
                p = jnp.dot(hs[at, :], w2s[k], preferred_element_type=F32)
                acc[s, pl.ds(pl.multiple_of(base + first, 8), m), k * half_d : (k + 1) * half_d] += p

            return body

        each(dispatch)
        finish(0, e)
        each(hidden(w1a, w3a, 0, cut))
        following(0, e)
        finish(1, e)
        each(hidden(w1b, w3b, cut, ff - cut))
        following(1, e)
        for k in range(2):
            finish(2 + k, e)
            each(project(k))
            following(2 + k, e)
            if k == 0:

                @pl.when(e == e_loc - 1)
                def _():
                    for c in out_copies(0):
                        c.start()

        return carry

    lax.fori_loop(0, e_loc, step, 0)
    for c in out_copies(1):
        c.start()
    for c in out_copies(0) + out_copies(1):
        c.wait()


def _combine_kernel(chips, pos_ref, idx_ref, g_ref, ma_ref, mb_ref, oa_ref, ob_ref, out_ref):
    core, me = lax.axis_index("ep"), lax.axis_index("tp")
    quarter, _ = ma_ref.shape
    t = idx_ref.shape[1]
    pos = pos_ref[me + core * chips]
    ids = lax.broadcasted_iota(jnp.int32, pos.shape, 0)
    row = lax.broadcasted_iota(jnp.int32, (quarter, t), 0)
    dims = (((0,), (0,)), ((), ()))
    total = None
    for j in range(2):
        pj = jnp.max(jnp.where(idx_ref[j : j + 1, :] == ids, pos, -1), axis=0, keepdims=True)
        y = None
        for ref, first in (
            (ma_ref, core * 2 * quarter),
            (mb_ref, core * 2 * quarter + quarter),
            (oa_ref, (1 - core) * 2 * quarter),
            (ob_ref, (1 - core) * 2 * quarter + quarter),
        ):
            hit = (row + first == pj).astype(F32).astype(BF16)
            part = lax.dot_general(hit, ref[...], dims, preferred_element_type=F32)
            y = part if y is None else y + part
        y = y * g_ref[:, j : j + 1]
        total = y if total is None else total + y
    out_ref[...] = total.astype(out_ref.dtype)


def solution(mesh):
    chips = mesh.shape["tp"]
    vmem = pl.BlockSpec(memory_space=pltpu.VMEM)
    anym = pl.BlockSpec(memory_space=pl.ANY)
    smem = pl.BlockSpec(memory_space=pltpu.SMEM)

    def layer(x, idx, g, cap, w1, w3, w2):
        t_loc, d = x.shape
        top = idx.shape[1]
        e_all = cap.shape[0]
        e_loc, _, ff = w1.shape
        c = (5 * top * t_loc // (2 * e_all) + 7) // 8 * 8
        rows = 2 * top * t_loc
        quarter = rows // 4
        cut = 512

        def swap(a):
            return lax.ppermute(a, "ep", [(0, 1), (1, 0)])

        def shift(a, r):
            return lax.ppermute(a, "tp", [(i, i ^ r) for i in range(chips)])

        def after(a, *first):
            return lax.optimization_barrier((a, *first))[0]

        idx_all = lax.all_gather(idx.T, ("ep", "tp"), axis=0)
        pos, off, cnt = pl.pallas_call(
            functools.partial(_meta_kernel, chips),
            out_shape=[
                jax.ShapeDtypeStruct((2 * chips, e_all, t_loc), jnp.int32),
                jax.ShapeDtypeStruct((chips, e_all, 128), jnp.int32),
                jax.ShapeDtypeStruct((chips, e_all, 128), jnp.int32),
            ],
            in_specs=[vmem] * 2,
            out_specs=[vmem] * 3,
            name="meta",
        )(idx_all, cap[:, None])

        small, tile = 96, 144
        span = (2 * c + 7 + tile - 1) // tile * tile

        def stage_call(turns, xs):
            n = len(turns)
            return pl.pallas_call(
                functools.partial(_expert_kernel, turns, small, tile, cut),
                out_shape=[jax.ShapeDtypeStruct((quarter, d), F32)] * (4 * n),
                in_specs=[smem, smem, vmem] + [anym] * (2 * n + 3),
                out_specs=[anym] * (4 * n),
                scratch_shapes=[
                    pltpu.VMEM((n, rows + tile, d), F32),
                    pltpu.VMEM((n, 2, t_loc, d), BF16),
                    pltpu.VMEM((n * span, d), BF16),
                    pltpu.VMEM((n * span, ff), BF16),
                    pltpu.VMEM((d, cut), BF16),
                    pltpu.VMEM((d, cut), BF16),
                    pltpu.VMEM((d, ff - cut), BF16),
                    pltpu.VMEM((d, ff - cut), BF16),
                    pltpu.VMEM((2, ff, d // 2), BF16),
                    pltpu.SemaphoreType.DMA((6,)),
                    pltpu.SemaphoreType.DMA((2, 4 * n)),
                    pltpu.SemaphoreType.DMA((2 * n,)),
                ],
                compiler_params=pltpu.CompilerParams(vmem_limit_bytes=67_043_328),
                cost_estimate=pl.CostEstimate(
                    flops=n * 3 * rows * d * ff, bytes_accessed=6 * e_loc * d * ff + 4 * n * rows * d, transcendentals=0
                ),
            )(off, cnt, pos, *xs, w1, w3, w2)

        def merge(parts):
            return [parts[q] + swap(parts[2 + q]) for q in range(2)]

        x_first = after(x, idx_all)
        x_d, x_x, x_y = shift(x_first, 3), shift(x_first, 1), shift(x_first, 2)

        diag = merge(stage_call((3,), (x_d, swap(x_d))))
        via_x, via_y = shift(diag[0], 1), shift(diag[1], 2)
        x_x, x_y = after(x_x, *diag), after(x_y, *diag)
        both = stage_call((1, 2), (x_x, swap(x_x), x_y, swap(x_y)))
        for_x, for_y = merge(both[:4]), merge(both[4:])
        near_a, near_b = shift(for_x[0], 1), shift(for_y[1], 2)
        far_a, far_b = for_y[0] + via_x, for_x[1] + via_y
        got_a, got_b = shift(far_a, 2), shift(far_b, 1)
        x_o = after(x, *for_x, *for_y)
        own = merge(stage_call((0,), (x_o, swap(x_o))))
        y_a = (own[0] + near_a + got_a).astype(BF16)
        y_b = (own[1] + near_b + got_b).astype(BF16)
        return pl.pallas_call(
            functools.partial(_combine_kernel, chips),
            out_shape=jax.ShapeDtypeStruct((t_loc, d), BF16),
            in_specs=[vmem] * 7,
            out_specs=vmem,
            compiler_params=pltpu.CompilerParams(vmem_limit_bytes=60_000_000),
            name="combine",
        )(pos, idx.T, g, y_a, y_b, swap(y_a), swap(y_b))

    rows = P(("ep", "tp"), None)
    return jax.shard_map(
        layer,
        mesh=mesh,
        in_specs=(rows, rows, rows, P(None), P("ep", None, "tp"), P("ep", None, "tp"), P("ep", "tp", None)),
        out_specs=rows,
        check_vma=False,
    )
```

time: 1800 us -> 333 us (0.18)
  blocking collectives: 1390 us -> 14.6 us
  matrix products: 128 us -> 0 us
  Pallas kernels: 0 us -> 126 us
  waiting for transfers between devices: 187 us -> 140 us
  local copies, waits for them, and re-layouts: 51.6 us -> 6.27 us
  starting transfers between devices: 0.01 us -> 26.9 us
    unnamed x1 -> x0, blocking collectives: 1380 us -> none
    all_gather x1 -> x0, waiting for transfers between devices: 187 us -> none  [local(): full = lax.all_gather(recv, 'tp', axis=0, tiled=True)]
    ppermute x0 -> x23, waiting for transfers between devices: none -> 140 us  [the longest x9 130 us: shift(): return lax.ppermute(a, 'tp', [(i, i ^ r) for i in range(chips)])]
    dot_general x3 -> x0, matrix products: 128 us -> none  [the longest x1 46.7 us: local(): jnp.einsum('secd,edf->secf', full, w1, preferred_element_type=jnp.float32)]
    pallas_call x0 -> x5, Pallas kernels: none -> 126 us  [the longest x3 118 us: stage_call(): pl.pallas_call(functools.partial(_expert_kernel, turns, small, tile, cut)...]
    ppermute x0 -> x23, starting transfers between devices: none -> 26.9 us  [the longest x14 16.3 us: swap(): return lax.ppermute(a, 'ep', [(0, 1), (1, 0)])]
    scatter x1 -> x0, local copies, waits for them, and re-layouts: 23.2 us -> none  [local(): jnp.zeros((e_all * c + 1, d), x.dtype).at[sid].set(x[tok])[:e_all * c]]
  transfers between devices with their start and end apart: 1 -> 23, of which waited for: 1 -> 12; matrix products, arithmetic and copies ran while one was open for 0% -> 6% of each run, Pallas kernels for 0% -> 11%
where the time goes in v1:
time: 333 us
  waiting for transfers between devices  140 us (42%)
  Pallas kernels  126 us (38%)
  starting transfers between devices  26.9 us (8%)
  other arithmetic  18.7 us (6%)
  blocking collectives  14.6 us (4%)
  local copies, waits for them, and re-layouts  6.27 us (2%)
    ppermute x9, waiting for transfers between devices, shift(): return lax.ppermute(a, 'tp', [(i, i ^ r) for i in range(chips)])  130 us
    pallas_call x3, Pallas kernels, stage_call(): pl.pallas_call(functools.partial(_expert_kernel, turns, small, tile, cut)...  118 us
    ppermute x14, starting transfers between devices, swap(): return lax.ppermute(a, 'ep', [(0, 1), (1, 0)])  16.3 us
    all_gather x1, blocking collectives, layer(): idx_all = lax.all_gather(idx.T, ('ep', 'tp'), axis=0)  14.6 us
    ppermute x9, starting transfers between devices, shift(): return lax.ppermute(a, 'tp', [(i, i ^ r) for i in range(chips)])  10.7 us
    add x4, other arithmetic, merge(): return [parts[q] + swap(parts[2 + q]) for q in range(2)]  10.1 us
    ppermute x14, waiting for transfers between devices, swap(): return lax.ppermute(a, 'ep', [(0, 1), (1, 0)])  9.77 us
  transfers between devices with their start and end apart: 23, of which 12 were waited for; matrix products, arithmetic and copies ran while one was open for 6% of the time, Pallas kernels for 11%

profile of v1, /device:TPU:0, one launch (start us, length us, event | category | flops | bytes accessed | tf_op | source)
XLA Modules:
  0.0 332.5 jit_solution(5778569201408559727)
XLA Ops:
  0.0 14.6 %all-gather.1.idx_ref = s32[8,2,256]{2,1,0:T(2,128)} all-gather(s32[1,2,256]{2,1,0:T(2,128)} %bitcast.4), channel_id=2, replica_groups=mesh['tp'=4,'ep'=2] {'ep','tp'}, dimensions={0}, use_global_device_ids=true | all-gather | bytes 18432 | tf_op jit(solution)/shard_map/all_gather | solution.py:244
  14.6 1.4 collective-permute-start.1
  16.0 23.5 %collective-permute-done.1.refs_3_ = bf16[256,2048]{1,0:T(8,128)(2,1)S(1)} collective-permute-done((bf16[256,2048]{1,0:T(8,128)(2,1)}, bf16[256,2048]{1,0:T(8,128)(2,1)S(1)}, u32[]{:S(2)}, u32[]{:S(2)}) %collective-permute-start.1) | collective-permute-done | bytes 1048608 | tf_op jit(solution)/shard_map/ppermute | solution.py:239
  39.5 1.0 copy-done.11
  40.5 1.3 copy.10.cap_ref
  41.8 1.6 meta.1
  43.4 1.0 copy-done.12
  44.4 31.4 %shard_map.73 = (f32[256,2048]{1,0:T(8,128)}, f32[256,2048]{1,0:T(8,128)}, f32[256,2048]{1,0:T(8,128)}, f32[256,2048]{1,0:T(8,128)}) custom-call(s32[4,8,128]{2,1,0:T(8,128)} %get-tuple-element.29.refs_0_, s32[4,8,128]{2,1,0:T(8,128)} %get-tuple-element.30.refs_1_, s32[8,8,256]{2,1,0:T(8,128)} %get-tuple-element.28.refs_2_.pos_ref, ...), custom_call_target="tpu_custom_call" | custom-call | flops 8858370048 | bytes 77594624 | tf_op jit(solution)/shard_map/pallas_call | solution.py:262
  75.8 6.4 %collective-permute-start.4 = (f32[256,2048]{1,0:T(8,128)}, f32[256,2048]{1,0:T(8,128)S(1)}, u32[]{:S(2)}, u32[]{:S(2)}) collective-permute-start(f32[256,2048]{1,0:T(8,128)} %get-tuple-element.35), channel_id=1, source_target_pairs={{0,1},{1,0},{2,3},{3,2},{4,5},{5,4},{6,7},{7,6}} | collective-permute-start | bytes 6291464 | tf_op jit(solution)/shard_map/ppermute | solution.py:236
  82.2 0.0 collective-permute-start.3
  82.2 4.0 %collective-permute-done.4 = f32[256,2048]{1,0:T(8,128)S(1)} collective-permute-done((f32[256,2048]{1,0:T(8,128)}, f32[256,2048]{1,0:T(8,128)S(1)}, u32[]{:S(2)}, u32[]{:S(2)}) %collective-permute-start.4) | collective-permute-done | bytes 2097184 | tf_op jit(solution)/shard_map/ppermute | solution.py:236
  86.2 3.4 %add.43 = f32[256,2048]{1,0:T(8,128)} add(f32[256,2048]{1,0:T(8,128)} %get-tuple-element.34, f32[256,2048]{1,0:T(8,128)S(1)} %collective-permute-done.4) | non-fusion elementwise | flops 524288 | bytes 6291456 | tf_op jit(solution)/shard_map/add | solution.py:288
  89.6 1.6 add.42
  91.2 16.8 %collective-permute-done.6.refs_5_ = bf16[256,2048]{1,0:T(8,128)(2,1)S(1)} collective-permute-done((bf16[256,2048]{1,0:T(8,128)(2,1)}, bf16[256,2048]{1,0:T(8,128)(2,1)S(1)}, u32[]{:S(2)}, u32[]{:S(2)}) %collective-permute-start.6) | collective-permute-done | bytes 1048608 | tf_op jit(solution)/shard_map/ppermute | solution.py:239
  108.0 1.0 copy-done.8
  109.0 0.5 collective-permute-start.5
  109.5 2.1 collective-permute-done.7.refs_6_
  111.7 1.0 copy-done.10
  112.6 0.7 collective-permute-done.5.refs_4_
  113.3 52.9 %shard_map.74 = (f32[256,2048]{1,0:T(8,128)}, f32[256,2048]{1,0:T(8,128)}, f32[256,2048]{1,0:T(8,128)}, f32[256,2048]{1,0:T(8,128)}, f32[256,2048]{1,0:T(8,128)}...) custom-call(s32[4,8,128]{2,1,0:T(8,128)} %get-tuple-element.29.refs_0_, ...), custom_call_target="tpu_custom_call" | custom-call | flops 17716740096 | bytes 85983232 | tf_op jit(solution)/shard_map/pallas_call | solution.py:262
  166.2 8.1 %collective-permute-start.11 = (f32[256,2048]{1,0:T(8,128)}, f32[256,2048]{1,0:T(8,128)S(1)}, u32[]{:S(2)}, u32[]{:S(2)}) collective-permute-start(f32[256,2048]{1,0:T(8,128)} %get-tuple-element.45), channel_id=1, source_target_pairs={{0,1},{1,0},{2,3},{3,2},{4,5},{5,4},{6,7},{7,6}} | collective-permute-start | bytes 6291464 | tf_op jit(solution)/shard_map/ppermute | solution.py:236
  174.4 0.0 collective-permute-start.8
  174.4 3.6 %collective-permute-start.19 = (f32[256,2048]{1,0:T(8,128)}, f32[256,2048]{1,0:T(8,128)S(1)}, u32[]{:S(2)}, u32[]{:S(2)}) collective-permute-start(f32[256,2048]{1,0:T(8,128)} %add.43), channel_id=1, source_target_pairs={{0,4},{2,6},{4,0},{6,2},{1,5},{3,7},{5,1},{7,3}} | collective-permute-start | bytes 6291464 | tf_op jit(solution)/shard_map/ppermute | solution.py:239
  178.0 0.2 collective-permute-start.9
  178.2 0.2 collective-permute-done.11
  178.4 0.4 collective-permute-start.10
  178.7 3.4 %add.47 = f32[256,2048]{1,0:T(8,128)} add(f32[256,2048]{1,0:T(8,128)} %get-tuple-element.44, f32[256,2048]{1,0:T(8,128)S(1)} %collective-permute-done.11) | non-fusion elementwise | flops 524288 | bytes 6291456 | tf_op jit(solution)/shard_map/add | solution.py:288
  182.2 1.6 add.44
  183.8 40.7 %collective-permute-done.19 = f32[256,2048]{1,0:T(8,128)S(1)} collective-permute-done((f32[256,2048]{1,0:T(8,128)}, f32[256,2048]{1,0:T(8,128)S(1)}, u32[]{:S(2)}, u32[]{:S(2)}) %collective-permute-start.19) | collective-permute-done | bytes 2097184 | tf_op jit(solution)/shard_map/ppermute | solution.py:239
  224.5 2.0 fusion
  226.5 2.0 fusion.1
  228.5 1.7 collective-permute-start.18
  230.2 1.0 collective-permute-done.12.refs_4_
  231.3 34.1 %shard_map.75 = (f32[256,2048]{1,0:T(8,128)}, f32[256,2048]{1,0:T(8,128)}, f32[256,2048]{1,0:T(8,128)}, f32[256,2048]{1,0:T(8,128)}) custom-call(s32[4,8,128]{2,1,0:T(8,128)} %get-tuple-element.29.refs_0_, s32[4,8,128]{2,1,0:T(8,128)} %get-tuple-element.30.refs_1_, s32[8,8,256]{2,1,0:T(8,128)} %get-tuple-element.28.refs_2_.pos_ref, bf16[256,2048]{1,0:T(8,128)(2,1)} %refs_3_, ...), custom_call_target="tpu_custom_call" | custom-call | flops 8858370048 | bytes 77594624 | tf_op jit(solution)/shard_map/pallas_call | solution.py:262
  265.4 0.5 collective-permute-start.17
  265.9 0.3 collective-permute-start.14
  266.2 3.6 %collective-permute-start.16 = (f32[256,2048]{1,0:T(8,128)}, f32[256,2048]{1,0:T(8,128)S(1)}, u32[]{:S(2)}, u32[]{:S(2)}) collective-permute-start(f32[256,2048]{1,0:T(8,128)} %fusion.1), channel_id=1, source_target_pairs={{0,4},{2,6},{4,0},{6,2},{1,5},{3,7},{5,1},{7,3}} | collective-permute-start | bytes 6291464 | tf_op jit(solution)/shard_map/ppermute | solution.py:239
  269.8 7.5 %collective-permute-done.18 = f32[256,2048]{1,0:T(8,128)} collective-permute-done((f32[256,2048]{1,0:T(8,128)}, f32[256,2048]{1,0:T(8,128)}, u32[]{:S(2)}, u32[]{:S(2)}) %collective-permute-start.18) | collective-permute-done | bytes 2097184 | tf_op jit(solution)/shard_map/ppermute | solution.py:239
  277.3 1.7 collective-permute-done.20
  279.1 3.7 %add_convert_fusion.mb_ref = bf16[256,2048]{1,0:T(8,128)(2,1)S(1)} fusion(f32[256,2048]{1,0:T(8,128)} %collective-permute-done.20, f32[256,2048]{1,0:T(8,128)} %collective-permute-done.18, f32[256,2048]{1,0:T(8,128)} %get-tuple-element.49, f32[256,2048]{1,0:T(8,128)S(1)} %collective-permute-done.17), kind=kLoop, calls=%fused_computation | loop fusion | flops 2097152 | bytes 9437184 | tf_op jit(solution)/shard_map/convert_element_type | solution.py:304
  282.8 0.0 collective-permute-start.22
  282.9 40.3 %collective-permute-done.14 = f32[256,2048]{1,0:T(8,128)S(1)} collective-permute-done((f32[256,2048]{1,0:T(8,128)}, f32[256,2048]{1,0:T(8,128)S(1)}, u32[]{:S(2)}, u32[]{:S(2)}) %collective-permute-start.14) | collective-permute-done | bytes 2097184 | tf_op jit(solution)/shard_map/ppermute | solution.py:239
  323.2 0.0 copy-start.14
  323.2 0.9 add_convert_fusion.1.ma_ref
  324.1 0.0 collective-permute-start.21
  324.2 1.0 copy.11.g_ref
  325.1 1.8 collective-permute-done.21.oa_ref
  326.9 5.6 %combine.1 = bf16[256,2048]{1,0:T(8,128)(2,1)} custom-call(s32[8,8,256]{2,1,0:T(8,128)} %get-tuple-element.28.refs_2_.pos_ref, s32[2,256]{1,0:T(2,128)} %bitcast.5, f32[256,2]{1,0:T(8,128)} %copy.11.g_ref, bf16[256,2048]{1,0:T(8,128)(2,1)} %copy-done.1, bf16[256,2048]{1,0:T(8,128)(2,1)} %copy-done, bf16[256,2048]{1,0:T(8,128)(2,1)} %collective-permute-done.21.oa_ref, ...), custom_call_target="tpu_custom_call" | custom-call | tf_op jit(solution)/shard_map/combine/pallas_call | solution.py:305
  (44 shorter events, 0.1 us)
Async XLA Ops:
  14.6 24.9 %collective-permute-start.1 = (bf16[256,2048]{1,0:T(8,128)(2,1)}, bf16[256,2048]{1,0:T(8,128)(2,1)S(1)}, u32[]{:S(2)}, u32[]{:S(2)}) collective-permute-start(bf16[256,2048]{1,0:T(8,128)(2,1)} %refs_3_), channel_id=1, source_target_pairs={{0,6},{2,4},{4,2},{6,0},{1,7},{3,5},{5,3},{7,1}} | collective-permute-start | bytes 3145736 | tf_op jit(solution)/shard_map/ppermute | solution.py:239
  39.5 1.0 copy-start.11
  40.5 2.9 collective-permute-start.2
  43.4 1.0 copy-start.12
  75.8 10.4 %collective-permute-start.4 = (f32[256,2048]{1,0:T(8,128)}, f32[256,2048]{1,0:T(8,128)S(1)}, u32[]{:S(2)}, u32[]{:S(2)}) collective-permute-start(f32[256,2048]{1,0:T(8,128)} %get-tuple-element.35), channel_id=1, source_target_pairs={{0,1},{1,0},{2,3},{3,2},{4,5},{5,4},{6,7},{7,6}} | collective-permute-start | bytes 6291464 | tf_op jit(solution)/shard_map/ppermute | solution.py:236
  82.2 7.4 %collective-permute-start.3 = (f32[256,2048]{1,0:T(8,128)}, f32[256,2048]{1,0:T(8,128)S(1)}, u32[]{:S(2)}, u32[]{:S(2)}) collective-permute-start(f32[256,2048]{1,0:T(8,128)} %get-tuple-element.33), channel_id=1, source_target_pairs={{0,1},{1,0},{2,3},{3,2},{4,5},{5,4},{6,7},{7,6}} | collective-permute-start | bytes 6291464 | tf_op jit(solution)/shard_map/ppermute | solution.py:236
  82.2 25.8 %collective-permute-start.6 = (bf16[256,2048]{1,0:T(8,128)(2,1)}, bf16[256,2048]{1,0:T(8,128)(2,1)S(1)}, u32[]{:S(2)}, u32[]{:S(2)}) collective-permute-start(bf16[256,2048]{1,0:T(8,128)(2,1)} %refs_3_), channel_id=1, source_target_pairs={{0,4},{2,6},{4,0},{6,2},{1,5},{3,7},{5,1},{7,3}} | collective-permute-start | bytes 3145736 | tf_op jit(solution)/shard_map/ppermute | solution.py:239
  82.2 26.8 %collective-permute-start = (bf16[256,2048]{1,0:T(8,128)(2,1)}, bf16[256,2048]{1,0:T(8,128)(2,1)S(1)}, u32[]{:S(2)}, u32[]{:S(2)}) collective-permute-start(bf16[256,2048]{1,0:T(8,128)(2,1)} %refs_3_), channel_id=1, source_target_pairs={{0,2},{2,0},{4,6},{6,4},{1,3},{3,1},{5,7},{7,5}} | collective-permute-start | bytes 3145736 | tf_op jit(solution)/shard_map/ppermute | solution.py:239
  86.2 3.4 %copy-start.3 = (f32[256,2048]{1,0:T(8,128)S(1)}, f32[256,2048]{1,0:T(8,128)}, u32[]{:S(2)}) copy-start(f32[256,2048]{1,0:T(8,128)} %get-tuple-element.32) | copy-start | bytes 6291460
  108.0 1.0 copy-start.8
  109.0 2.7 collective-permute-start.7
  109.0 2.7 copy-start.9
  109.0 4.3 %collective-permute-start.5 = (bf16[256,2048]{1,0:T(8,128)(2,1)S(1)}, bf16[256,2048]{1,0:T(8,128)(2,1)}, u32[]{:S(2)}, u32[]{:S(2)}) collective-permute-start(bf16[256,2048]{1,0:T(8,128)(2,1)S(1)} %collective-permute-done.refs_3_), channel_id=1, source_target_pairs={{0,1},{1,0},{2,3},{3,2},{4,5},{5,4},{6,7},{7,6}} | collective-permute-start | bytes 3145736 | tf_op jit(solution)/shard_map/ppermute | solution.py:236
  111.7 1.0 copy-start.10
  166.2 12.1 %collective-permute-start.11 = (f32[256,2048]{1,0:T(8,128)}, f32[256,2048]{1,0:T(8,128)S(1)}, u32[]{:S(2)}, u32[]{:S(2)}) collective-permute-start(f32[256,2048]{1,0:T(8,128)} %get-tuple-element.45), channel_id=1, source_target_pairs={{0,1},{1,0},{2,3},{3,2},{4,5},{5,4},{6,7},{7,6}} | collective-permute-start | bytes 6291464 | tf_op jit(solution)/shard_map/ppermute | solution.py:236
  174.4 7.8 %collective-permute-start.8 = (f32[256,2048]{1,0:T(8,128)}, f32[256,2048]{1,0:T(8,128)S(1)}, u32[]{:S(2)}, u32[]{:S(2)}) collective-permute-start(f32[256,2048]{1,0:T(8,128)} %get-tuple-element.39), channel_id=1, source_target_pairs={{0,1},{1,0},{2,3},{3,2},{4,5},{5,4},{6,7},{7,6}} | collective-permute-start | bytes 6291464 | tf_op jit(solution)/shard_map/ppermute | solution.py:236
  174.4 50.1 %collective-permute-start.19 = (f32[256,2048]{1,0:T(8,128)}, f32[256,2048]{1,0:T(8,128)S(1)}, u32[]{:S(2)}, u32[]{:S(2)}) collective-permute-start(f32[256,2048]{1,0:T(8,128)} %add.43), channel_id=1, source_target_pairs={{0,4},{2,6},{4,0},{6,2},{1,5},{3,7},{5,1},{7,3}} | collective-permute-start | bytes 6291464 | tf_op jit(solution)/shard_map/ppermute | solution.py:239
  178.0 46.5 %collective-permute-start.9 = (f32[256,2048]{1,0:T(8,128)}, f32[256,2048]{1,0:T(8,128)S(1)}, u32[]{:S(2)}, u32[]{:S(2)}) collective-permute-start(f32[256,2048]{1,0:T(8,128)} %get-tuple-element.41), channel_id=1, source_target_pairs={{0,1},{1,0},{2,3},{3,2},{4,5},{5,4},{6,7},{7,6}} | collective-permute-start | bytes 6291464 | tf_op jit(solution)/shard_map/ppermute | solution.py:236
  178.2 48.3 %collective-permute-start.15 = (f32[256,2048]{1,0:T(8,128)}, f32[256,2048]{1,0:T(8,128)S(1)}, u32[]{:S(2)}, u32[]{:S(2)}) collective-permute-start(f32[256,2048]{1,0:T(8,128)} %add.42), channel_id=1, source_target_pairs={{0,2},{2,0},{4,6},{6,4},{1,3},{3,1},{5,7},{7,5}} | collective-permute-start | bytes 6291464 | tf_op jit(solution)/shard_map/ppermute | solution.py:239
  178.4 48.1 %collective-permute-start.10 = (f32[256,2048]{1,0:T(8,128)}, f32[256,2048]{1,0:T(8,128)S(1)}, u32[]{:S(2)}, u32[]{:S(2)}) collective-permute-start(f32[256,2048]{1,0:T(8,128)} %get-tuple-element.43), channel_id=1, source_target_pairs={{0,1},{1,0},{2,3},{3,2},{4,5},{5,4},{6,7},{7,6}} | collective-permute-start | bytes 6291464 | tf_op jit(solution)/shard_map/ppermute | solution.py:236
  178.7 3.5 %copy-start.2 = (f32[256,2048]{1,0:T(8,128)S(1)}, f32[256,2048]{1,0:T(8,128)}, u32[]{:S(2)}) copy-start(f32[256,2048]{1,0:T(8,128)} %get-tuple-element.38) | copy-start | bytes 6291460
  182.2 42.3 %copy-start.5 = (f32[256,2048]{1,0:T(8,128)S(1)}, f32[256,2048]{1,0:T(8,128)}, u32[]{:S(2)}) copy-start(f32[256,2048]{1,0:T(8,128)} %get-tuple-element.40) | copy-start | bytes 6291460
  224.5 2.0 copy-start.4
  226.5 2.0 copy-start.7
  228.5 2.8 collective-permute-start.12
  228.5 48.8 %collective-permute-start.18 = (f32[256,2048]{1,0:T(8,128)}, f32[256,2048]{1,0:T(8,128)}, u32[]{:S(2)}, u32[]{:S(2)}) collective-permute-start(f32[256,2048]{1,0:T(8,128)} %add.47), channel_id=1, source_target_pairs={{0,4},{2,6},{4,0},{6,2},{1,5},{3,7},{5,1},{7,3}} | collective-permute-start | bytes 6291464 | tf_op jit(solution)/shard_map/ppermute | solution.py:239
  230.2 48.8 %collective-permute-start.20 = (f32[256,2048]{1,0:T(8,128)}, f32[256,2048]{1,0:T(8,128)}, u32[]{:S(2)}, u32[]{:S(2)}) collective-permute-start(f32[256,2048]{1,0:T(8,128)} %fusion), channel_id=1, source_target_pairs={{0,2},{2,0},{4,6},{6,4},{1,3},{3,1},{5,7},{7,5}} | collective-permute-start | bytes 6291464 | tf_op jit(solution)/shard_map/ppermute | solution.py:239
  265.4 13.7 %collective-permute-start.17 = (f32[256,2048]{1,0:T(8,128)}, f32[256,2048]{1,0:T(8,128)S(1)}, u32[]{:S(2)}, u32[]{:S(2)}) collective-permute-start(f32[256,2048]{1,0:T(8,128)} %get-tuple-element.50), channel_id=1, source_target_pairs={{0,1},{1,0},{2,3},{3,2},{4,5},{5,4},{6,7},{7,6}} | collective-permute-start | bytes 6291464 | tf_op jit(solution)/shard_map/ppermute | solution.py:236
  265.9 57.3 %collective-permute-start.14 = (f32[256,2048]{1,0:T(8,128)}, f32[256,2048]{1,0:T(8,128)S(1)}, u32[]{:S(2)}, u32[]{:S(2)}) collective-permute-start(f32[256,2048]{1,0:T(8,128)} %add.44), channel_id=1, source_target_pairs={{0,2},{2,0},{4,6},{6,4},{1,3},{3,1},{5,7},{7,5}} | collective-permute-start | bytes 6291464 | tf_op jit(solution)/shard_map/ppermute | solution.py:239
  266.2 56.9 %collective-permute-start.16 = (f32[256,2048]{1,0:T(8,128)}, f32[256,2048]{1,0:T(8,128)S(1)}, u32[]{:S(2)}, u32[]{:S(2)}) collective-permute-start(f32[256,2048]{1,0:T(8,128)} %fusion.1), channel_id=1, source_target_pairs={{0,4},{2,6},{4,0},{6,2},{1,5},{3,7},{5,1},{7,3}} | collective-permute-start | bytes 6291464 | tf_op jit(solution)/shard_map/ppermute | solution.py:239
  277.3 45.8 %collective-permute-start.13 = (f32[256,2048]{1,0:T(8,128)}, f32[256,2048]{1,0:T(8,128)S(1)}, u32[]{:S(2)}, u32[]{:S(2)}) collective-permute-start(f32[256,2048]{1,0:T(8,128)} %get-tuple-element.48), channel_id=1, source_target_pairs={{0,1},{1,0},{2,3},{3,2},{4,5},{5,4},{6,7},{7,6}} | collective-permute-start | bytes 6291464 | tf_op jit(solution)/shard_map/ppermute | solution.py:236
  279.1 44.1 %copy-start.6 = (f32[256,2048]{1,0:T(8,128)S(1)}, f32[256,2048]{1,0:T(8,128)}, u32[]{:S(2)}) copy-start(f32[256,2048]{1,0:T(8,128)} %get-tuple-element.47) | copy-start | bytes 6291460
  282.8 41.3 %copy-start = (bf16[256,2048]{1,0:T(8,128)(2,1)}, bf16[256,2048]{1,0:T(8,128)(2,1)S(1)}, u32[]{:S(2)}) copy-start(bf16[256,2048]{1,0:T(8,128)(2,1)S(1)} %add_convert_fusion.mb_ref) | copy-start | bytes 3145732
  282.8 42.3 %collective-permute-start.22 = (bf16[256,2048]{1,0:T(8,128)(2,1)S(1)}, bf16[256,2048]{1,0:T(8,128)(2,1)S(1)}, u32[]{:S(2)}, u32[]{:S(2)}) collective-permute-start(bf16[256,2048]{1,0:T(8,128)(2,1)S(1)} %add_convert_fusion.mb_ref), channel_id=1, source_target_pairs={{0,1},{1,0},{2,3},{3,2},{4,5},{5,4},{6,7},{7,6}} | collective-permute-start | bytes 3145736 | tf_op jit(solution)/shard_map/ppermute | solution.py:236
  323.2 1.0 copy-start.14
  324.1 2.8 copy-start.1
  324.1 2.8 collective-permute-start.21
  325.1 1.8 copy-start.13

commit v2 on v0

v2 whole, which is shorter than its diff:
```python
import functools

import jax
import jax.numpy as jnp
from jax import lax
from jax.experimental import pallas as pl
from jax.experimental.pallas import tpu as pltpu
from jax.sharding import PartitionSpec as P


F32 = jnp.float32
BF16 = jnp.bfloat16
VMEM_BYTES = 67_043_328


def _route_kernel(chips, idx_ref, g_ref, cap_ref, pos_ref, off_ref, cnt_ref, mine_ref, ids_all, send_sem, recv_sem):
    core, me = lax.axis_index("ep"), lax.axis_index("tp")
    blocks, top, t = ids_all.shape
    e_all = cap_ref.shape[0]
    here = core * chips + me
    peers = [
        (k, {"ep": jnp.bitwise_xor(core, k // chips), "tp": jnp.bitwise_xor(me, k % chips)}) for k in range(1, blocks)
    ]
    barrier = pltpu.get_barrier_semaphore()
    for _, peer in peers:
        pl.semaphore_signal(barrier, inc=1, device_id=peer, device_id_type=pl.DeviceIdType.MESH)
    pl.semaphore_wait(barrier, blocks - 1)
    copies = [
        pltpu.make_async_remote_copy(
            src_ref=idx_ref,
            dst_ref=ids_all.at[here],
            send_sem=send_sem.at[k],
            recv_sem=recv_sem.at[k],
            device_id=peer,
            device_id_type=pl.DeviceIdType.MESH,
        )
        for k, peer in peers
    ]
    for c in copies:
        c.start()
    ids_all[pl.ds(here, 1)] = idx_ref[...][None]
    before = (
        lax.broadcasted_iota(jnp.int32, (t, t), 0) < lax.broadcasted_iota(jnp.int32, (t, t), 1)
    ).astype(F32).astype(BF16)
    ids = lax.broadcasted_iota(jnp.int32, (e_all, t), 0)
    cap = jnp.broadcast_to(cap_ref[...], (e_all, t))
    for c in copies:
        c.wait()

    for b in range(blocks):
        hit = (ids_all[b, 0:1, :] == ids) | (ids_all[b, 1:2, :] == ids)
        one = hit.astype(F32)
        rank = jnp.dot(one.astype(BF16), before, preferred_element_type=F32).astype(jnp.int32)
        total = jnp.sum(one, axis=1, keepdims=True).astype(jnp.int32)
        count = jnp.minimum(jnp.broadcast_to(total, (e_all, t)), cap)
        first = jnp.zeros_like(count)
        for e in range(e_all - 1):
            first = first + jnp.where(ids > e, jnp.broadcast_to(count[e : e + 1, :], count.shape), 0)
        off_ref[b] = first[:, :128]
        cnt_ref[b] = count[:, :128]
        pos_ref[b] = jnp.where(hit & (rank < cap), first + rank, -1)
    pos = pos_ref[here]
    lines = [
        jnp.max(jnp.where(idx_ref[j : j + 1, :] == ids, pos, -1), axis=0, keepdims=True).astype(F32) for j in range(top)
    ]
    lines += [g_ref[j : j + 1, :] for j in range(top)]
    table = jnp.concatenate(lines + [jnp.zeros((8 - 2 * top, t), F32)], axis=0)
    mine_ref[...] = jnp.transpose(table)


def _expert_kernel(
    turns, sizes, cut, off_ref, cnt_ref, pos_ref, xm_hbm, xo_hbm, w1_hbm, w3_hbm, w2_hbm, *refs
):
    outs = refs[:4]
    acc, xbuf, w1a, w3a, w1b, w3b, w2s, wsem, osem, xsem = refs[4:]
    e_loc, d, ff = w1_hbm.shape
    _, rows, _ = acc.shape
    t = xbuf.shape[1]
    half_d, half = d // 2, rows // 2
    core, me = lax.axis_index("ep"), lax.axis_index("tp")
    chips = pos_ref.shape[0] // 2
    blocks = []
    for c in (core, 1 - core):
        turn = jnp.where(c == 0, turns[0], turns[1])
        blocks.append(c * chips + jnp.bitwise_xor(me, turn))

    def chunk(k, e):
        if k == 0:
            return [
                pltpu.make_async_copy(w1_hbm.at[e, :, pl.ds(0, cut)], w1a, wsem.at[0]),
                pltpu.make_async_copy(w3_hbm.at[e, :, pl.ds(0, cut)], w3a, wsem.at[1]),
            ]
        if k == 1:
            return [
                pltpu.make_async_copy(w1_hbm.at[e, :, pl.ds(cut, ff - cut)], w1b, wsem.at[2]),
                pltpu.make_async_copy(w3_hbm.at[e, :, pl.ds(cut, ff - cut)], w3b, wsem.at[3]),
            ]
        h = k - 2
        return [pltpu.make_async_copy(w2_hbm.at[e, :, pl.ds(h * half_d, half_d)], w2s.at[h], wsem.at[2 + k])]

    def start(k, e):
        for c in chunk(k, e):
            c.start()

    def finish(k, e):
        for c in chunk(k, e):
            c.wait()

    def following(k, e):
        @pl.when(e + 1 < e_loc)
        def _():
            start(k, e + 1)

    def out_copies(h):
        cols = pl.ds(h * half_d, half_d)
        return [
            pltpu.make_async_copy(
                acc.at[1 - i // 2, pl.ds((i % 2) * half, half), cols], outs[i].at[:, cols], osem.at[h, i]
            )
            for i in range(4)
        ]

    tokens = [
        pltpu.make_async_copy(xm_hbm, xbuf.at[0], xsem.at[0]),
        pltpu.make_async_copy(xo_hbm, xbuf.at[1], xsem.at[1]),
    ]
    for c in tokens:
        c.start()
    for k in range(4):
        start(k, 0)
    acc[...] = jnp.zeros_like(acc)
    for c in tokens:
        c.wait()

    def step(e, carry):
        expert = core * e_loc + e
        offs = [off_ref[b, expert, 0] for b in blocks]
        cnts = [cnt_ref[b, expert, 0] for b in blocks]
        need = functools.reduce(jnp.maximum, [jnp.where(k > 0, o - o // 8 * 8 + k, 0) for o, k in zip(offs, cnts)])

        def last(k):
            if k == 0:

                @pl.when(e == e_loc - 1)
                def _():
                    for c in out_copies(0):
                        c.start()

        def run(m):
            bases = [pl.multiple_of(jnp.minimum(o // 8 * 8, rows - m), 8) for o in offs]
            parts = []
            for s in range(2):
                row = lax.broadcasted_iota(jnp.int32, (m, t), 0) + bases[s]
                hit = (row == pos_ref[blocks[s], pl.ds(expert, 1), :]).astype(F32).astype(BF16)
                parts.append(jnp.dot(hit, xbuf[s], preferred_element_type=F32))
            xs = jnp.concatenate(parts, axis=0).astype(BF16)
            hs = []
            for k, (wa, wb) in enumerate(((w1a, w3a), (w1b, w3b))):
                finish(k, e)
                h1 = jnp.dot(xs, wa[...], preferred_element_type=F32)
                h3 = jnp.dot(xs, wb[...], preferred_element_type=F32)
                hs.append((jax.nn.silu(h1) * h3).astype(BF16))
                following(k, e)
            h = jnp.concatenate(hs, axis=1)
            for k in range(2):
                finish(2 + k, e)
                p = jnp.dot(h, w2s[k], preferred_element_type=F32)
                for s in range(2):
                    acc[s, pl.ds(bases[s], m), k * half_d : (k + 1) * half_d] += p[s * m : (s + 1) * m]
                following(2 + k, e)
                last(k)

        @pl.when(need == 0)
        def _():
            for k in range(4):
                finish(k, e)
                following(k, e)
                last(k - 2)

        lo = 0
        for m in sizes:
            pl.when((need > lo) & (need <= m))(functools.partial(run, m))
            lo = m
        return carry

    lax.fori_loop(0, e_loc, step, 0)
    for c in out_copies(1):
        c.start()
    for c in out_copies(0) + out_copies(1):
        c.wait()


def _combine_kernel(mine_ref, s0_ref, s1_ref, f0_ref, f1_ref, out_ref, hit):
    top, t, rows = hit.shape

    @pl.when(pl.program_id(0) == 0)
    def _():
        row = lax.broadcasted_iota(jnp.int32, (t, rows), 1)
        for j in range(top):
            hit[j] = (row == mine_ref[:, j : j + 1].astype(jnp.int32)).astype(F32).astype(BF16)

    y = jnp.concatenate([s0_ref[...] + f0_ref[...], s1_ref[...] + f1_ref[...]], axis=0).astype(BF16)
    total = None
    for j in range(top):
        part = jnp.dot(hit[j], y, preferred_element_type=F32) * mine_ref[:, top + j : top + j + 1]
        total = part if total is None else total + part
    out_ref[...] = total.astype(out_ref.dtype)


def solution(mesh):
    chips = mesh.shape["tp"]
    vmem = pl.BlockSpec(memory_space=pltpu.VMEM)
    anym = pl.BlockSpec(memory_space=pl.ANY)
    smem = pl.BlockSpec(memory_space=pltpu.SMEM)

    def layer(x, idx, g, cap, w1, w3, w2):
        t_loc, d = x.shape
        top = idx.shape[1]
        e_all = cap.shape[0]
        e_loc, _, ff = w1.shape
        c = (5 * top * t_loc // (2 * e_all) + 7) // 8 * 8
        rows = top * t_loc
        half = rows // 2
        cut = 512
        blocks = 2 * chips

        def swap(a):
            return lax.ppermute(a, "ep", [(0, 1), (1, 0)])

        def shift(a, turns):
            pairs = [(2 * k + i, 2 * (k ^ turns[i]) + i) for k in range(chips) for i in range(2)]
            return lax.ppermute(a, ("tp", "ep"), pairs)

        def after(a, *first):
            return lax.optimization_barrier((a, *first))[0]

        x_d = shift(x, (3, 3))
        pos, off, cnt, mine = pl.pallas_call(
            functools.partial(_route_kernel, chips),
            out_shape=[
                jax.ShapeDtypeStruct((blocks, e_all, t_loc), jnp.int32),
                jax.ShapeDtypeStruct((blocks, e_all, 128), jnp.int32),
                jax.ShapeDtypeStruct((blocks, e_all, 128), jnp.int32),
                jax.ShapeDtypeStruct((t_loc, 8), F32),
            ],
            in_specs=[vmem] * 3,
            out_specs=[vmem] * 4,
            scratch_shapes=[
                pltpu.VMEM((blocks, top, t_loc), jnp.int32),
                pltpu.SemaphoreType.DMA((blocks,)),
                pltpu.SemaphoreType.DMA((blocks,)),
            ],
            compiler_params=pltpu.CompilerParams(collective_id=0, has_side_effects=True, vmem_limit_bytes=VMEM_BYTES),
            name="route",
        )(idx.T, g.T, cap[:, None])

        sizes = (64, (c + 7 + 7) // 8 * 8)

        def stage(turns, mine, other, sizes=sizes):
            return pl.pallas_call(
                functools.partial(_expert_kernel, turns, sizes, cut),
                out_shape=[jax.ShapeDtypeStruct((half, d), F32)] * 4,
                in_specs=[smem, smem, vmem] + [anym] * 5,
                out_specs=[anym] * 4,
                scratch_shapes=[
                    pltpu.VMEM((2, rows, d), F32),
                    pltpu.VMEM((2, t_loc, d), BF16),
                    pltpu.VMEM((d, cut), BF16),
                    pltpu.VMEM((d, cut), BF16),
                    pltpu.VMEM((d, ff - cut), BF16),
                    pltpu.VMEM((d, ff - cut), BF16),
                    pltpu.VMEM((2, ff, d // 2), BF16),
                    pltpu.SemaphoreType.DMA((6,)),
                    pltpu.SemaphoreType.DMA((2, 4)),
                    pltpu.SemaphoreType.DMA((2,)),
                ],
                compiler_params=pltpu.CompilerParams(vmem_limit_bytes=VMEM_BYTES),
                cost_estimate=pl.CostEstimate(
                    flops=6 * rows * d * ff, bytes_accessed=6 * e_loc * d * ff + 8 * rows * d, transcendentals=0
                ),
            )(off, cnt, pos, mine, other, w1, w3, w2)

        def merge(parts):
            return [parts[2 + q] + swap(parts[q]) for q in range(2)]

        out, back = (1, 2), (2, 1)
        x_n, x_f = shift(x, out), shift(x, back)
        diag = merge(stage((3, 3), x_d, swap(x_d)))
        via = [shift(a, out) for a in diag]
        x_n, x_f = after(x_n, *diag), after(x_f, *diag)
        near = merge(stage(out, x_n, swap(x_n)))
        near = [shift(a, out) for a in near]
        part = stage(back, x_f, swap(x_f))
        far = merge(part)
        far = [a + b for a, b in zip(far, via)]
        x_o = after(x, *far)
        far = [shift(a, back) for a in far]
        own = merge(stage((0, 0), x_o, swap(x_o), sizes[-1:]))
        sums = [a + b for a, b in zip(own, near)]
        width = d // 4
        return pl.pallas_call(
            _combine_kernel,
            out_shape=jax.ShapeDtypeStruct((t_loc, d), BF16),
            grid=(4,),
            in_specs=[pl.BlockSpec((t_loc, 8), lambda i: (0, 0))] + [pl.BlockSpec((half, width), lambda i: (0, i))] * 4,
            out_specs=pl.BlockSpec((t_loc, width), lambda i: (0, i)),
            scratch_shapes=[pltpu.VMEM((top, t_loc, rows), BF16)],
            name="combine",
        )(mine, *sums, *far)

    rows = P(("ep", "tp"), None)
    return jax.shard_map(
        layer,
        mesh=mesh,
        in_specs=(rows, rows, rows, P(None), P("ep", None, "tp"), P("ep", None, "tp"), P("ep", "tp", None)),
        out_specs=rows,
        check_vma=False,
    )
```

time: 1800 us -> 309 us (0.17)
  blocking collectives: 1390 us -> 0 us
  Pallas kernels: 0 us -> 145 us
  matrix products: 128 us -> 0 us
  waiting for transfers between devices: 187 us -> 97.5 us
  local copies, waits for them, and re-layouts: 51.6 us -> 3.71 us
  starting transfers between devices: 0.01 us -> 37.8 us
    unnamed x1 -> x0, blocking collectives: 1380 us -> none
    all_gather x1 -> x0, waiting for transfers between devices: 187 us -> none  [local(): full = lax.all_gather(recv, 'tp', axis=0, tiled=True)]
    pallas_call x0 -> x6, Pallas kernels: none -> 145 us  [the longest x4 132 us: stage(): pl.pallas_call(functools.partial(_expert_kernel, turns, sizes, cut), out_...]
    dot_general x3 -> x0, matrix products: 128 us -> none  [the longest x1 46.7 us: local(): jnp.einsum('secd,edf->secf', full, w1, preferred_element_type=jnp.float32)]
    ppermute x0 -> x21, waiting for transfers between devices: none -> 97.5 us  [the longest x9 91.1 us: shift(): return lax.ppermute(a, ('tp', 'ep'), pairs)]
    ppermute x0 -> x21, starting transfers between devices: none -> 37.8 us  [the longest x12 19.1 us: swap(): return lax.ppermute(a, 'ep', [(0, 1), (1, 0)])]
    add x0 -> x8, other arithmetic: none -> 24 us  [the longest x2 9.29 us: layer(): far = [a + b for a, b in zip(far, via)]]
    scatter x1 -> x0, local copies, waits for them, and re-layouts: 23.2 us -> none  [local(): jnp.zeros((e_all * c + 1, d), x.dtype).at[sid].set(x[tok])[:e_all * c]]
  transfers between devices with their start and end apart: 1 -> 21, of which waited for: 1 -> 7; matrix products, arithmetic and copies ran while one was open for 0% -> 8% of each run, Pallas kernels for 0% -> 35%
where the time goes in v2:
time: 309 us; the launch traced here: 308 us
  Pallas kernels  145 us (47%)
  waiting for transfers between devices  97.5 us (32%)
  starting transfers between devices  37.8 us (12%)
  other arithmetic  24 us (8%)
  local copies, waits for them, and re-layouts  3.71 us (1%)
    pallas_call x4, Pallas kernels, stage(): pl.pallas_call(functools.partial(_expert_kernel, turns, sizes, cut), out_...  132 us
    ppermute x9, waiting for transfers between devices, shift(): return lax.ppermute(a, ('tp', 'ep'), pairs)  91.1 us
    ppermute x12, starting transfers between devices, swap(): return lax.ppermute(a, 'ep', [(0, 1), (1, 0)])  19.1 us
    ppermute x9, starting transfers between devices, shift(): return lax.ppermute(a, ('tp', 'ep'), pairs)  18.8 us
    add x2, other arithmetic, layer(): far = [a + b for a, b in zip(far, via)]  9.29 us
    add x4, other arithmetic, merge(): return [parts[2 + q] + swap(parts[q]) for q in range(2)]  9.27 us
    pallas_call x1, Pallas kernels, layer(): pl.pallas_call(functools.partial(_route_kernel, chips), out_shape=[jax.Sh...  6.79 us
    ppermute x12, waiting for transfers between devices, swap(): return lax.ppermute(a, 'ep', [(0, 1), (1, 0)])  6.35 us
  transfers between devices with their start and end apart: 21, of which 7 were waited for; matrix products, arithmetic and copies ran while one was open for 8% of the time, Pallas kernels for 35%

profile of v2, /device:TPU:0, one launch (start us, length us, event | category | flops | bytes accessed | tf_op | source)
XLA Modules:
  0.0 308.0 jit_solution(4513852716793279150)
XLA Ops:
  0.0 4.3 %collective-permute-start.1 = (bf16[256,2048]{1,0:T(8,128)(2,1)}, bf16[256,2048]{1,0:T(8,128)(2,1)}, u32[]{:S(2)}, u32[]{:S(2)}) collective-permute-start(bf16[256,2048]{1,0:T(8,128)(2,1)} %xm_hbm), channel_id=1, source_target_pairs={{0,6},{1,7},{2,4},{3,5},{4,2},{5,3},{6,0},{7,1}} | collective-permute-start | bytes 3145736 | tf_op jit(solution)/shard_map/ppermute | solution.py:232
  4.3 23.5 %collective-permute-done.1.xm_hbm = bf16[256,2048]{1,0:T(8,128)(2,1)} collective-permute-done((bf16[256,2048]{1,0:T(8,128)(2,1)}, bf16[256,2048]{1,0:T(8,128)(2,1)}, u32[]{:S(2)}, u32[]{:S(2)}) %collective-permute-start.1) | collective-permute-done | bytes 1048608 | tf_op jit(solution)/shard_map/ppermute | solution.py:232
  27.7 0.0 collective-permute-start.2
  27.7 1.3 copy.8.cap_ref
  29.1 6.8 %route.1 = (s32[8,8,256]{2,1,0:T(8,128)}, s32[8,8,128]{2,1,0:T(8,128)}, s32[8,8,128]{2,1,0:T(8,128)}, f32[256,8]{1,0:T(8,128)}) custom-call(s32[2,256]{1,0:T(2,128)} %bitcast.3, f32[2,256]{1,0:T(2,128)} %bitcast.4, s32[8,1]{1,0:T(8,128)} %copy.8.cap_ref), custom_call_target="tpu_custom_call" | custom-call | tf_op jit(solution)/shard_map/route/pallas_call | solution.py:238
  35.9 0.0 collective-permute-done.2.xo_hbm
  35.9 30.7 %shard_map.73 = (f32[256,2048]{1,0:T(8,128)}, f32[256,2048]{1,0:T(8,128)}, f32[256,2048]{1,0:T(8,128)}, f32[256,2048]{1,0:T(8,128)}) custom-call(s32[8,8,128]{2,1,0:T(8,128)} %get-tuple-element.29.off_ref, s32[8,8,128]{2,1,0:T(8,128)} %get-tuple-element.30.cnt_ref, s32[8,8,256]{2,1,0:T(8,128)} %get-tuple-element.31.pos_ref, ...), custom_call_target="tpu_custom_call" | custom-call | flops 8858370048 | bytes 77594624 | tf_op jit(solution)/shard_map/pallas_call | solution.py:260
  66.6 5.8 %collective-permute-start.3 = (f32[256,2048]{1,0:T(8,128)}, f32[256,2048]{1,0:T(8,128)S(1)}, u32[]{:S(2)}, u32[]{:S(2)}) collective-permute-start(f32[256,2048]{1,0:T(8,128)} %get-tuple-element.33), channel_id=1, source_target_pairs={{0,1},{1,0},{2,3},{3,2},{4,5},{5,4},{6,7},{7,6}} | collective-permute-start | bytes 6291464 | tf_op jit(solution)/shard_map/ppermute | solution.py:228
  72.3 0.0 collective-permute-start.4
  72.4 4.0 %collective-permute-done.3 = f32[256,2048]{1,0:T(8,128)S(1)} collective-permute-done((f32[256,2048]{1,0:T(8,128)}, f32[256,2048]{1,0:T(8,128)S(1)}, u32[]{:S(2)}, u32[]{:S(2)}) %collective-permute-start.3) | collective-permute-done | bytes 2097184 | tf_op jit(solution)/shard_map/ppermute | solution.py:228
  76.3 3.4 %add.36 = f32[256,2048]{1,0:T(8,128)} add(f32[256,2048]{1,0:T(8,128)} %get-tuple-element.32, f32[256,2048]{1,0:T(8,128)S(1)} %collective-permute-done.3) | non-fusion elementwise | flops 524288 | bytes 6291456 | tf_op jit(solution)/shard_map/add | solution.py:284
  79.8 1.6 add.37
  81.4 6.0 %collective-permute-done.xm_hbm = bf16[256,2048]{1,0:T(8,128)(2,1)S(1)} collective-permute-done((bf16[256,2048]{1,0:T(8,128)(2,1)}, bf16[256,2048]{1,0:T(8,128)(2,1)S(1)}, u32[]{:S(2)}, u32[]{:S(2)}) %collective-permute-start) | collective-permute-done | bytes 1048608 | tf_op jit(solution)/shard_map/ppermute | solution.py:232
  87.4 1.0 copy-done.9
  88.4 0.0 collective-permute-start.5
  88.4 1.3 collective-permute-start.12
  89.6 0.7 collective-permute-start.7
  90.4 0.8 collective-permute-done.5.xo_hbm
  91.2 28.0 %shard_map.74 = (f32[256,2048]{1,0:T(8,128)}, f32[256,2048]{1,0:T(8,128)}, f32[256,2048]{1,0:T(8,128)}, f32[256,2048]{1,0:T(8,128)}) custom-call(s32[8,8,128]{2,1,0:T(8,128)} %get-tuple-element.29.off_ref, s32[8,8,128]{2,1,0:T(8,128)} %get-tuple-element.30.cnt_ref, s32[8,8,256]{2,1,0:T(8,128)} %get-tuple-element.31.pos_ref, bf16[256,2048]{1,0:T(8,128)(2,1)} %copy-done.9, ...), custom_call_target="tpu_custom_call" | custom-call | flops 8858370048 | bytes 77594624 | tf_op jit(solution)/shard_map/pallas_call | solution.py:260
  119.1 9.2 %collective-permute-start.6 = (f32[256,2048]{1,0:T(8,128)}, f32[256,2048]{1,0:T(8,128)}, u32[]{:S(2)}, u32[]{:S(2)}) collective-permute-start(f32[256,2048]{1,0:T(8,128)} %get-tuple-element.38), channel_id=1, source_target_pairs={{0,1},{1,0},{2,3},{3,2},{4,5},{5,4},{6,7},{7,6}} | collective-permute-start | bytes 6291464 | tf_op jit(solution)/shard_map/ppermute | solution.py:228
  128.3 0.0 collective-permute-done.12.xm_hbm
  128.3 0.0 collective-permute-start.13
  128.3 1.3 collective-permute-start.9
  129.6 2.7 collective-permute-start.8
  132.3 1.6 collective-permute-done.13.xo_hbm
  133.9 33.0 %shard_map.76 = (f32[256,2048]{1,0:T(8,128)}, f32[256,2048]{1,0:T(8,128)}, f32[256,2048]{1,0:T(8,128)}, f32[256,2048]{1,0:T(8,128)}) custom-call(s32[8,8,128]{2,1,0:T(8,128)} %get-tuple-element.29.off_ref, s32[8,8,128]{2,1,0:T(8,128)} %get-tuple-element.30.cnt_ref, s32[8,8,256]{2,1,0:T(8,128)} %get-tuple-element.31.pos_ref, ...), custom_call_target="tpu_custom_call" | custom-call | flops 8858370048 | bytes 77594624 | tf_op jit(solution)/shard_map/pallas_call | solution.py:260
  166.9 0.8 collective-permute-start.14
  167.7 0.0 collective-permute-done.7
  167.7 0.0 collective-permute-done.6
  167.8 5.0 %add_add_fusion.3 = f32[256,2048]{1,0:T(8,128)} fusion(f32[256,2048]{1,0:T(8,128)} %collective-permute-done.7, f32[256,2048]{1,0:T(8,128)} %get-tuple-element.37, f32[256,2048]{1,0:T(8,128)} %collective-permute-done.6), kind=kLoop, calls=%fused_computation.3 | loop fusion | flops 1048576 | bytes 8388608 | tf_op jit(solution)/shard_map/add | solution.py:295
  172.8 0.0 collective-permute-done.9
  172.8 4.3 %add_add_fusion.2 = f32[256,2048]{1,0:T(8,128)} fusion(f32[256,2048]{1,0:T(8,128)} %collective-permute-done.9, f32[256,2048]{1,0:T(8,128)S(1)} %copy-done.4, f32[256,2048]{1,0:T(8,128)} %collective-permute-done.8), kind=kLoop, calls=%fused_computation.2 | loop fusion | flops 1048576 | bytes 8388608 | tf_op jit(solution)/shard_map/add | solution.py:295
  177.1 0.0 collective-permute-start.10
  177.1 0.5 collective-permute-start.17
  177.6 1.6 add.43
  179.2 7.8 %collective-permute-start.15 = (f32[256,2048]{1,0:T(8,128)}, f32[256,2048]{1,0:T(8,128)}, u32[]{:S(2)}, u32[]{:S(2)}) collective-permute-start(f32[256,2048]{1,0:T(8,128)} %add.43), channel_id=1, source_target_pairs={{0,2},{1,5},{2,0},{3,7},{4,6},{5,1},{6,4},{7,3}} | collective-permute-start | bytes 6291464 | tf_op jit(solution)/shard_map/ppermute | solution.py:232
  187.0 40.4 %shard_map.75 = (f32[256,2048]{1,0:T(8,128)}, f32[256,2048]{1,0:T(8,128)}, f32[256,2048]{1,0:T(8,128)}, f32[256,2048]{1,0:T(8,128)}) custom-call(s32[8,8,128]{2,1,0:T(8,128)} %get-tuple-element.29.off_ref, s32[8,8,128]{2,1,0:T(8,128)} %get-tuple-element.30.cnt_ref, s32[8,8,256]{2,1,0:T(8,128)} %get-tuple-element.31.pos_ref, bf16[256,2048]{1,0:T(8,128)(2,1)} %xm_hbm, ...), custom_call_target="tpu_custom_call" | custom-call | flops 8858370048 | bytes 77594624 | tf_op jit(solution)/shard_map/pallas_call | solution.py:260
  227.4 0.0 collective-permute-start.11
  227.5 2.6 add.46
  230.1 1.3 collective-permute-start.18
  231.5 0.9 collective-permute-start.19
  232.4 1.1 collective-permute-start.20
  233.5 3.6 %add_add_fusion.1.s0_ref = f32[256,2048]{1,0:T(8,128)} fusion(f32[256,2048]{1,0:T(8,128)} %collective-permute-done.15, f32[256,2048]{1,0:T(8,128)S(1)} %copy-done.6, f32[256,2048]{1,0:T(8,128)S(1)} %collective-permute-done.11), kind=kLoop, calls=%fused_computation.1 | loop fusion | flops 1048576 | bytes 8388608 | tf_op jit(solution)/shard_map/add | solution.py:299
  237.1 40.7 %collective-permute-done.18 = f32[256,2048]{1,0:T(8,128)S(1)} collective-permute-done((f32[256,2048]{1,0:T(8,128)S(1)}, f32[256,2048]{1,0:T(8,128)S(1)}, u32[]{:S(2)}, u32[]{:S(2)}) %collective-permute-start.18) | collective-permute-done | bytes 2097184 | tf_op jit(solution)/shard_map/ppermute | solution.py:232
  277.8 1.8 add_add_fusion.s1_ref
  279.6 21.0 %collective-permute-done.20.f1_ref = f32[256,2048]{1,0:T(8,128)S(1)} collective-permute-done((f32[256,2048]{1,0:T(8,128)S(1)}, f32[256,2048]{1,0:T(8,128)S(1)}, u32[]{:S(2)}, u32[]{:S(2)}) %collective-permute-start.20) | collective-permute-done | bytes 2097184 | tf_op jit(solution)/shard_map/ppermute | solution.py:232
  300.6 1.4 copy-done.8
  302.0 6.0 %combine.1 = bf16[256,2048]{1,0:T(8,128)(2,1)} custom-call(f32[256,8]{1,0:T(8,128)} %get-tuple-element.28.mine_ref, f32[256,2048]{1,0:T(8,128)} %add_add_fusion.1.s0_ref, f32[256,2048]{1,0:T(8,128)} %add_add_fusion.s1_ref, f32[256,2048]{1,0:T(8,128)} %copy-done.7, f32[256,2048]{1,0:T(8,128)} %copy-done.8), custom_call_target="tpu_custom_call" | custom-call | tf_op jit(solution)/shard_map/combine/pallas_call | solution.py:301
  (29 shorter events, 0.1 us)
Async XLA Ops:
  0.0 27.7 %collective-permute-start.1 = (bf16[256,2048]{1,0:T(8,128)(2,1)}, bf16[256,2048]{1,0:T(8,128)(2,1)}, u32[]{:S(2)}, u32[]{:S(2)}) collective-permute-start(bf16[256,2048]{1,0:T(8,128)(2,1)} %xm_hbm), channel_id=1, source_target_pairs={{0,6},{1,7},{2,4},{3,5},{4,2},{5,3},{6,0},{7,1}} | collective-permute-start | bytes 3145736 | tf_op jit(solution)/shard_map/ppermute | solution.py:232
  27.7 8.1 %collective-permute-start.2 = (bf16[256,2048]{1,0:T(8,128)(2,1)}, bf16[256,2048]{1,0:T(8,128)(2,1)}, u32[]{:S(2)}, u32[]{:S(2)}) collective-permute-start(bf16[256,2048]{1,0:T(8,128)(2,1)} %collective-permute-done.1.xm_hbm), channel_id=1, source_target_pairs={{0,1},{1,0},{2,3},{3,2},{4,5},{5,4},{6,7},{7,6}} | collective-permute-start | bytes 3145736 | tf_op jit(solution)/shard_map/ppermute | solution.py:228
  66.6 9.8 %collective-permute-start.3 = (f32[256,2048]{1,0:T(8,128)}, f32[256,2048]{1,0:T(8,128)S(1)}, u32[]{:S(2)}, u32[]{:S(2)}) collective-permute-start(f32[256,2048]{1,0:T(8,128)} %get-tuple-element.33), channel_id=1, source_target_pairs={{0,1},{1,0},{2,3},{3,2},{4,5},{5,4},{6,7},{7,6}} | collective-permute-start | bytes 6291464 | tf_op jit(solution)/shard_map/ppermute | solution.py:228
  72.3 7.4 %collective-permute-start.4 = (f32[256,2048]{1,0:T(8,128)}, f32[256,2048]{1,0:T(8,128)S(1)}, u32[]{:S(2)}, u32[]{:S(2)}) collective-permute-start(f32[256,2048]{1,0:T(8,128)} %get-tuple-element.35), channel_id=1, source_target_pairs={{0,1},{1,0},{2,3},{3,2},{4,5},{5,4},{6,7},{7,6}} | collective-permute-start | bytes 6291464 | tf_op jit(solution)/shard_map/ppermute | solution.py:228
  72.4 15.0 %collective-permute-start = (bf16[256,2048]{1,0:T(8,128)(2,1)}, bf16[256,2048]{1,0:T(8,128)(2,1)S(1)}, u32[]{:S(2)}, u32[]{:S(2)}) collective-permute-start(bf16[256,2048]{1,0:T(8,128)(2,1)} %xm_hbm), channel_id=1, source_target_pairs={{0,4},{1,3},{2,6},{3,1},{4,0},{5,7},{6,2},{7,5}} | collective-permute-start | bytes 3145736 | tf_op jit(solution)/shard_map/ppermute | solution.py:232
  76.3 3.4 %copy-start.1 = (f32[256,2048]{1,0:T(8,128)S(1)}, f32[256,2048]{1,0:T(8,128)}, u32[]{:S(2)}) copy-start(f32[256,2048]{1,0:T(8,128)} %get-tuple-element.34) | copy-start | bytes 6291460
  87.4 1.0 copy-start.9
  88.4 2.8 collective-permute-start.5
  88.4 39.9 %collective-permute-start.12 = (bf16[256,2048]{1,0:T(8,128)(2,1)}, bf16[256,2048]{1,0:T(8,128)(2,1)}, u32[]{:S(2)}, u32[]{:S(2)}) collective-permute-start(bf16[256,2048]{1,0:T(8,128)(2,1)} %xm_hbm), channel_id=1, source_target_pairs={{0,2},{1,5},{2,0},{3,7},{4,6},{5,1},{6,4},{7,3}} | collective-permute-start | bytes 3145736 | tf_op jit(solution)/shard_map/ppermute | solution.py:232
  89.6 78.1 %collective-permute-start.7 = (f32[256,2048]{1,0:T(8,128)}, f32[256,2048]{1,0:T(8,128)}, u32[]{:S(2)}, u32[]{:S(2)}) collective-permute-start(f32[256,2048]{1,0:T(8,128)} %add.36), channel_id=1, source_target_pairs={{0,2},{1,5},{2,0},{3,7},{4,6},{5,1},{6,4},{7,3}} | collective-permute-start | bytes 6291464 | tf_op jit(solution)/shard_map/ppermute | solution.py:232
  119.1 48.6 %collective-permute-start.6 = (f32[256,2048]{1,0:T(8,128)}, f32[256,2048]{1,0:T(8,128)}, u32[]{:S(2)}, u32[]{:S(2)}) collective-permute-start(f32[256,2048]{1,0:T(8,128)} %get-tuple-element.38), channel_id=1, source_target_pairs={{0,1},{1,0},{2,3},{3,2},{4,5},{5,4},{6,7},{7,6}} | collective-permute-start | bytes 6291464 | tf_op jit(solution)/shard_map/ppermute | solution.py:228
  128.3 5.6 %collective-permute-start.13 = (bf16[256,2048]{1,0:T(8,128)(2,1)}, bf16[256,2048]{1,0:T(8,128)(2,1)}, u32[]{:S(2)}, u32[]{:S(2)}) collective-permute-start(bf16[256,2048]{1,0:T(8,128)(2,1)} %collective-permute-done.12.xm_hbm), channel_id=1, source_target_pairs={{0,1},{1,0},{2,3},{3,2},{4,5},{5,4},{6,7},{7,6}} | collective-permute-start | bytes 3145736 | tf_op jit(solution)/shard_map/ppermute | solution.py:228
  128.3 44.4 %collective-permute-start.9 = (f32[256,2048]{1,0:T(8,128)}, f32[256,2048]{1,0:T(8,128)}, u32[]{:S(2)}, u32[]{:S(2)}) collective-permute-start(f32[256,2048]{1,0:T(8,128)} %add.37), channel_id=1, source_target_pairs={{0,2},{1,5},{2,0},{3,7},{4,6},{5,1},{6,4},{7,3}} | collective-permute-start | bytes 6291464 | tf_op jit(solution)/shard_map/ppermute | solution.py:232
  129.6 43.2 %collective-permute-start.8 = (f32[256,2048]{1,0:T(8,128)}, f32[256,2048]{1,0:T(8,128)}, u32[]{:S(2)}, u32[]{:S(2)}) collective-permute-start(f32[256,2048]{1,0:T(8,128)} %get-tuple-element.40), channel_id=1, source_target_pairs={{0,1},{1,0},{2,3},{3,2},{4,5},{5,4},{6,7},{7,6}} | collective-permute-start | bytes 6291464 | tf_op jit(solution)/shard_map/ppermute | solution.py:228
  166.9 10.7 %collective-permute-start.14 = (f32[256,2048]{1,0:T(8,128)}, f32[256,2048]{1,0:T(8,128)S(1)}, u32[]{:S(2)}, u32[]{:S(2)}) collective-permute-start(f32[256,2048]{1,0:T(8,128)} %get-tuple-element.46), channel_id=1, source_target_pairs={{0,1},{1,0},{2,3},{3,2},{4,5},{5,4},{6,7},{7,6}} | collective-permute-start | bytes 6291464 | tf_op jit(solution)/shard_map/ppermute | solution.py:228
  167.8 5.0 %copy-start.4 = (f32[256,2048]{1,0:T(8,128)S(1)}, f32[256,2048]{1,0:T(8,128)}, u32[]{:S(2)}) copy-start(f32[256,2048]{1,0:T(8,128)} %get-tuple-element.39) | copy-start | bytes 6291460
  172.8 4.8 %copy-start = (f32[256,2048]{1,0:T(8,128)S(1)}, f32[256,2048]{1,0:T(8,128)}, u32[]{:S(2)}) copy-start(f32[256,2048]{1,0:T(8,128)} %get-tuple-element.45) | copy-start | bytes 6291460
  177.1 10.0 %collective-permute-start.10 = (bf16[256,2048]{1,0:T(8,128)(2,1)}, bf16[256,2048]{1,0:T(8,128)(2,1)}, u32[]{:S(2)}, u32[]{:S(2)}) collective-permute-start(bf16[256,2048]{1,0:T(8,128)(2,1)} %xm_hbm), channel_id=1, source_target_pairs={{0,1},{1,0},{2,3},{3,2},{4,5},{5,4},{6,7},{7,6}} | collective-permute-start | bytes 3145736 | tf_op jit(solution)/shard_map/ppermute | solution.py:228
  177.1 50.3 %collective-permute-start.17 = (f32[256,2048]{1,0:T(8,128)}, f32[256,2048]{1,0:T(8,128)}, u32[]{:S(2)}, u32[]{:S(2)}) collective-permute-start(f32[256,2048]{1,0:T(8,128)} %get-tuple-element.50), channel_id=1, source_target_pairs={{0,1},{1,0},{2,3},{3,2},{4,5},{5,4},{6,7},{7,6}} | collective-permute-start | bytes 6291464 | tf_op jit(solution)/shard_map/ppermute | solution.py:228
  179.2 53.2 %collective-permute-start.15 = (f32[256,2048]{1,0:T(8,128)}, f32[256,2048]{1,0:T(8,128)}, u32[]{:S(2)}, u32[]{:S(2)}) collective-permute-start(f32[256,2048]{1,0:T(8,128)} %add.43), channel_id=1, source_target_pairs={{0,2},{1,5},{2,0},{3,7},{4,6},{5,1},{6,4},{7,3}} | collective-permute-start | bytes 6291464 | tf_op jit(solution)/shard_map/ppermute | solution.py:232
  227.4 6.1 %collective-permute-start.11 = (f32[256,2048]{1,0:T(8,128)}, f32[256,2048]{1,0:T(8,128)S(1)}, u32[]{:S(2)}, u32[]{:S(2)}) collective-permute-start(f32[256,2048]{1,0:T(8,128)} %get-tuple-element.43), channel_id=1, source_target_pairs={{0,1},{1,0},{2,3},{3,2},{4,5},{5,4},{6,7},{7,6}} | collective-permute-start | bytes 6291464 | tf_op jit(solution)/shard_map/ppermute | solution.py:228
  227.4 4.0 %copy-start.2 = (f32[256,2048]{1,0:T(8,128)S(1)}, f32[256,2048]{1,0:T(8,128)}, u32[]{:S(2)}) copy-start(f32[256,2048]{1,0:T(8,128)} %add_add_fusion.3) | copy-start | bytes 6291460
  227.5 4.9 %copy-start.3 = (f32[256,2048]{1,0:T(8,128)S(1)}, f32[256,2048]{1,0:T(8,128)}, u32[]{:S(2)}) copy-start(f32[256,2048]{1,0:T(8,128)} %add_add_fusion.2) | copy-start | bytes 6291460
  227.5 6.0 %copy-start.6 = (f32[256,2048]{1,0:T(8,128)S(1)}, f32[256,2048]{1,0:T(8,128)}, u32[]{:S(2)}) copy-start(f32[256,2048]{1,0:T(8,128)} %get-tuple-element.42) | copy-start | bytes 6291460
  230.1 47.7 %collective-permute-start.18 = (f32[256,2048]{1,0:T(8,128)S(1)}, f32[256,2048]{1,0:T(8,128)S(1)}, u32[]{:S(2)}, u32[]{:S(2)}) collective-permute-start(f32[256,2048]{1,0:T(8,128)S(1)} %add.46), channel_id=1, source_target_pairs={{0,2},{1,5},{2,0},{3,7},{4,6},{5,1},{6,4},{7,3}} | collective-permute-start | bytes 6291464 | tf_op jit(solution)/shard_map/ppermute | solution.py:232
  231.4 46.3 %collective-permute-start.16 = (f32[256,2048]{1,0:T(8,128)}, f32[256,2048]{1,0:T(8,128)S(1)}, u32[]{:S(2)}, u32[]{:S(2)}) collective-permute-start(f32[256,2048]{1,0:T(8,128)} %get-tuple-element.48), channel_id=1, source_target_pairs={{0,1},{1,0},{2,3},{3,2},{4,5},{5,4},{6,7},{7,6}} | collective-permute-start | bytes 6291464 | tf_op jit(solution)/shard_map/ppermute | solution.py:228
  231.5 48.2 %collective-permute-start.19 = (f32[256,2048]{1,0:T(8,128)S(1)}, f32[256,2048]{1,0:T(8,128)S(1)}, u32[]{:S(2)}, u32[]{:S(2)}) collective-permute-start(f32[256,2048]{1,0:T(8,128)S(1)} %copy-done.2), channel_id=1, source_target_pairs={{0,4},{1,3},{2,6},{3,1},{4,0},{5,7},{6,2},{7,5}} | collective-permute-start | bytes 6291464 | tf_op jit(solution)/shard_map/ppermute | solution.py:232
  232.4 68.2 %collective-permute-start.20 = (f32[256,2048]{1,0:T(8,128)S(1)}, f32[256,2048]{1,0:T(8,128)S(1)}, u32[]{:S(2)}, u32[]{:S(2)}) collective-permute-start(f32[256,2048]{1,0:T(8,128)S(1)} %copy-done.3), channel_id=1, source_target_pairs={{0,4},{1,3},{2,6},{3,1},{4,0},{5,7},{6,2},{7,5}} | collective-permute-start | bytes 6291464 | tf_op jit(solution)/shard_map/ppermute | solution.py:232
  233.5 44.3 %copy-start.5 = (f32[256,2048]{1,0:T(8,128)S(1)}, f32[256,2048]{1,0:T(8,128)}, u32[]{:S(2)}) copy-start(f32[256,2048]{1,0:T(8,128)} %get-tuple-element.47) | copy-start | bytes 6291460
  279.6 22.4 %copy-start.7 = (f32[256,2048]{1,0:T(8,128)}, f32[256,2048]{1,0:T(8,128)S(1)}, u32[]{:S(2)}) copy-start(f32[256,2048]{1,0:T(8,128)S(1)} %collective-permute-done.19.f0_ref) | copy-start | bytes 6291460
  300.6 1.4 copy-start.8

commit v3 on v2

--- a/solution.py
+++ b/solution.py
@@ -13,17 +13,19 @@
 VMEM_BYTES = 67_043_328
 
 
-def _route_kernel(chips, idx_ref, g_ref, cap_ref, pos_ref, off_ref, cnt_ref, mine_ref, ids_all, send_sem, recv_sem):
+def _route_kernel(chips, turns, idx_ref, g_ref, cap_ref, x_ref, *refs):
+    pos_ref, off_ref, cnt_ref, mine_ref, xm_ref, xo_ref, ids_all, send_sem, recv_sem, xsend, xrecv = refs
     core, me = lax.axis_index("ep"), lax.axis_index("tp")
     blocks, top, t = ids_all.shape
     e_all = cap_ref.shape[0]
     here = core * chips + me
+    mesh_id = pl.DeviceIdType.MESH
     peers = [
         (k, {"ep": jnp.bitwise_xor(core, k // chips), "tp": jnp.bitwise_xor(me, k % chips)}) for k in range(1, blocks)
     ]
     barrier = pltpu.get_barrier_semaphore()
     for _, peer in peers:
-        pl.semaphore_signal(barrier, inc=1, device_id=peer, device_id_type=pl.DeviceIdType.MESH)
+        pl.semaphore_signal(barrier, inc=1, device_id=peer, device_id_type=mesh_id)
     pl.semaphore_wait(barrier, blocks - 1)
     copies = [
         pltpu.make_async_remote_copy(
@@ -32,11 +34,30 @@
             send_sem=send_sem.at[k],
             recv_sem=recv_sem.at[k],
             device_id=peer,
-            device_id_type=pl.DeviceIdType.MESH,
+            device_id_type=mesh_id,
         )
         for k, peer in peers
     ]
     for c in copies:
+        c.start()
+    pieces = xsend.shape[1]
+    turn = turns[0] + (turns[1] - turns[0]) * core
+    piece = x_ref.shape[0] // pieces
+
+    def tokens(hop, i, src, dst, peer):
+        part = pl.ds(i * piece, piece)
+        return pltpu.make_async_remote_copy(
+            src_ref=src.at[part],
+            dst_ref=dst.at[part],
+            send_sem=xsend.at[hop, i],
+            recv_sem=xrecv.at[hop, i],
+            device_id=peer,
+            device_id_type=mesh_id,
+        )
+
+    arrive = [tokens(0, i, x_ref, xm_ref, {"ep": core, "tp": jnp.bitwise_xor(me, turn)}) for i in range(pieces)]
+    forward = [tokens(1, i, xm_ref, xo_ref, {"ep": 1 - core, "tp": me}) for i in range(pieces)]
+    for c in arrive:
         c.start()
     ids_all[pl.ds(here, 1)] = idx_ref[...][None]
     before = (
@@ -66,6 +87,12 @@
     lines += [g_ref[j : j + 1, :] for j in range(top)]
     table = jnp.concatenate(lines + [jnp.zeros((8 - 2 * top, t), F32)], axis=0)
     mine_ref[...] = jnp.transpose(table)
+    for c, f in zip(arrive, forward):
+        c.wait_recv()
+        f.start()
+    for c, f in zip(arrive, forward):
+        c.wait_send()
+        f.wait()
 
 
 def _expert_kernel(
@@ -85,18 +112,19 @@
         blocks.append(c * chips + jnp.bitwise_xor(me, turn))
 
     def chunk(k, e):
-        if k == 0:
+        if isinstance(k, int) and k == 0:
             return [
                 pltpu.make_async_copy(w1_hbm.at[e, :, pl.ds(0, cut)], w1a, wsem.at[0]),
                 pltpu.make_async_copy(w3_hbm.at[e, :, pl.ds(0, cut)], w3a, wsem.at[1]),
             ]
-        if k == 1:
+        if isinstance(k, int) and k == 1:
             return [
                 pltpu.make_async_copy(w1_hbm.at[e, :, pl.ds(cut, ff - cut)], w1b, wsem.at[2]),
                 pltpu.make_async_copy(w3_hbm.at[e, :, pl.ds(cut, ff - cut)], w3b, wsem.at[3]),
             ]
         h = k - 2
-        return [pltpu.make_async_copy(w2_hbm.at[e, :, pl.ds(h * half_d, half_d)], w2s.at[h], wsem.at[2 + k])]
+        cols = pl.ds(pl.multiple_of(h * half_d, half_d), half_d)
+        return [pltpu.make_async_copy(w2_hbm.at[e, :, cols], w2s.at[h], wsem.at[2 + k])]
 
     def start(k, e):
         for c in chunk(k, e):
@@ -139,12 +167,10 @@
         need = functools.reduce(jnp.maximum, [jnp.where(k > 0, o - o // 8 * 8 + k, 0) for o, k in zip(offs, cnts)])
 
         def last(k):
-            if k == 0:
-
-                @pl.when(e == e_loc - 1)
-                def _():
-                    for c in out_copies(0):
-                        c.start()
+            @pl.when((e == e_loc - 1) & (k == 0))
+            def _():
+                for c in out_copies(0):
+                    c.start()
 
         def run(m):
             bases = [pl.multiple_of(jnp.minimum(o // 8 * 8, rows - m), 8) for o in offs]
@@ -162,13 +188,18 @@
                 hs.append((jax.nn.silu(h1) * h3).astype(BF16))
                 following(k, e)
             h = jnp.concatenate(hs, axis=1)
-            for k in range(2):
+
+            def project(k, carry):
                 finish(2 + k, e)
                 p = jnp.dot(h, w2s[k], preferred_element_type=F32)
+                cols = pl.ds(pl.multiple_of(k * half_d, half_d), half_d)
                 for s in range(2):
-                    acc[s, pl.ds(bases[s], m), k * half_d : (k + 1) * half_d] += p[s * m : (s + 1) * m]
+                    acc[s, pl.ds(bases[s], m), cols] += p[s * m : (s + 1) * m]
                 following(2 + k, e)
                 last(k)
+                return carry
+
+            lax.fori_loop(0, 2, project, 0)
 
         @pl.when(need == 0)
         def _():
@@ -234,25 +265,30 @@
         def after(a, *first):
             return lax.optimization_barrier((a, *first))[0]
 
-        x_d = shift(x, (3, 3))
-        pos, off, cnt, mine = pl.pallas_call(
-            functools.partial(_route_kernel, chips),
+        out, back = (1, 2), (2, 1)
+        pieces = 4
+        pos, off, cnt, mine, xn_mine, xn_other = pl.pallas_call(
+            functools.partial(_route_kernel, chips, out),
             out_shape=[
                 jax.ShapeDtypeStruct((blocks, e_all, t_loc), jnp.int32),
                 jax.ShapeDtypeStruct((blocks, e_all, 128), jnp.int32),
                 jax.ShapeDtypeStruct((blocks, e_all, 128), jnp.int32),
                 jax.ShapeDtypeStruct((t_loc, 8), F32),
+                jax.ShapeDtypeStruct((t_loc, d), BF16),
+                jax.ShapeDtypeStruct((t_loc, d), BF16),
             ],
-            in_specs=[vmem] * 3,
-            out_specs=[vmem] * 4,
+            in_specs=[vmem] * 3 + [anym],
+            out_specs=[vmem] * 4 + [anym] * 2,
             scratch_shapes=[
                 pltpu.VMEM((blocks, top, t_loc), jnp.int32),
                 pltpu.SemaphoreType.DMA((blocks,)),
                 pltpu.SemaphoreType.DMA((blocks,)),
+                pltpu.SemaphoreType.DMA((2, pieces)),
+                pltpu.SemaphoreType.DMA((2, pieces)),
             ],
             compiler_params=pltpu.CompilerParams(collective_id=0, has_side_effects=True, vmem_limit_bytes=VMEM_BYTES),
             name="route",
-        )(idx.T, g.T, cap[:, None])
+        )(idx.T, g.T, cap[:, None], x)
 
         sizes = (64, (c + 7 + 7) // 8 * 8)
 
@@ -280,23 +316,25 @@
                 ),
             )(off, cnt, pos, mine, other, w1, w3, w2)
 
-        def merge(parts):
-            return [parts[2 + q] + swap(parts[q]) for q in range(2)]
-
-        out, back = (1, 2), (2, 1)
-        x_n, x_f = shift(x, out), shift(x, back)
+        def merge(parts, *more):
+            sums = []
+            for q in range(2):
+                other = swap(parts[q])
+                sums.append(functools.reduce(jnp.add, [m[q] for m in more], parts[2 + q] + other))
+            return sums
+
+        x_next = after(x, pos)
+        x_d, x_f = shift(x_next, (3, 3)), shift(x_next, back)
+        near = merge(stage(out, xn_mine, xn_other))
+        x_d = after(x_d, *near)
+        near = [shift(a, out) for a in near]
         diag = merge(stage((3, 3), x_d, swap(x_d)))
+        x_f = after(x_f, *diag)
         via = [shift(a, out) for a in diag]
-        x_n, x_f = after(x_n, *diag), after(x_f, *diag)
-        near = merge(stage(out, x_n, swap(x_n)))
-        near = [shift(a, out) for a in near]
-        part = stage(back, x_f, swap(x_f))
-        far = merge(part)
-        far = [a + b for a, b in zip(far, via)]
+        far = merge(stage(back, x_f, swap(x_f)), via)
         x_o = after(x, *far)
         far = [shift(a, back) for a in far]
-        own = merge(stage((0, 0), x_o, swap(x_o), sizes[-1:]))
-        sums = [a + b for a, b in zip(own, near)]
+        sums = merge(stage((0, 0), x_o, swap(x_o)), near)
         width = d // 4
         return pl.pallas_call(
             _combine_kernel,

time: 309 us -> 329 us (1.065)
  waiting for transfers between devices: 97.5 us -> 112 us
  Pallas kernels: 145 us -> 156 us
    pallas_call x1, Pallas kernels: 6.79 us -> 21.1 us  [layer(): pl.pallas_call(functools.partial(_route_kernel, chips, out), out_shape=[j...]
    ppermute x9 -> x8, waiting for transfers between devices: 91.1 us -> 103 us  [shift(): return lax.ppermute(a, ('tp', 'ep'), pairs)]
    ppermute x9 -> x8, starting transfers between devices: 18.8 us -> 14.4 us  [shift(): return lax.ppermute(a, ('tp', 'ep'), pairs)]
    pallas_call x4, Pallas kernels: 132 us -> 128 us  [stage(): pl.pallas_call(functools.partial(_expert_kernel, turns, sizes, cut), out_...]
    ppermute x12 -> x11, waiting for transfers between devices: 6.35 us -> 8.72 us  [swap(): return lax.ppermute(a, 'ep', [(0, 1), (1, 0)])]
    ppermute x12 -> x11, starting transfers between devices: 19.1 us -> 20.7 us  [swap(): return lax.ppermute(a, 'ep', [(0, 1), (1, 0)])]
  transfers between devices with their start and end apart: 21 -> 19, of which waited for: 7 -> 10; matrix products, arithmetic and copies ran while one was open for 8% -> 6% of each run, Pallas kernels for 35% -> 20%
where the time goes in v3:
time: 329 us; the launch traced here: 328 us
  Pallas kernels  156 us (47%)
  waiting for transfers between devices  112 us (34%)
  starting transfers between devices  35.1 us (11%)
  other arithmetic  22.2 us (7%)
    pallas_call x4, Pallas kernels, stage(): pl.pallas_call(functools.partial(_expert_kernel, turns, sizes, cut), out_...  128 us
    ppermute x8, waiting for transfers between devices, shift(): return lax.ppermute(a, ('tp', 'ep'), pairs)  103 us
    pallas_call x1, Pallas kernels, layer(): pl.pallas_call(functools.partial(_route_kernel, chips, out), out_shape=[j...  21.1 us
    ppermute x11, starting transfers between devices, swap(): return lax.ppermute(a, 'ep', [(0, 1), (1, 0)])  20.7 us
    ppermute x8, starting transfers between devices, shift(): return lax.ppermute(a, ('tp', 'ep'), pairs)  14.4 us
    add x4, other arithmetic, merge(): functools.reduce(jnp.add, [m[q] for m in more], parts[2 + q] + other)  12.2 us
    add x4, other arithmetic, merge(): parts[2 + q] + other  10 us
    ppermute x11, waiting for transfers between devices, swap(): return lax.ppermute(a, 'ep', [(0, 1), (1, 0)])  8.72 us
  transfers between devices with their start and end apart: 19, of which 10 were waited for; matrix products, arithmetic and copies ran while one was open for 6% of the time, Pallas kernels for 20%

profile of v3, /device:TPU:0, one launch (start us, length us, event | category | flops | bytes accessed | tf_op | source)
XLA Modules:
  0.0 328.1 jit_solution(16772263122306995611)
XLA Ops:
  0.0 1.3 copy.8.cap_ref
  1.3 21.1 %route.1 = (s32[8,8,256]{2,1,0:T(8,128)}, s32[8,8,128]{2,1,0:T(8,128)}, s32[8,8,128]{2,1,0:T(8,128)}, f32[256,8]{1,0:T(8,128)}, bf16[256,2048]{1,0:T(8,128)(2,1)}, /*index=5*/bf16[256,2048]{1,0:T(8,128)(2,1)}) custom-call(s32[2,256]{1,0:T(2,128)} %bitcast.3, f32[2,256]{1,0:T(2,128)} %bitcast.4, s32[8,1]{1,0:T(8,128)} %copy.8.cap_ref, bf16[256,2048]{1,0:T(8,128)(2,1)} %xm_hbm), custom_call_target="tpu_custom_call" | custom-call | tf_op jit(solution)/shard_map/route/pallas_call | solution.py:270
  22.5 33.1 %shard_map.73 = (f32[256,2048]{1,0:T(8,128)}, f32[256,2048]{1,0:T(8,128)}, f32[256,2048]{1,0:T(8,128)}, f32[256,2048]{1,0:T(8,128)}) custom-call(s32[8,8,128]{2,1,0:T(8,128)} %get-tuple-element.32.off_ref, s32[8,8,128]{2,1,0:T(8,128)} %get-tuple-element.33.cnt_ref, s32[8,8,256]{2,1,0:T(8,128)} %get-tuple-element.34.pos_ref, ...), custom_call_target="tpu_custom_call" | custom-call | flops 8858370048 | bytes 77594624 | tf_op jit(solution)/shard_map/pallas_call | solution.py:296
  55.5 0.8 collective-permute-start.2
  56.4 0.0 collective-permute-start.3
  56.4 5.0 %collective-permute-start.1 = (bf16[256,2048]{1,0:T(8,128)(2,1)}, bf16[256,2048]{1,0:T(8,128)(2,1)S(1)}, u32[]{:S(2)}, u32[]{:S(2)}) collective-permute-start(bf16[256,2048]{1,0:T(8,128)(2,1)} %xm_hbm), channel_id=1, source_target_pairs={{0,6},{1,7},{2,4},{3,5},{4,2},{5,3},{6,0},{7,1}} | collective-permute-start | bytes 3145736 | tf_op jit(solution)/shard_map/ppermute | solution.py:263
  61.4 0.0 collective-permute-done.2
  61.4 3.3 %add.36 = f32[256,2048]{1,0:T(8,128)} add(f32[256,2048]{1,0:T(8,128)} %get-tuple-element.38, f32[256,2048]{1,0:T(8,128)S(1)} %collective-permute-done.2) | non-fusion elementwise | flops 524288 | bytes 6291456 | tf_op jit(solution)/shard_map/add | solution.py:323
  64.8 1.6 add.37
  66.4 19.0 %collective-permute-done.1.xm_hbm = bf16[256,2048]{1,0:T(8,128)(2,1)S(1)} collective-permute-done((bf16[256,2048]{1,0:T(8,128)(2,1)}, bf16[256,2048]{1,0:T(8,128)(2,1)S(1)}, u32[]{:S(2)}, u32[]{:S(2)}) %collective-permute-start.1) | collective-permute-done | bytes 1048608 | tf_op jit(solution)/shard_map/ppermute | solution.py:263
  85.4 1.0 copy-done.7
  86.4 0.0 collective-permute-start.4
  86.4 2.8 collective-permute-done.4.xo_hbm
  89.2 30.8 %shard_map.74 = (f32[256,2048]{1,0:T(8,128)}, f32[256,2048]{1,0:T(8,128)}, f32[256,2048]{1,0:T(8,128)}, f32[256,2048]{1,0:T(8,128)}) custom-call(s32[8,8,128]{2,1,0:T(8,128)} %get-tuple-element.32.off_ref, s32[8,8,128]{2,1,0:T(8,128)} %get-tuple-element.33.cnt_ref, s32[8,8,256]{2,1,0:T(8,128)} %get-tuple-element.34.pos_ref, bf16[256,2048]{1,0:T(8,128)(2,1)} %copy-done.7, ...), custom_call_target="tpu_custom_call" | custom-call | flops 8858370048 | bytes 77594624 | tf_op jit(solution)/shard_map/pallas_call | solution.py:296
  120.0 5.8 %collective-permute-start.5 = (f32[256,2048]{1,0:T(8,128)}, f32[256,2048]{1,0:T(8,128)S(1)}, u32[]{:S(2)}, u32[]{:S(2)}) collective-permute-start(f32[256,2048]{1,0:T(8,128)} %get-tuple-element.44), channel_id=1, source_target_pairs={{0,1},{1,0},{2,3},{3,2},{4,5},{5,4},{6,7},{7,6}} | collective-permute-start | bytes 6291464 | tf_op jit(solution)/shard_map/ppermute | solution.py:259
  125.8 0.0 collective-permute-start.6
  125.9 1.5 collective-permute-start
  127.4 2.5 collective-permute-done.5
  129.8 3.4 %add.38 = f32[256,2048]{1,0:T(8,128)} add(f32[256,2048]{1,0:T(8,128)} %get-tuple-element.43, f32[256,2048]{1,0:T(8,128)S(1)} %collective-permute-done.5) | non-fusion elementwise | flops 524288 | bytes 6291456 | tf_op jit(solution)/shard_map/add | solution.py:323
  133.3 0.0 collective-permute-done.6
  133.3 1.6 add.39
  134.9 6.0 %collective-permute-done.xm_hbm = bf16[256,2048]{1,0:T(8,128)(2,1)S(1)} collective-permute-done((bf16[256,2048]{1,0:T(8,128)(2,1)}, bf16[256,2048]{1,0:T(8,128)(2,1)S(1)}, u32[]{:S(2)}, u32[]{:S(2)}) %collective-permute-start) | collective-permute-done | bytes 1048608 | tf_op jit(solution)/shard_map/ppermute | solution.py:263
  140.9 1.0 copy-done.6
  141.9 0.3 collective-permute-start.7
  142.2 2.4 collective-permute-start.9
  144.6 0.1 collective-permute-done.7.xo_hbm
  144.7 28.0 %shard_map.75 = (f32[256,2048]{1,0:T(8,128)}, f32[256,2048]{1,0:T(8,128)}, f32[256,2048]{1,0:T(8,128)}, f32[256,2048]{1,0:T(8,128)}) custom-call(s32[8,8,128]{2,1,0:T(8,128)} %get-tuple-element.32.off_ref, s32[8,8,128]{2,1,0:T(8,128)} %get-tuple-element.33.cnt_ref, s32[8,8,256]{2,1,0:T(8,128)} %get-tuple-element.34.pos_ref, bf16[256,2048]{1,0:T(8,128)(2,1)} %copy-done.6, ...), custom_call_target="tpu_custom_call" | custom-call | flops 8858370048 | bytes 77594624 | tf_op jit(solution)/shard_map/pallas_call | solution.py:296
  172.7 9.4 %collective-permute-start.8 = (f32[256,2048]{1,0:T(8,128)}, f32[256,2048]{1,0:T(8,128)S(1)}, u32[]{:S(2)}, u32[]{:S(2)}) collective-permute-start(f32[256,2048]{1,0:T(8,128)} %get-tuple-element.49), channel_id=1, source_target_pairs={{0,1},{1,0},{2,3},{3,2},{4,5},{5,4},{6,7},{7,6}} | collective-permute-start | bytes 6291464 | tf_op jit(solution)/shard_map/ppermute | solution.py:259
  182.1 2.5 collective-permute-start.11
  184.6 2.2 collective-permute-start.10
  186.8 4.3 %add_add_fusion.3 = f32[256,2048]{1,0:T(8,128)} fusion(f32[256,2048]{1,0:T(8,128)} %collective-permute-done.9, f32[256,2048]{1,0:T(8,128)} %get-tuple-element.48, f32[256,2048]{1,0:T(8,128)S(1)} %collective-permute-done.8), kind=kLoop, calls=%fused_computation.3 | loop fusion | flops 1048576 | bytes 8388608 | tf_op jit(solution)/shard_map/add | solution.py:323
  191.1 17.8 %collective-permute-done.11 = f32[256,2048]{1,0:T(8,128)S(1)} collective-permute-done((f32[256,2048]{1,0:T(8,128)}, f32[256,2048]{1,0:T(8,128)S(1)}, u32[]{:S(2)}, u32[]{:S(2)}) %collective-permute-start.11) | collective-permute-done | bytes 2097184 | tf_op jit(solution)/shard_map/ppermute | solution.py:263
  208.9 1.9 add_add_fusion.2
  210.8 1.6 collective-permute-start.12
  212.4 0.4 collective-permute-start.14
  212.8 2.0 collective-permute-done.12.xo_hbm
  214.8 36.5 %shard_map.76 = (f32[256,2048]{1,0:T(8,128)}, f32[256,2048]{1,0:T(8,128)}, f32[256,2048]{1,0:T(8,128)}, f32[256,2048]{1,0:T(8,128)}) custom-call(s32[8,8,128]{2,1,0:T(8,128)} %get-tuple-element.32.off_ref, s32[8,8,128]{2,1,0:T(8,128)} %get-tuple-element.33.cnt_ref, s32[8,8,256]{2,1,0:T(8,128)} %get-tuple-element.34.pos_ref, bf16[256,2048]{1,0:T(8,128)(2,1)} %xm_hbm, ...), custom_call_target="tpu_custom_call" | custom-call | flops 8858370048 | bytes 77594624 | tf_op jit(solution)/shard_map/pallas_call | solution.py:296
  251.3 0.0 collective-permute-start.13
  251.3 0.0 collective-permute-start.16
  251.4 0.5 collective-permute-start.15
  251.8 2.4 collective-permute-start.17
  254.3 0.0 collective-permute-start.18
  254.3 1.4 collective-permute-done.13
  255.7 4.2 %add_add_fusion.1.s0_ref = f32[256,2048]{1,0:T(8,128)} fusion(f32[256,2048]{1,0:T(8,128)} %collective-permute-done.14, f32[256,2048]{1,0:T(8,128)} %get-tuple-element.53, f32[256,2048]{1,0:T(8,128)S(1)} %collective-permute-done.13), kind=kLoop, calls=%fused_computation.1 | loop fusion | flops 1048576 | bytes 8388608 | tf_op jit(solution)/shard_map/add | solution.py:323
  259.9 40.1 %collective-permute-done.16 = f32[256,2048]{1,0:T(8,128)S(1)} collective-permute-done((f32[256,2048]{1,0:T(8,128)}, f32[256,2048]{1,0:T(8,128)S(1)}, u32[]{:S(2)}, u32[]{:S(2)}) %collective-permute-start.16) | collective-permute-done | bytes 2097184 | tf_op jit(solution)/shard_map/ppermute | solution.py:263
  300.1 1.9 add_add_fusion.s1_ref
  301.9 20.2 %collective-permute-done.18.f1_ref = f32[256,2048]{1,0:T(8,128)} collective-permute-done((f32[256,2048]{1,0:T(8,128)}, f32[256,2048]{1,0:T(8,128)}, u32[]{:S(2)}, u32[]{:S(2)}) %collective-permute-start.18) | collective-permute-done | bytes 2097184 | tf_op jit(solution)/shard_map/ppermute | solution.py:263
  322.1 6.0 %combine.1 = bf16[256,2048]{1,0:T(8,128)(2,1)} custom-call(f32[256,8]{1,0:T(8,128)} %get-tuple-element.31.mine_ref, f32[256,2048]{1,0:T(8,128)} %add_add_fusion.1.s0_ref, f32[256,2048]{1,0:T(8,128)} %add_add_fusion.s1_ref, f32[256,2048]{1,0:T(8,128)} %copy-done.4, f32[256,2048]{1,0:T(8,128)} %collective-permute-done.18.f1_ref), custom_call_target="tpu_custom_call" | custom-call | tf_op jit(solution)/shard_map/combine/pallas_call | solution.py:339
  (21 shorter events, 0.0 us)
Async XLA Ops:
  55.5 5.9 %collective-permute-start.2 = (f32[256,2048]{1,0:T(8,128)}, f32[256,2048]{1,0:T(8,128)S(1)}, u32[]{:S(2)}, u32[]{:S(2)}) collective-permute-start(f32[256,2048]{1,0:T(8,128)} %get-tuple-element.39), channel_id=1, source_target_pairs={{0,1},{1,0},{2,3},{3,2},{4,5},{5,4},{6,7},{7,6}} | collective-permute-start | bytes 6291464 | tf_op jit(solution)/shard_map/ppermute | solution.py:259
  56.4 8.4 %collective-permute-start.3 = (f32[256,2048]{1,0:T(8,128)}, f32[256,2048]{1,0:T(8,128)S(1)}, u32[]{:S(2)}, u32[]{:S(2)}) collective-permute-start(f32[256,2048]{1,0:T(8,128)} %get-tuple-element.41), channel_id=1, source_target_pairs={{0,1},{1,0},{2,3},{3,2},{4,5},{5,4},{6,7},{7,6}} | collective-permute-start | bytes 6291464 | tf_op jit(solution)/shard_map/ppermute | solution.py:259
  56.4 29.0 %collective-permute-start.1 = (bf16[256,2048]{1,0:T(8,128)(2,1)}, bf16[256,2048]{1,0:T(8,128)(2,1)S(1)}, u32[]{:S(2)}, u32[]{:S(2)}) collective-permute-start(bf16[256,2048]{1,0:T(8,128)(2,1)} %xm_hbm), channel_id=1, source_target_pairs={{0,6},{1,7},{2,4},{3,5},{4,2},{5,3},{6,0},{7,1}} | collective-permute-start | bytes 3145736 | tf_op jit(solution)/shard_map/ppermute | solution.py:263
  61.4 3.4 %copy-start.1 = (f32[256,2048]{1,0:T(8,128)S(1)}, f32[256,2048]{1,0:T(8,128)}, u32[]{:S(2)}) copy-start(f32[256,2048]{1,0:T(8,128)} %get-tuple-element.40) | copy-start | bytes 6291460
  85.4 1.0 copy-start.7
  86.4 2.8 collective-permute-start.4
  120.0 9.8 %collective-permute-start.5 = (f32[256,2048]{1,0:T(8,128)}, f32[256,2048]{1,0:T(8,128)S(1)}, u32[]{:S(2)}, u32[]{:S(2)}) collective-permute-start(f32[256,2048]{1,0:T(8,128)} %get-tuple-element.44), channel_id=1, source_target_pairs={{0,1},{1,0},{2,3},{3,2},{4,5},{5,4},{6,7},{7,6}} | collective-permute-start | bytes 6291464 | tf_op jit(solution)/shard_map/ppermute | solution.py:259
  125.8 7.4 %collective-permute-start.6 = (f32[256,2048]{1,0:T(8,128)}, f32[256,2048]{1,0:T(8,128)S(1)}, u32[]{:S(2)}, u32[]{:S(2)}) collective-permute-start(f32[256,2048]{1,0:T(8,128)} %get-tuple-element.46), channel_id=1, source_target_pairs={{0,1},{1,0},{2,3},{3,2},{4,5},{5,4},{6,7},{7,6}} | collective-permute-start | bytes 6291464 | tf_op jit(solution)/shard_map/ppermute | solution.py:259
  125.9 15.0 %collective-permute-start = (bf16[256,2048]{1,0:T(8,128)(2,1)}, bf16[256,2048]{1,0:T(8,128)(2,1)S(1)}, u32[]{:S(2)}, u32[]{:S(2)}) collective-permute-start(bf16[256,2048]{1,0:T(8,128)(2,1)} %xm_hbm), channel_id=1, source_target_pairs={{0,4},{1,3},{2,6},{3,1},{4,0},{5,7},{6,2},{7,5}} | collective-permute-start | bytes 3145736 | tf_op jit(solution)/shard_map/ppermute | solution.py:263
  129.8 3.4 %copy-start.2 = (f32[256,2048]{1,0:T(8,128)S(1)}, f32[256,2048]{1,0:T(8,128)}, u32[]{:S(2)}) copy-start(f32[256,2048]{1,0:T(8,128)} %get-tuple-element.45) | copy-start | bytes 6291460
  140.9 1.0 copy-start.6
  141.9 2.8 collective-permute-start.7
  142.2 44.7 %collective-permute-start.9 = (f32[256,2048]{1,0:T(8,128)}, f32[256,2048]{1,0:T(8,128)}, u32[]{:S(2)}, u32[]{:S(2)}) collective-permute-start(f32[256,2048]{1,0:T(8,128)} %add.38), channel_id=1, source_target_pairs={{0,2},{1,5},{2,0},{3,7},{4,6},{5,1},{6,4},{7,3}} | collective-permute-start | bytes 6291464 | tf_op jit(solution)/shard_map/ppermute | solution.py:263
  172.7 14.1 %collective-permute-start.8 = (f32[256,2048]{1,0:T(8,128)}, f32[256,2048]{1,0:T(8,128)S(1)}, u32[]{:S(2)}, u32[]{:S(2)}) collective-permute-start(f32[256,2048]{1,0:T(8,128)} %get-tuple-element.49), channel_id=1, source_target_pairs={{0,1},{1,0},{2,3},{3,2},{4,5},{5,4},{6,7},{7,6}} | collective-permute-start | bytes 6291464 | tf_op jit(solution)/shard_map/ppermute | solution.py:259
  182.1 26.8 %collective-permute-start.11 = (f32[256,2048]{1,0:T(8,128)}, f32[256,2048]{1,0:T(8,128)S(1)}, u32[]{:S(2)}, u32[]{:S(2)}) collective-permute-start(f32[256,2048]{1,0:T(8,128)} %add.39), channel_id=1, source_target_pairs={{0,2},{1,5},{2,0},{3,7},{4,6},{5,1},{6,4},{7,3}} | collective-permute-start | bytes 6291464 | tf_op jit(solution)/shard_map/ppermute | solution.py:263
  184.6 24.2 %collective-permute-start.10 = (f32[256,2048]{1,0:T(8,128)}, f32[256,2048]{1,0:T(8,128)S(1)}, u32[]{:S(2)}, u32[]{:S(2)}) collective-permute-start(f32[256,2048]{1,0:T(8,128)} %get-tuple-element.51), channel_id=1, source_target_pairs={{0,1},{1,0},{2,3},{3,2},{4,5},{5,4},{6,7},{7,6}} | collective-permute-start | bytes 6291464 | tf_op jit(solution)/shard_map/ppermute | solution.py:259
  186.8 22.0 %copy-start.5 = (f32[256,2048]{1,0:T(8,128)S(1)}, f32[256,2048]{1,0:T(8,128)}, u32[]{:S(2)}) copy-start(f32[256,2048]{1,0:T(8,128)} %get-tuple-element.50) | copy-start | bytes 6291460
  208.9 1.9 copy-start
  210.8 4.0 %collective-permute-start.12 = (bf16[256,2048]{1,0:T(8,128)(2,1)S(1)}, bf16[256,2048]{1,0:T(8,128)(2,1)}, u32[]{:S(2)}, u32[]{:S(2)}) collective-permute-start(bf16[256,2048]{1,0:T(8,128)(2,1)S(1)} %copy-done), channel_id=1, source_target_pairs={{0,1},{1,0},{2,3},{3,2},{4,5},{5,4},{6,7},{7,6}} | collective-permute-start | bytes 3145736 | tf_op jit(solution)/shard_map/ppermute | solution.py:259
  212.4 41.9 %collective-permute-start.14 = (f32[256,2048]{1,0:T(8,128)}, f32[256,2048]{1,0:T(8,128)}, u32[]{:S(2)}, u32[]{:S(2)}) collective-permute-start(f32[256,2048]{1,0:T(8,128)} %add.36), channel_id=1, source_target_pairs={{0,2},{1,5},{2,0},{3,7},{4,6},{5,1},{6,4},{7,3}} | collective-permute-start | bytes 6291464 | tf_op jit(solution)/shard_map/ppermute | solution.py:263
  251.3 4.4 %collective-permute-start.13 = (f32[256,2048]{1,0:T(8,128)}, f32[256,2048]{1,0:T(8,128)S(1)}, u32[]{:S(2)}, u32[]{:S(2)}) collective-permute-start(f32[256,2048]{1,0:T(8,128)} %get-tuple-element.54), channel_id=1, source_target_pairs={{0,1},{1,0},{2,3},{3,2},{4,5},{5,4},{6,7},{7,6}} | collective-permute-start | bytes 6291464 | tf_op jit(solution)/shard_map/ppermute | solution.py:259
  251.3 48.7 %collective-permute-start.16 = (f32[256,2048]{1,0:T(8,128)}, f32[256,2048]{1,0:T(8,128)S(1)}, u32[]{:S(2)}, u32[]{:S(2)}) collective-permute-start(f32[256,2048]{1,0:T(8,128)} %add.37), channel_id=1, source_target_pairs={{0,2},{1,5},{2,0},{3,7},{4,6},{5,1},{6,4},{7,3}} | collective-permute-start | bytes 6291464 | tf_op jit(solution)/shard_map/ppermute | solution.py:263
  251.4 48.7 %collective-permute-start.15 = (f32[256,2048]{1,0:T(8,128)}, f32[256,2048]{1,0:T(8,128)S(1)}, u32[]{:S(2)}, u32[]{:S(2)}) collective-permute-start(f32[256,2048]{1,0:T(8,128)} %get-tuple-element.56), channel_id=1, source_target_pairs={{0,1},{1,0},{2,3},{3,2},{4,5},{5,4},{6,7},{7,6}} | collective-permute-start | bytes 6291464 | tf_op jit(solution)/shard_map/ppermute | solution.py:259
  251.8 50.1 %collective-permute-start.17 = (f32[256,2048]{1,0:T(8,128)}, f32[256,2048]{1,0:T(8,128)S(1)}, u32[]{:S(2)}, u32[]{:S(2)}) collective-permute-start(f32[256,2048]{1,0:T(8,128)} %add_add_fusion.3), channel_id=1, source_target_pairs={{0,4},{1,3},{2,6},{3,1},{4,0},{5,7},{6,2},{7,5}} | collective-permute-start | bytes 6291464 | tf_op jit(solution)/shard_map/ppermute | solution.py:263
  254.3 67.9 %collective-permute-start.18 = (f32[256,2048]{1,0:T(8,128)}, f32[256,2048]{1,0:T(8,128)}, u32[]{:S(2)}, u32[]{:S(2)}) collective-permute-start(f32[256,2048]{1,0:T(8,128)} %add_add_fusion.2), channel_id=1, source_target_pairs={{0,4},{1,3},{2,6},{3,1},{4,0},{5,7},{6,2},{7,5}} | collective-permute-start | bytes 6291464 | tf_op jit(solution)/shard_map/ppermute | solution.py:263
  255.7 44.4 %copy-start.3 = (f32[256,2048]{1,0:T(8,128)S(1)}, f32[256,2048]{1,0:T(8,128)}, u32[]{:S(2)}) copy-start(f32[256,2048]{1,0:T(8,128)} %get-tuple-element.55) | copy-start | bytes 6291460
  301.9 20.2 %copy-start.4 = (f32[256,2048]{1,0:T(8,128)}, f32[256,2048]{1,0:T(8,128)S(1)}, u32[]{:S(2)}) copy-start(f32[256,2048]{1,0:T(8,128)S(1)} %collective-permute-done.17.f0_ref) | copy-start | bytes 6291460

commit v4 on v3

--- a/solution.py
+++ b/solution.py
@@ -17,7 +17,7 @@
     pos_ref, off_ref, cnt_ref, mine_ref, xm_ref, xo_ref, ids_all, send_sem, recv_sem, xsend, xrecv = refs
     core, me = lax.axis_index("ep"), lax.axis_index("tp")
     blocks, top, t = ids_all.shape
-    e_all = cap_ref.shape[0]
+    e_all = pos_ref.shape[1]
     here = core * chips + me
     mesh_id = pl.DeviceIdType.MESH
     peers = [
@@ -64,7 +64,9 @@
         lax.broadcasted_iota(jnp.int32, (t, t), 0) < lax.broadcasted_iota(jnp.int32, (t, t), 1)
     ).astype(F32).astype(BF16)
     ids = lax.broadcasted_iota(jnp.int32, (e_all, t), 0)
-    cap = jnp.broadcast_to(cap_ref[...], (e_all, t))
+    cap = jnp.zeros((e_all, t), jnp.int32)
+    for e in range(e_all):
+        cap = jnp.where(ids == e, cap_ref[e], cap)
     for c in copies:
         c.wait()
 
@@ -103,7 +105,7 @@
     e_loc, d, ff = w1_hbm.shape
     _, rows, _ = acc.shape
     t = xbuf.shape[1]
-    half_d, half = d // 2, rows // 2
+    half_d = d // 2
     core, me = lax.axis_index("ep"), lax.axis_index("tp")
     chips = pos_ref.shape[0] // 2
     blocks = []
@@ -111,42 +113,44 @@
         turn = jnp.where(c == 0, turns[0], turns[1])
         blocks.append(c * chips + jnp.bitwise_xor(me, turn))
 
-    def chunk(k, e):
-        if isinstance(k, int) and k == 0:
-            return [
-                pltpu.make_async_copy(w1_hbm.at[e, :, pl.ds(0, cut)], w1a, wsem.at[0]),
-                pltpu.make_async_copy(w3_hbm.at[e, :, pl.ds(0, cut)], w3a, wsem.at[1]),
-            ]
-        if isinstance(k, int) and k == 1:
-            return [
-                pltpu.make_async_copy(w1_hbm.at[e, :, pl.ds(cut, ff - cut)], w1b, wsem.at[2]),
-                pltpu.make_async_copy(w3_hbm.at[e, :, pl.ds(cut, ff - cut)], w3b, wsem.at[3]),
-            ]
-        h = k - 2
-        cols = pl.ds(pl.multiple_of(h * half_d, half_d), half_d)
-        return [pltpu.make_async_copy(w2_hbm.at[e, :, cols], w2s.at[h], wsem.at[2 + k])]
-
-    def start(k, e):
-        for c in chunk(k, e):
-            c.start()
-
-    def finish(k, e):
-        for c in chunk(k, e):
+    def first(e):
+        cols, b = pl.ds(0, cut), e % 2
+        return [
+            pltpu.make_async_copy(w1_hbm.at[e, :, cols], w1a.at[b], wsem.at[b, 0]),
+            pltpu.make_async_copy(w3_hbm.at[e, :, cols], w3a.at[b], wsem.at[b, 1]),
+        ]
+
+    def second(e):
+        cols, b = pl.ds(cut, ff - cut), e % 2
+        return [
+            pltpu.make_async_copy(w1_hbm.at[e, :, cols], w1b.at[b], wsem.at[b, 2]),
+            pltpu.make_async_copy(w3_hbm.at[e, :, cols], w3b.at[b], wsem.at[b, 3]),
+        ]
+
+    def third(k):
+        def copies(e):
+            cols, b = pl.ds(pl.multiple_of(k * half_d, half_d), half_d), e % 2
+            return [pltpu.make_async_copy(w2_hbm.at[e, :, cols], w2s.at[b, k], wsem.at[b, 4 + k])]
+
+        return copies
+
+    def arrive(chunk, e):
+        for c in chunk(e):
             c.wait()
 
-    def following(k, e):
         @pl.when(e + 1 < e_loc)
         def _():
-            start(k, e + 1)
+            for c in chunk(e + 1):
+                c.start()
 
     def out_copies(h):
         cols = pl.ds(h * half_d, half_d)
-        return [
-            pltpu.make_async_copy(
-                acc.at[1 - i // 2, pl.ds((i % 2) * half, half), cols], outs[i].at[:, cols], osem.at[h, i]
-            )
-            for i in range(4)
-        ]
+        copies = []
+        for i in range(4):
+            size = outs[i].shape[0]
+            part = pl.ds(0 if i % 2 == 0 else rows - size, size)
+            copies.append(pltpu.make_async_copy(acc.at[1 - i // 2, part, cols], outs[i].at[:, cols], osem.at[h, i]))
+        return copies
 
     tokens = [
         pltpu.make_async_copy(xm_hbm, xbuf.at[0], xsem.at[0]),
@@ -154,8 +158,9 @@
     ]
     for c in tokens:
         c.start()
-    for k in range(4):
-        start(k, 0)
+    for chunk in (first, second, third(0), third(1)):
+        for c in chunk(0):
+            c.start()
     acc[...] = jnp.zeros_like(acc)
     for c in tokens:
         c.wait()
@@ -181,21 +186,19 @@
                 parts.append(jnp.dot(hit, xbuf[s], preferred_element_type=F32))
             xs = jnp.concatenate(parts, axis=0).astype(BF16)
             hs = []
-            for k, (wa, wb) in enumerate(((w1a, w3a), (w1b, w3b))):
-                finish(k, e)
-                h1 = jnp.dot(xs, wa[...], preferred_element_type=F32)
-                h3 = jnp.dot(xs, wb[...], preferred_element_type=F32)
+            for chunk, wa, wb in ((first, w1a, w3a), (second, w1b, w3b)):
+                arrive(chunk, e)
+                h1 = jnp.dot(xs, wa[e % 2], preferred_element_type=F32)
+                h3 = jnp.dot(xs, wb[e % 2], preferred_element_type=F32)
                 hs.append((jax.nn.silu(h1) * h3).astype(BF16))
-                following(k, e)
             h = jnp.concatenate(hs, axis=1)
 
             def project(k, carry):
-                finish(2 + k, e)
-                p = jnp.dot(h, w2s[k], preferred_element_type=F32)
+                arrive(third(k), e)
+                p = jnp.dot(h, w2s[e % 2, k], preferred_element_type=F32)
                 cols = pl.ds(pl.multiple_of(k * half_d, half_d), half_d)
                 for s in range(2):
                     acc[s, pl.ds(bases[s], m), cols] += p[s * m : (s + 1) * m]
-                following(2 + k, e)
                 last(k)
                 return carry
 
@@ -203,10 +206,9 @@
 
         @pl.when(need == 0)
         def _():
-            for k in range(4):
-                finish(k, e)
-                following(k, e)
-                last(k - 2)
+            for chunk in (first, second, third(0), third(1)):
+                arrive(chunk, e)
+            last(0)
 
         lo = 0
         for m in sizes:
@@ -221,17 +223,18 @@
         c.wait()
 
 
-def _combine_kernel(mine_ref, s0_ref, s1_ref, f0_ref, f1_ref, out_ref, hit):
+def _combine_kernel(first, mine_ref, sum_ref, last_ref, *refs):
+    out_ref, hit = refs[-2:]
     top, t, rows = hit.shape
 
     @pl.when(pl.program_id(0) == 0)
     def _():
-        row = lax.broadcasted_iota(jnp.int32, (t, rows), 1)
+        row = lax.broadcasted_iota(jnp.int32, (t, rows), 1) + first
         for j in range(top):
             hit[j] = (row == mine_ref[:, j : j + 1].astype(jnp.int32)).astype(F32).astype(BF16)
 
-    y = jnp.concatenate([s0_ref[...] + f0_ref[...], s1_ref[...] + f1_ref[...]], axis=0).astype(BF16)
-    total = None
+    y = (sum_ref[...] + last_ref[...]).astype(BF16)
+    total = refs[0][...] if len(refs) == 3 else None
     for j in range(top):
         part = jnp.dot(hit[j], y, preferred_element_type=F32) * mine_ref[:, top + j : top + j + 1]
         total = part if total is None else total + part
@@ -251,7 +254,6 @@
         e_loc, _, ff = w1.shape
         c = (5 * top * t_loc // (2 * e_all) + 7) // 8 * 8
         rows = top * t_loc
-        half = rows // 2
         cut = 512
         blocks = 2 * chips
 
@@ -277,7 +279,7 @@
                 jax.ShapeDtypeStruct((t_loc, d), BF16),
                 jax.ShapeDtypeStruct((t_loc, d), BF16),
             ],
-            in_specs=[vmem] * 3 + [anym],
+            in_specs=[vmem, vmem, smem, anym],
             out_specs=[vmem] * 4 + [anym] * 2,
             scratch_shapes=[
                 pltpu.VMEM((blocks, top, t_loc), jnp.int32),
@@ -288,25 +290,25 @@
             ],
             compiler_params=pltpu.CompilerParams(collective_id=0, has_side_effects=True, vmem_limit_bytes=VMEM_BYTES),
             name="route",
-        )(idx.T, g.T, cap[:, None], x)
+        )(idx.T, g.T, cap, x)
 
         sizes = (64, (c + 7 + 7) // 8 * 8)
 
-        def stage(turns, mine, other, sizes=sizes):
+        def stage(turns, mine, other, split):
             return pl.pallas_call(
                 functools.partial(_expert_kernel, turns, sizes, cut),
-                out_shape=[jax.ShapeDtypeStruct((half, d), F32)] * 4,
+                out_shape=[jax.ShapeDtypeStruct((n, d), F32) for n in split * 2],
                 in_specs=[smem, smem, vmem] + [anym] * 5,
                 out_specs=[anym] * 4,
                 scratch_shapes=[
                     pltpu.VMEM((2, rows, d), F32),
                     pltpu.VMEM((2, t_loc, d), BF16),
-                    pltpu.VMEM((d, cut), BF16),
-                    pltpu.VMEM((d, cut), BF16),
-                    pltpu.VMEM((d, ff - cut), BF16),
-                    pltpu.VMEM((d, ff - cut), BF16),
-                    pltpu.VMEM((2, ff, d // 2), BF16),
-                    pltpu.SemaphoreType.DMA((6,)),
+                    pltpu.VMEM((2, d, cut), BF16),
+                    pltpu.VMEM((2, d, cut), BF16),
+                    pltpu.VMEM((2, d, ff - cut), BF16),
+                    pltpu.VMEM((2, d, ff - cut), BF16),
+                    pltpu.VMEM((2, 2, ff, d // 2), BF16),
+                    pltpu.SemaphoreType.DMA((2, 6)),
                     pltpu.SemaphoreType.DMA((2, 4)),
                     pltpu.SemaphoreType.DMA((2,)),
                 ],
@@ -325,26 +327,35 @@
 
         x_next = after(x, pos)
         x_d, x_f = shift(x_next, (3, 3)), shift(x_next, back)
-        near = merge(stage(out, xn_mine, xn_other))
+        early, late = (rows // 4, rows - rows // 4), (rows - rows // 4, rows // 4)
+        near = merge(stage(out, xn_mine, xn_other, early))
         x_d = after(x_d, *near)
         near = [shift(a, out) for a in near]
-        diag = merge(stage((3, 3), x_d, swap(x_d)))
+        diag = merge(stage((3, 3), x_d, swap(x_d), late))
         x_f = after(x_f, *diag)
         via = [shift(a, out) for a in diag]
-        far = merge(stage(back, x_f, swap(x_f)), via)
+        far = merge(stage(back, x_f, swap(x_f), late), via)
         x_o = after(x, *far)
         far = [shift(a, back) for a in far]
-        sums = merge(stage((0, 0), x_o, swap(x_o)), near)
+        near = jnp.concatenate(near, axis=0)
+        near = [near[: late[0]], near[late[0] :]]
+        sums = merge(stage((0, 0), x_o, swap(x_o), late), near)
         width = d // 4
-        return pl.pallas_call(
-            _combine_kernel,
-            out_shape=jax.ShapeDtypeStruct((t_loc, d), BF16),
-            grid=(4,),
-            in_specs=[pl.BlockSpec((t_loc, 8), lambda i: (0, 0))] + [pl.BlockSpec((half, width), lambda i: (0, i))] * 4,
-            out_specs=pl.BlockSpec((t_loc, width), lambda i: (0, i)),
-            scratch_shapes=[pltpu.VMEM((top, t_loc, rows), BF16)],
-            name="combine",
-        )(mine, *sums, *far)
+        total = None
+        for q in range(2):
+            table = pl.BlockSpec((t_loc, 8), lambda i: (0, 0))
+            part = pl.BlockSpec((late[q], width), lambda i: (0, i))
+            wide = pl.BlockSpec((t_loc, width), lambda i: (0, i))
+            total = pl.pallas_call(
+                functools.partial(_combine_kernel, q * late[0]),
+                out_shape=jax.ShapeDtypeStruct((t_loc, d), (F32, BF16)[q]),
+                grid=(4,),
+                in_specs=[table, part, part] + [wide] * q,
+                out_specs=wide,
+                scratch_shapes=[pltpu.VMEM((top, t_loc, late[q]), BF16)],
+                cost_estimate=pl.CostEstimate(flops=8 * t_loc * late[q] * d, bytes_accessed=16 * late[q] * d, transcendentals=0),
+            )(mine, sums[q], far[q], *([total] * q))
+        return total
 
     rows = P(("ep", "tp"), None)
     return jax.shard_map(

time: 329 us -> 310 us (0.942)
  waiting for transfers between devices: 112 us -> 87 us
  Pallas kernels: 156 us -> 160 us
    ppermute x8, waiting for transfers between devices: 103 us -> 69.9 us  [shift(): return lax.ppermute(a, ('tp', 'ep'), pairs)]
    ppermute x11, waiting for transfers between devices: 8.72 us -> 17.1 us  [swap(): return lax.ppermute(a, 'ep', [(0, 1), (1, 0)])]
    pallas_call x1 -> x2, Pallas kernels: 6.01 us -> 10.4 us  [layer(): pl.pallas_call(functools.partial(_combine_kernel, q * late[0]), out_shape...]
  transfers between devices with their start and end apart: 19 -> 19, of which waited for: 10 -> 12; matrix products, arithmetic and copies ran while one was open for 6% -> 6% of each run, Pallas kernels for 20% -> 23%
where the time goes in v4:
time: 310 us; the launch traced here: 309 us
  Pallas kernels  160 us (52%)
  waiting for transfers between devices  87 us (28%)
  starting transfers between devices  35.3 us (11%)
  other arithmetic  23.2 us (7%)
  local copies, waits for them, and re-layouts  3.66 us (1%)
    pallas_call x4, Pallas kernels, stage(): pl.pallas_call(functools.partial(_expert_kernel, turns, sizes, cut), out_...  128 us
    ppermute x8, waiting for transfers between devices, shift(): return lax.ppermute(a, ('tp', 'ep'), pairs)  69.9 us
    ppermute x11, starting transfers between devices, swap(): return lax.ppermute(a, 'ep', [(0, 1), (1, 0)])  21.4 us
    pallas_call x1, Pallas kernels, layer(): pl.pallas_call(functools.partial(_route_kernel, chips, out), out_shape=[j...  21.3 us
    ppermute x11, waiting for transfers between devices, swap(): return lax.ppermute(a, 'ep', [(0, 1), (1, 0)])  17.1 us
    ppermute x8, starting transfers between devices, shift(): return lax.ppermute(a, ('tp', 'ep'), pairs)  13.9 us
    add x4, other arithmetic, merge(): functools.reduce(jnp.add, [m[q] for m in more], parts[2 + q] + other)  13.8 us
    pallas_call x2, Pallas kernels, layer(): pl.pallas_call(functools.partial(_combine_kernel, q * late[0]), out_shape...  10.4 us
  transfers between devices with their start and end apart: 19, of which 12 were waited for; matrix products, arithmetic and copies ran while one was open for 6% of the time, Pallas kernels for 23%

profile of v4, /device:TPU:0, one launch (start us, length us, event | category | flops | bytes accessed | tf_op | source)
XLA Modules:
  0.0 308.9 jit_solution(9969265593217354074)
XLA Ops:
  0.0 21.3 %route.1 = (s32[8,8,256]{2,1,0:T(8,128)}, s32[8,8,128]{2,1,0:T(8,128)}, s32[8,8,128]{2,1,0:T(8,128)}, f32[256,8]{1,0:T(8,128)}, bf16[256,2048]{1,0:T(8,128)(2,1)}, /*index=5*/bf16[256,2048]{1,0:T(8,128)(2,1)}) custom-call(s32[2,256]{1,0:T(2,128)} %bitcast.2, f32[2,256]{1,0:T(2,128)} %bitcast.3, s32[8]{0:T(128)} %cap_ref.1, bf16[256,2048]{1,0:T(8,128)(2,1)} %xm_hbm), custom_call_target="tpu_custom_call" | custom-call | tf_op jit(solution)/shard_map/route/pallas_call | solution.py:272
  21.3 33.2 %shard_map.73 = (f32[128,2048]{1,0:T(8,128)}, f32[384,2048]{1,0:T(8,128)}, f32[128,2048]{1,0:T(8,128)}, f32[384,2048]{1,0:T(8,128)}) custom-call(s32[8,8,128]{2,1,0:T(8,128)} %get-tuple-element.32.off_ref, s32[8,8,128]{2,1,0:T(8,128)} %get-tuple-element.33.cnt_ref, s32[8,8,256]{2,1,0:T(8,128)} %get-tuple-element.34.pos_ref, ...), custom_call_target="tpu_custom_call" | custom-call | flops 8858370048 | bytes 77594624 | tf_op jit(solution)/shard_map/pallas_call | solution.py:298
  54.5 0.5 collective-permute-start.3
  55.0 0.1 collective-permute-start.2
  55.0 5.3 %collective-permute-start.1 = (bf16[256,2048]{1,0:T(8,128)(2,1)}, bf16[256,2048]{1,0:T(8,128)(2,1)S(1)}, u32[]{:S(2)}, u32[]{:S(2)}) collective-permute-start(bf16[256,2048]{1,0:T(8,128)(2,1)} %xm_hbm), channel_id=1, source_target_pairs={{0,6},{1,7},{2,4},{3,5},{4,2},{5,3},{6,0},{7,1}} | collective-permute-start | bytes 3145736 | tf_op jit(solution)/shard_map/ppermute | solution.py:265
  60.4 1.6 collective-permute-done.2
  62.0 2.3 add.36
  64.3 2.3 add.37
  66.6 17.8 %collective-permute-done.1.xm_hbm = bf16[256,2048]{1,0:T(8,128)(2,1)S(1)} collective-permute-done((bf16[256,2048]{1,0:T(8,128)(2,1)}, bf16[256,2048]{1,0:T(8,128)(2,1)S(1)}, u32[]{:S(2)}, u32[]{:S(2)}) %collective-permute-start.1) | collective-permute-done | bytes 1048608 | tf_op jit(solution)/shard_map/ppermute | solution.py:265
  84.4 1.0 copy-done.7
  85.3 2.8 collective-permute-done.4.xo_hbm
  88.1 30.5 %shard_map.74 = (f32[384,2048]{1,0:T(8,128)}, f32[128,2048]{1,0:T(8,128)}, f32[384,2048]{1,0:T(8,128)}, f32[128,2048]{1,0:T(8,128)}) custom-call(s32[8,8,128]{2,1,0:T(8,128)} %get-tuple-element.32.off_ref, s32[8,8,128]{2,1,0:T(8,128)} %get-tuple-element.33.cnt_ref, s32[8,8,256]{2,1,0:T(8,128)} %get-tuple-element.34.pos_ref, bf16[256,2048]{1,0:T(8,128)(2,1)} %copy-done.7, ...), custom_call_target="tpu_custom_call" | custom-call | flops 8858370048 | bytes 77594624 | tf_op jit(solution)/shard_map/pallas_call | solution.py:298
  118.7 6.1 %collective-permute-start.5 = (f32[384,2048]{1,0:T(8,128)}, f32[384,2048]{1,0:T(8,128)S(1)}, u32[]{:S(2)}, u32[]{:S(2)}) collective-permute-start(f32[384,2048]{1,0:T(8,128)} %get-tuple-element.44), channel_id=1, source_target_pairs={{0,1},{1,0},{2,3},{3,2},{4,5},{5,4},{6,7},{7,6}} | collective-permute-start | bytes 9437192 | tf_op jit(solution)/shard_map/ppermute | solution.py:261
  124.8 0.0 collective-permute-start.6
  124.8 1.5 collective-permute-start
  126.3 5.5 %collective-permute-done.6 = f32[128,2048]{1,0:T(8,128)S(1)} collective-permute-done((f32[128,2048]{1,0:T(8,128)}, f32[128,2048]{1,0:T(8,128)S(1)}, u32[]{:S(2)}, u32[]{:S(2)}) %collective-permute-start.6) | collective-permute-done | bytes 1048608 | tf_op jit(solution)/shard_map/ppermute | solution.py:261
  131.8 2.3 add.39
  134.1 2.4 add.38
  136.5 3.4 %collective-permute-done.xm_hbm = bf16[256,2048]{1,0:T(8,128)(2,1)S(1)} collective-permute-done((bf16[256,2048]{1,0:T(8,128)(2,1)}, bf16[256,2048]{1,0:T(8,128)(2,1)S(1)}, u32[]{:S(2)}, u32[]{:S(2)}) %collective-permute-start) | collective-permute-done | bytes 1048608 | tf_op jit(solution)/shard_map/ppermute | solution.py:265
  139.9 1.0 copy-done.6
  140.8 0.1 collective-permute-start.7
  140.9 2.2 collective-permute-start.9
  143.2 0.5 collective-permute-done.7.xo_hbm
  143.6 27.7 %shard_map.75 = (f32[384,2048]{1,0:T(8,128)}, f32[128,2048]{1,0:T(8,128)}, f32[384,2048]{1,0:T(8,128)}, f32[128,2048]{1,0:T(8,128)}) custom-call(s32[8,8,128]{2,1,0:T(8,128)} %get-tuple-element.32.off_ref, s32[8,8,128]{2,1,0:T(8,128)} %get-tuple-element.33.cnt_ref, s32[8,8,256]{2,1,0:T(8,128)} %get-tuple-element.34.pos_ref, bf16[256,2048]{1,0:T(8,128)(2,1)} %copy-done.6, ...), custom_call_target="tpu_custom_call" | custom-call | flops 8858370048 | bytes 77594624 | tf_op jit(solution)/shard_map/pallas_call | solution.py:298
  171.4 9.5 %collective-permute-start.8 = (f32[384,2048]{1,0:T(8,128)}, f32[384,2048]{1,0:T(8,128)S(1)}, u32[]{:S(2)}, u32[]{:S(2)}) collective-permute-start(f32[384,2048]{1,0:T(8,128)} %get-tuple-element.49), channel_id=1, source_target_pairs={{0,1},{1,0},{2,3},{3,2},{4,5},{5,4},{6,7},{7,6}} | collective-permute-start | bytes 9437192 | tf_op jit(solution)/shard_map/ppermute | solution.py:261
  180.9 2.3 collective-permute-start.11
  183.2 2.6 collective-permute-start.10
  185.8 10.4 %collective-permute-done.11 = f32[128,2048]{1,0:T(8,128)S(1)} collective-permute-done((f32[128,2048]{1,0:T(8,128)}, f32[128,2048]{1,0:T(8,128)S(1)}, u32[]{:S(2)}, u32[]{:S(2)}) %collective-permute-start.11) | collective-permute-done | bytes 1048608 | tf_op jit(solution)/shard_map/ppermute | solution.py:265
  196.2 2.4 add_add_fusion.1
  198.7 4.6 %add_add_fusion = f32[384,2048]{1,0:T(8,128)} fusion(f32[384,2048]{1,0:T(8,128)} %collective-permute-done.9, f32[384,2048]{1,0:T(8,128)S(1)} %copy-done.2, f32[384,2048]{1,0:T(8,128)S(1)} %collective-permute-done.8), kind=kLoop, calls=%fused_computation.2 | loop fusion | flops 1572864 | bytes 12582912 | tf_op jit(solution)/shard_map/add | solution.py:325
  203.2 2.0 collective-permute-start.12
  205.2 0.1 collective-permute-start.14
  205.3 2.4 collective-permute-done.12.xo_hbm
  207.6 36.5 %shard_map.76 = (f32[384,2048]{1,0:T(8,128)}, f32[128,2048]{1,0:T(8,128)}, f32[384,2048]{1,0:T(8,128)}, f32[128,2048]{1,0:T(8,128)}) custom-call(s32[8,8,128]{2,1,0:T(8,128)} %get-tuple-element.32.off_ref, s32[8,8,128]{2,1,0:T(8,128)} %get-tuple-element.33.cnt_ref, s32[8,8,256]{2,1,0:T(8,128)} %get-tuple-element.34.pos_ref, bf16[256,2048]{1,0:T(8,128)(2,1)} %xm_hbm, ...), custom_call_target="tpu_custom_call" | custom-call | flops 8858370048 | bytes 77594624 | tf_op jit(solution)/shard_map/pallas_call | solution.py:298
  244.1 0.0 collective-permute-start.16
  244.2 0.0 collective-permute-start.18
  244.2 0.5 collective-permute-start.13
  244.7 2.4 collective-permute-start.17
  247.1 0.1 collective-permute-start.15
  247.1 4.4 %collective-permute-done.13 = f32[128,2048]{1,0:T(8,128)S(1)} collective-permute-done((f32[128,2048]{1,0:T(8,128)}, f32[128,2048]{1,0:T(8,128)S(1)}, u32[]{:S(2)}, u32[]{:S(2)}) %collective-permute-start.13) | collective-permute-done | bytes 1048608 | tf_op jit(solution)/shard_map/ppermute | solution.py:261
  251.5 2.7 slice_add_fusion.sum_ref
  254.2 17.1 %collective-permute-done.17 = f32[128,2048]{1,0:T(8,128)S(1)} collective-permute-done((f32[128,2048]{1,0:T(8,128)}, f32[128,2048]{1,0:T(8,128)S(1)}, u32[]{:S(2)}, u32[]{:S(2)}) %collective-permute-start.17) | collective-permute-done | bytes 1048608 | tf_op jit(solution)/shard_map/ppermute | solution.py:265
  271.3 4.1 %fusion.sum_ref = f32[384,2048]{1,0:T(8,128)} fusion(f32[384,2048]{1,0:T(8,128)} %collective-permute-done.14, f32[128,2048]{1,0:T(8,128)S(1)} %collective-permute-done.17, f32[384,2048]{1,0:T(8,128)S(1)} %copy-done.5, f32[384,2048]{1,0:T(8,128)S(1)} %collective-permute-done.16), kind=kLoop, calls=%fused_computation.1 | loop fusion | flops 2359296 | bytes 13631488 | tf_op jit(solution)/shard_map/add | solution.py:325
  275.4 17.4 %collective-permute-done.18.last_ref = f32[384,2048]{1,0:T(8,128)S(1)} collective-permute-done((f32[384,2048]{1,0:T(8,128)}, f32[384,2048]{1,0:T(8,128)S(1)}, u32[]{:S(2)}, u32[]{:S(2)}) %collective-permute-start.18) | collective-permute-done | bytes 3145760 | tf_op jit(solution)/shard_map/ppermute | solution.py:265
  292.8 1.7 copy-done.1
  294.5 5.7 %shard_map.77.refs_0_ = f32[256,2048]{1,0:T(8,128)} custom-call(f32[256,8]{1,0:T(8,128)} %get-tuple-element.31.mine_ref, f32[384,2048]{1,0:T(8,128)} %fusion.sum_ref, f32[384,2048]{1,0:T(8,128)} %copy-done.1), custom_call_target="tpu_custom_call" | custom-call | flops 1610612736 | bytes 12582912 | tf_op jit(solution)/shard_map/pallas_call | solution.py:349
  300.2 3.9 %collective-permute-done.15.last_ref = f32[128,2048]{1,0:T(8,128)} collective-permute-done((f32[128,2048]{1,0:T(8,128)}, f32[128,2048]{1,0:T(8,128)}, u32[]{:S(2)}, u32[]{:S(2)}) %collective-permute-start.15) | collective-permute-done | bytes 1048608 | tf_op jit(solution)/shard_map/ppermute | solution.py:265
  304.2 4.7 %shard_map.78 = bf16[256,2048]{1,0:T(8,128)(2,1)} custom-call(f32[256,8]{1,0:T(8,128)} %get-tuple-element.31.mine_ref, f32[128,2048]{1,0:T(8,128)} %slice_add_fusion.sum_ref, f32[128,2048]{1,0:T(8,128)} %collective-permute-done.15.last_ref, f32[256,2048]{1,0:T(8,128)} %shard_map.77.refs_0_), custom_call_target="tpu_custom_call" | custom-call | flops 536870912 | bytes 4194304 | tf_op jit(solution)/shard_map/pallas_call | solution.py:349
  (21 shorter events, 0.0 us)
Async XLA Ops:
  54.5 9.8 %copy-start.3 = (f32[384,2048]{1,0:T(8,128)S(1)}, f32[384,2048]{1,0:T(8,128)}, u32[]{:S(2)}) copy-start(f32[384,2048]{1,0:T(8,128)} %get-tuple-element.40) | copy-start | bytes 9437188
  54.5 9.8 %collective-permute-start.3 = (f32[384,2048]{1,0:T(8,128)}, f32[384,2048]{1,0:T(8,128)S(1)}, u32[]{:S(2)}, u32[]{:S(2)}) collective-permute-start(f32[384,2048]{1,0:T(8,128)} %get-tuple-element.41), channel_id=1, source_target_pairs={{0,1},{1,0},{2,3},{3,2},{4,5},{5,4},{6,7},{7,6}} | collective-permute-start | bytes 9437192 | tf_op jit(solution)/shard_map/ppermute | solution.py:261
  55.0 7.0 %collective-permute-start.2 = (f32[128,2048]{1,0:T(8,128)}, f32[128,2048]{1,0:T(8,128)S(1)}, u32[]{:S(2)}, u32[]{:S(2)}) collective-permute-start(f32[128,2048]{1,0:T(8,128)} %get-tuple-element.39), channel_id=1, source_target_pairs={{0,1},{1,0},{2,3},{3,2},{4,5},{5,4},{6,7},{7,6}} | collective-permute-start | bytes 3145736 | tf_op jit(solution)/shard_map/ppermute | solution.py:261
  55.0 29.3 %collective-permute-start.1 = (bf16[256,2048]{1,0:T(8,128)(2,1)}, bf16[256,2048]{1,0:T(8,128)(2,1)S(1)}, u32[]{:S(2)}, u32[]{:S(2)}) collective-permute-start(bf16[256,2048]{1,0:T(8,128)(2,1)} %xm_hbm), channel_id=1, source_target_pairs={{0,6},{1,7},{2,4},{3,5},{4,2},{5,3},{6,0},{7,1}} | collective-permute-start | bytes 3145736 | tf_op jit(solution)/shard_map/ppermute | solution.py:265
  84.4 1.0 copy-start.7
  85.3 2.8 collective-permute-start.4
  118.6 15.5 %copy-start.4 = (f32[384,2048]{1,0:T(8,128)S(1)}, f32[384,2048]{1,0:T(8,128)}, u32[]{:S(2)}) copy-start(f32[384,2048]{1,0:T(8,128)} %get-tuple-element.43) | copy-start | bytes 9437188
  118.7 15.5 %collective-permute-start.5 = (f32[384,2048]{1,0:T(8,128)}, f32[384,2048]{1,0:T(8,128)S(1)}, u32[]{:S(2)}, u32[]{:S(2)}) collective-permute-start(f32[384,2048]{1,0:T(8,128)} %get-tuple-element.44), channel_id=1, source_target_pairs={{0,1},{1,0},{2,3},{3,2},{4,5},{5,4},{6,7},{7,6}} | collective-permute-start | bytes 9437192 | tf_op jit(solution)/shard_map/ppermute | solution.py:261
  124.8 7.0 %collective-permute-start.6 = (f32[128,2048]{1,0:T(8,128)}, f32[128,2048]{1,0:T(8,128)S(1)}, u32[]{:S(2)}, u32[]{:S(2)}) collective-permute-start(f32[128,2048]{1,0:T(8,128)} %get-tuple-element.46), channel_id=1, source_target_pairs={{0,1},{1,0},{2,3},{3,2},{4,5},{5,4},{6,7},{7,6}} | collective-permute-start | bytes 3145736 | tf_op jit(solution)/shard_map/ppermute | solution.py:261
  124.8 15.0 %collective-permute-start = (bf16[256,2048]{1,0:T(8,128)(2,1)}, bf16[256,2048]{1,0:T(8,128)(2,1)S(1)}, u32[]{:S(2)}, u32[]{:S(2)}) collective-permute-start(bf16[256,2048]{1,0:T(8,128)(2,1)} %xm_hbm), channel_id=1, source_target_pairs={{0,4},{1,3},{2,6},{3,1},{4,0},{5,7},{6,2},{7,5}} | collective-permute-start | bytes 3145736 | tf_op jit(solution)/shard_map/ppermute | solution.py:265
  139.8 1.0 copy-start.6
  140.8 2.8 collective-permute-start.7
  140.9 57.7 %collective-permute-start.9 = (f32[384,2048]{1,0:T(8,128)}, f32[384,2048]{1,0:T(8,128)}, u32[]{:S(2)}, u32[]{:S(2)}) collective-permute-start(f32[384,2048]{1,0:T(8,128)} %add.38), channel_id=1, source_target_pairs={{0,2},{1,5},{2,0},{3,7},{4,6},{5,1},{6,4},{7,3}} | collective-permute-start | bytes 9437192 | tf_op jit(solution)/shard_map/ppermute | solution.py:265
  171.4 27.3 %copy-start.2 = (f32[384,2048]{1,0:T(8,128)S(1)}, f32[384,2048]{1,0:T(8,128)}, u32[]{:S(2)}) copy-start(f32[384,2048]{1,0:T(8,128)} %get-tuple-element.48) | copy-start | bytes 9437188
  171.4 27.2 %collective-permute-start.8 = (f32[384,2048]{1,0:T(8,128)}, f32[384,2048]{1,0:T(8,128)S(1)}, u32[]{:S(2)}, u32[]{:S(2)}) collective-permute-start(f32[384,2048]{1,0:T(8,128)} %get-tuple-element.49), channel_id=1, source_target_pairs={{0,1},{1,0},{2,3},{3,2},{4,5},{5,4},{6,7},{7,6}} | collective-permute-start | bytes 9437192 | tf_op jit(solution)/shard_map/ppermute | solution.py:261
  180.9 15.3 %collective-permute-start.11 = (f32[128,2048]{1,0:T(8,128)}, f32[128,2048]{1,0:T(8,128)S(1)}, u32[]{:S(2)}, u32[]{:S(2)}) collective-permute-start(f32[128,2048]{1,0:T(8,128)} %add.39), channel_id=1, source_target_pairs={{0,2},{1,5},{2,0},{3,7},{4,6},{5,1},{6,4},{7,3}} | collective-permute-start | bytes 3145736 | tf_op jit(solution)/shard_map/ppermute | solution.py:265
  183.2 13.0 %collective-permute-start.10 = (f32[128,2048]{1,0:T(8,128)}, f32[128,2048]{1,0:T(8,128)S(1)}, u32[]{:S(2)}, u32[]{:S(2)}) collective-permute-start(f32[128,2048]{1,0:T(8,128)} %get-tuple-element.51), channel_id=1, source_target_pairs={{0,1},{1,0},{2,3},{3,2},{4,5},{5,4},{6,7},{7,6}} | collective-permute-start | bytes 3145736 | tf_op jit(solution)/shard_map/ppermute | solution.py:261
  198.6 4.6 %copy-start = (bf16[256,2048]{1,0:T(8,128)(2,1)S(1)}, bf16[256,2048]{1,0:T(8,128)(2,1)}, u32[]{:S(2)}) copy-start(bf16[256,2048]{1,0:T(8,128)(2,1)} %xm_hbm) | copy-start | bytes 3145732
  203.2 4.4 %collective-permute-start.12 = (bf16[256,2048]{1,0:T(8,128)(2,1)S(1)}, bf16[256,2048]{1,0:T(8,128)(2,1)}, u32[]{:S(2)}, u32[]{:S(2)}) collective-permute-start(bf16[256,2048]{1,0:T(8,128)(2,1)S(1)} %copy-done), channel_id=1, source_target_pairs={{0,1},{1,0},{2,3},{3,2},{4,5},{5,4},{6,7},{7,6}} | collective-permute-start | bytes 3145736 | tf_op jit(solution)/shard_map/ppermute | solution.py:261
  205.2 41.9 %collective-permute-start.14 = (f32[384,2048]{1,0:T(8,128)}, f32[384,2048]{1,0:T(8,128)}, u32[]{:S(2)}, u32[]{:S(2)}) collective-permute-start(f32[384,2048]{1,0:T(8,128)} %add.37), channel_id=1, source_target_pairs={{0,2},{1,5},{2,0},{3,7},{4,6},{5,1},{6,4},{7,3}} | collective-permute-start | bytes 9437192 | tf_op jit(solution)/shard_map/ppermute | solution.py:265
  244.1 27.2 %copy-start.5 = (f32[384,2048]{1,0:T(8,128)S(1)}, f32[384,2048]{1,0:T(8,128)}, u32[]{:S(2)}) copy-start(f32[384,2048]{1,0:T(8,128)} %get-tuple-element.55) | copy-start | bytes 9437188
  244.1 27.2 %collective-permute-start.16 = (f32[384,2048]{1,0:T(8,128)}, f32[384,2048]{1,0:T(8,128)S(1)}, u32[]{:S(2)}, u32[]{:S(2)}) collective-permute-start(f32[384,2048]{1,0:T(8,128)} %get-tuple-element.56), channel_id=1, source_target_pairs={{0,1},{1,0},{2,3},{3,2},{4,5},{5,4},{6,7},{7,6}} | collective-permute-start | bytes 9437192 | tf_op jit(solution)/shard_map/ppermute | solution.py:261
  244.2 48.7 %collective-permute-start.18 = (f32[384,2048]{1,0:T(8,128)}, f32[384,2048]{1,0:T(8,128)S(1)}, u32[]{:S(2)}, u32[]{:S(2)}) collective-permute-start(f32[384,2048]{1,0:T(8,128)} %add_add_fusion), channel_id=1, source_target_pairs={{0,4},{1,3},{2,6},{3,1},{4,0},{5,7},{6,2},{7,5}} | collective-permute-start | bytes 9437192 | tf_op jit(solution)/shard_map/ppermute | solution.py:265
  244.2 7.3 %collective-permute-start.13 = (f32[128,2048]{1,0:T(8,128)}, f32[128,2048]{1,0:T(8,128)S(1)}, u32[]{:S(2)}, u32[]{:S(2)}) collective-permute-start(f32[128,2048]{1,0:T(8,128)} %get-tuple-element.54), channel_id=1, source_target_pairs={{0,1},{1,0},{2,3},{3,2},{4,5},{5,4},{6,7},{7,6}} | collective-permute-start | bytes 3145736 | tf_op jit(solution)/shard_map/ppermute | solution.py:261
  244.7 26.6 %collective-permute-start.17 = (f32[128,2048]{1,0:T(8,128)}, f32[128,2048]{1,0:T(8,128)S(1)}, u32[]{:S(2)}, u32[]{:S(2)}) collective-permute-start(f32[128,2048]{1,0:T(8,128)} %add.36), channel_id=1, source_target_pairs={{0,2},{1,5},{2,0},{3,7},{4,6},{5,1},{6,4},{7,3}} | collective-permute-start | bytes 3145736 | tf_op jit(solution)/shard_map/ppermute | solution.py:265
  247.1 57.1 %collective-permute-start.15 = (f32[128,2048]{1,0:T(8,128)}, f32[128,2048]{1,0:T(8,128)}, u32[]{:S(2)}, u32[]{:S(2)}) collective-permute-start(f32[128,2048]{1,0:T(8,128)} %add_add_fusion.1), channel_id=1, source_target_pairs={{0,4},{1,3},{2,6},{3,1},{4,0},{5,7},{6,2},{7,5}} | collective-permute-start | bytes 3145736 | tf_op jit(solution)/shard_map/ppermute | solution.py:265
  292.8 1.7 copy-start.1

commit v5 on v4

--- a/solution.py
+++ b/solution.py
@@ -14,7 +14,7 @@
 
 
 def _route_kernel(chips, turns, idx_ref, g_ref, cap_ref, x_ref, *refs):
-    pos_ref, off_ref, cnt_ref, mine_ref, xm_ref, xo_ref, ids_all, send_sem, recv_sem, xsend, xrecv = refs
+    pos_ref, table_ref, mine_ref, xm_ref, xo_ref, ids_all, send_sem, recv_sem, xsend, xrecv = refs
     core, me = lax.axis_index("ep"), lax.axis_index("tp")
     blocks, top, t = ids_all.shape
     e_all = pos_ref.shape[1]
@@ -67,6 +67,7 @@
     cap = jnp.zeros((e_all, t), jnp.int32)
     for e in range(e_all):
         cap = jnp.where(ids == e, cap_ref[e], cap)
+    sub, lane = (lax.broadcasted_iota(jnp.int32, (e_all, 128), i) for i in range(2))
     for c in copies:
         c.wait()
 
@@ -79,8 +80,8 @@
         first = jnp.zeros_like(count)
         for e in range(e_all - 1):
             first = first + jnp.where(ids > e, jnp.broadcast_to(count[e : e + 1, :], count.shape), 0)
-        off_ref[b] = first[:, :128]
-        cnt_ref[b] = count[:, :128]
+        pair = jnp.where(lane == sub, first[:, :128], 0) + jnp.where(lane == sub + e_all, count[:, :128], 0)
+        table_ref[pl.ds(b, 1)] = jnp.sum(pair, axis=0, keepdims=True)
         pos_ref[b] = jnp.where(hit & (rank < cap), first + rank, -1)
     pos = pos_ref[here]
     lines = [
@@ -98,7 +99,7 @@
 
 
 def _expert_kernel(
-    turns, sizes, cut, off_ref, cnt_ref, pos_ref, xm_hbm, xo_hbm, w1_hbm, w3_hbm, w2_hbm, *refs
+    turns, sizes, cut, table_ref, pos_ref, xm_hbm, xo_hbm, w1_hbm, w3_hbm, w2_hbm, *refs
 ):
     outs = refs[:4]
     acc, xbuf, w1a, w3a, w1b, w3b, w2s, wsem, osem, xsem = refs[4:]
@@ -167,8 +168,8 @@
 
     def step(e, carry):
         expert = core * e_loc + e
-        offs = [off_ref[b, expert, 0] for b in blocks]
-        cnts = [cnt_ref[b, expert, 0] for b in blocks]
+        offs = [table_ref[b, expert] for b in blocks]
+        cnts = [table_ref[b, 2 * e_loc + expert] for b in blocks]
         need = functools.reduce(jnp.maximum, [jnp.where(k > 0, o - o // 8 * 8 + k, 0) for o, k in zip(offs, cnts)])
 
         def last(k):
@@ -223,18 +224,17 @@
         c.wait()
 
 
-def _combine_kernel(first, mine_ref, sum_ref, last_ref, *refs):
-    out_ref, hit = refs[-2:]
+def _combine_kernel(mine_ref, s0_ref, s1_ref, f0_ref, f1_ref, out_ref, hit):
     top, t, rows = hit.shape
 
     @pl.when(pl.program_id(0) == 0)
     def _():
-        row = lax.broadcasted_iota(jnp.int32, (t, rows), 1) + first
+        row = lax.broadcasted_iota(jnp.int32, (t, rows), 1)
         for j in range(top):
             hit[j] = (row == mine_ref[:, j : j + 1].astype(jnp.int32)).astype(F32).astype(BF16)
 
-    y = (sum_ref[...] + last_ref[...]).astype(BF16)
-    total = refs[0][...] if len(refs) == 3 else None
+    y = jnp.concatenate([s0_ref[...] + f0_ref[...], s1_ref[...] + f1_ref[...]], axis=0).astype(BF16)
+    total = None
     for j in range(top):
         part = jnp.dot(hit[j], y, preferred_element_type=F32) * mine_ref[:, top + j : top + j + 1]
         total = part if total is None else total + part
@@ -269,18 +269,17 @@
 
         out, back = (1, 2), (2, 1)
         pieces = 4
-        pos, off, cnt, mine, xn_mine, xn_other = pl.pallas_call(
+        pos, groups, mine, xn_mine, xn_other = pl.pallas_call(
             functools.partial(_route_kernel, chips, out),
             out_shape=[
                 jax.ShapeDtypeStruct((blocks, e_all, t_loc), jnp.int32),
-                jax.ShapeDtypeStruct((blocks, e_all, 128), jnp.int32),
-                jax.ShapeDtypeStruct((blocks, e_all, 128), jnp.int32),
+                jax.ShapeDtypeStruct((blocks, 128), jnp.int32),
                 jax.ShapeDtypeStruct((t_loc, 8), F32),
                 jax.ShapeDtypeStruct((t_loc, d), BF16),
                 jax.ShapeDtypeStruct((t_loc, d), BF16),
             ],
             in_specs=[vmem, vmem, smem, anym],
-            out_specs=[vmem] * 4 + [anym] * 2,
+            out_specs=[vmem] * 3 + [anym] * 2,
             scratch_shapes=[
                 pltpu.VMEM((blocks, top, t_loc), jnp.int32),
                 pltpu.SemaphoreType.DMA((blocks,)),
@@ -298,7 +297,7 @@
             return pl.pallas_call(
                 functools.partial(_expert_kernel, turns, sizes, cut),
                 out_shape=[jax.ShapeDtypeStruct((n, d), F32) for n in split * 2],
-                in_specs=[smem, smem, vmem] + [anym] * 5,
+                in_specs=[smem, vmem] + [anym] * 5,
                 out_specs=[anym] * 4,
                 scratch_shapes=[
                     pltpu.VMEM((2, rows, d), F32),
@@ -316,7 +315,7 @@
                 cost_estimate=pl.CostEstimate(
                     flops=6 * rows * d * ff, bytes_accessed=6 * e_loc * d * ff + 8 * rows * d, transcendentals=0
                 ),
-            )(off, cnt, pos, mine, other, w1, w3, w2)
+            )(groups, pos, mine, other, w1, w3, w2)
 
         def merge(parts, *more):
             sums = []
@@ -327,35 +326,28 @@
 
         x_next = after(x, pos)
         x_d, x_f = shift(x_next, (3, 3)), shift(x_next, back)
-        early, late = (rows // 4, rows - rows // 4), (rows - rows // 4, rows // 4)
-        near = merge(stage(out, xn_mine, xn_other, early))
+        halves = (rows // 2, rows // 2)
+        near = merge(stage(out, xn_mine, xn_other, halves))
         x_d = after(x_d, *near)
         near = [shift(a, out) for a in near]
-        diag = merge(stage((3, 3), x_d, swap(x_d), late))
+        diag = merge(stage((3, 3), x_d, swap(x_d), halves))
         x_f = after(x_f, *diag)
         via = [shift(a, out) for a in diag]
-        far = merge(stage(back, x_f, swap(x_f), late), via)
+        far = merge(stage(back, x_f, swap(x_f), halves), via)
         x_o = after(x, *far)
         far = [shift(a, back) for a in far]
-        near = jnp.concatenate(near, axis=0)
-        near = [near[: late[0]], near[late[0] :]]
-        sums = merge(stage((0, 0), x_o, swap(x_o), late), near)
+        sums = merge(stage((0, 0), x_o, swap(x_o), halves), near)
         width = d // 4
-        total = None
-        for q in range(2):
-            table = pl.BlockSpec((t_loc, 8), lambda i: (0, 0))
-            part = pl.BlockSpec((late[q], width), lambda i: (0, i))
-            wide = pl.BlockSpec((t_loc, width), lambda i: (0, i))
-            total = pl.pallas_call(
-                functools.partial(_combine_kernel, q * late[0]),
-                out_shape=jax.ShapeDtypeStruct((t_loc, d), (F32, BF16)[q]),
-                grid=(4,),
-                in_specs=[table, part, part] + [wide] * q,
-                out_specs=wide,
-                scratch_shapes=[pltpu.VMEM((top, t_loc, late[q]), BF16)],
-                cost_estimate=pl.CostEstimate(flops=8 * t_loc * late[q] * d, bytes_accessed=16 * late[q] * d, transcendentals=0),
-            )(mine, sums[q], far[q], *([total] * q))
-        return total
+        part = pl.BlockSpec((rows // 2, width), lambda i: (0, i))
+        return pl.pallas_call(
+            _combine_kernel,
+            out_shape=jax.ShapeDtypeStruct((t_loc, d), BF16),
+            grid=(4,),
+            in_specs=[pl.BlockSpec((t_loc, 8), lambda i: (0, 0))] + [part] * 4,
+            out_specs=pl.BlockSpec((t_loc, width), lambda i: (0, i)),
+            scratch_shapes=[pltpu.VMEM((top, t_loc, rows), BF16)],
+            name="combine",
+        )(mine, *sums, *far)
 
     rows = P(("ep", "tp"), None)
     return jax.shard_map(

time: 310 us -> 324 us (1.045)
  waiting for transfers between devices: 87 us -> 112 us
  Pallas kernels: 160 us -> 152 us
    ppermute x8, waiting for transfers between devices: 69.9 us -> 103 us  [shift(): return lax.ppermute(a, ('tp', 'ep'), pairs)]
    ppermute x11, waiting for transfers between devices: 17.1 us -> 9.51 us  [swap(): return lax.ppermute(a, 'ep', [(0, 1), (1, 0)])]
    pallas_call x2 -> x1, Pallas kernels: 10.4 us -> 6.01 us  [layer(): pl.pallas_call(_combine_kernel, out_shape=jax.ShapeDtypeStruct((t_loc, d)...]
    pallas_call x4, Pallas kernels: 128 us -> 125 us  [stage(): pl.pallas_call(functools.partial(_expert_kernel, turns, sizes, cut), out_...]
  transfers between devices with their start and end apart: 19 -> 19, of which waited for: 12 -> 10; matrix products, arithmetic and copies ran while one was open for 6% -> 6% of each run, Pallas kernels for 23% -> 19%
where the time goes in v5:
time: 324 us
  Pallas kernels  152 us (47%)
  waiting for transfers between devices  112 us (35%)
  starting transfers between devices  35.2 us (11%)
  other arithmetic  22.2 us (7%)
    pallas_call x4, Pallas kernels, stage(): pl.pallas_call(functools.partial(_expert_kernel, turns, sizes, cut), out_...  125 us
    ppermute x8, waiting for transfers between devices, shift(): return lax.ppermute(a, ('tp', 'ep'), pairs)  103 us
    ppermute x11, starting transfers between devices, swap(): return lax.ppermute(a, 'ep', [(0, 1), (1, 0)])  21.3 us
    pallas_call x1, Pallas kernels, layer(): pl.pallas_call(functools.partial(_route_kernel, chips, out), out_shape=[j...  21.2 us
    ppermute x8, starting transfers between devices, shift(): return lax.ppermute(a, ('tp', 'ep'), pairs)  13.9 us
    add x4, other arithmetic, merge(): functools.reduce(jnp.add, [m[q] for m in more], parts[2 + q] + other)  12.2 us
    add x4, other arithmetic, merge(): parts[2 + q] + other  10 us
    ppermute x11, waiting for transfers between devices, swap(): return lax.ppermute(a, 'ep', [(0, 1), (1, 0)])  9.51 us
  transfers between devices with their start and end apart: 19, of which 10 were waited for; matrix products, arithmetic and copies ran while one was open for 6% of the time, Pallas kernels for 19%

profile of v5, /device:TPU:0, one launch (start us, length us, event | category | flops | bytes accessed | tf_op | source)
XLA Modules:
  0.0 323.6 jit_solution(633092411384337379)
XLA Ops:
  0.0 21.2 %route.1 = (s32[8,8,256]{2,1,0:T(8,128)}, s32[8,128]{1,0:T(8,128)}, f32[256,8]{1,0:T(8,128)}, bf16[256,2048]{1,0:T(8,128)(2,1)}, bf16[256,2048]{1,0:T(8,128)(2,1)}) custom-call(s32[2,256]{1,0:T(2,128)} %bitcast.2, f32[2,256]{1,0:T(2,128)} %bitcast.3, s32[8]{0:T(128)} %cap_ref.1, bf16[256,2048]{1,0:T(8,128)(2,1)} %xm_hbm), custom_call_target="tpu_custom_call" | custom-call | tf_op jit(solution)/shard_map/route/pallas_call | solution.py:272
  21.2 32.3 %shard_map.73 = (f32[256,2048]{1,0:T(8,128)}, f32[256,2048]{1,0:T(8,128)}, f32[256,2048]{1,0:T(8,128)}, f32[256,2048]{1,0:T(8,128)}) custom-call(s32[8,128]{1,0:T(8,128)} %get-tuple-element.31.table_ref, s32[8,8,256]{2,1,0:T(8,128)} %get-tuple-element.32.pos_ref, bf16[256,2048]{1,0:T(8,128)(2,1)} %get-tuple-element.34.xm_hbm, ...), custom_call_target="tpu_custom_call" | custom-call | flops 8858370048 | bytes 77594624 | tf_op jit(solution)/shard_map/pallas_call | solution.py:297
  53.5 0.4 collective-permute-start.2
  53.9 0.1 collective-permute-start.3
  54.0 5.3 %collective-permute-start.1 = (bf16[256,2048]{1,0:T(8,128)(2,1)}, bf16[256,2048]{1,0:T(8,128)(2,1)S(1)}, u32[]{:S(2)}, u32[]{:S(2)}) collective-permute-start(bf16[256,2048]{1,0:T(8,128)(2,1)} %xm_hbm), channel_id=1, source_target_pairs={{0,6},{1,7},{2,4},{3,5},{4,2},{5,3},{6,0},{7,1}} | collective-permute-start | bytes 3145736 | tf_op jit(solution)/shard_map/ppermute | solution.py:265
  59.4 0.0 collective-permute-done.2
  59.4 3.3 %add.36 = f32[256,2048]{1,0:T(8,128)} add(f32[256,2048]{1,0:T(8,128)} %get-tuple-element.36, f32[256,2048]{1,0:T(8,128)S(1)} %collective-permute-done.2) | non-fusion elementwise | flops 524288 | bytes 6291456 | tf_op jit(solution)/shard_map/add | solution.py:324
  62.7 0.0 collective-permute-done.3
  62.7 1.6 add.37
  64.3 19.0 %collective-permute-done.1.xm_hbm = bf16[256,2048]{1,0:T(8,128)(2,1)S(1)} collective-permute-done((bf16[256,2048]{1,0:T(8,128)(2,1)}, bf16[256,2048]{1,0:T(8,128)(2,1)S(1)}, u32[]{:S(2)}, u32[]{:S(2)}) %collective-permute-start.1) | collective-permute-done | bytes 1048608 | tf_op jit(solution)/shard_map/ppermute | solution.py:265
  83.4 1.0 copy-done.7
  84.3 2.8 collective-permute-done.4.xo_hbm
  87.1 29.7 %shard_map.74 = (f32[256,2048]{1,0:T(8,128)}, f32[256,2048]{1,0:T(8,128)}, f32[256,2048]{1,0:T(8,128)}, f32[256,2048]{1,0:T(8,128)}) custom-call(s32[8,128]{1,0:T(8,128)} %get-tuple-element.31.table_ref, s32[8,8,256]{2,1,0:T(8,128)} %get-tuple-element.32.pos_ref, bf16[256,2048]{1,0:T(8,128)(2,1)} %copy-done.7, ...), custom_call_target="tpu_custom_call" | custom-call | flops 8858370048 | bytes 77594624 | tf_op jit(solution)/shard_map/pallas_call | solution.py:297
  116.8 6.1 %collective-permute-start.5 = (f32[256,2048]{1,0:T(8,128)}, f32[256,2048]{1,0:T(8,128)S(1)}, u32[]{:S(2)}, u32[]{:S(2)}) collective-permute-start(f32[256,2048]{1,0:T(8,128)} %get-tuple-element.42), channel_id=1, source_target_pairs={{0,1},{1,0},{2,3},{3,2},{4,5},{5,4},{6,7},{7,6}} | collective-permute-start | bytes 6291464 | tf_op jit(solution)/shard_map/ppermute | solution.py:261
  123.0 0.0 collective-permute-start.6
  123.0 1.5 collective-permute-start
  124.4 2.5 collective-permute-done.5
  127.0 3.4 %add.38 = f32[256,2048]{1,0:T(8,128)} add(f32[256,2048]{1,0:T(8,128)} %get-tuple-element.41, f32[256,2048]{1,0:T(8,128)S(1)} %collective-permute-done.5) | non-fusion elementwise | flops 524288 | bytes 6291456 | tf_op jit(solution)/shard_map/add | solution.py:324
  130.4 0.0 collective-permute-done.6
  130.4 1.6 add.39
  132.0 6.0 %collective-permute-done.xm_hbm = bf16[256,2048]{1,0:T(8,128)(2,1)S(1)} collective-permute-done((bf16[256,2048]{1,0:T(8,128)(2,1)}, bf16[256,2048]{1,0:T(8,128)(2,1)S(1)}, u32[]{:S(2)}, u32[]{:S(2)}) %collective-permute-start) | collective-permute-done | bytes 1048608 | tf_op jit(solution)/shard_map/ppermute | solution.py:265
  138.0 1.0 copy-done.6
  139.0 0.1 collective-permute-start.7
  139.1 2.2 collective-permute-start.9
  141.3 0.5 collective-permute-done.7.xo_hbm
  141.8 26.9 %shard_map.75 = (f32[256,2048]{1,0:T(8,128)}, f32[256,2048]{1,0:T(8,128)}, f32[256,2048]{1,0:T(8,128)}, f32[256,2048]{1,0:T(8,128)}) custom-call(s32[8,128]{1,0:T(8,128)} %get-tuple-element.31.table_ref, s32[8,8,256]{2,1,0:T(8,128)} %get-tuple-element.32.pos_ref, bf16[256,2048]{1,0:T(8,128)(2,1)} %copy-done.6, ...), custom_call_target="tpu_custom_call" | custom-call | flops 8858370048 | bytes 77594624 | tf_op jit(solution)/shard_map/pallas_call | solution.py:297
  168.7 9.5 %collective-permute-start.8 = (f32[256,2048]{1,0:T(8,128)}, f32[256,2048]{1,0:T(8,128)S(1)}, u32[]{:S(2)}, u32[]{:S(2)}) collective-permute-start(f32[256,2048]{1,0:T(8,128)} %get-tuple-element.47), channel_id=1, source_target_pairs={{0,1},{1,0},{2,3},{3,2},{4,5},{5,4},{6,7},{7,6}} | collective-permute-start | bytes 6291464 | tf_op jit(solution)/shard_map/ppermute | solution.py:261
  178.2 2.3 collective-permute-start.11
  180.5 2.5 collective-permute-start.10
  183.0 0.0 collective-permute-done.9
  183.1 4.3 %add_add_fusion.3 = f32[256,2048]{1,0:T(8,128)} fusion(f32[256,2048]{1,0:T(8,128)} %collective-permute-done.9, f32[256,2048]{1,0:T(8,128)} %get-tuple-element.46, f32[256,2048]{1,0:T(8,128)S(1)} %collective-permute-done.8), kind=kLoop, calls=%fused_computation.3 | loop fusion | flops 1048576 | bytes 8388608 | tf_op jit(solution)/shard_map/add | solution.py:324
  187.3 17.4 %collective-permute-done.11 = f32[256,2048]{1,0:T(8,128)S(1)} collective-permute-done((f32[256,2048]{1,0:T(8,128)}, f32[256,2048]{1,0:T(8,128)S(1)}, u32[]{:S(2)}, u32[]{:S(2)}) %collective-permute-start.11) | collective-permute-done | bytes 2097184 | tf_op jit(solution)/shard_map/ppermute | solution.py:265
  204.7 1.9 add_add_fusion.2
  206.6 1.9 collective-permute-start.12
  208.6 0.1 collective-permute-start.14
  208.7 2.3 collective-permute-done.12.xo_hbm
  211.0 35.7 %shard_map.76 = (f32[256,2048]{1,0:T(8,128)}, f32[256,2048]{1,0:T(8,128)}, f32[256,2048]{1,0:T(8,128)}, f32[256,2048]{1,0:T(8,128)}) custom-call(s32[8,128]{1,0:T(8,128)} %get-tuple-element.31.table_ref, s32[8,8,256]{2,1,0:T(8,128)} %get-tuple-element.32.pos_ref, bf16[256,2048]{1,0:T(8,128)(2,1)} %xm_hbm, bf16[256,2048]{1,0:T(8,128)(2,1)} %collective-permute-done.12.xo_hbm, ...), custom_call_target="tpu_custom_call" | custom-call | flops 8858370048 | bytes 77594624 | tf_op jit(solution)/shard_map/pallas_call | solution.py:297
  246.7 0.0 collective-permute-start.13
  246.7 0.0 collective-permute-start.16
  246.8 0.5 collective-permute-start.15
  247.2 2.4 collective-permute-start.17
  249.7 0.0 collective-permute-start.18
  249.7 1.4 collective-permute-done.13
  251.1 4.2 %add_add_fusion.1.s0_ref = f32[256,2048]{1,0:T(8,128)} fusion(f32[256,2048]{1,0:T(8,128)} %collective-permute-done.14, f32[256,2048]{1,0:T(8,128)} %get-tuple-element.51, f32[256,2048]{1,0:T(8,128)S(1)} %collective-permute-done.13), kind=kLoop, calls=%fused_computation.1 | loop fusion | flops 1048576 | bytes 8388608 | tf_op jit(solution)/shard_map/add | solution.py:324
  255.3 40.2 %collective-permute-done.16 = f32[256,2048]{1,0:T(8,128)S(1)} collective-permute-done((f32[256,2048]{1,0:T(8,128)}, f32[256,2048]{1,0:T(8,128)S(1)}, u32[]{:S(2)}, u32[]{:S(2)}) %collective-permute-start.16) | collective-permute-done | bytes 2097184 | tf_op jit(solution)/shard_map/ppermute | solution.py:265
  295.5 1.9 add_add_fusion.s1_ref
  297.4 20.2 %collective-permute-done.18.f1_ref = f32[256,2048]{1,0:T(8,128)} collective-permute-done((f32[256,2048]{1,0:T(8,128)}, f32[256,2048]{1,0:T(8,128)}, u32[]{:S(2)}, u32[]{:S(2)}) %collective-permute-start.18) | collective-permute-done | bytes 2097184 | tf_op jit(solution)/shard_map/ppermute | solution.py:265
  317.6 6.0 %combine.1 = bf16[256,2048]{1,0:T(8,128)(2,1)} custom-call(f32[256,8]{1,0:T(8,128)} %get-tuple-element.30.mine_ref, f32[256,2048]{1,0:T(8,128)} %add_add_fusion.1.s0_ref, f32[256,2048]{1,0:T(8,128)} %add_add_fusion.s1_ref, f32[256,2048]{1,0:T(8,128)} %copy-done.4, f32[256,2048]{1,0:T(8,128)} %collective-permute-done.18.f1_ref), custom_call_target="tpu_custom_call" | custom-call | tf_op jit(solution)/shard_map/combine/pallas_call | solution.py:342
  (20 shorter events, 0.0 us)
Async XLA Ops:
  53.5 5.9 %collective-permute-start.2 = (f32[256,2048]{1,0:T(8,128)}, f32[256,2048]{1,0:T(8,128)S(1)}, u32[]{:S(2)}, u32[]{:S(2)}) collective-permute-start(f32[256,2048]{1,0:T(8,128)} %get-tuple-element.37), channel_id=1, source_target_pairs={{0,1},{1,0},{2,3},{3,2},{4,5},{5,4},{6,7},{7,6}} | collective-permute-start | bytes 6291464 | tf_op jit(solution)/shard_map/ppermute | solution.py:261
  53.9 8.8 %collective-permute-start.3 = (f32[256,2048]{1,0:T(8,128)}, f32[256,2048]{1,0:T(8,128)S(1)}, u32[]{:S(2)}, u32[]{:S(2)}) collective-permute-start(f32[256,2048]{1,0:T(8,128)} %get-tuple-element.39), channel_id=1, source_target_pairs={{0,1},{1,0},{2,3},{3,2},{4,5},{5,4},{6,7},{7,6}} | collective-permute-start | bytes 6291464 | tf_op jit(solution)/shard_map/ppermute | solution.py:261
  54.0 29.3 %collective-permute-start.1 = (bf16[256,2048]{1,0:T(8,128)(2,1)}, bf16[256,2048]{1,0:T(8,128)(2,1)S(1)}, u32[]{:S(2)}, u32[]{:S(2)}) collective-permute-start(bf16[256,2048]{1,0:T(8,128)(2,1)} %xm_hbm), channel_id=1, source_target_pairs={{0,6},{1,7},{2,4},{3,5},{4,2},{5,3},{6,0},{7,1}} | collective-permute-start | bytes 3145736 | tf_op jit(solution)/shard_map/ppermute | solution.py:265
  59.4 3.4 %copy-start.1 = (f32[256,2048]{1,0:T(8,128)S(1)}, f32[256,2048]{1,0:T(8,128)}, u32[]{:S(2)}) copy-start(f32[256,2048]{1,0:T(8,128)} %get-tuple-element.38) | copy-start | bytes 6291460
  83.4 1.0 copy-start.7
  84.3 2.8 collective-permute-start.4
  116.8 10.1 %collective-permute-start.5 = (f32[256,2048]{1,0:T(8,128)}, f32[256,2048]{1,0:T(8,128)S(1)}, u32[]{:S(2)}, u32[]{:S(2)}) collective-permute-start(f32[256,2048]{1,0:T(8,128)} %get-tuple-element.42), channel_id=1, source_target_pairs={{0,1},{1,0},{2,3},{3,2},{4,5},{5,4},{6,7},{7,6}} | collective-permute-start | bytes 6291464 | tf_op jit(solution)/shard_map/ppermute | solution.py:261
  123.0 7.4 %collective-permute-start.6 = (f32[256,2048]{1,0:T(8,128)}, f32[256,2048]{1,0:T(8,128)S(1)}, u32[]{:S(2)}, u32[]{:S(2)}) collective-permute-start(f32[256,2048]{1,0:T(8,128)} %get-tuple-element.44), channel_id=1, source_target_pairs={{0,1},{1,0},{2,3},{3,2},{4,5},{5,4},{6,7},{7,6}} | collective-permute-start | bytes 6291464 | tf_op jit(solution)/shard_map/ppermute | solution.py:261
  123.0 15.0 %collective-permute-start = (bf16[256,2048]{1,0:T(8,128)(2,1)}, bf16[256,2048]{1,0:T(8,128)(2,1)S(1)}, u32[]{:S(2)}, u32[]{:S(2)}) collective-permute-start(bf16[256,2048]{1,0:T(8,128)(2,1)} %xm_hbm), channel_id=1, source_target_pairs={{0,4},{1,3},{2,6},{3,1},{4,0},{5,7},{6,2},{7,5}} | collective-permute-start | bytes 3145736 | tf_op jit(solution)/shard_map/ppermute | solution.py:265
  126.9 3.4 %copy-start.2 = (f32[256,2048]{1,0:T(8,128)S(1)}, f32[256,2048]{1,0:T(8,128)}, u32[]{:S(2)}) copy-start(f32[256,2048]{1,0:T(8,128)} %get-tuple-element.43) | copy-start | bytes 6291460
  138.0 1.0 copy-start.6
  139.0 2.8 collective-permute-start.7
  139.1 44.0 %collective-permute-start.9 = (f32[256,2048]{1,0:T(8,128)}, f32[256,2048]{1,0:T(8,128)}, u32[]{:S(2)}, u32[]{:S(2)}) collective-permute-start(f32[256,2048]{1,0:T(8,128)} %add.38), channel_id=1, source_target_pairs={{0,2},{1,5},{2,0},{3,7},{4,6},{5,1},{6,4},{7,3}} | collective-permute-start | bytes 6291464 | tf_op jit(solution)/shard_map/ppermute | solution.py:265
  168.7 14.4 %collective-permute-start.8 = (f32[256,2048]{1,0:T(8,128)}, f32[256,2048]{1,0:T(8,128)S(1)}, u32[]{:S(2)}, u32[]{:S(2)}) collective-permute-start(f32[256,2048]{1,0:T(8,128)} %get-tuple-element.47), channel_id=1, source_target_pairs={{0,1},{1,0},{2,3},{3,2},{4,5},{5,4},{6,7},{7,6}} | collective-permute-start | bytes 6291464 | tf_op jit(solution)/shard_map/ppermute | solution.py:261
  178.2 26.6 %collective-permute-start.11 = (f32[256,2048]{1,0:T(8,128)}, f32[256,2048]{1,0:T(8,128)S(1)}, u32[]{:S(2)}, u32[]{:S(2)}) collective-permute-start(f32[256,2048]{1,0:T(8,128)} %add.39), channel_id=1, source_target_pairs={{0,2},{1,5},{2,0},{3,7},{4,6},{5,1},{6,4},{7,3}} | collective-permute-start | bytes 6291464 | tf_op jit(solution)/shard_map/ppermute | solution.py:265
  180.5 24.2 %collective-permute-start.10 = (f32[256,2048]{1,0:T(8,128)}, f32[256,2048]{1,0:T(8,128)S(1)}, u32[]{:S(2)}, u32[]{:S(2)}) collective-permute-start(f32[256,2048]{1,0:T(8,128)} %get-tuple-element.49), channel_id=1, source_target_pairs={{0,1},{1,0},{2,3},{3,2},{4,5},{5,4},{6,7},{7,6}} | collective-permute-start | bytes 6291464 | tf_op jit(solution)/shard_map/ppermute | solution.py:261
  183.0 21.7 %copy-start.5 = (f32[256,2048]{1,0:T(8,128)S(1)}, f32[256,2048]{1,0:T(8,128)}, u32[]{:S(2)}) copy-start(f32[256,2048]{1,0:T(8,128)} %get-tuple-element.48) | copy-start | bytes 6291460
  204.7 1.9 copy-start
  206.6 4.4 %collective-permute-start.12 = (bf16[256,2048]{1,0:T(8,128)(2,1)S(1)}, bf16[256,2048]{1,0:T(8,128)(2,1)}, u32[]{:S(2)}, u32[]{:S(2)}) collective-permute-start(bf16[256,2048]{1,0:T(8,128)(2,1)S(1)} %copy-done), channel_id=1, source_target_pairs={{0,1},{1,0},{2,3},{3,2},{4,5},{5,4},{6,7},{7,6}} | collective-permute-start | bytes 3145736 | tf_op jit(solution)/shard_map/ppermute | solution.py:261
  208.6 41.1 %collective-permute-start.14 = (f32[256,2048]{1,0:T(8,128)}, f32[256,2048]{1,0:T(8,128)}, u32[]{:S(2)}, u32[]{:S(2)}) collective-permute-start(f32[256,2048]{1,0:T(8,128)} %add.36), channel_id=1, source_target_pairs={{0,2},{1,5},{2,0},{3,7},{4,6},{5,1},{6,4},{7,3}} | collective-permute-start | bytes 6291464 | tf_op jit(solution)/shard_map/ppermute | solution.py:265
  246.7 4.4 %collective-permute-start.13 = (f32[256,2048]{1,0:T(8,128)}, f32[256,2048]{1,0:T(8,128)S(1)}, u32[]{:S(2)}, u32[]{:S(2)}) collective-permute-start(f32[256,2048]{1,0:T(8,128)} %get-tuple-element.52), channel_id=1, source_target_pairs={{0,1},{1,0},{2,3},{3,2},{4,5},{5,4},{6,7},{7,6}} | collective-permute-start | bytes 6291464 | tf_op jit(solution)/shard_map/ppermute | solution.py:261
  246.7 48.7 %collective-permute-start.16 = (f32[256,2048]{1,0:T(8,128)}, f32[256,2048]{1,0:T(8,128)S(1)}, u32[]{:S(2)}, u32[]{:S(2)}) collective-permute-start(f32[256,2048]{1,0:T(8,128)} %add.37), channel_id=1, source_target_pairs={{0,2},{1,5},{2,0},{3,7},{4,6},{5,1},{6,4},{7,3}} | collective-permute-start | bytes 6291464 | tf_op jit(solution)/shard_map/ppermute | solution.py:265
  246.8 48.7 %collective-permute-start.15 = (f32[256,2048]{1,0:T(8,128)}, f32[256,2048]{1,0:T(8,128)S(1)}, u32[]{:S(2)}, u32[]{:S(2)}) collective-permute-start(f32[256,2048]{1,0:T(8,128)} %get-tuple-element.54), channel_id=1, source_target_pairs={{0,1},{1,0},{2,3},{3,2},{4,5},{5,4},{6,7},{7,6}} | collective-permute-start | bytes 6291464 | tf_op jit(solution)/shard_map/ppermute | solution.py:261
  247.2 50.1 %collective-permute-start.17 = (f32[256,2048]{1,0:T(8,128)}, f32[256,2048]{1,0:T(8,128)S(1)}, u32[]{:S(2)}, u32[]{:S(2)}) collective-permute-start(f32[256,2048]{1,0:T(8,128)} %add_add_fusion.3), channel_id=1, source_target_pairs={{0,4},{1,3},{2,6},{3,1},{4,0},{5,7},{6,2},{7,5}} | collective-permute-start | bytes 6291464 | tf_op jit(solution)/shard_map/ppermute | solution.py:265
  249.7 67.9 %collective-permute-start.18 = (f32[256,2048]{1,0:T(8,128)}, f32[256,2048]{1,0:T(8,128)}, u32[]{:S(2)}, u32[]{:S(2)}) collective-permute-start(f32[256,2048]{1,0:T(8,128)} %add_add_fusion.2), channel_id=1, source_target_pairs={{0,4},{1,3},{2,6},{3,1},{4,0},{5,7},{6,2},{7,5}} | collective-permute-start | bytes 6291464 | tf_op jit(solution)/shard_map/ppermute | solution.py:265
  251.1 44.4 %copy-start.3 = (f32[256,2048]{1,0:T(8,128)S(1)}, f32[256,2048]{1,0:T(8,128)}, u32[]{:S(2)}) copy-start(f32[256,2048]{1,0:T(8,128)} %get-tuple-element.53) | copy-start | bytes 6291460
  297.3 20.2 %copy-start.4 = (f32[256,2048]{1,0:T(8,128)}, f32[256,2048]{1,0:T(8,128)S(1)}, u32[]{:S(2)}) copy-start(f32[256,2048]{1,0:T(8,128)S(1)} %collective-permute-done.17.f0_ref) | copy-start | bytes 6291460

commit v6 on v5

--- a/solution.py
+++ b/solution.py
@@ -14,7 +14,7 @@
 
 
 def _route_kernel(chips, turns, idx_ref, g_ref, cap_ref, x_ref, *refs):
-    pos_ref, table_ref, mine_ref, xm_ref, xo_ref, ids_all, send_sem, recv_sem, xsend, xrecv = refs
+    pos_ref, table_ref, hit_ref, gate_ref, xm_ref, xo_ref, ids_all, send_sem, recv_sem, xsend, xrecv = refs
     core, me = lax.axis_index("ep"), lax.axis_index("tp")
     blocks, top, t = ids_all.shape
     e_all = pos_ref.shape[1]
@@ -89,7 +89,11 @@
     ]
     lines += [g_ref[j : j + 1, :] for j in range(top)]
     table = jnp.concatenate(lines + [jnp.zeros((8 - 2 * top, t), F32)], axis=0)
-    mine_ref[...] = jnp.transpose(table)
+    table = jnp.transpose(table)
+    gate_ref[...] = table
+    row = lax.broadcasted_iota(jnp.int32, hit_ref.shape[1:], 1)
+    for j in range(top):
+        hit_ref[j] = (row == table[:, j : j + 1].astype(jnp.int32)).astype(F32).astype(BF16)
     for c, f in zip(arrive, forward):
         c.wait_recv()
         f.start()
@@ -99,11 +103,13 @@
 
 
 def _expert_kernel(
-    turns, sizes, cut, table_ref, pos_ref, xm_hbm, xo_hbm, w1_hbm, w3_hbm, w2_hbm, *refs
+    turns, sizes, cuts, table_ref, pos_ref, xm_hbm, xo_hbm, w1_hbm, w3_hbm, w2_hbm, *refs
 ):
     outs = refs[:4]
-    acc, xbuf, w1a, w3a, w1b, w3b, w2s, wsem, osem, xsem = refs[4:]
-    e_loc, d, ff = w1_hbm.shape
+    acc, xbuf, *ws, w2s, wsem, osem, xsem = refs[4:]
+    w1s, w3s = ws[: len(ws) // 2], ws[len(ws) // 2 :]
+    ahead = 2
+    e_loc, d, _ = w1_hbm.shape
     _, rows, _ = acc.shape
     t = xbuf.shape[1]
     half_d = d // 2
@@ -114,35 +120,38 @@
         turn = jnp.where(c == 0, turns[0], turns[1])
         blocks.append(c * chips + jnp.bitwise_xor(me, turn))
 
-    def first(e):
-        cols, b = pl.ds(0, cut), e % 2
-        return [
-            pltpu.make_async_copy(w1_hbm.at[e, :, cols], w1a.at[b], wsem.at[b, 0]),
-            pltpu.make_async_copy(w3_hbm.at[e, :, cols], w3a.at[b], wsem.at[b, 1]),
-        ]
-
-    def second(e):
-        cols, b = pl.ds(cut, ff - cut), e % 2
-        return [
-            pltpu.make_async_copy(w1_hbm.at[e, :, cols], w1b.at[b], wsem.at[b, 2]),
-            pltpu.make_async_copy(w3_hbm.at[e, :, cols], w3b.at[b], wsem.at[b, 3]),
-        ]
-
-    def third(k):
+    def columns(k):
+        def copies(e):
+            cols, b = pl.ds(cuts[k], cuts[k + 1] - cuts[k]), e % 2
+            return [
+                pltpu.make_async_copy(w1_hbm.at[e, :, cols], w1s[k].at[b], wsem.at[b, 2 * k]),
+                pltpu.make_async_copy(w3_hbm.at[e, :, cols], w3s[k].at[b], wsem.at[b, 2 * k + 1]),
+            ]
+
+        return copies
+
+    def output(k):
         def copies(e):
             cols, b = pl.ds(pl.multiple_of(k * half_d, half_d), half_d), e % 2
-            return [pltpu.make_async_copy(w2_hbm.at[e, :, cols], w2s.at[b, k], wsem.at[b, 4 + k])]
+            return [pltpu.make_async_copy(w2_hbm.at[e, :, cols], w2s.at[b, k], wsem.at[b, 2 * len(w1s) + k])]
 
         return copies
 
-    def arrive(chunk, e):
-        for c in chunk(e):
+    chunks = [columns(k) for k in range(len(w1s))] + [output(k) for k in range(2)]
+
+    def arrive(i, e):
+        for c in chunks[i](e):
             c.wait()
-
-        @pl.when(e + 1 < e_loc)
-        def _():
-            for c in chunk(e + 1):
+        i += ahead
+        if i < len(chunks):
+            for c in chunks[i](e):
                 c.start()
+        else:
+
+            @pl.when(e + 1 < e_loc)
+            def _():
+                for c in chunks[i - len(chunks)](e + 1):
+                    c.start()
 
     def out_copies(h):
         cols = pl.ds(h * half_d, half_d)
@@ -159,8 +168,8 @@
     ]
     for c in tokens:
         c.start()
-    for chunk in (first, second, third(0), third(1)):
-        for c in chunk(0):
+    for i in range(ahead):
+        for c in chunks[i](0):
             c.start()
     acc[...] = jnp.zeros_like(acc)
     for c in tokens:
@@ -187,15 +196,16 @@
                 parts.append(jnp.dot(hit, xbuf[s], preferred_element_type=F32))
             xs = jnp.concatenate(parts, axis=0).astype(BF16)
             hs = []
-            for chunk, wa, wb in ((first, w1a, w3a), (second, w1b, w3b)):
-                arrive(chunk, e)
+            for i, (wa, wb) in enumerate(zip(w1s, w3s)):
+                arrive(i, e)
                 h1 = jnp.dot(xs, wa[e % 2], preferred_element_type=F32)
                 h3 = jnp.dot(xs, wb[e % 2], preferred_element_type=F32)
                 hs.append((jax.nn.silu(h1) * h3).astype(BF16))
             h = jnp.concatenate(hs, axis=1)
 
             def project(k, carry):
-                arrive(third(k), e)
+                for i in range(2):
+                    pl.when(k == i)(functools.partial(arrive, len(w1s) + i, e))
                 p = jnp.dot(h, w2s[e % 2, k], preferred_element_type=F32)
                 cols = pl.ds(pl.multiple_of(k * half_d, half_d), half_d)
                 for s in range(2):
@@ -207,8 +217,8 @@
 
         @pl.when(need == 0)
         def _():
-            for chunk in (first, second, third(0), third(1)):
-                arrive(chunk, e)
+            for i in range(len(chunks)):
+                arrive(i, e)
             last(0)
 
         lo = 0
@@ -224,19 +234,12 @@
         c.wait()
 
 
-def _combine_kernel(mine_ref, s0_ref, s1_ref, f0_ref, f1_ref, out_ref, hit):
-    top, t, rows = hit.shape
-
-    @pl.when(pl.program_id(0) == 0)
-    def _():
-        row = lax.broadcasted_iota(jnp.int32, (t, rows), 1)
-        for j in range(top):
-            hit[j] = (row == mine_ref[:, j : j + 1].astype(jnp.int32)).astype(F32).astype(BF16)
-
+def _combine_kernel(hit_ref, gate_ref, s0_ref, s1_ref, f0_ref, f1_ref, out_ref):
+    top = hit_ref.shape[0]
     y = jnp.concatenate([s0_ref[...] + f0_ref[...], s1_ref[...] + f1_ref[...]], axis=0).astype(BF16)
     total = None
     for j in range(top):
-        part = jnp.dot(hit[j], y, preferred_element_type=F32) * mine_ref[:, top + j : top + j + 1]
+        part = jnp.dot(hit_ref[j], y, preferred_element_type=F32) * gate_ref[:, top + j : top + j + 1]
         total = part if total is None else total + part
     out_ref[...] = total.astype(out_ref.dtype)
 
@@ -254,7 +257,8 @@
         e_loc, _, ff = w1.shape
         c = (5 * top * t_loc // (2 * e_all) + 7) // 8 * 8
         rows = top * t_loc
-        cut = 512
+        cuts = (0, 512, 1024, ff)
+        widths = [b - a for a, b in zip(cuts, cuts[1:])]
         blocks = 2 * chips
 
         def swap(a):
@@ -269,17 +273,18 @@
 
         out, back = (1, 2), (2, 1)
         pieces = 4
-        pos, groups, mine, xn_mine, xn_other = pl.pallas_call(
+        pos, groups, hit, gate, xn_mine, xn_other = pl.pallas_call(
             functools.partial(_route_kernel, chips, out),
             out_shape=[
                 jax.ShapeDtypeStruct((blocks, e_all, t_loc), jnp.int32),
                 jax.ShapeDtypeStruct((blocks, 128), jnp.int32),
+                jax.ShapeDtypeStruct((top, t_loc, rows), BF16),
                 jax.ShapeDtypeStruct((t_loc, 8), F32),
                 jax.ShapeDtypeStruct((t_loc, d), BF16),
                 jax.ShapeDtypeStruct((t_loc, d), BF16),
             ],
             in_specs=[vmem, vmem, smem, anym],
-            out_specs=[vmem] * 3 + [anym] * 2,
+            out_specs=[vmem] * 4 + [anym] * 2,
             scratch_shapes=[
                 pltpu.VMEM((blocks, top, t_loc), jnp.int32),
                 pltpu.SemaphoreType.DMA((blocks,)),
@@ -295,19 +300,16 @@
 
         def stage(turns, mine, other, split):
             return pl.pallas_call(
-                functools.partial(_expert_kernel, turns, sizes, cut),
+                functools.partial(_expert_kernel, turns, sizes, cuts),
                 out_shape=[jax.ShapeDtypeStruct((n, d), F32) for n in split * 2],
                 in_specs=[smem, vmem] + [anym] * 5,
                 out_specs=[anym] * 4,
                 scratch_shapes=[
                     pltpu.VMEM((2, rows, d), F32),
                     pltpu.VMEM((2, t_loc, d), BF16),
-                    pltpu.VMEM((2, d, cut), BF16),
-                    pltpu.VMEM((2, d, cut), BF16),
-                    pltpu.VMEM((2, d, ff - cut), BF16),
-                    pltpu.VMEM((2, d, ff - cut), BF16),
+                    *[pltpu.VMEM((2, d, w), BF16) for w in widths * 2],
                     pltpu.VMEM((2, 2, ff, d // 2), BF16),
-                    pltpu.SemaphoreType.DMA((2, 6)),
+                    pltpu.SemaphoreType.DMA((2, 2 * len(widths) + 2)),
                     pltpu.SemaphoreType.DMA((2, 4)),
                     pltpu.SemaphoreType.DMA((2,)),
                 ],
@@ -337,17 +339,16 @@
         x_o = after(x, *far)
         far = [shift(a, back) for a in far]
         sums = merge(stage((0, 0), x_o, swap(x_o), halves), near)
-        width = d // 4
-        part = pl.BlockSpec((rows // 2, width), lambda i: (0, i))
+        steps = 8
+        part = pl.BlockSpec((rows // 2, d // steps), lambda i: (0, i))
         return pl.pallas_call(
             _combine_kernel,
             out_shape=jax.ShapeDtypeStruct((t_loc, d), BF16),
-            grid=(4,),
-            in_specs=[pl.BlockSpec((t_loc, 8), lambda i: (0, 0))] + [part] * 4,
-            out_specs=pl.BlockSpec((t_loc, width), lambda i: (0, i)),
-            scratch_shapes=[pltpu.VMEM((top, t_loc, rows), BF16)],
+            grid=(steps,),
+            in_specs=[vmem, vmem] + [part] * 4,
+            out_specs=pl.BlockSpec((t_loc, d // steps), lambda i: (0, i)),
             name="combine",
-        )(mine, *sums, *far)
+        )(hit, gate, *sums, *far)
 
     rows = P(("ep", "tp"), None)
     return jax.shard_map(

time: 324 us -> 324 us (level)
  Pallas kernels: 152 us -> 159 us
  starting transfers between devices: 35.2 us -> 28.6 us
    ppermute x11, starting transfers between devices: 21.3 us -> 15.2 us  [swap(): return lax.ppermute(a, 'ep', [(0, 1), (1, 0)])]
    pallas_call x4, Pallas kernels: 125 us -> 129 us  [stage(): pl.pallas_call(functools.partial(_expert_kernel, turns, sizes, cuts), out...]
  transfers between devices with their start and end apart: 19 -> 19, of which waited for: 10 -> 11; matrix products, arithmetic and copies ran while one was open for 6% -> 6% of each run, Pallas kernels for 19% -> 20%
where the time goes in v6:
time: 324 us; the launch traced here: 323 us
  Pallas kernels  159 us (49%)
  waiting for transfers between devices  112 us (35%)
  starting transfers between devices  28.6 us (9%)
  other arithmetic  22.3 us (7%)
    pallas_call x4, Pallas kernels, stage(): pl.pallas_call(functools.partial(_expert_kernel, turns, sizes, cuts), out...  129 us
    ppermute x8, waiting for transfers between devices, shift(): return lax.ppermute(a, ('tp', 'ep'), pairs)  103 us
    pallas_call x1, Pallas kernels, layer(): pl.pallas_call(functools.partial(_route_kernel, chips, out), out_shape=[j...  21.4 us
    ppermute x11, starting transfers between devices, swap(): return lax.ppermute(a, 'ep', [(0, 1), (1, 0)])  15.2 us
    ppermute x8, starting transfers between devices, shift(): return lax.ppermute(a, ('tp', 'ep'), pairs)  13.5 us
    add x4, other arithmetic, merge(): functools.reduce(jnp.add, [m[q] for m in more], parts[2 + q] + other)  12.3 us
    add x4, other arithmetic, merge(): parts[2 + q] + other  10 us
    ppermute x11, waiting for transfers between devices, swap(): return lax.ppermute(a, 'ep', [(0, 1), (1, 0)])  8.54 us
  transfers between devices with their start and end apart: 19, of which 11 were waited for; matrix products, arithmetic and copies ran while one was open for 6% of the time, Pallas kernels for 20%

profile of v6, /device:TPU:0, one launch (start us, length us, event | category | flops | bytes accessed | tf_op | source)
XLA Modules:
  0.0 323.4 jit_solution(11194533370211343336)
XLA Ops:
  0.0 21.4 %route.1 = (s32[8,8,256]{2,1,0:T(8,128)}, s32[8,128]{1,0:T(8,128)}, bf16[2,256,512]{2,1,0:T(8,128)(2,1)}, f32[256,8]{1,0:T(8,128)}, bf16[256,2048]{1,0:T(8,128)(2,1)}, /*index=5*/bf16[256,2048]{1,0:T(8,128)(2,1)}) custom-call(s32[2,256]{1,0:T(2,128)} %bitcast.2, f32[2,256]{1,0:T(2,128)} %bitcast.3, s32[8]{0:T(128)} %cap_ref.1, bf16[256,2048]{1,0:T(8,128)(2,1)} %xm_hbm), custom_call_target="tpu_custom_call" | custom-call | tf_op jit(solution)/shard_map/route/pallas_call | solution.py:276
  21.4 32.9 %shard_map.73 = (f32[256,2048]{1,0:T(8,128)}, f32[256,2048]{1,0:T(8,128)}, f32[256,2048]{1,0:T(8,128)}, f32[256,2048]{1,0:T(8,128)}) custom-call(s32[8,128]{1,0:T(8,128)} %get-tuple-element.33.table_ref, s32[8,8,256]{2,1,0:T(8,128)} %get-tuple-element.34.pos_ref, bf16[256,2048]{1,0:T(8,128)(2,1)} %get-tuple-element.36.xm_hbm, ...), custom_call_target="tpu_custom_call" | custom-call | flops 8858370048 | bytes 77594624 | tf_op jit(solution)/shard_map/pallas_call | solution.py:302
  54.4 1.1 collective-permute-start.2
  55.4 0.0 collective-permute-start.3
  55.5 3.4 %collective-permute-start.1 = (bf16[256,2048]{1,0:T(8,128)(2,1)}, bf16[256,2048]{1,0:T(8,128)(2,1)S(1)}, u32[]{:S(2)}, u32[]{:S(2)}) collective-permute-start(bf16[256,2048]{1,0:T(8,128)(2,1)} %xm_hbm), channel_id=1, source_target_pairs={{0,6},{1,7},{2,4},{3,5},{4,2},{5,3},{6,0},{7,1}} | collective-permute-start | bytes 3145736 | tf_op jit(solution)/shard_map/ppermute | solution.py:269
  58.8 0.6 collective-permute-done.2
  59.4 3.3 %add.36 = f32[256,2048]{1,0:T(8,128)} add(f32[256,2048]{1,0:T(8,128)} %get-tuple-element.38, f32[256,2048]{1,0:T(8,128)S(1)} %collective-permute-done.2) | non-fusion elementwise | flops 524288 | bytes 6291456 | tf_op jit(solution)/shard_map/add | solution.py:326
  62.8 1.6 add.37
  64.4 18.4 %collective-permute-done.1.xm_hbm = bf16[256,2048]{1,0:T(8,128)(2,1)S(1)} collective-permute-done((bf16[256,2048]{1,0:T(8,128)(2,1)}, bf16[256,2048]{1,0:T(8,128)(2,1)S(1)}, u32[]{:S(2)}, u32[]{:S(2)}) %collective-permute-start.1) | collective-permute-done | bytes 1048608 | tf_op jit(solution)/shard_map/ppermute | solution.py:269
  82.8 1.0 copy-done.7
  83.8 0.0 collective-permute-start.4
  83.8 2.8 collective-permute-done.4.xo_hbm
  86.6 31.5 %shard_map.74 = (f32[256,2048]{1,0:T(8,128)}, f32[256,2048]{1,0:T(8,128)}, f32[256,2048]{1,0:T(8,128)}, f32[256,2048]{1,0:T(8,128)}) custom-call(s32[8,128]{1,0:T(8,128)} %get-tuple-element.33.table_ref, s32[8,8,256]{2,1,0:T(8,128)} %get-tuple-element.34.pos_ref, bf16[256,2048]{1,0:T(8,128)(2,1)} %copy-done.7, ...), custom_call_target="tpu_custom_call" | custom-call | flops 8858370048 | bytes 77594624 | tf_op jit(solution)/shard_map/pallas_call | solution.py:302
  118.1 4.3 %collective-permute-start.5 = (f32[256,2048]{1,0:T(8,128)}, f32[256,2048]{1,0:T(8,128)S(1)}, u32[]{:S(2)}, u32[]{:S(2)}) collective-permute-start(f32[256,2048]{1,0:T(8,128)} %get-tuple-element.44), channel_id=1, source_target_pairs={{0,1},{1,0},{2,3},{3,2},{4,5},{5,4},{6,7},{7,6}} | collective-permute-start | bytes 6291464 | tf_op jit(solution)/shard_map/ppermute | solution.py:265
  122.4 0.0 collective-permute-start.6
  122.4 1.5 collective-permute-start
  123.9 2.5 collective-permute-done.5
  126.4 3.4 %add.38 = f32[256,2048]{1,0:T(8,128)} add(f32[256,2048]{1,0:T(8,128)} %get-tuple-element.43, f32[256,2048]{1,0:T(8,128)S(1)} %collective-permute-done.5) | non-fusion elementwise | flops 524288 | bytes 6291456 | tf_op jit(solution)/shard_map/add | solution.py:326
  129.8 0.0 collective-permute-done.6
  129.8 1.6 add.39
  131.4 6.0 %collective-permute-done.xm_hbm = bf16[256,2048]{1,0:T(8,128)(2,1)S(1)} collective-permute-done((bf16[256,2048]{1,0:T(8,128)(2,1)}, bf16[256,2048]{1,0:T(8,128)(2,1)S(1)}, u32[]{:S(2)}, u32[]{:S(2)}) %collective-permute-start) | collective-permute-done | bytes 1048608 | tf_op jit(solution)/shard_map/ppermute | solution.py:269
  137.4 1.0 copy-done.6
  138.4 0.6 collective-permute-start.7
  138.9 2.4 collective-permute-start.9
  141.4 0.0 collective-permute-done.7.xo_hbm
  141.4 29.2 %shard_map.75 = (f32[256,2048]{1,0:T(8,128)}, f32[256,2048]{1,0:T(8,128)}, f32[256,2048]{1,0:T(8,128)}, f32[256,2048]{1,0:T(8,128)}) custom-call(s32[8,128]{1,0:T(8,128)} %get-tuple-element.33.table_ref, s32[8,8,256]{2,1,0:T(8,128)} %get-tuple-element.34.pos_ref, bf16[256,2048]{1,0:T(8,128)(2,1)} %copy-done.6, ...), custom_call_target="tpu_custom_call" | custom-call | flops 8858370048 | bytes 77594624 | tf_op jit(solution)/shard_map/pallas_call | solution.py:302
  170.6 6.7 %collective-permute-start.8 = (f32[256,2048]{1,0:T(8,128)}, f32[256,2048]{1,0:T(8,128)S(1)}, u32[]{:S(2)}, u32[]{:S(2)}) collective-permute-start(f32[256,2048]{1,0:T(8,128)} %get-tuple-element.49), channel_id=1, source_target_pairs={{0,1},{1,0},{2,3},{3,2},{4,5},{5,4},{6,7},{7,6}} | collective-permute-start | bytes 6291464 | tf_op jit(solution)/shard_map/ppermute | solution.py:265
  177.3 2.6 collective-permute-start.11
  179.9 1.2 collective-permute-start.10
  181.0 0.3 collective-permute-done.8
  181.3 4.3 %add_add_fusion.3 = f32[256,2048]{1,0:T(8,128)} fusion(f32[256,2048]{1,0:T(8,128)} %collective-permute-done.9, f32[256,2048]{1,0:T(8,128)} %get-tuple-element.48, f32[256,2048]{1,0:T(8,128)S(1)} %collective-permute-done.8), kind=kLoop, calls=%fused_computation.3 | loop fusion | flops 1048576 | bytes 8388608 | tf_op jit(solution)/shard_map/add | solution.py:326
  185.6 18.5 %collective-permute-done.11 = f32[256,2048]{1,0:T(8,128)S(1)} collective-permute-done((f32[256,2048]{1,0:T(8,128)}, f32[256,2048]{1,0:T(8,128)S(1)}, u32[]{:S(2)}, u32[]{:S(2)}) %collective-permute-start.11) | collective-permute-done | bytes 2097184 | tf_op jit(solution)/shard_map/ppermute | solution.py:269
  204.1 1.9 add_add_fusion.2
  206.0 0.6 collective-permute-start.12
  206.6 1.4 collective-permute-start.14
  208.0 1.0 collective-permute-done.12.xo_hbm
  209.0 35.5 %shard_map.76 = (f32[256,2048]{1,0:T(8,128)}, f32[256,2048]{1,0:T(8,128)}, f32[256,2048]{1,0:T(8,128)}, f32[256,2048]{1,0:T(8,128)}) custom-call(s32[8,128]{1,0:T(8,128)} %get-tuple-element.33.table_ref, s32[8,8,256]{2,1,0:T(8,128)} %get-tuple-element.34.pos_ref, bf16[256,2048]{1,0:T(8,128)(2,1)} %xm_hbm, bf16[256,2048]{1,0:T(8,128)(2,1)} %collective-permute-done.12.xo_hbm, ...), custom_call_target="tpu_custom_call" | custom-call | flops 8858370048 | bytes 77594624 | tf_op jit(solution)/shard_map/pallas_call | solution.py:302
  244.5 0.0 collective-permute-start.13
  244.6 0.0 collective-permute-start.16
  244.6 0.7 collective-permute-start.15
  245.3 2.2 collective-permute-start.17
  247.5 0.0 collective-permute-start.18
  247.5 1.4 collective-permute-done.13
  248.9 4.3 %add_add_fusion.1.s0_ref = f32[256,2048]{1,0:T(8,128)} fusion(f32[256,2048]{1,0:T(8,128)} %collective-permute-done.14, f32[256,2048]{1,0:T(8,128)} %get-tuple-element.53, f32[256,2048]{1,0:T(8,128)S(1)} %collective-permute-done.13), kind=kLoop, calls=%fused_computation.1 | loop fusion | flops 1048576 | bytes 8388608 | tf_op jit(solution)/shard_map/add | solution.py:326
  253.2 40.1 %collective-permute-done.16 = f32[256,2048]{1,0:T(8,128)S(1)} collective-permute-done((f32[256,2048]{1,0:T(8,128)}, f32[256,2048]{1,0:T(8,128)S(1)}, u32[]{:S(2)}, u32[]{:S(2)}) %collective-permute-start.16) | collective-permute-done | bytes 2097184 | tf_op jit(solution)/shard_map/ppermute | solution.py:269
  293.3 1.9 add_add_fusion.s1_ref
  295.2 20.2 %collective-permute-done.18.f1_ref = f32[256,2048]{1,0:T(8,128)} collective-permute-done((f32[256,2048]{1,0:T(8,128)}, f32[256,2048]{1,0:T(8,128)}, u32[]{:S(2)}, u32[]{:S(2)}) %collective-permute-start.18) | collective-permute-done | bytes 2097184 | tf_op jit(solution)/shard_map/ppermute | solution.py:269
  315.4 8.0 %combine.1 = bf16[256,2048]{1,0:T(8,128)(2,1)} custom-call(bf16[2,256,512]{2,1,0:T(8,128)(2,1)} %get-tuple-element.31.hit_ref, f32[256,8]{1,0:T(8,128)} %get-tuple-element.32.gate_ref, f32[256,2048]{1,0:T(8,128)} %add_add_fusion.1.s0_ref, f32[256,2048]{1,0:T(8,128)} %add_add_fusion.s1_ref, f32[256,2048]{1,0:T(8,128)} %copy-done.1, ...), custom_call_target="tpu_custom_call" | custom-call | tf_op jit(solution)/shard_map/combine/pallas_call | solution.py:344
  (20 shorter events, 0.0 us)
Async XLA Ops:
  54.4 5.1 %collective-permute-start.2 = (f32[256,2048]{1,0:T(8,128)}, f32[256,2048]{1,0:T(8,128)S(1)}, u32[]{:S(2)}, u32[]{:S(2)}) collective-permute-start(f32[256,2048]{1,0:T(8,128)} %get-tuple-element.39), channel_id=1, source_target_pairs={{0,1},{1,0},{2,3},{3,2},{4,5},{5,4},{6,7},{7,6}} | collective-permute-start | bytes 6291464 | tf_op jit(solution)/shard_map/ppermute | solution.py:265
  55.4 7.3 %collective-permute-start.3 = (f32[256,2048]{1,0:T(8,128)}, f32[256,2048]{1,0:T(8,128)S(1)}, u32[]{:S(2)}, u32[]{:S(2)}) collective-permute-start(f32[256,2048]{1,0:T(8,128)} %get-tuple-element.41), channel_id=1, source_target_pairs={{0,1},{1,0},{2,3},{3,2},{4,5},{5,4},{6,7},{7,6}} | collective-permute-start | bytes 6291464 | tf_op jit(solution)/shard_map/ppermute | solution.py:265
  55.5 27.4 %collective-permute-start.1 = (bf16[256,2048]{1,0:T(8,128)(2,1)}, bf16[256,2048]{1,0:T(8,128)(2,1)S(1)}, u32[]{:S(2)}, u32[]{:S(2)}) collective-permute-start(bf16[256,2048]{1,0:T(8,128)(2,1)} %xm_hbm), channel_id=1, source_target_pairs={{0,6},{1,7},{2,4},{3,5},{4,2},{5,3},{6,0},{7,1}} | collective-permute-start | bytes 3145736 | tf_op jit(solution)/shard_map/ppermute | solution.py:269
  59.4 3.4 %copy-start.2 = (f32[256,2048]{1,0:T(8,128)S(1)}, f32[256,2048]{1,0:T(8,128)}, u32[]{:S(2)}) copy-start(f32[256,2048]{1,0:T(8,128)} %get-tuple-element.40) | copy-start | bytes 6291460
  82.8 1.0 copy-start.7
  83.8 2.8 collective-permute-start.4
  118.1 8.3 %collective-permute-start.5 = (f32[256,2048]{1,0:T(8,128)}, f32[256,2048]{1,0:T(8,128)S(1)}, u32[]{:S(2)}, u32[]{:S(2)}) collective-permute-start(f32[256,2048]{1,0:T(8,128)} %get-tuple-element.44), channel_id=1, source_target_pairs={{0,1},{1,0},{2,3},{3,2},{4,5},{5,4},{6,7},{7,6}} | collective-permute-start | bytes 6291464 | tf_op jit(solution)/shard_map/ppermute | solution.py:265
  122.4 7.4 %collective-permute-start.6 = (f32[256,2048]{1,0:T(8,128)}, f32[256,2048]{1,0:T(8,128)S(1)}, u32[]{:S(2)}, u32[]{:S(2)}) collective-permute-start(f32[256,2048]{1,0:T(8,128)} %get-tuple-element.46), channel_id=1, source_target_pairs={{0,1},{1,0},{2,3},{3,2},{4,5},{5,4},{6,7},{7,6}} | collective-permute-start | bytes 6291464 | tf_op jit(solution)/shard_map/ppermute | solution.py:265
  122.4 15.0 %collective-permute-start = (bf16[256,2048]{1,0:T(8,128)(2,1)}, bf16[256,2048]{1,0:T(8,128)(2,1)S(1)}, u32[]{:S(2)}, u32[]{:S(2)}) collective-permute-start(bf16[256,2048]{1,0:T(8,128)(2,1)} %xm_hbm), channel_id=1, source_target_pairs={{0,4},{1,3},{2,6},{3,1},{4,0},{5,7},{6,2},{7,5}} | collective-permute-start | bytes 3145736 | tf_op jit(solution)/shard_map/ppermute | solution.py:269
  126.4 3.4 %copy-start.3 = (f32[256,2048]{1,0:T(8,128)S(1)}, f32[256,2048]{1,0:T(8,128)}, u32[]{:S(2)}) copy-start(f32[256,2048]{1,0:T(8,128)} %get-tuple-element.45) | copy-start | bytes 6291460
  137.4 1.0 copy-start.6
  138.4 3.0 collective-permute-start.7
  138.9 42.1 %collective-permute-start.9 = (f32[256,2048]{1,0:T(8,128)}, f32[256,2048]{1,0:T(8,128)}, u32[]{:S(2)}, u32[]{:S(2)}) collective-permute-start(f32[256,2048]{1,0:T(8,128)} %add.38), channel_id=1, source_target_pairs={{0,2},{1,5},{2,0},{3,7},{4,6},{5,1},{6,4},{7,3}} | collective-permute-start | bytes 6291464 | tf_op jit(solution)/shard_map/ppermute | solution.py:269
  170.6 10.7 %collective-permute-start.8 = (f32[256,2048]{1,0:T(8,128)}, f32[256,2048]{1,0:T(8,128)S(1)}, u32[]{:S(2)}, u32[]{:S(2)}) collective-permute-start(f32[256,2048]{1,0:T(8,128)} %get-tuple-element.49), channel_id=1, source_target_pairs={{0,1},{1,0},{2,3},{3,2},{4,5},{5,4},{6,7},{7,6}} | collective-permute-start | bytes 6291464 | tf_op jit(solution)/shard_map/ppermute | solution.py:265
  177.3 26.8 %collective-permute-start.11 = (f32[256,2048]{1,0:T(8,128)}, f32[256,2048]{1,0:T(8,128)S(1)}, u32[]{:S(2)}, u32[]{:S(2)}) collective-permute-start(f32[256,2048]{1,0:T(8,128)} %add.39), channel_id=1, source_target_pairs={{0,2},{1,5},{2,0},{3,7},{4,6},{5,1},{6,4},{7,3}} | collective-permute-start | bytes 6291464 | tf_op jit(solution)/shard_map/ppermute | solution.py:269
  179.9 24.2 %collective-permute-start.10 = (f32[256,2048]{1,0:T(8,128)}, f32[256,2048]{1,0:T(8,128)S(1)}, u32[]{:S(2)}, u32[]{:S(2)}) collective-permute-start(f32[256,2048]{1,0:T(8,128)} %get-tuple-element.51), channel_id=1, source_target_pairs={{0,1},{1,0},{2,3},{3,2},{4,5},{5,4},{6,7},{7,6}} | collective-permute-start | bytes 6291464 | tf_op jit(solution)/shard_map/ppermute | solution.py:265
  181.3 22.8 %copy-start.5 = (f32[256,2048]{1,0:T(8,128)S(1)}, f32[256,2048]{1,0:T(8,128)}, u32[]{:S(2)}) copy-start(f32[256,2048]{1,0:T(8,128)} %get-tuple-element.50) | copy-start | bytes 6291460
  204.1 1.9 copy-start
  206.0 3.0 collective-permute-start.12
  206.6 40.9 %collective-permute-start.14 = (f32[256,2048]{1,0:T(8,128)}, f32[256,2048]{1,0:T(8,128)}, u32[]{:S(2)}, u32[]{:S(2)}) collective-permute-start(f32[256,2048]{1,0:T(8,128)} %add.36), channel_id=1, source_target_pairs={{0,2},{1,5},{2,0},{3,7},{4,6},{5,1},{6,4},{7,3}} | collective-permute-start | bytes 6291464 | tf_op jit(solution)/shard_map/ppermute | solution.py:269
  244.5 4.4 %collective-permute-start.13 = (f32[256,2048]{1,0:T(8,128)}, f32[256,2048]{1,0:T(8,128)S(1)}, u32[]{:S(2)}, u32[]{:S(2)}) collective-permute-start(f32[256,2048]{1,0:T(8,128)} %get-tuple-element.54), channel_id=1, source_target_pairs={{0,1},{1,0},{2,3},{3,2},{4,5},{5,4},{6,7},{7,6}} | collective-permute-start | bytes 6291464 | tf_op jit(solution)/shard_map/ppermute | solution.py:265
  244.6 48.7 %collective-permute-start.16 = (f32[256,2048]{1,0:T(8,128)}, f32[256,2048]{1,0:T(8,128)S(1)}, u32[]{:S(2)}, u32[]{:S(2)}) collective-permute-start(f32[256,2048]{1,0:T(8,128)} %add.37), channel_id=1, source_target_pairs={{0,2},{1,5},{2,0},{3,7},{4,6},{5,1},{6,4},{7,3}} | collective-permute-start | bytes 6291464 | tf_op jit(solution)/shard_map/ppermute | solution.py:269
  244.6 48.7 %collective-permute-start.15 = (f32[256,2048]{1,0:T(8,128)}, f32[256,2048]{1,0:T(8,128)S(1)}, u32[]{:S(2)}, u32[]{:S(2)}) collective-permute-start(f32[256,2048]{1,0:T(8,128)} %get-tuple-element.56), channel_id=1, source_target_pairs={{0,1},{1,0},{2,3},{3,2},{4,5},{5,4},{6,7},{7,6}} | collective-permute-start | bytes 6291464 | tf_op jit(solution)/shard_map/ppermute | solution.py:265
  245.3 49.9 %collective-permute-start.17 = (f32[256,2048]{1,0:T(8,128)}, f32[256,2048]{1,0:T(8,128)S(1)}, u32[]{:S(2)}, u32[]{:S(2)}) collective-permute-start(f32[256,2048]{1,0:T(8,128)} %add_add_fusion.3), channel_id=1, source_target_pairs={{0,4},{1,3},{2,6},{3,1},{4,0},{5,7},{6,2},{7,5}} | collective-permute-start | bytes 6291464 | tf_op jit(solution)/shard_map/ppermute | solution.py:269
  247.5 67.9 %collective-permute-start.18 = (f32[256,2048]{1,0:T(8,128)}, f32[256,2048]{1,0:T(8,128)}, u32[]{:S(2)}, u32[]{:S(2)}) collective-permute-start(f32[256,2048]{1,0:T(8,128)} %add_add_fusion.2), channel_id=1, source_target_pairs={{0,4},{1,3},{2,6},{3,1},{4,0},{5,7},{6,2},{7,5}} | collective-permute-start | bytes 6291464 | tf_op jit(solution)/shard_map/ppermute | solution.py:269
  248.9 44.4 %copy-start.4 = (f32[256,2048]{1,0:T(8,128)S(1)}, f32[256,2048]{1,0:T(8,128)}, u32[]{:S(2)}) copy-start(f32[256,2048]{1,0:T(8,128)} %get-tuple-element.55) | copy-start | bytes 6291460
  295.2 20.2 %copy-start.1 = (f32[256,2048]{1,0:T(8,128)}, f32[256,2048]{1,0:T(8,128)S(1)}, u32[]{:S(2)}) copy-start(f32[256,2048]{1,0:T(8,128)S(1)} %collective-permute-done.17.f0_ref) | copy-start | bytes 6291460

commit v7 on v6

--- a/solution.py
+++ b/solution.py
@@ -14,7 +14,7 @@
 
 
 def _route_kernel(chips, turns, idx_ref, g_ref, cap_ref, x_ref, *refs):
-    pos_ref, table_ref, hit_ref, gate_ref, xm_ref, xo_ref, ids_all, send_sem, recv_sem, xsend, xrecv = refs
+    pos_ref, table_ref, hit_ref, gate_ref, pair_ref, xo_ref, ids_all, held, landed, send_sem, recv_sem, xsend, xrecv, lsem = refs
     core, me = lax.axis_index("ep"), lax.axis_index("tp")
     blocks, top, t = ids_all.shape
     e_all = pos_ref.shape[1]
@@ -23,6 +23,8 @@
     peers = [
         (k, {"ep": jnp.bitwise_xor(core, k // chips), "tp": jnp.bitwise_xor(me, k % chips)}) for k in range(1, blocks)
     ]
+    load = pltpu.make_async_copy(x_ref, held, lsem.at[0])
+    load.start()
     barrier = pltpu.get_barrier_semaphore()
     for _, peer in peers:
         pl.semaphore_signal(barrier, inc=1, device_id=peer, device_id_type=mesh_id)
@@ -55,10 +57,19 @@
             device_id_type=mesh_id,
         )
 
-    arrive = [tokens(0, i, x_ref, xm_ref, {"ep": core, "tp": jnp.bitwise_xor(me, turn)}) for i in range(pieces)]
-    forward = [tokens(1, i, xm_ref, xo_ref, {"ep": 1 - core, "tp": me}) for i in range(pieces)]
+    arrive = [tokens(0, i, held, landed, {"ep": core, "tp": jnp.bitwise_xor(me, turn)}) for i in range(pieces)]
+    forward = [tokens(1, i, landed, xo_ref, {"ep": 1 - core, "tp": me}) for i in range(pieces)]
+    keep = [
+        pltpu.make_async_copy(
+            landed.at[pl.ds(i * piece, piece)], pair_ref.at[pl.ds(i * piece, piece)], lsem.at[2 + i]
+        )
+        for i in range(pieces)
+    ]
+    own = pltpu.make_async_copy(held, pair_ref.at[pl.ds(t, t)], lsem.at[1])
+    load.wait()
     for c in arrive:
         c.start()
+    own.start()
     ids_all[pl.ds(here, 1)] = idx_ref[...][None]
     before = (
         lax.broadcasted_iota(jnp.int32, (t, t), 0) < lax.broadcasted_iota(jnp.int32, (t, t), 1)
@@ -94,21 +105,24 @@
     row = lax.broadcasted_iota(jnp.int32, hit_ref.shape[1:], 1)
     for j in range(top):
         hit_ref[j] = (row == table[:, j : j + 1].astype(jnp.int32)).astype(F32).astype(BF16)
-    for c, f in zip(arrive, forward):
+    for c, f, k in zip(arrive, forward, keep):
         c.wait_recv()
         f.start()
-    for c, f in zip(arrive, forward):
+        k.start()
+    for c, f, k in zip(arrive, forward, keep):
         c.wait_send()
+        k.wait()
         f.wait()
+    own.wait()
 
 
 def _expert_kernel(
-    turns, sizes, cuts, table_ref, pos_ref, xm_hbm, xo_hbm, w1_hbm, w3_hbm, w2_hbm, *refs
+    turns, rows0, sizes, cuts, table_ref, pos_ref, xm_hbm, xo_hbm, w1_hbm, w3_hbm, w2_hbm, *refs
 ):
     outs = refs[:4]
     acc, xbuf, *ws, w2s, wsem, osem, xsem = refs[4:]
     w1s, w3s = ws[: len(ws) // 2], ws[len(ws) // 2 :]
-    ahead = 2
+    ahead = len(w1s) + 2
     e_loc, d, _ = w1_hbm.shape
     _, rows, _ = acc.shape
     t = xbuf.shape[1]
@@ -163,8 +177,7 @@
         return copies
 
     tokens = [
-        pltpu.make_async_copy(xm_hbm, xbuf.at[0], xsem.at[0]),
-        pltpu.make_async_copy(xo_hbm, xbuf.at[1], xsem.at[1]),
+        pltpu.make_async_copy(ref.at[pl.ds(rows0[i], t)], xbuf.at[i], xsem.at[i]) for i, ref in enumerate((xm_hbm, xo_hbm))
     ]
     for c in tokens:
         c.start()
@@ -257,7 +270,7 @@
         e_loc, _, ff = w1.shape
         c = (5 * top * t_loc // (2 * e_all) + 7) // 8 * 8
         rows = top * t_loc
-        cuts = (0, 512, 1024, ff)
+        cuts = (0, 512, ff)
         widths = [b - a for a, b in zip(cuts, cuts[1:])]
         blocks = 2 * chips
 
@@ -268,29 +281,29 @@
             pairs = [(2 * k + i, 2 * (k ^ turns[i]) + i) for k in range(chips) for i in range(2)]
             return lax.ppermute(a, ("tp", "ep"), pairs)
 
-        def after(a, *first):
-            return lax.optimization_barrier((a, *first))[0]
-
         out, back = (1, 2), (2, 1)
         pieces = 4
-        pos, groups, hit, gate, xn_mine, xn_other = pl.pallas_call(
+        pos, groups, hit, gate, pair, x_near = pl.pallas_call(
             functools.partial(_route_kernel, chips, out),
             out_shape=[
                 jax.ShapeDtypeStruct((blocks, e_all, t_loc), jnp.int32),
                 jax.ShapeDtypeStruct((blocks, 128), jnp.int32),
                 jax.ShapeDtypeStruct((top, t_loc, rows), BF16),
                 jax.ShapeDtypeStruct((t_loc, 8), F32),
-                jax.ShapeDtypeStruct((t_loc, d), BF16),
+                jax.ShapeDtypeStruct((2 * t_loc, d), BF16),
                 jax.ShapeDtypeStruct((t_loc, d), BF16),
             ],
             in_specs=[vmem, vmem, smem, anym],
             out_specs=[vmem] * 4 + [anym] * 2,
             scratch_shapes=[
                 pltpu.VMEM((blocks, top, t_loc), jnp.int32),
+                pltpu.VMEM((t_loc, d), BF16),
+                pltpu.VMEM((t_loc, d), BF16),
                 pltpu.SemaphoreType.DMA((blocks,)),
                 pltpu.SemaphoreType.DMA((blocks,)),
                 pltpu.SemaphoreType.DMA((2, pieces)),
                 pltpu.SemaphoreType.DMA((2, pieces)),
+                pltpu.SemaphoreType.DMA((2 + pieces,)),
             ],
             compiler_params=pltpu.CompilerParams(collective_id=0, has_side_effects=True, vmem_limit_bytes=VMEM_BYTES),
             name="route",
@@ -298,9 +311,9 @@
 
         sizes = (64, (c + 7 + 7) // 8 * 8)
 
-        def stage(turns, mine, other, split):
+        def stage(turns, mine, other, split, rows0=(0, 0)):
             return pl.pallas_call(
-                functools.partial(_expert_kernel, turns, sizes, cuts),
+                functools.partial(_expert_kernel, turns, rows0, sizes, cuts),
                 out_shape=[jax.ShapeDtypeStruct((n, d), F32) for n in split * 2],
                 in_specs=[smem, vmem] + [anym] * 5,
                 out_specs=[anym] * 4,
@@ -326,20 +339,20 @@
                 sums.append(functools.reduce(jnp.add, [m[q] for m in more], parts[2 + q] + other))
             return sums
 
-        x_next = after(x, pos)
-        x_d, x_f = shift(x_next, (3, 3)), shift(x_next, back)
-        halves = (rows // 2, rows // 2)
-        near = merge(stage(out, xn_mine, xn_other, halves))
-        x_d = after(x_d, *near)
+        halves, early = (rows // 2, rows // 2), (rows // 4, rows - rows // 4)
+        rest = shift(pair, back)
+        rest_other = swap(rest)
+        own_x = swap(x)
+        near = merge(stage(out, pair, x_near, early))
         near = [shift(a, out) for a in near]
-        diag = merge(stage((3, 3), x_d, swap(x_d), halves))
-        x_f = after(x_f, *diag)
+        diag = merge(stage((3, 3), rest, rest_other, halves))
         via = [shift(a, out) for a in diag]
-        far = merge(stage(back, x_f, swap(x_f), halves), via)
-        x_o = after(x, *far)
+        far = merge(stage(back, rest, rest_other, halves, (t_loc, t_loc)), via)
         far = [shift(a, back) for a in far]
-        sums = merge(stage((0, 0), x_o, swap(x_o), halves), near)
-        steps = 8
+        near = jnp.concatenate(near, axis=0)
+        near = [near[: halves[0]], near[halves[0] :]]
+        sums = merge(stage((0, 0), x, own_x, halves), near)
+        steps = 4
         part = pl.BlockSpec((rows // 2, d // steps), lambda i: (0, i))
         return pl.pallas_call(
             _combine_kernel,

time: 324 us -> 309 us (0.954)
  waiting for transfers between devices: 112 us -> 103 us
  Pallas kernels: 159 us -> 152 us
  other arithmetic: 22.3 us -> 25.8 us
    ppermute x11 -> x10, waiting for transfers between devices: 8.54 us -> 0.03 us  [swap(): return lax.ppermute(a, 'ep', [(0, 1), (1, 0)])]
    pallas_call x4, Pallas kernels: 129 us -> 125 us  [stage(): pl.pallas_call(functools.partial(_expert_kernel, turns, rows0, sizes, cut...]
    add x4, other arithmetic: 10 us -> 14.2 us  [merge(): parts[2 + q] + other]
    ppermute x8 -> x7, starting transfers between devices: 13.5 us -> 10.5 us  [shift(): return lax.ppermute(a, ('tp', 'ep'), pairs)]
    ppermute x11 -> x10, starting transfers between devices: 15.2 us -> 17.1 us  [swap(): return lax.ppermute(a, 'ep', [(0, 1), (1, 0)])]
    ppermute x8 -> x7, waiting for transfers between devices: 103 us -> 103 us  [shift(): return lax.ppermute(a, ('tp', 'ep'), pairs)]
    add x4 -> x3, other arithmetic: 12.3 us -> 11.6 us  [merge(): functools.reduce(jnp.add, [m[q] for m in more], parts[2 + q] + other)]
  transfers between devices with their start and end apart: 19 -> 17, of which waited for: 11 -> 3; matrix products, arithmetic and copies ran while one was open for 6% -> 8% of each run, Pallas kernels for 20% -> 40%
where the time goes in v7:
time: 309 us
  Pallas kernels  152 us (49%)
  waiting for transfers between devices  103 us (33%)
  starting transfers between devices  27.6 us (9%)
  other arithmetic  25.8 us (8%)
    pallas_call x4, Pallas kernels, stage(): pl.pallas_call(functools.partial(_expert_kernel, turns, rows0, sizes, cut...  125 us
    ppermute x7, waiting for transfers between devices, shift(): return lax.ppermute(a, ('tp', 'ep'), pairs)  103 us
    pallas_call x1, Pallas kernels, layer(): pl.pallas_call(functools.partial(_route_kernel, chips, out), out_shape=[j...  21 us
    ppermute x10, starting transfers between devices, swap(): return lax.ppermute(a, 'ep', [(0, 1), (1, 0)])  17.1 us
    add x4, other arithmetic, merge(): parts[2 + q] + other  14.2 us
    add x3, other arithmetic, merge(): functools.reduce(jnp.add, [m[q] for m in more], parts[2 + q] + other)  11.6 us
    ppermute x7, starting transfers between devices, shift(): return lax.ppermute(a, ('tp', 'ep'), pairs)  10.5 us
  transfers between devices with their start and end apart: 17, of which 3 were waited for; matrix products, arithmetic and copies ran while one was open for 8% of the time, Pallas kernels for 40%

profile of v7, /device:TPU:0, one launch (start us, length us, event | category | flops | bytes accessed | tf_op | source)
XLA Modules:
  0.0 308.7 jit_solution(7001788129484114450)
XLA Ops:
  0.0 21.0 %route.1 = (s32[8,8,256]{2,1,0:T(8,128)}, s32[8,128]{1,0:T(8,128)}, bf16[2,256,512]{2,1,0:T(8,128)(2,1)}, f32[256,8]{1,0:T(8,128)}, bf16[512,2048]{1,0:T(8,128)(2,1)}, /*index=5*/bf16[256,2048]{1,0:T(8,128)(2,1)}) custom-call(s32[2,256]{1,0:T(2,128)} %bitcast.2, f32[2,256]{1,0:T(2,128)} %bitcast.3, s32[8]{0:T(128)} %cap_ref.1, bf16[256,2048]{1,0:T(8,128)(2,1)} %xm_hbm.1), custom_call_target="tpu_custom_call" | custom-call | tf_op jit(solution)/shard_map/route/pallas_call | solution.py:286
  21.0 1.1 collective-permute-start.7
  22.2 25.2 %collective-permute-done.7.xm_hbm = bf16[512,2048]{1,0:T(8,128)(2,1)} collective-permute-done((bf16[512,2048]{1,0:T(8,128)(2,1)}, bf16[512,2048]{1,0:T(8,128)(2,1)}, u32[]{:S(2)}, u32[]{:S(2)}) %collective-permute-start.7) | collective-permute-done | bytes 2097184 | tf_op jit(solution)/shard_map/ppermute | solution.py:282
  47.4 0.0 collective-permute-start.8
  47.4 32.4 %shard_map.74 = (f32[128,2048]{1,0:T(8,128)}, f32[384,2048]{1,0:T(8,128)}, f32[128,2048]{1,0:T(8,128)}, f32[384,2048]{1,0:T(8,128)}) custom-call(s32[8,128]{1,0:T(8,128)} %get-tuple-element.29.table_ref, s32[8,8,256]{2,1,0:T(8,128)} %get-tuple-element.30.pos_ref, bf16[512,2048]{1,0:T(8,128)(2,1)} %get-tuple-element.33.xm_hbm, ...), custom_call_target="tpu_custom_call" | custom-call | flops 8858370048 | bytes 77594624 | tf_op jit(solution)/shard_map/pallas_call | solution.py:315
  79.8 0.6 collective-permute-start.4
  80.3 0.0 collective-permute-done.8.xo_hbm
  80.3 29.6 %shard_map.76 = (f32[256,2048]{1,0:T(8,128)}, f32[256,2048]{1,0:T(8,128)}, f32[256,2048]{1,0:T(8,128)}, f32[256,2048]{1,0:T(8,128)}) custom-call(s32[8,128]{1,0:T(8,128)} %get-tuple-element.29.table_ref, s32[8,8,256]{2,1,0:T(8,128)} %get-tuple-element.30.pos_ref, bf16[512,2048]{1,0:T(8,128)(2,1)} %collective-permute-done.7.xm_hbm, ...), custom_call_target="tpu_custom_call" | custom-call | flops 8858370048 | bytes 77594624 | tf_op jit(solution)/shard_map/pallas_call | solution.py:315
  109.9 6.0 %collective-permute-start.14 = (f32[256,2048]{1,0:T(8,128)}, f32[256,2048]{1,0:T(8,128)}, u32[]{:S(2)}, u32[]{:S(2)}) collective-permute-start(f32[256,2048]{1,0:T(8,128)} %get-tuple-element.48), channel_id=1, source_target_pairs={{0,1},{1,0},{2,3},{3,2},{4,5},{5,4},{6,7},{7,6}} | collective-permute-start | bytes 6291464 | tf_op jit(solution)/shard_map/ppermute | solution.py:278
  116.0 0.0 collective-permute-start.10
  116.0 0.5 collective-permute-start.2
  116.5 27.0 %shard_map.75 = (f32[256,2048]{1,0:T(8,128)}, f32[256,2048]{1,0:T(8,128)}, f32[256,2048]{1,0:T(8,128)}, f32[256,2048]{1,0:T(8,128)}) custom-call(s32[8,128]{1,0:T(8,128)} %get-tuple-element.29.table_ref, s32[8,8,256]{2,1,0:T(8,128)} %get-tuple-element.30.pos_ref, bf16[512,2048]{1,0:T(8,128)(2,1)} %collective-permute-done.7.xm_hbm, ...), custom_call_target="tpu_custom_call" | custom-call | flops 8858370048 | bytes 77594624 | tf_op jit(solution)/shard_map/pallas_call | solution.py:315
  143.5 9.4 %collective-permute-start.13 = (f32[256,2048]{1,0:T(8,128)}, f32[256,2048]{1,0:T(8,128)}, u32[]{:S(2)}, u32[]{:S(2)}) collective-permute-start(f32[256,2048]{1,0:T(8,128)} %get-tuple-element.46), channel_id=1, source_target_pairs={{0,1},{1,0},{2,3},{3,2},{4,5},{5,4},{6,7},{7,6}} | collective-permute-start | bytes 6291464 | tf_op jit(solution)/shard_map/ppermute | solution.py:278
  152.9 0.0 collective-permute-done.14
  152.9 0.0 collective-permute-start.9
  152.9 4.0 %add.46 = f32[256,2048]{1,0:T(8,128)} add(f32[256,2048]{1,0:T(8,128)} %get-tuple-element.47, f32[256,2048]{1,0:T(8,128)} %collective-permute-done.14) | non-fusion elementwise | flops 524288 | bytes 6291456 | tf_op jit(solution)/shard_map/add | solution.py:339
  157.0 0.0 collective-permute-done.2
  157.0 5.4 %collective-permute-start.15 = (f32[256,2048]{1,0:T(8,128)}, f32[256,2048]{1,0:T(8,128)}, u32[]{:S(2)}, u32[]{:S(2)}) collective-permute-start(f32[256,2048]{1,0:T(8,128)} %add.46), channel_id=1, source_target_pairs={{0,2},{1,5},{2,0},{3,7},{4,6},{5,1},{6,4},{7,3}} | collective-permute-start | bytes 6291464 | tf_op jit(solution)/shard_map/ppermute | solution.py:282
  162.4 0.0 collective-permute-done.10
  162.4 0.0 collective-permute-start
  162.4 3.3 %add.43 = f32[256,2048]{1,0:T(8,128)} add(f32[256,2048]{1,0:T(8,128)S(1)} %copy-done.4, f32[256,2048]{1,0:T(8,128)} %collective-permute-done.10) | non-fusion elementwise | flops 524288 | bytes 6291456 | tf_op jit(solution)/shard_map/add | solution.py:339
  165.7 0.0 collective-permute-done.4
  165.7 0.5 collective-permute-start.11
  166.2 2.6 add.37
  168.8 4.3 %add.38 = f32[384,2048]{1,0:T(8,128)} add(f32[384,2048]{1,0:T(8,128)S(1)} %copy-done.1, f32[384,2048]{1,0:T(8,128)} %collective-permute-done.4) | non-fusion elementwise | flops 786432 | bytes 9437184 | tf_op jit(solution)/shard_map/add | solution.py:339
  173.0 0.0 collective-permute-done.xo_hbm
  173.1 1.0 copy-done.8
  174.0 1.3 collective-permute-start.5
  175.3 35.7 %shard_map.73 = (f32[256,2048]{1,0:T(8,128)}, f32[256,2048]{1,0:T(8,128)}, f32[256,2048]{1,0:T(8,128)}, f32[256,2048]{1,0:T(8,128)}) custom-call(s32[8,128]{1,0:T(8,128)} %get-tuple-element.29.table_ref, s32[8,8,256]{2,1,0:T(8,128)} %get-tuple-element.30.pos_ref, bf16[256,2048]{1,0:T(8,128)(2,1)} %xm_hbm.1, bf16[256,2048]{1,0:T(8,128)(2,1)} %copy-done.8, ...), custom_call_target="tpu_custom_call" | custom-call | flops 8858370048 | bytes 77594624 | tf_op jit(solution)/shard_map/pallas_call | solution.py:315
  211.0 0.0 collective-permute-done.13
  211.0 0.0 collective-permute-start.3
  211.0 0.0 collective-permute-done.9
  211.1 0.0 collective-permute-start.1
  211.1 0.0 collective-permute-done.15
  211.1 0.5 collective-permute-start.6
  211.6 3.5 %add_add_fusion = f32[256,2048]{1,0:T(8,128)S(1)} fusion(f32[256,2048]{1,0:T(8,128)} %collective-permute-done.15, f32[256,2048]{1,0:T(8,128)} %get-tuple-element.45, f32[256,2048]{1,0:T(8,128)} %collective-permute-done.13), kind=kLoop, calls=%fused_computation.3 | loop fusion | flops 1048576 | bytes 8388608 | tf_op jit(solution)/shard_map/add | solution.py:339
  215.1 0.0 collective-permute-done.11
  215.1 0.0 collective-permute-start.16
  215.2 2.9 add_add_fusion.1
  218.1 58.4 %collective-permute-done.3 = f32[128,2048]{1,0:T(8,128)S(1)} collective-permute-done((f32[128,2048]{1,0:T(8,128)}, f32[128,2048]{1,0:T(8,128)S(1)}, u32[]{:S(2)}, u32[]{:S(2)}) %collective-permute-start.3) | collective-permute-done | bytes 1048608 | tf_op jit(solution)/shard_map/ppermute | solution.py:282
  276.5 2.1 collective-permute-start.12
  278.6 0.0 collective-permute-done.1
  278.6 0.0 collective-permute-done.6
  278.6 0.0 collective-permute-done.5
  278.6 5.2 %slice_add_fusion = (f32[256,2048]{1,0:T(8,128)}, f32[256,2048]{1,0:T(8,128)}) fusion(f32[384,2048]{1,0:T(8,128)} %collective-permute-done.5, f32[256,2048]{1,0:T(8,128)S(1)} %copy-done.3, f32[256,2048]{1,0:T(8,128)S(1)} %collective-permute-done.6, f32[128,2048]{1,0:T(8,128)S(1)} %collective-permute-done.3, f32[256,2048]{1,0:T(8,128)S(1)} %copy-done.2, ...), kind=kLoop, calls=%fused_computation | loop fusion | flops 2621440 | bytes 18874368 | tf_op jit(solution)/shard_map/add | solution.py:339
  283.8 0.0 collective-permute-done.16.f1_ref
  283.8 18.9 %collective-permute-done.12.f0_ref = f32[256,2048]{1,0:T(8,128)} collective-permute-done((f32[256,2048]{1,0:T(8,128)S(1)}, f32[256,2048]{1,0:T(8,128)}, u32[]{:S(2)}, u32[]{:S(2)}) %collective-permute-start.12) | collective-permute-done | bytes 2097184 | tf_op jit(solution)/shard_map/ppermute | solution.py:282
  302.7 6.0 %combine.1 = bf16[256,2048]{1,0:T(8,128)(2,1)} custom-call(bf16[2,256,512]{2,1,0:T(8,128)(2,1)} %get-tuple-element.27.hit_ref, f32[256,8]{1,0:T(8,128)} %get-tuple-element.28.gate_ref, f32[256,2048]{1,0:T(8,128)} %get-tuple-element.50.s0_ref, f32[256,2048]{1,0:T(8,128)} %get-tuple-element.49.s1_ref, f32[256,2048]{1,0:T(8,128)} %collective-permute-done.12.f0_ref, ...), custom_call_target="tpu_custom_call" | custom-call | tf_op jit(solution)/shard_map/combine/pallas_call | solution.py:357
  (17 shorter events, 0.0 us)
Async XLA Ops:
  21.0 26.4 %collective-permute-start.7 = (bf16[512,2048]{1,0:T(8,128)(2,1)}, bf16[512,2048]{1,0:T(8,128)(2,1)}, u32[]{:S(2)}, u32[]{:S(2)}) collective-permute-start(bf16[512,2048]{1,0:T(8,128)(2,1)} %get-tuple-element.33.xm_hbm), channel_id=1, source_target_pairs={{0,4},{1,3},{2,6},{3,1},{4,0},{5,7},{6,2},{7,5}} | collective-permute-start | bytes 6291464 | tf_op jit(solution)/shard_map/ppermute | solution.py:282
  47.4 32.9 %collective-permute-start.8 = (bf16[512,2048]{1,0:T(8,128)(2,1)}, bf16[512,2048]{1,0:T(8,128)(2,1)}, u32[]{:S(2)}, u32[]{:S(2)}) collective-permute-start(bf16[512,2048]{1,0:T(8,128)(2,1)} %collective-permute-done.7.xm_hbm), channel_id=1, source_target_pairs={{0,1},{1,0},{2,3},{3,2},{4,5},{5,4},{6,7},{7,6}} | collective-permute-start | bytes 6291464 | tf_op jit(solution)/shard_map/ppermute | solution.py:278
  79.8 85.9 %collective-permute-start.4 = (f32[384,2048]{1,0:T(8,128)}, f32[384,2048]{1,0:T(8,128)}, u32[]{:S(2)}, u32[]{:S(2)}) collective-permute-start(f32[384,2048]{1,0:T(8,128)} %get-tuple-element.38), channel_id=1, source_target_pairs={{0,1},{1,0},{2,3},{3,2},{4,5},{5,4},{6,7},{7,6}} | collective-permute-start | bytes 9437192 | tf_op jit(solution)/shard_map/ppermute | solution.py:278
  109.9 43.0 %collective-permute-start.14 = (f32[256,2048]{1,0:T(8,128)}, f32[256,2048]{1,0:T(8,128)}, u32[]{:S(2)}, u32[]{:S(2)}) collective-permute-start(f32[256,2048]{1,0:T(8,128)} %get-tuple-element.48), channel_id=1, source_target_pairs={{0,1},{1,0},{2,3},{3,2},{4,5},{5,4},{6,7},{7,6}} | collective-permute-start | bytes 6291464 | tf_op jit(solution)/shard_map/ppermute | solution.py:278
  116.0 46.4 %collective-permute-start.10 = (f32[256,2048]{1,0:T(8,128)}, f32[256,2048]{1,0:T(8,128)}, u32[]{:S(2)}, u32[]{:S(2)}) collective-permute-start(f32[256,2048]{1,0:T(8,128)} %get-tuple-element.44), channel_id=1, source_target_pairs={{0,1},{1,0},{2,3},{3,2},{4,5},{5,4},{6,7},{7,6}} | collective-permute-start | bytes 6291464 | tf_op jit(solution)/shard_map/ppermute | solution.py:278
  116.0 41.0 %collective-permute-start.2 = (f32[128,2048]{1,0:T(8,128)}, f32[128,2048]{1,0:T(8,128)}, u32[]{:S(2)}, u32[]{:S(2)}) collective-permute-start(f32[128,2048]{1,0:T(8,128)} %get-tuple-element.36), channel_id=1, source_target_pairs={{0,1},{1,0},{2,3},{3,2},{4,5},{5,4},{6,7},{7,6}} | collective-permute-start | bytes 3145736 | tf_op jit(solution)/shard_map/ppermute | solution.py:278
  143.5 67.5 %collective-permute-start.13 = (f32[256,2048]{1,0:T(8,128)}, f32[256,2048]{1,0:T(8,128)}, u32[]{:S(2)}, u32[]{:S(2)}) collective-permute-start(f32[256,2048]{1,0:T(8,128)} %get-tuple-element.46), channel_id=1, source_target_pairs={{0,1},{1,0},{2,3},{3,2},{4,5},{5,4},{6,7},{7,6}} | collective-permute-start | bytes 6291464 | tf_op jit(solution)/shard_map/ppermute | solution.py:278
  152.9 58.2 %collective-permute-start.9 = (f32[256,2048]{1,0:T(8,128)}, f32[256,2048]{1,0:T(8,128)}, u32[]{:S(2)}, u32[]{:S(2)}) collective-permute-start(f32[256,2048]{1,0:T(8,128)} %get-tuple-element.42), channel_id=1, source_target_pairs={{0,1},{1,0},{2,3},{3,2},{4,5},{5,4},{6,7},{7,6}} | collective-permute-start | bytes 6291464 | tf_op jit(solution)/shard_map/ppermute | solution.py:278
  152.9 9.4 %copy-start = (bf16[256,2048]{1,0:T(8,128)(2,1)S(1)}, bf16[256,2048]{1,0:T(8,128)(2,1)}, u32[]{:S(2)}) copy-start(bf16[256,2048]{1,0:T(8,128)(2,1)} %xm_hbm.1) | copy-start | bytes 3145732
  152.9 9.4 %copy-start.4 = (f32[256,2048]{1,0:T(8,128)S(1)}, f32[256,2048]{1,0:T(8,128)}, u32[]{:S(2)}) copy-start(f32[256,2048]{1,0:T(8,128)} %get-tuple-element.43) | copy-start | bytes 6291460
  157.0 54.1 %collective-permute-start.15 = (f32[256,2048]{1,0:T(8,128)}, f32[256,2048]{1,0:T(8,128)}, u32[]{:S(2)}, u32[]{:S(2)}) collective-permute-start(f32[256,2048]{1,0:T(8,128)} %add.46), channel_id=1, source_target_pairs={{0,2},{1,5},{2,0},{3,7},{4,6},{5,1},{6,4},{7,3}} | collective-permute-start | bytes 6291464 | tf_op jit(solution)/shard_map/ppermute | solution.py:282
  162.4 10.7 %collective-permute-start = (bf16[256,2048]{1,0:T(8,128)(2,1)S(1)}, bf16[256,2048]{1,0:T(8,128)(2,1)S(1)}, u32[]{:S(2)}, u32[]{:S(2)}) collective-permute-start(bf16[256,2048]{1,0:T(8,128)(2,1)S(1)} %copy-done), channel_id=1, source_target_pairs={{0,1},{1,0},{2,3},{3,2},{4,5},{5,4},{6,7},{7,6}} | collective-permute-start | bytes 3145736 | tf_op jit(solution)/shard_map/ppermute | solution.py:278
  162.4 3.8 %copy-start.7 = (f32[128,2048]{1,0:T(8,128)S(1)}, f32[128,2048]{1,0:T(8,128)}, u32[]{:S(2)}) copy-start(f32[128,2048]{1,0:T(8,128)} %get-tuple-element.35) | copy-start | bytes 3145732
  165.7 3.1 %copy-start.1 = (f32[384,2048]{1,0:T(8,128)S(1)}, f32[384,2048]{1,0:T(8,128)}, u32[]{:S(2)}) copy-start(f32[384,2048]{1,0:T(8,128)} %get-tuple-element.37) | copy-start | bytes 9437188
  165.7 49.4 %collective-permute-start.11 = (f32[256,2048]{1,0:T(8,128)}, f32[256,2048]{1,0:T(8,128)}, u32[]{:S(2)}, u32[]{:S(2)}) collective-permute-start(f32[256,2048]{1,0:T(8,128)} %add.43), channel_id=1, source_target_pairs={{0,2},{1,5},{2,0},{3,7},{4,6},{5,1},{6,4},{7,3}} | collective-permute-start | bytes 6291464 | tf_op jit(solution)/shard_map/ppermute | solution.py:282
  173.0 1.0 copy-start.8
  174.0 104.6 %collective-permute-start.5 = (f32[384,2048]{1,0:T(8,128)}, f32[384,2048]{1,0:T(8,128)}, u32[]{:S(2)}, u32[]{:S(2)}) collective-permute-start(f32[384,2048]{1,0:T(8,128)} %add.38), channel_id=1, source_target_pairs={{0,2},{1,5},{2,0},{3,7},{4,6},{5,1},{6,4},{7,3}} | collective-permute-start | bytes 9437192 | tf_op jit(solution)/shard_map/ppermute | solution.py:282
  211.0 65.5 %collective-permute-start.3 = (f32[128,2048]{1,0:T(8,128)}, f32[128,2048]{1,0:T(8,128)S(1)}, u32[]{:S(2)}, u32[]{:S(2)}) collective-permute-start(f32[128,2048]{1,0:T(8,128)} %add.37), channel_id=1, source_target_pairs={{0,2},{1,5},{2,0},{3,7},{4,6},{5,1},{6,4},{7,3}} | collective-permute-start | bytes 3145736 | tf_op jit(solution)/shard_map/ppermute | solution.py:282
  211.1 67.5 %collective-permute-start.1 = (f32[256,2048]{1,0:T(8,128)}, f32[256,2048]{1,0:T(8,128)S(1)}, u32[]{:S(2)}, u32[]{:S(2)}) collective-permute-start(f32[256,2048]{1,0:T(8,128)} %get-tuple-element.32), channel_id=1, source_target_pairs={{0,1},{1,0},{2,3},{3,2},{4,5},{5,4},{6,7},{7,6}} | collective-permute-start | bytes 6291464 | tf_op jit(solution)/shard_map/ppermute | solution.py:278
  211.1 67.5 %collective-permute-start.6 = (f32[256,2048]{1,0:T(8,128)}, f32[256,2048]{1,0:T(8,128)S(1)}, u32[]{:S(2)}, u32[]{:S(2)}) collective-permute-start(f32[256,2048]{1,0:T(8,128)} %get-tuple-element.40), channel_id=1, source_target_pairs={{0,1},{1,0},{2,3},{3,2},{4,5},{5,4},{6,7},{7,6}} | collective-permute-start | bytes 6291464 | tf_op jit(solution)/shard_map/ppermute | solution.py:278
  211.6 3.6 %copy-start.6 = (f32[256,2048]{1,0:T(8,128)S(1)}, f32[256,2048]{1,0:T(8,128)}, u32[]{:S(2)}) copy-start(f32[256,2048]{1,0:T(8,128)} %get-tuple-element.41) | copy-start | bytes 6291460
  215.1 68.7 %collective-permute-start.16 = (f32[256,2048]{1,0:T(8,128)S(1)}, f32[256,2048]{1,0:T(8,128)S(1)}, u32[]{:S(2)}, u32[]{:S(2)}) collective-permute-start(f32[256,2048]{1,0:T(8,128)S(1)} %add_add_fusion), channel_id=1, source_target_pairs={{0,4},{1,3},{2,6},{3,1},{4,0},{5,7},{6,2},{7,5}} | collective-permute-start | bytes 6291464 | tf_op jit(solution)/shard_map/ppermute | solution.py:282
  215.2 63.4 %copy-start.2 = (f32[256,2048]{1,0:T(8,128)S(1)}, f32[256,2048]{1,0:T(8,128)}, u32[]{:S(2)}) copy-start(f32[256,2048]{1,0:T(8,128)} %get-tuple-element.31) | copy-start | bytes 6291460
  215.2 63.4 %copy-start.3 = (f32[256,2048]{1,0:T(8,128)S(1)}, f32[256,2048]{1,0:T(8,128)}, u32[]{:S(2)}) copy-start(f32[256,2048]{1,0:T(8,128)} %get-tuple-element.39) | copy-start | bytes 6291460
  276.5 26.2 %collective-permute-start.12 = (f32[256,2048]{1,0:T(8,128)S(1)}, f32[256,2048]{1,0:T(8,128)}, u32[]{:S(2)}, u32[]{:S(2)}) collective-permute-start(f32[256,2048]{1,0:T(8,128)S(1)} %add_add_fusion.1), channel_id=1, source_target_pairs={{0,4},{1,3},{2,6},{3,1},{4,0},{5,7},{6,2},{7,5}} | collective-permute-start | bytes 6291464 | tf_op jit(solution)/shard_map/ppermute | solution.py:282
  283.8 18.9 %copy-start.5 = (f32[256,2048]{1,0:T(8,128)}, f32[256,2048]{1,0:T(8,128)S(1)}, u32[]{:S(2)}) copy-start(f32[256,2048]{1,0:T(8,128)S(1)} %collective-permute-done.16.f1_ref) | copy-start | bytes 6291460

commit v8 on v7

--- a/solution.py
+++ b/solution.py
@@ -339,26 +339,26 @@
                 sums.append(functools.reduce(jnp.add, [m[q] for m in more], parts[2 + q] + other))
             return sums
 
-        halves, early = (rows // 2, rows // 2), (rows // 4, rows - rows // 4)
+        early, late = (rows // 4, rows - rows // 4), (rows - rows // 4, rows // 4)
         rest = shift(pair, back)
         rest_other = swap(rest)
         own_x = swap(x)
         near = merge(stage(out, pair, x_near, early))
         near = [shift(a, out) for a in near]
-        diag = merge(stage((3, 3), rest, rest_other, halves))
+        diag = merge(stage((3, 3), rest, rest_other, late))
         via = [shift(a, out) for a in diag]
-        far = merge(stage(back, rest, rest_other, halves, (t_loc, t_loc)), via)
+        far = merge(stage(back, rest, rest_other, late, (t_loc, t_loc)), via)
         far = [shift(a, back) for a in far]
         near = jnp.concatenate(near, axis=0)
-        near = [near[: halves[0]], near[halves[0] :]]
-        sums = merge(stage((0, 0), x, own_x, halves), near)
+        near = [near[: late[0]], near[late[0] :]]
+        sums = merge(stage((0, 0), x, own_x, late), near)
         steps = 4
-        part = pl.BlockSpec((rows // 2, d // steps), lambda i: (0, i))
+        parts = [pl.BlockSpec((n, d // steps), lambda i: (0, i)) for n in late]
         return pl.pallas_call(
             _combine_kernel,
             out_shape=jax.ShapeDtypeStruct((t_loc, d), BF16),
             grid=(steps,),
-            in_specs=[vmem, vmem] + [part] * 4,
+            in_specs=[vmem, vmem] + parts * 2,
             out_specs=pl.BlockSpec((t_loc, d // steps), lambda i: (0, i)),
             name="combine",
         )(hit, gate, *sums, *far)

time: 309 us -> 321 us (1.039)
  waiting for transfers between devices: 103 us -> 110 us
  local copies, waits for them, and re-layouts: 1 us -> 6.35 us
    unnamed x18 -> x26, local copies, waits for them, and re-layouts: 1 us -> 6.35 us
    ppermute x10, waiting for transfers between devices: 0.03 us -> 4.18 us  [swap(): return lax.ppermute(a, 'ep', [(0, 1), (1, 0)])]
    ppermute x7, waiting for transfers between devices: 103 us -> 106 us  [shift(): return lax.ppermute(a, ('tp', 'ep'), pairs)]
    add x3 -> x4, other arithmetic: 11.6 us -> 11.7 us  [merge(): functools.reduce(jnp.add, [m[q] for m in more], parts[2 + q] + other)]
  transfers between devices with their start and end apart: 17 -> 17, of which waited for: 3 -> 4; matrix products, arithmetic and copies ran while one was open for 8% -> 8% of each run, Pallas kernels for 40% -> 30%
where the time goes in v8:
time: 321 us
  Pallas kernels  152 us (47%)
  waiting for transfers between devices  110 us (34%)
  starting transfers between devices  27.7 us (9%)
  other arithmetic  24.3 us (8%)
  local copies, waits for them, and re-layouts  6.35 us (2%)
    pallas_call x4, Pallas kernels, stage(): pl.pallas_call(functools.partial(_expert_kernel, turns, rows0, sizes, cut...  125 us
    ppermute x7, waiting for transfers between devices, shift(): return lax.ppermute(a, ('tp', 'ep'), pairs)  106 us
    pallas_call x1, Pallas kernels, layer(): pl.pallas_call(functools.partial(_route_kernel, chips, out), out_shape=[j...  21 us
    ppermute x10, starting transfers between devices, swap(): return lax.ppermute(a, 'ep', [(0, 1), (1, 0)])  17.1 us
    add x4, other arithmetic, merge(): parts[2 + q] + other  12.6 us
    add x4, other arithmetic, merge(): functools.reduce(jnp.add, [m[q] for m in more], parts[2 + q] + other)  11.7 us
    ppermute x7, starting transfers between devices, shift(): return lax.ppermute(a, ('tp', 'ep'), pairs)  10.6 us
  transfers between devices with their start and end apart: 17, of which 4 were waited for; matrix products, arithmetic and copies ran while one was open for 8% of the time, Pallas kernels for 30%

profile of v8, /device:TPU:0, one launch (start us, length us, event | category | flops | bytes accessed | tf_op | source)
XLA Modules:
  0.0 320.6 jit_solution(214579703637660807)
XLA Ops:
  0.0 21.0 %route.1 = (s32[8,8,256]{2,1,0:T(8,128)}, s32[8,128]{1,0:T(8,128)}, bf16[2,256,512]{2,1,0:T(8,128)(2,1)}, f32[256,8]{1,0:T(8,128)}, bf16[512,2048]{1,0:T(8,128)(2,1)}, /*index=5*/bf16[256,2048]{1,0:T(8,128)(2,1)}) custom-call(s32[2,256]{1,0:T(2,128)} %bitcast.2, f32[2,256]{1,0:T(2,128)} %bitcast.3, s32[8]{0:T(128)} %cap_ref.1, bf16[256,2048]{1,0:T(8,128)(2,1)} %xm_hbm.1), custom_call_target="tpu_custom_call" | custom-call | tf_op jit(solution)/shard_map/route/pallas_call | solution.py:286
  21.0 1.1 collective-permute-start.7
  22.1 25.1 %collective-permute-done.7.xm_hbm = bf16[512,2048]{1,0:T(8,128)(2,1)S(1)} collective-permute-done((bf16[512,2048]{1,0:T(8,128)(2,1)}, bf16[512,2048]{1,0:T(8,128)(2,1)S(1)}, u32[]{:S(2)}, u32[]{:S(2)}) %collective-permute-start.7) | collective-permute-done | bytes 2097184 | tf_op jit(solution)/shard_map/ppermute | solution.py:282
  47.3 1.3 copy-done
  48.6 0.0 collective-permute-start.8
  48.6 4.2 %collective-permute-done.8.xo_hbm = bf16[512,2048]{1,0:T(8,128)(2,1)S(1)} collective-permute-done((bf16[512,2048]{1,0:T(8,128)(2,1)S(1)}, bf16[512,2048]{1,0:T(8,128)(2,1)S(1)}, u32[]{:S(2)}, u32[]{:S(2)}) %collective-permute-start.8) | collective-permute-done | bytes 2097184 | tf_op jit(solution)/shard_map/ppermute | solution.py:278
  52.7 1.3 copy-done.1
  54.0 29.7 %shard_map.76 = (f32[384,2048]{1,0:T(8,128)}, f32[128,2048]{1,0:T(8,128)}, f32[384,2048]{1,0:T(8,128)}, f32[128,2048]{1,0:T(8,128)}) custom-call(s32[8,128]{1,0:T(8,128)} %get-tuple-element.29.table_ref, s32[8,8,256]{2,1,0:T(8,128)} %get-tuple-element.30.pos_ref, bf16[512,2048]{1,0:T(8,128)(2,1)} %copy-done, bf16[512,2048]{1,0:T(8,128)(2,1)} %copy-done.1, ...), custom_call_target="tpu_custom_call" | custom-call | flops 8858370048 | bytes 77594624 | tf_op jit(solution)/shard_map/pallas_call | solution.py:315
  83.7 6.2 %collective-permute-start.10 = (f32[384,2048]{1,0:T(8,128)}, f32[384,2048]{1,0:T(8,128)}, u32[]{:S(2)}, u32[]{:S(2)}) collective-permute-start(f32[384,2048]{1,0:T(8,128)} %get-tuple-element.44), channel_id=1, source_target_pairs={{0,1},{1,0},{2,3},{3,2},{4,5},{5,4},{6,7},{7,6}} | collective-permute-start | bytes 9437192 | tf_op jit(solution)/shard_map/ppermute | solution.py:278
  89.9 32.4 %shard_map.74 = (f32[128,2048]{1,0:T(8,128)}, f32[384,2048]{1,0:T(8,128)}, f32[128,2048]{1,0:T(8,128)}, f32[384,2048]{1,0:T(8,128)}) custom-call(s32[8,128]{1,0:T(8,128)} %get-tuple-element.29.table_ref, s32[8,8,256]{2,1,0:T(8,128)} %get-tuple-element.30.pos_ref, bf16[512,2048]{1,0:T(8,128)(2,1)} %get-tuple-element.33.xm_hbm, ...), custom_call_target="tpu_custom_call" | custom-call | flops 8858370048 | bytes 77594624 | tf_op jit(solution)/shard_map/pallas_call | solution.py:315
  122.3 0.1 collective-permute-start.4
  122.4 27.0 %shard_map.75 = (f32[384,2048]{1,0:T(8,128)}, f32[128,2048]{1,0:T(8,128)}, f32[384,2048]{1,0:T(8,128)}, f32[128,2048]{1,0:T(8,128)}) custom-call(s32[8,128]{1,0:T(8,128)} %get-tuple-element.29.table_ref, s32[8,8,256]{2,1,0:T(8,128)} %get-tuple-element.30.pos_ref, bf16[512,2048]{1,0:T(8,128)(2,1)} %copy-done, bf16[512,2048]{1,0:T(8,128)(2,1)} %copy-done.1, ...), custom_call_target="tpu_custom_call" | custom-call | flops 8858370048 | bytes 77594624 | tf_op jit(solution)/shard_map/pallas_call | solution.py:315
  149.4 9.8 %collective-permute-start.9 = (f32[384,2048]{1,0:T(8,128)}, f32[384,2048]{1,0:T(8,128)}, u32[]{:S(2)}, u32[]{:S(2)}) collective-permute-start(f32[384,2048]{1,0:T(8,128)} %get-tuple-element.42), channel_id=1, source_target_pairs={{0,1},{1,0},{2,3},{3,2},{4,5},{5,4},{6,7},{7,6}} | collective-permute-start | bytes 9437192 | tf_op jit(solution)/shard_map/ppermute | solution.py:278
  159.3 0.0 collective-permute-done.10
  159.3 5.4 %add.43 = f32[384,2048]{1,0:T(8,128)} add(f32[384,2048]{1,0:T(8,128)} %get-tuple-element.43, f32[384,2048]{1,0:T(8,128)} %collective-permute-done.10) | non-fusion elementwise | flops 786432 | bytes 9437184 | tf_op jit(solution)/shard_map/add | solution.py:339
  164.6 5.4 %collective-permute-start.11 = (f32[384,2048]{1,0:T(8,128)}, f32[384,2048]{1,0:T(8,128)}, u32[]{:S(2)}, u32[]{:S(2)}) collective-permute-start(f32[384,2048]{1,0:T(8,128)} %add.43), channel_id=1, source_target_pairs={{0,2},{1,5},{2,0},{3,7},{4,6},{5,1},{6,4},{7,3}} | collective-permute-start | bytes 9437192 | tf_op jit(solution)/shard_map/ppermute | solution.py:282
  170.1 0.0 collective-permute-start
  170.1 0.5 collective-permute-start.2
  170.6 0.0 collective-permute-done.4
  170.6 4.3 %add.38 = f32[384,2048]{1,0:T(8,128)} add(f32[384,2048]{1,0:T(8,128)S(1)} %copy-done.4, f32[384,2048]{1,0:T(8,128)} %collective-permute-done.4) | non-fusion elementwise | flops 786432 | bytes 9437184 | tf_op jit(solution)/shard_map/add | solution.py:339
  174.9 0.0 collective-permute-start.5
  174.9 0.0 collective-permute-done.xo_hbm
  174.9 1.0 copy-done.11
  175.9 0.0 collective-permute-start.14
  175.9 35.6 %shard_map.73 = (f32[384,2048]{1,0:T(8,128)}, f32[128,2048]{1,0:T(8,128)}, f32[384,2048]{1,0:T(8,128)}, f32[128,2048]{1,0:T(8,128)}) custom-call(s32[8,128]{1,0:T(8,128)} %get-tuple-element.29.table_ref, s32[8,8,256]{2,1,0:T(8,128)} %get-tuple-element.30.pos_ref, bf16[256,2048]{1,0:T(8,128)(2,1)} %xm_hbm.1, bf16[256,2048]{1,0:T(8,128)(2,1)} %copy-done.11, ...), custom_call_target="tpu_custom_call" | custom-call | flops 8858370048 | bytes 77594624 | tf_op jit(solution)/shard_map/pallas_call | solution.py:315
  211.5 0.0 collective-permute-start.1
  211.6 0.0 collective-permute-done.11
  211.6 0.5 collective-permute-start.13
  212.1 4.7 %add_add_fusion = f32[384,2048]{1,0:T(8,128)S(1)} fusion(f32[384,2048]{1,0:T(8,128)} %collective-permute-done.11, f32[384,2048]{1,0:T(8,128)} %get-tuple-element.41, f32[384,2048]{1,0:T(8,128)} %collective-permute-done.9), kind=kLoop, calls=%fused_computation.2 | loop fusion | flops 1572864 | bytes 12582912 | tf_op jit(solution)/shard_map/add | solution.py:339
  216.8 0.0 collective-permute-done.14
  216.8 0.0 collective-permute-start.12
  216.9 1.5 add.46
  218.4 1.5 collective-permute-start.15
  219.9 0.0 collective-permute-start.6
  220.0 1.4 add.37
  221.4 61.4 %collective-permute-done.15 = f32[128,2048]{1,0:T(8,128)S(1)} collective-permute-done((f32[128,2048]{1,0:T(8,128)S(1)}, f32[128,2048]{1,0:T(8,128)S(1)}, u32[]{:S(2)}, u32[]{:S(2)}) %collective-permute-start.15) | collective-permute-done | bytes 1048608 | tf_op jit(solution)/shard_map/ppermute | solution.py:282
  282.8 2.5 collective-permute-start.3
  285.2 0.2 add_add_fusion.1
  285.5 0.0 collective-permute-start.16
  285.5 0.0 collective-permute-done.5
  285.5 2.6 slice_add_fusion.s1_ref
  288.1 19.7 %collective-permute-done.3 = f32[128,2048]{1,0:T(8,128)S(1)} collective-permute-done((f32[128,2048]{1,0:T(8,128)S(1)}, f32[128,2048]{1,0:T(8,128)S(1)}, u32[]{:S(2)}, u32[]{:S(2)}) %collective-permute-start.3) | collective-permute-done | bytes 1048608 | tf_op jit(solution)/shard_map/ppermute | solution.py:282
  307.8 0.0 collective-permute-done.1
  307.8 4.2 %fusion.s0_ref = f32[384,2048]{1,0:T(8,128)} fusion(f32[384,2048]{1,0:T(8,128)} %collective-permute-done.5, f32[128,2048]{1,0:T(8,128)S(1)} %collective-permute-done.3, f32[384,2048]{1,0:T(8,128)S(1)} %copy-done.5, f32[384,2048]{1,0:T(8,128)S(1)} %collective-permute-done.1), kind=kLoop, calls=%fused_computation.1 | loop fusion | flops 2359296 | bytes 13631488 | tf_op jit(solution)/shard_map/add | solution.py:339
  312.0 0.0 collective-permute-done.12.f0_ref
  312.0 1.1 copy-done.8
  313.0 1.6 copy-done.3
  314.7 5.9 %combine.1 = bf16[256,2048]{1,0:T(8,128)(2,1)} custom-call(bf16[2,256,512]{2,1,0:T(8,128)(2,1)} %get-tuple-element.27.hit_ref, f32[256,8]{1,0:T(8,128)} %get-tuple-element.28.gate_ref, f32[384,2048]{1,0:T(8,128)} %fusion.s0_ref, f32[128,2048]{1,0:T(8,128)} %slice_add_fusion.s1_ref, f32[384,2048]{1,0:T(8,128)} %copy-done.3, f32[128,2048]{1,0:T(8,128)} %copy-done.8), custom_call_target="tpu_custom_call" | custom-call | tf_op jit(solution)/shard_map/combine/pallas_call | solution.py:357
  (26 shorter events, 0.1 us)
Async XLA Ops:
  21.0 26.3 %collective-permute-start.7 = (bf16[512,2048]{1,0:T(8,128)(2,1)}, bf16[512,2048]{1,0:T(8,128)(2,1)S(1)}, u32[]{:S(2)}, u32[]{:S(2)}) collective-permute-start(bf16[512,2048]{1,0:T(8,128)(2,1)} %get-tuple-element.33.xm_hbm), channel_id=1, source_target_pairs={{0,4},{1,3},{2,6},{3,1},{4,0},{5,7},{6,2},{7,5}} | collective-permute-start | bytes 6291464 | tf_op jit(solution)/shard_map/ppermute | solution.py:282
  47.3 1.3 copy-start
  48.6 4.2 %collective-permute-start.8 = (bf16[512,2048]{1,0:T(8,128)(2,1)S(1)}, bf16[512,2048]{1,0:T(8,128)(2,1)S(1)}, u32[]{:S(2)}, u32[]{:S(2)}) collective-permute-start(bf16[512,2048]{1,0:T(8,128)(2,1)S(1)} %collective-permute-done.7.xm_hbm), channel_id=1, source_target_pairs={{0,1},{1,0},{2,3},{3,2},{4,5},{5,4},{6,7},{7,6}} | collective-permute-start | bytes 6291464 | tf_op jit(solution)/shard_map/ppermute | solution.py:278
  52.7 1.3 copy-start.1
  83.7 75.5 %collective-permute-start.10 = (f32[384,2048]{1,0:T(8,128)}, f32[384,2048]{1,0:T(8,128)}, u32[]{:S(2)}, u32[]{:S(2)}) collective-permute-start(f32[384,2048]{1,0:T(8,128)} %get-tuple-element.44), channel_id=1, source_target_pairs={{0,1},{1,0},{2,3},{3,2},{4,5},{5,4},{6,7},{7,6}} | collective-permute-start | bytes 9437192 | tf_op jit(solution)/shard_map/ppermute | solution.py:278
  122.3 48.3 %collective-permute-start.4 = (f32[384,2048]{1,0:T(8,128)}, f32[384,2048]{1,0:T(8,128)}, u32[]{:S(2)}, u32[]{:S(2)}) collective-permute-start(f32[384,2048]{1,0:T(8,128)} %get-tuple-element.38), channel_id=1, source_target_pairs={{0,1},{1,0},{2,3},{3,2},{4,5},{5,4},{6,7},{7,6}} | collective-permute-start | bytes 9437192 | tf_op jit(solution)/shard_map/ppermute | solution.py:278
  149.4 62.1 %collective-permute-start.9 = (f32[384,2048]{1,0:T(8,128)}, f32[384,2048]{1,0:T(8,128)}, u32[]{:S(2)}, u32[]{:S(2)}) collective-permute-start(f32[384,2048]{1,0:T(8,128)} %get-tuple-element.42), channel_id=1, source_target_pairs={{0,1},{1,0},{2,3},{3,2},{4,5},{5,4},{6,7},{7,6}} | collective-permute-start | bytes 9437192 | tf_op jit(solution)/shard_map/ppermute | solution.py:278
  159.3 10.8 %copy-start.2 = (bf16[256,2048]{1,0:T(8,128)(2,1)S(1)}, bf16[256,2048]{1,0:T(8,128)(2,1)}, u32[]{:S(2)}) copy-start(bf16[256,2048]{1,0:T(8,128)(2,1)} %xm_hbm.1) | copy-start | bytes 3145732
  159.3 11.3 %copy-start.4 = (f32[384,2048]{1,0:T(8,128)S(1)}, f32[384,2048]{1,0:T(8,128)}, u32[]{:S(2)}) copy-start(f32[384,2048]{1,0:T(8,128)} %get-tuple-element.37) | copy-start | bytes 9437188
  164.6 46.9 %collective-permute-start.11 = (f32[384,2048]{1,0:T(8,128)}, f32[384,2048]{1,0:T(8,128)}, u32[]{:S(2)}, u32[]{:S(2)}) collective-permute-start(f32[384,2048]{1,0:T(8,128)} %add.43), channel_id=1, source_target_pairs={{0,2},{1,5},{2,0},{3,7},{4,6},{5,1},{6,4},{7,3}} | collective-permute-start | bytes 9437192 | tf_op jit(solution)/shard_map/ppermute | solution.py:282
  170.1 4.8 %collective-permute-start = (bf16[256,2048]{1,0:T(8,128)(2,1)S(1)}, bf16[256,2048]{1,0:T(8,128)(2,1)S(1)}, u32[]{:S(2)}, u32[]{:S(2)}) collective-permute-start(bf16[256,2048]{1,0:T(8,128)(2,1)S(1)} %copy-done.2), channel_id=1, source_target_pairs={{0,1},{1,0},{2,3},{3,2},{4,5},{5,4},{6,7},{7,6}} | collective-permute-start | bytes 3145736 | tf_op jit(solution)/shard_map/ppermute | solution.py:278
  170.1 48.3 %collective-permute-start.2 = (f32[128,2048]{1,0:T(8,128)}, f32[128,2048]{1,0:T(8,128)}, u32[]{:S(2)}, u32[]{:S(2)}) collective-permute-start(f32[128,2048]{1,0:T(8,128)} %get-tuple-element.36), channel_id=1, source_target_pairs={{0,1},{1,0},{2,3},{3,2},{4,5},{5,4},{6,7},{7,6}} | collective-permute-start | bytes 3145736 | tf_op jit(solution)/shard_map/ppermute | solution.py:278
  174.9 110.6 %collective-permute-start.5 = (f32[384,2048]{1,0:T(8,128)}, f32[384,2048]{1,0:T(8,128)}, u32[]{:S(2)}, u32[]{:S(2)}) collective-permute-start(f32[384,2048]{1,0:T(8,128)} %add.38), channel_id=1, source_target_pairs={{0,2},{1,5},{2,0},{3,7},{4,6},{5,1},{6,4},{7,3}} | collective-permute-start | bytes 9437192 | tf_op jit(solution)/shard_map/ppermute | solution.py:282
  174.9 1.0 copy-start.11
  175.9 41.0 %collective-permute-start.14 = (f32[128,2048]{1,0:T(8,128)}, f32[128,2048]{1,0:T(8,128)}, u32[]{:S(2)}, u32[]{:S(2)}) collective-permute-start(f32[128,2048]{1,0:T(8,128)} %get-tuple-element.48), channel_id=1, source_target_pairs={{0,1},{1,0},{2,3},{3,2},{4,5},{5,4},{6,7},{7,6}} | collective-permute-start | bytes 3145736 | tf_op jit(solution)/shard_map/ppermute | solution.py:278
  211.5 96.2 %collective-permute-start.1 = (f32[384,2048]{1,0:T(8,128)}, f32[384,2048]{1,0:T(8,128)S(1)}, u32[]{:S(2)}, u32[]{:S(2)}) collective-permute-start(f32[384,2048]{1,0:T(8,128)} %get-tuple-element.32), channel_id=1, source_target_pairs={{0,1},{1,0},{2,3},{3,2},{4,5},{5,4},{6,7},{7,6}} | collective-permute-start | bytes 9437192 | tf_op jit(solution)/shard_map/ppermute | solution.py:278
  211.6 8.4 %collective-permute-start.13 = (f32[128,2048]{1,0:T(8,128)}, f32[128,2048]{1,0:T(8,128)S(1)}, u32[]{:S(2)}, u32[]{:S(2)}) collective-permute-start(f32[128,2048]{1,0:T(8,128)} %get-tuple-element.46), channel_id=1, source_target_pairs={{0,1},{1,0},{2,3},{3,2},{4,5},{5,4},{6,7},{7,6}} | collective-permute-start | bytes 3145736 | tf_op jit(solution)/shard_map/ppermute | solution.py:278
  212.1 4.8 %copy-start.7 = (f32[128,2048]{1,0:T(8,128)S(1)}, f32[128,2048]{1,0:T(8,128)}, u32[]{:S(2)}) copy-start(f32[128,2048]{1,0:T(8,128)} %get-tuple-element.47) | copy-start | bytes 3145732
  216.8 3.1 copy-start.12
  216.8 3.1 copy-start.6
  216.8 95.1 %collective-permute-start.12 = (f32[384,2048]{1,0:T(8,128)S(1)}, f32[384,2048]{1,0:T(8,128)S(1)}, u32[]{:S(2)}, u32[]{:S(2)}) collective-permute-start(f32[384,2048]{1,0:T(8,128)S(1)} %add_add_fusion), channel_id=1, source_target_pairs={{0,4},{1,3},{2,6},{3,1},{4,0},{5,7},{6,2},{7,5}} | collective-permute-start | bytes 9437192 | tf_op jit(solution)/shard_map/ppermute | solution.py:282
  216.9 68.3 %copy-start.9 = (f32[128,2048]{1,0:T(8,128)S(1)}, f32[128,2048]{1,0:T(8,128)}, u32[]{:S(2)}) copy-start(f32[128,2048]{1,0:T(8,128)} %get-tuple-element.45) | copy-start | bytes 3145732
  218.4 64.3 %collective-permute-start.15 = (f32[128,2048]{1,0:T(8,128)S(1)}, f32[128,2048]{1,0:T(8,128)S(1)}, u32[]{:S(2)}, u32[]{:S(2)}) collective-permute-start(f32[128,2048]{1,0:T(8,128)S(1)} %add.46), channel_id=1, source_target_pairs={{0,2},{1,5},{2,0},{3,7},{4,6},{5,1},{6,4},{7,3}} | collective-permute-start | bytes 3145736 | tf_op jit(solution)/shard_map/ppermute | solution.py:282
  219.9 65.5 %collective-permute-start.6 = (f32[128,2048]{1,0:T(8,128)S(1)}, f32[128,2048]{1,0:T(8,128)S(1)}, u32[]{:S(2)}, u32[]{:S(2)}) collective-permute-start(f32[128,2048]{1,0:T(8,128)S(1)} %copy-done.12), channel_id=1, source_target_pairs={{0,1},{1,0},{2,3},{3,2},{4,5},{5,4},{6,7},{7,6}} | collective-permute-start | bytes 3145736 | tf_op jit(solution)/shard_map/ppermute | solution.py:278
  219.9 65.6 %copy-start.10 = (f32[128,2048]{1,0:T(8,128)S(1)}, f32[128,2048]{1,0:T(8,128)}, u32[]{:S(2)}) copy-start(f32[128,2048]{1,0:T(8,128)} %get-tuple-element.39) | copy-start | bytes 3145732
  282.8 25.0 %collective-permute-start.3 = (f32[128,2048]{1,0:T(8,128)S(1)}, f32[128,2048]{1,0:T(8,128)S(1)}, u32[]{:S(2)}, u32[]{:S(2)}) collective-permute-start(f32[128,2048]{1,0:T(8,128)S(1)} %add.37), channel_id=1, source_target_pairs={{0,2},{1,5},{2,0},{3,7},{4,6},{5,1},{6,4},{7,3}} | collective-permute-start | bytes 3145736 | tf_op jit(solution)/shard_map/ppermute | solution.py:282
  285.5 22.3 %copy-start.5 = (f32[384,2048]{1,0:T(8,128)S(1)}, f32[384,2048]{1,0:T(8,128)}, u32[]{:S(2)}) copy-start(f32[384,2048]{1,0:T(8,128)} %get-tuple-element.31) | copy-start | bytes 9437188
  285.5 26.5 %collective-permute-start.16 = (f32[128,2048]{1,0:T(8,128)S(1)}, f32[128,2048]{1,0:T(8,128)S(1)}, u32[]{:S(2)}, u32[]{:S(2)}) collective-permute-start(f32[128,2048]{1,0:T(8,128)S(1)} %add_add_fusion.1), channel_id=1, source_target_pairs={{0,4},{1,3},{2,6},{3,1},{4,0},{5,7},{6,2},{7,5}} | collective-permute-start | bytes 3145736 | tf_op jit(solution)/shard_map/ppermute | solution.py:282
  312.0 1.1 copy-start.8
  313.0 1.6 copy-start.3

commit v9 on v8

--- a/solution.py
+++ b/solution.py
@@ -122,7 +122,6 @@
     outs = refs[:4]
     acc, xbuf, *ws, w2s, wsem, osem, xsem = refs[4:]
     w1s, w3s = ws[: len(ws) // 2], ws[len(ws) // 2 :]
-    ahead = len(w1s) + 2
     e_loc, d, _ = w1_hbm.shape
     _, rows, _ = acc.shape
     t = xbuf.shape[1]
@@ -156,16 +155,19 @@
     def arrive(i, e):
         for c in chunks[i](e):
             c.wait()
-        i += ahead
-        if i < len(chunks):
-            for c in chunks[i](e):
+        if i == 0:
+
+            @pl.when((e == 0) & (e_loc > 1))
+            def _():
+                for later in chunks:
+                    for c in later(1):
+                        c.start()
+
+    def used(i, e):
+        @pl.when(e + 2 < e_loc)
+        def _():
+            for c in chunks[i](e + 2):
                 c.start()
-        else:
-
-            @pl.when(e + 1 < e_loc)
-            def _():
-                for c in chunks[i - len(chunks)](e + 1):
-                    c.start()
 
     def out_copies(h):
         cols = pl.ds(h * half_d, half_d)
@@ -181,8 +183,8 @@
     ]
     for c in tokens:
         c.start()
-    for i in range(ahead):
-        for c in chunks[i](0):
+    for chunk in chunks:
+        for c in chunk(0):
             c.start()
     acc[...] = jnp.zeros_like(acc)
     for c in tokens:
@@ -214,6 +216,7 @@
                 h1 = jnp.dot(xs, wa[e % 2], preferred_element_type=F32)
                 h3 = jnp.dot(xs, wb[e % 2], preferred_element_type=F32)
                 hs.append((jax.nn.silu(h1) * h3).astype(BF16))
+                used(i, e)
             h = jnp.concatenate(hs, axis=1)
 
             def project(k, carry):
@@ -223,6 +226,8 @@
                 cols = pl.ds(pl.multiple_of(k * half_d, half_d), half_d)
                 for s in range(2):
                     acc[s, pl.ds(bases[s], m), cols] += p[s * m : (s + 1) * m]
+                for i in range(2):
+                    pl.when(k == i)(functools.partial(used, len(w1s) + i, e))
                 last(k)
                 return carry
 
@@ -232,6 +237,7 @@
         def _():
             for i in range(len(chunks)):
                 arrive(i, e)
+                used(i, e)
             last(0)
 
         lo = 0
@@ -247,14 +253,27 @@
         c.wait()
 
 
-def _combine_kernel(hit_ref, gate_ref, s0_ref, s1_ref, f0_ref, f1_ref, out_ref):
-    top = hit_ref.shape[0]
-    y = jnp.concatenate([s0_ref[...] + f0_ref[...], s1_ref[...] + f1_ref[...]], axis=0).astype(BF16)
-    total = None
+def _weigh(hit, gate_ref, y, total=None):
+    top = len(hit)
     for j in range(top):
-        part = jnp.dot(hit_ref[j], y, preferred_element_type=F32) * gate_ref[:, top + j : top + j + 1]
+        part = jnp.dot(hit[j], y, preferred_element_type=F32) * gate_ref[:, top + j : top + j + 1]
         total = part if total is None else total + part
-    out_ref[...] = total.astype(out_ref.dtype)
+    return total
+
+
+def _combine_kernel(hit_ref, gate_ref, k0_ref, k1_ref, o0_ref, o1_ref, n0_ref, n1_ref, f0_ref, total_ref, sum_ref):
+    most = f0_ref.shape[0]
+    near = jnp.concatenate([n0_ref[...], n1_ref[...]], axis=0)
+    y = (k0_ref[...] + o0_ref[...] + near[:most] + f0_ref[...]).astype(BF16)
+    total_ref[...] = _weigh([hit_ref[j, :, :most] for j in range(hit_ref.shape[0])], gate_ref, y)
+    sum_ref[...] = k1_ref[...] + o1_ref[...] + near[most:]
+
+
+def _close_kernel(hit_ref, gate_ref, total_ref, sum_ref, f1_ref, out_ref):
+    most = hit_ref.shape[2] - f1_ref.shape[0]
+    y = (sum_ref[...] + f1_ref[...]).astype(BF16)
+    hit = [hit_ref[j, :, most:] for j in range(hit_ref.shape[0])]
+    out_ref[...] = _weigh(hit, gate_ref, y, total_ref[...]).astype(out_ref.dtype)
 
 
 def solution(mesh):
@@ -339,7 +358,7 @@
                 sums.append(functools.reduce(jnp.add, [m[q] for m in more], parts[2 + q] + other))
             return sums
 
-        early, late = (rows // 4, rows - rows // 4), (rows - rows // 4, rows // 4)
+        early, late = (rows // 8, rows - rows // 8), (rows - rows // 4, rows // 4)
         rest = shift(pair, back)
         rest_other = swap(rest)
         own_x = swap(x)
@@ -349,19 +368,34 @@
         via = [shift(a, out) for a in diag]
         far = merge(stage(back, rest, rest_other, late, (t_loc, t_loc)), via)
         far = [shift(a, back) for a in far]
-        near = jnp.concatenate(near, axis=0)
-        near = [near[: late[0]], near[late[0] :]]
-        sums = merge(stage((0, 0), x, own_x, late), near)
-        steps = 4
-        parts = [pl.BlockSpec((n, d // steps), lambda i: (0, i)) for n in late]
+        own = stage((0, 0), x, own_x, late)
+        other = [swap(own[q]) for q in range(2)]
+
+        def by_columns(steps):
+            def part(n):
+                return pl.BlockSpec((n, d // steps), lambda i: (0, i))
+
+            return dict(grid=(steps,)), part
+
+        grid, part = by_columns(4)
+        total, last = pl.pallas_call(
+            _combine_kernel,
+            out_shape=[jax.ShapeDtypeStruct((t_loc, d), F32), jax.ShapeDtypeStruct((late[1], d), F32)],
+            in_specs=[vmem, vmem] + [part(n) for n in late * 2 + early + late[:1]],
+            out_specs=[part(t_loc), part(late[1])],
+            compiler_params=pltpu.CompilerParams(vmem_limit_bytes=VMEM_BYTES),
+            name="combine",
+            **grid,
+        )(hit, gate, *own[2:], *other, *near, far[0])
+        grid, part = by_columns(2)
         return pl.pallas_call(
-            _combine_kernel,
+            _close_kernel,
             out_shape=jax.ShapeDtypeStruct((t_loc, d), BF16),
-            grid=(steps,),
-            in_specs=[vmem, vmem] + parts * 2,
-            out_specs=pl.BlockSpec((t_loc, d // steps), lambda i: (0, i)),
-            name="combine",
-        )(hit, gate, *sums, *far)
+            in_specs=[vmem, vmem] + [part(n) for n in (t_loc, late[1], late[1])],
+            out_specs=part(t_loc),
+            name="close",
+            **grid,
+        )(hit, gate, total, last, far[1])
 
     rows = P(("ep", "tp"), None)
     return jax.shard_map(

time: 321 us -> 325 us (1.012)
  other arithmetic: 24.3 us -> 15.4 us
  waiting for transfers between devices: 110 us -> 118 us
  Pallas kernels: 152 us -> 157 us
    add x4 -> x2, other arithmetic: 11.7 us -> 5.03 us  [merge(): functools.reduce(jnp.add, [m[q] for m in more], parts[2 + q] + other)]
    pallas_call x1 -> x2, Pallas kernels: 5.9 us -> 12.3 us  [the longest x1 8.64 us: layer(): pl.pallas_call(_combine_kernel, out_shape=[jax.ShapeDtypeStruct((t_loc, d...]
    ppermute x7, waiting for transfers between devices: 106 us -> 111 us  [shift(): return lax.ppermute(a, ('tp', 'ep'), pairs)]
    ppermute x10, waiting for transfers between devices: 4.18 us -> 7.45 us  [swap(): return lax.ppermute(a, 'ep', [(0, 1), (1, 0)])]
  transfers between devices with their start and end apart: 17 -> 17, of which waited for: 4 -> 7; matrix products, arithmetic and copies ran while one was open for 8% -> 5% of each run, Pallas kernels for 30% -> 32%
where the time goes in v9:
time: 325 us
  Pallas kernels  157 us (48%)
  waiting for transfers between devices  118 us (36%)
  starting transfers between devices  27.8 us (9%)
  other arithmetic  15.4 us (5%)
  local copies, waits for them, and re-layouts  6.12 us (2%)
    pallas_call x4, Pallas kernels, stage(): pl.pallas_call(functools.partial(_expert_kernel, turns, rows0, sizes, cut...  123 us
    ppermute x7, waiting for transfers between devices, shift(): return lax.ppermute(a, ('tp', 'ep'), pairs)  111 us
    pallas_call x1, Pallas kernels, layer(): pl.pallas_call(functools.partial(_route_kernel, chips, out), out_shape=[j...  21 us
    ppermute x10, starting transfers between devices, swap(): return lax.ppermute(a, 'ep', [(0, 1), (1, 0)])  18.5 us
    add x4, other arithmetic, merge(): parts[2 + q] + other  10.4 us
    ppermute x7, starting transfers between devices, shift(): return lax.ppermute(a, ('tp', 'ep'), pairs)  9.4 us
    pallas_call x1, Pallas kernels, layer(): pl.pallas_call(_combine_kernel, out_shape=[jax.ShapeDtypeStruct((t_loc, d...  8.64 us
    ppermute x10, waiting for transfers between devices, swap(): return lax.ppermute(a, 'ep', [(0, 1), (1, 0)])  7.45 us
  transfers between devices with their start and end apart: 17, of which 7 were waited for; matrix products, arithmetic and copies ran while one was open for 5% of the time, Pallas kernels for 32%

profile of v9, /device:TPU:0, one launch (start us, length us, event | category | flops | bytes accessed | tf_op | source)
XLA Modules:
  0.0 324.8 jit_solution(13025857034925692311)
XLA Ops:
  0.0 21.0 %route.1 = (s32[8,8,256]{2,1,0:T(8,128)}, s32[8,128]{1,0:T(8,128)}, bf16[2,256,512]{2,1,0:T(8,128)(2,1)}, f32[256,8]{1,0:T(8,128)}, bf16[512,2048]{1,0:T(8,128)(2,1)}, /*index=5*/bf16[256,2048]{1,0:T(8,128)(2,1)}) custom-call(s32[2,256]{1,0:T(2,128)} %bitcast.2, f32[2,256]{1,0:T(2,128)} %bitcast.3, s32[8]{0:T(128)} %cap_ref.1, bf16[256,2048]{1,0:T(8,128)(2,1)} %xm_hbm.1), custom_call_target="tpu_custom_call" | custom-call | tf_op jit(solution)/shard_map/route/pallas_call | solution.py:305
  21.1 1.1 collective-permute-start.7
  22.2 25.1 %collective-permute-done.7.xm_hbm = bf16[512,2048]{1,0:T(8,128)(2,1)S(1)} collective-permute-done((bf16[512,2048]{1,0:T(8,128)(2,1)}, bf16[512,2048]{1,0:T(8,128)(2,1)S(1)}, u32[]{:S(2)}, u32[]{:S(2)}) %collective-permute-start.7) | collective-permute-done | bytes 2097184 | tf_op jit(solution)/shard_map/ppermute | solution.py:301
  47.3 1.4 copy-done
  48.7 0.0 collective-permute-start.8
  48.7 4.2 %collective-permute-done.8.xo_hbm = bf16[512,2048]{1,0:T(8,128)(2,1)S(1)} collective-permute-done((bf16[512,2048]{1,0:T(8,128)(2,1)S(1)}, bf16[512,2048]{1,0:T(8,128)(2,1)S(1)}, u32[]{:S(2)}, u32[]{:S(2)}) %collective-permute-start.8) | collective-permute-done | bytes 2097184 | tf_op jit(solution)/shard_map/ppermute | solution.py:297
  52.9 1.3 copy-done.1
  54.2 28.4 %shard_map.76 = (f32[384,2048]{1,0:T(8,128)}, f32[128,2048]{1,0:T(8,128)}, f32[384,2048]{1,0:T(8,128)}, f32[128,2048]{1,0:T(8,128)}) custom-call(s32[8,128]{1,0:T(8,128)} %get-tuple-element.31.table_ref, s32[8,8,256]{2,1,0:T(8,128)} %get-tuple-element.32.pos_ref, bf16[512,2048]{1,0:T(8,128)(2,1)} %copy-done, bf16[512,2048]{1,0:T(8,128)(2,1)} %copy-done.1, ...), custom_call_target="tpu_custom_call" | custom-call | flops 8858370048 | bytes 77594624 | tf_op jit(solution)/shard_map/pallas_call | solution.py:334
  82.6 7.5 %collective-permute-start.10 = (f32[384,2048]{1,0:T(8,128)}, f32[384,2048]{1,0:T(8,128)}, u32[]{:S(2)}, u32[]{:S(2)}) collective-permute-start(f32[384,2048]{1,0:T(8,128)} %get-tuple-element.46), channel_id=1, source_target_pairs={{0,1},{1,0},{2,3},{3,2},{4,5},{5,4},{6,7},{7,6}} | collective-permute-start | bytes 9437192 | tf_op jit(solution)/shard_map/ppermute | solution.py:297
  90.1 32.4 %shard_map.74 = (f32[64,2048]{1,0:T(8,128)}, f32[448,2048]{1,0:T(8,128)}, f32[64,2048]{1,0:T(8,128)}, f32[448,2048]{1,0:T(8,128)}) custom-call(s32[8,128]{1,0:T(8,128)} %get-tuple-element.31.table_ref, s32[8,8,256]{2,1,0:T(8,128)} %get-tuple-element.32.pos_ref, bf16[512,2048]{1,0:T(8,128)(2,1)} %get-tuple-element.37.xm_hbm, ...), custom_call_target="tpu_custom_call" | custom-call | flops 8858370048 | bytes 77594624 | tf_op jit(solution)/shard_map/pallas_call | solution.py:334
  122.5 0.0 collective-permute-start.5
  122.5 27.1 %shard_map.75 = (f32[384,2048]{1,0:T(8,128)}, f32[128,2048]{1,0:T(8,128)}, f32[384,2048]{1,0:T(8,128)}, f32[128,2048]{1,0:T(8,128)}) custom-call(s32[8,128]{1,0:T(8,128)} %get-tuple-element.31.table_ref, s32[8,8,256]{2,1,0:T(8,128)} %get-tuple-element.32.pos_ref, bf16[512,2048]{1,0:T(8,128)(2,1)} %copy-done, bf16[512,2048]{1,0:T(8,128)(2,1)} %copy-done.1, ...), custom_call_target="tpu_custom_call" | custom-call | flops 8858370048 | bytes 77594624 | tf_op jit(solution)/shard_map/pallas_call | solution.py:334
  149.6 9.9 %collective-permute-start.9 = (f32[384,2048]{1,0:T(8,128)}, f32[384,2048]{1,0:T(8,128)}, u32[]{:S(2)}, u32[]{:S(2)}) collective-permute-start(f32[384,2048]{1,0:T(8,128)} %get-tuple-element.44), channel_id=1, source_target_pairs={{0,1},{1,0},{2,3},{3,2},{4,5},{5,4},{6,7},{7,6}} | collective-permute-start | bytes 9437192 | tf_op jit(solution)/shard_map/ppermute | solution.py:297
  159.4 0.0 collective-permute-done.10
  159.4 5.2 %add.27 = f32[384,2048]{1,0:T(8,128)} add(f32[384,2048]{1,0:T(8,128)} %get-tuple-element.45, f32[384,2048]{1,0:T(8,128)} %collective-permute-done.10) | non-fusion elementwise | flops 786432 | bytes 9437184 | tf_op jit(solution)/shard_map/add | solution.py:358
  164.7 5.4 %collective-permute-start.11 = (f32[384,2048]{1,0:T(8,128)}, f32[384,2048]{1,0:T(8,128)}, u32[]{:S(2)}, u32[]{:S(2)}) collective-permute-start(f32[384,2048]{1,0:T(8,128)} %add.27), channel_id=1, source_target_pairs={{0,2},{1,5},{2,0},{3,7},{4,6},{5,1},{6,4},{7,3}} | collective-permute-start | bytes 9437192 | tf_op jit(solution)/shard_map/ppermute | solution.py:301
  170.1 0.0 collective-permute-start
  170.1 0.5 collective-permute-start.3
  170.6 2.3 collective-permute-done.xo_hbm
  172.9 35.6 %shard_map.73 = (f32[384,2048]{1,0:T(8,128)}, f32[128,2048]{1,0:T(8,128)}, f32[384,2048]{1,0:T(8,128)}, f32[128,2048]{1,0:T(8,128)}) custom-call(s32[8,128]{1,0:T(8,128)} %get-tuple-element.31.table_ref, s32[8,8,256]{2,1,0:T(8,128)} %get-tuple-element.32.pos_ref, bf16[256,2048]{1,0:T(8,128)(2,1)} %xm_hbm.1, bf16[256,2048]{1,0:T(8,128)(2,1)} %collective-permute-done.xo_hbm, ...), custom_call_target="tpu_custom_call" | custom-call | flops 8858370048 | bytes 77594624 | tf_op jit(solution)/shard_map/pallas_call | solution.py:334
  208.5 0.0 collective-permute-start.1
  208.6 0.0 collective-permute-done.5
  208.6 3.9 %add.25 = f32[448,2048]{1,0:T(8,128)S(1)} add(f32[448,2048]{1,0:T(8,128)} %get-tuple-element.41, f32[448,2048]{1,0:T(8,128)} %collective-permute-done.5) | non-fusion elementwise | flops 917504 | bytes 11010048 | tf_op jit(solution)/shard_map/add | solution.py:358
  212.5 0.0 collective-permute-start.6
  212.6 0.5 collective-permute-start.14
  213.1 3.9 %add_add_fusion = f32[384,2048]{1,0:T(8,128)S(1)} fusion(f32[384,2048]{1,0:T(8,128)} %collective-permute-done.11, f32[384,2048]{1,0:T(8,128)S(1)} %copy-done.3, f32[384,2048]{1,0:T(8,128)} %collective-permute-done.9), kind=kLoop, calls=%fused_computation | loop fusion | flops 1572864 | bytes 12582912 | tf_op jit(solution)/shard_map/add | solution.py:358
  217.0 0.0 copy-start.12
  217.0 1.7 collective-permute-start.12
  218.7 0.0 collective-permute-done.14
  218.8 0.0 collective-permute-start.13
  218.8 0.1 add.30
  218.9 0.0 collective-permute-done.3
  218.9 0.4 collective-permute-start.15
  219.3 1.1 add.24
  220.4 1.0 collective-permute-done.13
  221.4 0.7 collective-permute-start.4
  222.1 78.3 %collective-permute-done.15 = f32[128,2048]{1,0:T(8,128)S(1)} collective-permute-done((f32[128,2048]{1,0:T(8,128)S(1)}, f32[128,2048]{1,0:T(8,128)S(1)}, u32[]{:S(2)}, u32[]{:S(2)}) %collective-permute-start.15) | collective-permute-done | bytes 1048608 | tf_op jit(solution)/shard_map/ppermute | solution.py:301
  300.4 0.0 collective-permute-start.2
  300.4 1.1 add_add_fusion.1
  301.5 4.5 %collective-permute-done.4.n0_ref = f32[64,2048]{1,0:T(8,128)S(1)} collective-permute-done((f32[64,2048]{1,0:T(8,128)S(1)}, f32[64,2048]{1,0:T(8,128)S(1)}, u32[]{:S(2)}, u32[]{:S(2)}) %collective-permute-start.4) | collective-permute-done | bytes 524320 | tf_op jit(solution)/shard_map/ppermute | solution.py:301
  306.0 0.0 collective-permute-start.16
  306.0 0.0 collective-permute-done.2.o1_ref
  306.0 0.0 copy-start.7
  306.1 1.7 copy-done.4
  307.8 1.7 copy-done.5
  309.5 8.6 %combine.1 = (f32[256,2048]{1,0:T(8,128)}, f32[128,2048]{1,0:T(8,128)}) custom-call(bf16[2,256,512]{2,1,0:T(8,128)(2,1)} %get-tuple-element.29.hit_ref, f32[256,8]{1,0:T(8,128)} %get-tuple-element.30.gate_ref, f32[384,2048]{1,0:T(8,128)} %get-tuple-element.33.k0_ref, f32[128,2048]{1,0:T(8,128)} %get-tuple-element.34.k1_ref, f32[384,2048]{1,0:T(8,128)} %copy-done.4, ...), custom_call_target="tpu_custom_call" | custom-call | tf_op jit(solution)/shard_map/combine/pallas_call | solution.py:381
  318.1 3.0 collective-permute-done.16.f1_ref
  321.1 3.6 %close.1 = bf16[256,2048]{1,0:T(8,128)(2,1)} custom-call(bf16[2,256,512]{2,1,0:T(8,128)(2,1)} %get-tuple-element.29.hit_ref, f32[256,8]{1,0:T(8,128)} %get-tuple-element.30.gate_ref, f32[256,2048]{1,0:T(8,128)} %get-tuple-element.47.total_ref, f32[128,2048]{1,0:T(8,128)} %get-tuple-element.48.sum_ref, f32[128,2048]{1,0:T(8,128)} %collective-permute-done.16.f1_ref), custom_call_target="tpu_custom_call" | custom-call | tf_op jit(solution)/shard_map/close/pallas_call | solution.py:391
  (27 shorter events, 0.1 us)
Async XLA Ops:
  21.1 26.3 %collective-permute-start.7 = (bf16[512,2048]{1,0:T(8,128)(2,1)}, bf16[512,2048]{1,0:T(8,128)(2,1)S(1)}, u32[]{:S(2)}, u32[]{:S(2)}) collective-permute-start(bf16[512,2048]{1,0:T(8,128)(2,1)} %get-tuple-element.37.xm_hbm), channel_id=1, source_target_pairs={{0,4},{1,3},{2,6},{3,1},{4,0},{5,7},{6,2},{7,5}} | collective-permute-start | bytes 6291464 | tf_op jit(solution)/shard_map/ppermute | solution.py:301
  47.3 1.4 copy-start
  48.7 4.2 %collective-permute-start.8 = (bf16[512,2048]{1,0:T(8,128)(2,1)S(1)}, bf16[512,2048]{1,0:T(8,128)(2,1)S(1)}, u32[]{:S(2)}, u32[]{:S(2)}) collective-permute-start(bf16[512,2048]{1,0:T(8,128)(2,1)S(1)} %collective-permute-done.7.xm_hbm), channel_id=1, source_target_pairs={{0,1},{1,0},{2,3},{3,2},{4,5},{5,4},{6,7},{7,6}} | collective-permute-start | bytes 6291464 | tf_op jit(solution)/shard_map/ppermute | solution.py:297
  52.9 1.3 copy-start.1
  82.6 76.8 %collective-permute-start.10 = (f32[384,2048]{1,0:T(8,128)}, f32[384,2048]{1,0:T(8,128)}, u32[]{:S(2)}, u32[]{:S(2)}) collective-permute-start(f32[384,2048]{1,0:T(8,128)} %get-tuple-element.46), channel_id=1, source_target_pairs={{0,1},{1,0},{2,3},{3,2},{4,5},{5,4},{6,7},{7,6}} | collective-permute-start | bytes 9437192 | tf_op jit(solution)/shard_map/ppermute | solution.py:297
  122.5 86.1 %collective-permute-start.5 = (f32[448,2048]{1,0:T(8,128)}, f32[448,2048]{1,0:T(8,128)}, u32[]{:S(2)}, u32[]{:S(2)}) collective-permute-start(f32[448,2048]{1,0:T(8,128)} %get-tuple-element.42), channel_id=1, source_target_pairs={{0,1},{1,0},{2,3},{3,2},{4,5},{5,4},{6,7},{7,6}} | collective-permute-start | bytes 11010056 | tf_op jit(solution)/shard_map/ppermute | solution.py:297
  149.6 63.0 %collective-permute-start.9 = (f32[384,2048]{1,0:T(8,128)}, f32[384,2048]{1,0:T(8,128)}, u32[]{:S(2)}, u32[]{:S(2)}) collective-permute-start(f32[384,2048]{1,0:T(8,128)} %get-tuple-element.44), channel_id=1, source_target_pairs={{0,1},{1,0},{2,3},{3,2},{4,5},{5,4},{6,7},{7,6}} | collective-permute-start | bytes 9437192 | tf_op jit(solution)/shard_map/ppermute | solution.py:297
  159.4 10.7 %copy-start.2 = (bf16[256,2048]{1,0:T(8,128)(2,1)S(1)}, bf16[256,2048]{1,0:T(8,128)(2,1)}, u32[]{:S(2)}) copy-start(bf16[256,2048]{1,0:T(8,128)(2,1)} %xm_hbm.1) | copy-start | bytes 3145732
  164.7 48.4 %collective-permute-start.11 = (f32[384,2048]{1,0:T(8,128)}, f32[384,2048]{1,0:T(8,128)}, u32[]{:S(2)}, u32[]{:S(2)}) collective-permute-start(f32[384,2048]{1,0:T(8,128)} %add.27), channel_id=1, source_target_pairs={{0,2},{1,5},{2,0},{3,7},{4,6},{5,1},{6,4},{7,3}} | collective-permute-start | bytes 9437192 | tf_op jit(solution)/shard_map/ppermute | solution.py:301
  170.1 2.8 collective-permute-start
  170.1 48.8 %collective-permute-start.3 = (f32[64,2048]{1,0:T(8,128)}, f32[64,2048]{1,0:T(8,128)}, u32[]{:S(2)}, u32[]{:S(2)}) collective-permute-start(f32[64,2048]{1,0:T(8,128)} %get-tuple-element.40), channel_id=1, source_target_pairs={{0,1},{1,0},{2,3},{3,2},{4,5},{5,4},{6,7},{7,6}} | collective-permute-start | bytes 1572872 | tf_op jit(solution)/shard_map/ppermute | solution.py:297
  208.5 97.5 %collective-permute-start.1 = (f32[384,2048]{1,0:T(8,128)}, f32[384,2048]{1,0:T(8,128)S(1)}, u32[]{:S(2)}, u32[]{:S(2)}) collective-permute-start(f32[384,2048]{1,0:T(8,128)} %get-tuple-element.35), channel_id=1, source_target_pairs={{0,1},{1,0},{2,3},{3,2},{4,5},{5,4},{6,7},{7,6}} | collective-permute-start | bytes 9437192 | tf_op jit(solution)/shard_map/ppermute | solution.py:297
  208.6 4.0 %copy-start.13 = (f32[128,2048]{1,0:T(8,128)S(1)}, f32[128,2048]{1,0:T(8,128)}, u32[]{:S(2)}) copy-start(f32[128,2048]{1,0:T(8,128)} %get-tuple-element.52) | copy-start | bytes 3145732
  208.6 4.5 %copy-start.3 = (f32[384,2048]{1,0:T(8,128)S(1)}, f32[384,2048]{1,0:T(8,128)}, u32[]{:S(2)}) copy-start(f32[384,2048]{1,0:T(8,128)} %get-tuple-element.43) | copy-start | bytes 9437188
  212.5 93.5 %collective-permute-start.6 = (f32[448,2048]{1,0:T(8,128)S(1)}, f32[448,2048]{1,0:T(8,128)}, u32[]{:S(2)}, u32[]{:S(2)}) collective-permute-start(f32[448,2048]{1,0:T(8,128)S(1)} %add.25), channel_id=1, source_target_pairs={{0,2},{1,5},{2,0},{3,7},{4,6},{5,1},{6,4},{7,3}} | collective-permute-start | bytes 11010056 | tf_op jit(solution)/shard_map/ppermute | solution.py:301
  212.6 6.2 %collective-permute-start.14 = (f32[128,2048]{1,0:T(8,128)S(1)}, f32[128,2048]{1,0:T(8,128)S(1)}, u32[]{:S(2)}, u32[]{:S(2)}) collective-permute-start(f32[128,2048]{1,0:T(8,128)S(1)} %copy-done.13), channel_id=1, source_target_pairs={{0,1},{1,0},{2,3},{3,2},{4,5},{5,4},{6,7},{7,6}} | collective-permute-start | bytes 3145736 | tf_op jit(solution)/shard_map/ppermute | solution.py:297
  213.1 5.7 %copy-start.11 = (f32[128,2048]{1,0:T(8,128)S(1)}, f32[128,2048]{1,0:T(8,128)}, u32[]{:S(2)}) copy-start(f32[128,2048]{1,0:T(8,128)} %get-tuple-element.50) | copy-start | bytes 3145732
  213.1 5.7 %copy-start.6 = (f32[128,2048]{1,0:T(8,128)S(1)}, f32[128,2048]{1,0:T(8,128)}, u32[]{:S(2)}) copy-start(f32[128,2048]{1,0:T(8,128)} %get-tuple-element.51) | copy-start | bytes 3145732
  217.0 2.3 copy-start.9
  217.0 83.4 %copy-start.12 = (f32[128,2048]{1,0:T(8,128)S(1)}, f32[128,2048]{1,0:T(8,128)}, u32[]{:S(2)}) copy-start(f32[128,2048]{1,0:T(8,128)} %get-tuple-element.36) | copy-start | bytes 3145732
  217.0 83.4 %copy-start.8 = (f32[128,2048]{1,0:T(8,128)S(1)}, f32[128,2048]{1,0:T(8,128)}, u32[]{:S(2)}) copy-start(f32[128,2048]{1,0:T(8,128)} %get-tuple-element.49) | copy-start | bytes 3145732
  217.0 89.0 %collective-permute-start.12 = (f32[384,2048]{1,0:T(8,128)S(1)}, f32[384,2048]{1,0:T(8,128)S(1)}, u32[]{:S(2)}, u32[]{:S(2)}) collective-permute-start(f32[384,2048]{1,0:T(8,128)S(1)} %add_add_fusion), channel_id=1, source_target_pairs={{0,4},{1,3},{2,6},{3,1},{4,0},{5,7},{6,2},{7,5}} | collective-permute-start | bytes 9437192 | tf_op jit(solution)/shard_map/ppermute | solution.py:301
  218.8 2.7 collective-permute-start.13
  218.9 81.5 %collective-permute-start.15 = (f32[128,2048]{1,0:T(8,128)S(1)}, f32[128,2048]{1,0:T(8,128)S(1)}, u32[]{:S(2)}, u32[]{:S(2)}) collective-permute-start(f32[128,2048]{1,0:T(8,128)S(1)} %add.30), channel_id=1, source_target_pairs={{0,2},{1,5},{2,0},{3,7},{4,6},{5,1},{6,4},{7,3}} | collective-permute-start | bytes 3145736 | tf_op jit(solution)/shard_map/ppermute | solution.py:301
  221.4 84.6 %collective-permute-start.4 = (f32[64,2048]{1,0:T(8,128)S(1)}, f32[64,2048]{1,0:T(8,128)S(1)}, u32[]{:S(2)}, u32[]{:S(2)}) collective-permute-start(f32[64,2048]{1,0:T(8,128)S(1)} %add.24), channel_id=1, source_target_pairs={{0,2},{1,5},{2,0},{3,7},{4,6},{5,1},{6,4},{7,3}} | collective-permute-start | bytes 1572872 | tf_op jit(solution)/shard_map/ppermute | solution.py:301
  300.4 5.6 %collective-permute-start.2 = (f32[128,2048]{1,0:T(8,128)S(1)}, f32[128,2048]{1,0:T(8,128)S(1)}, u32[]{:S(2)}, u32[]{:S(2)}) collective-permute-start(f32[128,2048]{1,0:T(8,128)S(1)} %copy-done.12), channel_id=1, source_target_pairs={{0,1},{1,0},{2,3},{3,2},{4,5},{5,4},{6,7},{7,6}} | collective-permute-start | bytes 3145736 | tf_op jit(solution)/shard_map/ppermute | solution.py:297
  306.0 3.5 %copy-start.10 = (f32[64,2048]{1,0:T(8,128)}, f32[64,2048]{1,0:T(8,128)S(1)}, u32[]{:S(2)}) copy-start(f32[64,2048]{1,0:T(8,128)S(1)} %collective-permute-done.4.n0_ref) | copy-start | bytes 1572868
  306.0 15.1 %collective-permute-start.16 = (f32[128,2048]{1,0:T(8,128)}, f32[128,2048]{1,0:T(8,128)}, u32[]{:S(2)}, u32[]{:S(2)}) collective-permute-start(f32[128,2048]{1,0:T(8,128)} %add_add_fusion.1), channel_id=1, source_target_pairs={{0,4},{1,3},{2,6},{3,1},{4,0},{5,7},{6,2},{7,5}} | collective-permute-start | bytes 3145736 | tf_op jit(solution)/shard_map/ppermute | solution.py:301
  306.0 3.4 %copy-start.7 = (f32[128,2048]{1,0:T(8,128)}, f32[128,2048]{1,0:T(8,128)S(1)}, u32[]{:S(2)}) copy-start(f32[128,2048]{1,0:T(8,128)S(1)} %collective-permute-done.2.o1_ref) | copy-start | bytes 3145732
  306.0 1.7 copy-start.4
  307.8 1.7 copy-start.5

commit v10 on v9

--- a/solution.py
+++ b/solution.py
@@ -40,8 +40,6 @@
         )
         for k, peer in peers
     ]
-    for c in copies:
-        c.start()
     pieces = xsend.shape[1]
     turn = turns[0] + (turns[1] - turns[0]) * core
     piece = x_ref.shape[0] // pieces
@@ -67,7 +65,10 @@
     ]
     own = pltpu.make_async_copy(held, pair_ref.at[pl.ds(t, t)], lsem.at[1])
     load.wait()
-    for c in arrive:
+    arrive[0].start()
+    for c in copies:
+        c.start()
+    for c in arrive[1:]:
         c.start()
     own.start()
     ids_all[pl.ds(here, 1)] = idx_ref[...][None]
@@ -203,35 +204,42 @@
                     c.start()
 
         def run(m):
-            bases = [pl.multiple_of(jnp.minimum(o // 8 * 8, rows - m), 8) for o in offs]
-            parts = []
-            for s in range(2):
-                row = lax.broadcasted_iota(jnp.int32, (m, t), 0) + bases[s]
-                hit = (row == pos_ref[blocks[s], pl.ds(expert, 1), :]).astype(F32).astype(BF16)
-                parts.append(jnp.dot(hit, xbuf[s], preferred_element_type=F32))
-            xs = jnp.concatenate(parts, axis=0).astype(BF16)
-            hs = []
-            for i, (wa, wb) in enumerate(zip(w1s, w3s)):
-                arrive(i, e)
-                h1 = jnp.dot(xs, wa[e % 2], preferred_element_type=F32)
-                h3 = jnp.dot(xs, wb[e % 2], preferred_element_type=F32)
-                hs.append((jax.nn.silu(h1) * h3).astype(BF16))
-                used(i, e)
-            h = jnp.concatenate(hs, axis=1)
-
-            def project(k, carry):
-                for i in range(2):
-                    pl.when(k == i)(functools.partial(arrive, len(w1s) + i, e))
-                p = jnp.dot(h, w2s[e % 2, k], preferred_element_type=F32)
-                cols = pl.ds(pl.multiple_of(k * half_d, half_d), half_d)
+            tiles = (need + m - 1) // m
+
+            def once(i, carry):
+                opens, closes = i == 0, i == tiles - 1
+                starts = [o // 8 * 8 + i * m for o in offs]
+                bases = [pl.multiple_of(jnp.minimum(b, rows - m), 8) for b in starts]
+                parts = []
                 for s in range(2):
-                    acc[s, pl.ds(bases[s], m), cols] += p[s * m : (s + 1) * m]
-                for i in range(2):
-                    pl.when(k == i)(functools.partial(used, len(w1s) + i, e))
-                last(k)
-                return carry
-
-            lax.fori_loop(0, 2, project, 0)
+                    row = lax.broadcasted_iota(jnp.int32, (m, t), 0) + bases[s]
+                    hit = (row == pos_ref[blocks[s], pl.ds(expert, 1), :]) & (row >= starts[s])
+                    parts.append(jnp.dot(hit.astype(F32).astype(BF16), xbuf[s], preferred_element_type=F32))
+                xs = jnp.concatenate(parts, axis=0).astype(BF16)
+                hs = []
+                for c, (wa, wb) in enumerate(zip(w1s, w3s)):
+                    pl.when(opens)(functools.partial(arrive, c, e))
+                    h1 = jnp.dot(xs, wa[e % 2], preferred_element_type=F32)
+                    h3 = jnp.dot(xs, wb[e % 2], preferred_element_type=F32)
+                    hs.append((jax.nn.silu(h1) * h3).astype(BF16))
+                    pl.when(closes)(functools.partial(used, c, e))
+                h = jnp.concatenate(hs, axis=1)
+
+                def project(k, carry):
+                    for c in range(2):
+                        pl.when(opens & (k == c))(functools.partial(arrive, len(w1s) + c, e))
+                    p = jnp.dot(h, w2s[e % 2, k], preferred_element_type=F32)
+                    cols = pl.ds(pl.multiple_of(k * half_d, half_d), half_d)
+                    for s in range(2):
+                        acc[s, pl.ds(bases[s], m), cols] += p[s * m : (s + 1) * m]
+                    for c in range(2):
+                        pl.when(closes & (k == c))(functools.partial(used, len(w1s) + c, e))
+                    pl.when(closes)(functools.partial(last, k))
+                    return carry
+
+                return lax.fori_loop(0, 2, project, carry)
+
+            lax.fori_loop(0, tiles, once, 0)
 
         @pl.when(need == 0)
         def _():
@@ -240,10 +248,9 @@
                 used(i, e)
             last(0)
 
-        lo = 0
-        for m in sizes:
-            pl.when((need > lo) & (need <= m))(functools.partial(run, m))
-            lo = m
+        small, large = sizes
+        pl.when((need > 0) & (need <= small))(functools.partial(run, small))
+        pl.when(need > small)(functools.partial(run, large))
         return carry
 
     lax.fori_loop(0, e_loc, step, 0)
@@ -287,7 +294,6 @@
         top = idx.shape[1]
         e_all = cap.shape[0]
         e_loc, _, ff = w1.shape
-        c = (5 * top * t_loc // (2 * e_all) + 7) // 8 * 8
         rows = top * t_loc
         cuts = (0, 512, ff)
         widths = [b - a for a, b in zip(cuts, cuts[1:])]
@@ -301,7 +307,7 @@
             return lax.ppermute(a, ("tp", "ep"), pairs)
 
         out, back = (1, 2), (2, 1)
-        pieces = 4
+        pieces = 2
         pos, groups, hit, gate, pair, x_near = pl.pallas_call(
             functools.partial(_route_kernel, chips, out),
             out_shape=[
@@ -328,7 +334,7 @@
             name="route",
         )(idx.T, g.T, cap, x)
 
-        sizes = (64, (c + 7 + 7) // 8 * 8)
+        sizes = (64, 152)
 
         def stage(turns, mine, other, split, rows0=(0, 0)):
             return pl.pallas_call(
@@ -358,7 +364,7 @@
                 sums.append(functools.reduce(jnp.add, [m[q] for m in more], parts[2 + q] + other))
             return sums
 
-        early, late = (rows // 8, rows - rows // 8), (rows - rows // 4, rows // 4)
+        early, late = (rows // 4, rows - rows // 4), (rows - rows // 4, rows // 4)
         rest = shift(pair, back)
         rest_other = swap(rest)
         own_x = swap(x)

time: 325 us -> 318 us (0.978)
  Pallas kernels: 157 us -> 153 us
    pallas_call x4, Pallas kernels: 123 us -> 120 us  [stage(): pl.pallas_call(functools.partial(_expert_kernel, turns, rows0, sizes, cut...]
    ppermute x10, starting transfers between devices: 18.5 us -> 15 us  [swap(): return lax.ppermute(a, 'ep', [(0, 1), (1, 0)])]
    unnamed x28 -> x30, local copies, waits for them, and re-layouts: 6.12 us -> 8.05 us
  transfers between devices with their start and end apart: 17 -> 17, of which waited for: 7 -> 6; matrix products, arithmetic and copies ran while one was open for 5% -> 5% of each run, Pallas kernels for 32% -> 32%
where the time goes in v10:
time: 318 us
  Pallas kernels  153 us (48%)
  waiting for transfers between devices  115 us (36%)
  starting transfers between devices  24.9 us (8%)
  other arithmetic  16.7 us (5%)
  local copies, waits for them, and re-layouts  8.05 us (3%)
    pallas_call x4, Pallas kernels, stage(): pl.pallas_call(functools.partial(_expert_kernel, turns, rows0, sizes, cut...  120 us
    ppermute x7, waiting for transfers between devices, shift(): return lax.ppermute(a, ('tp', 'ep'), pairs)  109 us
    pallas_call x1, Pallas kernels, layer(): pl.pallas_call(functools.partial(_route_kernel, chips, out), out_shape=[j...  21.3 us
    ppermute x10, starting transfers between devices, swap(): return lax.ppermute(a, 'ep', [(0, 1), (1, 0)])  15 us
    add x4, other arithmetic, merge(): parts[2 + q] + other  11.7 us
    ppermute x7, starting transfers between devices, shift(): return lax.ppermute(a, ('tp', 'ep'), pairs)  9.96 us
    pallas_call x1, Pallas kernels, layer(): pl.pallas_call(_combine_kernel, out_shape=[jax.ShapeDtypeStruct((t_loc, d...  8.6 us
    unnamed x30, local copies, waits for them, and re-layouts  8.05 us
  transfers between devices with their start and end apart: 17, of which 6 were waited for; matrix products, arithmetic and copies ran while one was open for 5% of the time, Pallas kernels for 32%

profile of v10, /device:TPU:0, one launch (start us, length us, event | category | flops | bytes accessed | tf_op | source)
XLA Modules:
  0.0 317.9 jit_solution(13262747893544091990)
XLA Ops:
  0.0 21.3 %route.1 = (s32[8,8,256]{2,1,0:T(8,128)}, s32[8,128]{1,0:T(8,128)}, bf16[2,256,512]{2,1,0:T(8,128)(2,1)}, f32[256,8]{1,0:T(8,128)}, bf16[512,2048]{1,0:T(8,128)(2,1)}, /*index=5*/bf16[256,2048]{1,0:T(8,128)(2,1)}) custom-call(s32[2,256]{1,0:T(2,128)} %bitcast.2, f32[2,256]{1,0:T(2,128)} %bitcast.3, s32[8]{0:T(128)} %cap_ref.1, bf16[256,2048]{1,0:T(8,128)(2,1)} %xm_hbm.1), custom_call_target="tpu_custom_call" | custom-call | tf_op jit(solution)/shard_map/route/pallas_call | solution.py:311
  21.3 1.2 collective-permute-start.7
  22.6 25.0 %collective-permute-done.7.xm_hbm = bf16[512,2048]{1,0:T(8,128)(2,1)S(1)} collective-permute-done((bf16[512,2048]{1,0:T(8,128)(2,1)}, bf16[512,2048]{1,0:T(8,128)(2,1)S(1)}, u32[]{:S(2)}, u32[]{:S(2)}) %collective-permute-start.7) | collective-permute-done | bytes 2097184 | tf_op jit(solution)/shard_map/ppermute | solution.py:307
  47.6 1.3 copy-done
  48.9 4.2 %collective-permute-done.8.xo_hbm = bf16[512,2048]{1,0:T(8,128)(2,1)S(1)} collective-permute-done((bf16[512,2048]{1,0:T(8,128)(2,1)S(1)}, bf16[512,2048]{1,0:T(8,128)(2,1)S(1)}, u32[]{:S(2)}, u32[]{:S(2)}) %collective-permute-start.8) | collective-permute-done | bytes 2097184 | tf_op jit(solution)/shard_map/ppermute | solution.py:303
  53.1 1.4 copy-done.1
  54.5 27.7 %shard_map.76 = (f32[384,2048]{1,0:T(8,128)}, f32[128,2048]{1,0:T(8,128)}, f32[384,2048]{1,0:T(8,128)}, f32[128,2048]{1,0:T(8,128)}) custom-call(s32[8,128]{1,0:T(8,128)} %get-tuple-element.31.table_ref, s32[8,8,256]{2,1,0:T(8,128)} %get-tuple-element.32.pos_ref, bf16[512,2048]{1,0:T(8,128)(2,1)} %copy-done, bf16[512,2048]{1,0:T(8,128)(2,1)} %copy-done.1, ...), custom_call_target="tpu_custom_call" | custom-call | flops 8858370048 | bytes 77594624 | tf_op jit(solution)/shard_map/pallas_call | solution.py:340
  82.1 6.3 %collective-permute-start.10 = (f32[384,2048]{1,0:T(8,128)}, f32[384,2048]{1,0:T(8,128)}, u32[]{:S(2)}, u32[]{:S(2)}) collective-permute-start(f32[384,2048]{1,0:T(8,128)} %get-tuple-element.46), channel_id=1, source_target_pairs={{0,1},{1,0},{2,3},{3,2},{4,5},{5,4},{6,7},{7,6}} | collective-permute-start | bytes 9437192 | tf_op jit(solution)/shard_map/ppermute | solution.py:303
  88.5 31.2 %shard_map.74 = (f32[128,2048]{1,0:T(8,128)}, f32[384,2048]{1,0:T(8,128)}, f32[128,2048]{1,0:T(8,128)}, f32[384,2048]{1,0:T(8,128)}) custom-call(s32[8,128]{1,0:T(8,128)} %get-tuple-element.31.table_ref, s32[8,8,256]{2,1,0:T(8,128)} %get-tuple-element.32.pos_ref, bf16[512,2048]{1,0:T(8,128)(2,1)} %get-tuple-element.37.xm_hbm, ...), custom_call_target="tpu_custom_call" | custom-call | flops 8858370048 | bytes 77594624 | tf_op jit(solution)/shard_map/pallas_call | solution.py:340
  119.7 0.0 collective-permute-start.5
  119.7 26.9 %shard_map.75 = (f32[384,2048]{1,0:T(8,128)}, f32[128,2048]{1,0:T(8,128)}, f32[384,2048]{1,0:T(8,128)}, f32[128,2048]{1,0:T(8,128)}) custom-call(s32[8,128]{1,0:T(8,128)} %get-tuple-element.31.table_ref, s32[8,8,256]{2,1,0:T(8,128)} %get-tuple-element.32.pos_ref, bf16[512,2048]{1,0:T(8,128)(2,1)} %copy-done, bf16[512,2048]{1,0:T(8,128)(2,1)} %copy-done.1, ...), custom_call_target="tpu_custom_call" | custom-call | flops 8858370048 | bytes 77594624 | tf_op jit(solution)/shard_map/pallas_call | solution.py:340
  146.6 8.0 %collective-permute-start.9 = (f32[384,2048]{1,0:T(8,128)}, f32[384,2048]{1,0:T(8,128)}, u32[]{:S(2)}, u32[]{:S(2)}) collective-permute-start(f32[384,2048]{1,0:T(8,128)} %get-tuple-element.44), channel_id=1, source_target_pairs={{0,1},{1,0},{2,3},{3,2},{4,5},{5,4},{6,7},{7,6}} | collective-permute-start | bytes 9437192 | tf_op jit(solution)/shard_map/ppermute | solution.py:303
  154.6 0.0 collective-permute-done.10
  154.6 5.3 %add.27 = f32[384,2048]{1,0:T(8,128)} add(f32[384,2048]{1,0:T(8,128)} %get-tuple-element.45, f32[384,2048]{1,0:T(8,128)} %collective-permute-done.10) | non-fusion elementwise | flops 786432 | bytes 9437184 | tf_op jit(solution)/shard_map/add | solution.py:364
  159.9 4.8 %collective-permute-start.11 = (f32[384,2048]{1,0:T(8,128)}, f32[384,2048]{1,0:T(8,128)}, u32[]{:S(2)}, u32[]{:S(2)}) collective-permute-start(f32[384,2048]{1,0:T(8,128)} %add.27), channel_id=1, source_target_pairs={{0,2},{1,5},{2,0},{3,7},{4,6},{5,1},{6,4},{7,3}} | collective-permute-start | bytes 9437192 | tf_op jit(solution)/shard_map/ppermute | solution.py:307
  164.7 0.0 collective-permute-start
  164.7 0.5 collective-permute-start.3
  165.2 2.1 collective-permute-done.xo_hbm
  167.3 1.0 copy-done.12
  168.3 0.1 collective-permute-start.14
  168.4 33.8 %shard_map.73 = (f32[384,2048]{1,0:T(8,128)}, f32[128,2048]{1,0:T(8,128)}, f32[384,2048]{1,0:T(8,128)}, f32[128,2048]{1,0:T(8,128)}) custom-call(s32[8,128]{1,0:T(8,128)} %get-tuple-element.31.table_ref, s32[8,8,256]{2,1,0:T(8,128)} %get-tuple-element.32.pos_ref, bf16[256,2048]{1,0:T(8,128)(2,1)} %xm_hbm.1, bf16[256,2048]{1,0:T(8,128)(2,1)} %copy-done.12, ...), custom_call_target="tpu_custom_call" | custom-call | flops 8858370048 | bytes 77594624 | tf_op jit(solution)/shard_map/pallas_call | solution.py:340
  202.2 0.0 collective-permute-start.1
  202.3 3.5 %add.25 = f32[384,2048]{1,0:T(8,128)S(1)} add(f32[384,2048]{1,0:T(8,128)} %get-tuple-element.41, f32[384,2048]{1,0:T(8,128)} %collective-permute-done.5) | non-fusion elementwise | flops 786432 | bytes 9437184 | tf_op jit(solution)/shard_map/add | solution.py:364
  205.8 0.0 collective-permute-start.6
  205.8 0.2 copy-done.3
  206.0 3.9 %add_add_fusion = f32[384,2048]{1,0:T(8,128)S(1)} fusion(f32[384,2048]{1,0:T(8,128)} %collective-permute-done.11, f32[384,2048]{1,0:T(8,128)S(1)} %copy-done.3, f32[384,2048]{1,0:T(8,128)} %collective-permute-done.9), kind=kLoop, calls=%fused_computation | loop fusion | flops 1572864 | bytes 12582912 | tf_op jit(solution)/shard_map/add | solution.py:364
  209.9 1.8 collective-permute-start.12
  211.8 0.0 collective-permute-start.13
  211.8 1.5 add.30
  213.3 0.0 collective-permute-done.3
  213.3 0.4 collective-permute-start.15
  213.7 1.4 add.24
  215.1 0.0 collective-permute-done.13
  215.1 1.7 collective-permute-start.4
  216.8 71.2 %collective-permute-done.15 = f32[128,2048]{1,0:T(8,128)S(1)} collective-permute-done((f32[128,2048]{1,0:T(8,128)S(1)}, f32[128,2048]{1,0:T(8,128)S(1)}, u32[]{:S(2)}, u32[]{:S(2)}) %collective-permute-start.15) | collective-permute-done | bytes 1048608 | tf_op jit(solution)/shard_map/ppermute | solution.py:307
  288.0 0.0 collective-permute-start.2
  288.0 1.1 add_add_fusion.1
  289.1 10.1 %collective-permute-done.4.n0_ref = f32[128,2048]{1,0:T(8,128)S(1)} collective-permute-done((f32[128,2048]{1,0:T(8,128)S(1)}, f32[128,2048]{1,0:T(8,128)S(1)}, u32[]{:S(2)}, u32[]{:S(2)}) %collective-permute-start.4) | collective-permute-done | bytes 1048608 | tf_op jit(solution)/shard_map/ppermute | solution.py:307
  299.2 0.0 collective-permute-start.16
  299.2 0.0 collective-permute-done.2.o1_ref
  299.2 0.0 copy-start.10
  299.3 1.7 copy-done.4
  301.0 1.0 copy-done.5
  302.0 1.1 copy-done.6
  303.1 0.3 copy-done.10
  303.5 8.6 %combine.1 = (f32[256,2048]{1,0:T(8,128)}, f32[128,2048]{1,0:T(8,128)}) custom-call(bf16[2,256,512]{2,1,0:T(8,128)(2,1)} %get-tuple-element.29.hit_ref, f32[256,8]{1,0:T(8,128)} %get-tuple-element.30.gate_ref, f32[384,2048]{1,0:T(8,128)} %get-tuple-element.33.k0_ref, f32[128,2048]{1,0:T(8,128)} %get-tuple-element.34.k1_ref, f32[384,2048]{1,0:T(8,128)} %copy-done.4, ...), custom_call_target="tpu_custom_call" | custom-call | tf_op jit(solution)/shard_map/combine/pallas_call | solution.py:387
  312.1 2.3 collective-permute-done.16.f1_ref
  314.3 3.6 %close.1 = bf16[256,2048]{1,0:T(8,128)(2,1)} custom-call(bf16[2,256,512]{2,1,0:T(8,128)(2,1)} %get-tuple-element.29.hit_ref, f32[256,8]{1,0:T(8,128)} %get-tuple-element.30.gate_ref, f32[256,2048]{1,0:T(8,128)} %get-tuple-element.47.total_ref, f32[128,2048]{1,0:T(8,128)} %get-tuple-element.48.sum_ref, f32[128,2048]{1,0:T(8,128)} %collective-permute-done.16.f1_ref), custom_call_target="tpu_custom_call" | custom-call | tf_op jit(solution)/shard_map/close/pallas_call | solution.py:397
  (29 shorter events, 0.1 us)
Async XLA Ops:
  21.3 26.3 %collective-permute-start.7 = (bf16[512,2048]{1,0:T(8,128)(2,1)}, bf16[512,2048]{1,0:T(8,128)(2,1)S(1)}, u32[]{:S(2)}, u32[]{:S(2)}) collective-permute-start(bf16[512,2048]{1,0:T(8,128)(2,1)} %get-tuple-element.37.xm_hbm), channel_id=1, source_target_pairs={{0,4},{1,3},{2,6},{3,1},{4,0},{5,7},{6,2},{7,5}} | collective-permute-start | bytes 6291464 | tf_op jit(solution)/shard_map/ppermute | solution.py:307
  47.6 1.3 copy-start
  48.9 4.2 %collective-permute-start.8 = (bf16[512,2048]{1,0:T(8,128)(2,1)S(1)}, bf16[512,2048]{1,0:T(8,128)(2,1)S(1)}, u32[]{:S(2)}, u32[]{:S(2)}) collective-permute-start(bf16[512,2048]{1,0:T(8,128)(2,1)S(1)} %collective-permute-done.7.xm_hbm), channel_id=1, source_target_pairs={{0,1},{1,0},{2,3},{3,2},{4,5},{5,4},{6,7},{7,6}} | collective-permute-start | bytes 6291464 | tf_op jit(solution)/shard_map/ppermute | solution.py:303
  53.1 1.4 copy-start.1
  82.1 72.4 %collective-permute-start.10 = (f32[384,2048]{1,0:T(8,128)}, f32[384,2048]{1,0:T(8,128)}, u32[]{:S(2)}, u32[]{:S(2)}) collective-permute-start(f32[384,2048]{1,0:T(8,128)} %get-tuple-element.46), channel_id=1, source_target_pairs={{0,1},{1,0},{2,3},{3,2},{4,5},{5,4},{6,7},{7,6}} | collective-permute-start | bytes 9437192 | tf_op jit(solution)/shard_map/ppermute | solution.py:303
  119.7 82.5 %collective-permute-start.5 = (f32[384,2048]{1,0:T(8,128)}, f32[384,2048]{1,0:T(8,128)}, u32[]{:S(2)}, u32[]{:S(2)}) collective-permute-start(f32[384,2048]{1,0:T(8,128)} %get-tuple-element.42), channel_id=1, source_target_pairs={{0,1},{1,0},{2,3},{3,2},{4,5},{5,4},{6,7},{7,6}} | collective-permute-start | bytes 9437192 | tf_op jit(solution)/shard_map/ppermute | solution.py:303
  146.6 59.1 %collective-permute-start.9 = (f32[384,2048]{1,0:T(8,128)}, f32[384,2048]{1,0:T(8,128)}, u32[]{:S(2)}, u32[]{:S(2)}) collective-permute-start(f32[384,2048]{1,0:T(8,128)} %get-tuple-element.44), channel_id=1, source_target_pairs={{0,1},{1,0},{2,3},{3,2},{4,5},{5,4},{6,7},{7,6}} | collective-permute-start | bytes 9437192 | tf_op jit(solution)/shard_map/ppermute | solution.py:303
  154.6 10.1 %copy-start.2 = (bf16[256,2048]{1,0:T(8,128)(2,1)S(1)}, bf16[256,2048]{1,0:T(8,128)(2,1)}, u32[]{:S(2)}) copy-start(bf16[256,2048]{1,0:T(8,128)(2,1)} %xm_hbm.1) | copy-start | bytes 3145732
  159.9 45.9 %collective-permute-start.11 = (f32[384,2048]{1,0:T(8,128)}, f32[384,2048]{1,0:T(8,128)}, u32[]{:S(2)}, u32[]{:S(2)}) collective-permute-start(f32[384,2048]{1,0:T(8,128)} %add.27), channel_id=1, source_target_pairs={{0,2},{1,5},{2,0},{3,7},{4,6},{5,1},{6,4},{7,3}} | collective-permute-start | bytes 9437192 | tf_op jit(solution)/shard_map/ppermute | solution.py:307
  164.7 2.7 collective-permute-start
  164.7 48.7 %collective-permute-start.3 = (f32[128,2048]{1,0:T(8,128)}, f32[128,2048]{1,0:T(8,128)}, u32[]{:S(2)}, u32[]{:S(2)}) collective-permute-start(f32[128,2048]{1,0:T(8,128)} %get-tuple-element.40), channel_id=1, source_target_pairs={{0,1},{1,0},{2,3},{3,2},{4,5},{5,4},{6,7},{7,6}} | collective-permute-start | bytes 3145736 | tf_op jit(solution)/shard_map/ppermute | solution.py:303
  167.3 1.0 copy-start.12
  168.3 43.5 %collective-permute-start.14 = (f32[128,2048]{1,0:T(8,128)}, f32[128,2048]{1,0:T(8,128)}, u32[]{:S(2)}, u32[]{:S(2)}) collective-permute-start(f32[128,2048]{1,0:T(8,128)} %get-tuple-element.52), channel_id=1, source_target_pairs={{0,1},{1,0},{2,3},{3,2},{4,5},{5,4},{6,7},{7,6}} | collective-permute-start | bytes 3145736 | tf_op jit(solution)/shard_map/ppermute | solution.py:303
  202.2 97.0 %collective-permute-start.1 = (f32[384,2048]{1,0:T(8,128)}, f32[384,2048]{1,0:T(8,128)S(1)}, u32[]{:S(2)}, u32[]{:S(2)}) collective-permute-start(f32[384,2048]{1,0:T(8,128)} %get-tuple-element.35), channel_id=1, source_target_pairs={{0,1},{1,0},{2,3},{3,2},{4,5},{5,4},{6,7},{7,6}} | collective-permute-start | bytes 9437192 | tf_op jit(solution)/shard_map/ppermute | solution.py:303
  202.3 3.7 %copy-start.3 = (f32[384,2048]{1,0:T(8,128)S(1)}, f32[384,2048]{1,0:T(8,128)}, u32[]{:S(2)}) copy-start(f32[384,2048]{1,0:T(8,128)} %get-tuple-element.43) | copy-start | bytes 9437188
  205.8 93.5 %collective-permute-start.6 = (f32[384,2048]{1,0:T(8,128)S(1)}, f32[384,2048]{1,0:T(8,128)S(1)}, u32[]{:S(2)}, u32[]{:S(2)}) collective-permute-start(f32[384,2048]{1,0:T(8,128)S(1)} %add.25), channel_id=1, source_target_pairs={{0,2},{1,5},{2,0},{3,7},{4,6},{5,1},{6,4},{7,3}} | collective-permute-start | bytes 9437192 | tf_op jit(solution)/shard_map/ppermute | solution.py:307
  206.0 5.8 %copy-start.13 = (f32[128,2048]{1,0:T(8,128)S(1)}, f32[128,2048]{1,0:T(8,128)}, u32[]{:S(2)}) copy-start(f32[128,2048]{1,0:T(8,128)} %get-tuple-element.50) | copy-start | bytes 3145732
  206.0 5.8 %copy-start.8 = (f32[128,2048]{1,0:T(8,128)S(1)}, f32[128,2048]{1,0:T(8,128)}, u32[]{:S(2)}) copy-start(f32[128,2048]{1,0:T(8,128)} %get-tuple-element.51) | copy-start | bytes 3145732
  209.9 3.8 %copy-start.7 = (f32[128,2048]{1,0:T(8,128)S(1)}, f32[128,2048]{1,0:T(8,128)}, u32[]{:S(2)}) copy-start(f32[128,2048]{1,0:T(8,128)} %get-tuple-element.39) | copy-start | bytes 3145732
  209.9 89.4 %collective-permute-start.12 = (f32[384,2048]{1,0:T(8,128)S(1)}, f32[384,2048]{1,0:T(8,128)S(1)}, u32[]{:S(2)}, u32[]{:S(2)}) collective-permute-start(f32[384,2048]{1,0:T(8,128)S(1)} %add_add_fusion), channel_id=1, source_target_pairs={{0,4},{1,3},{2,6},{3,1},{4,0},{5,7},{6,2},{7,5}} | collective-permute-start | bytes 9437192 | tf_op jit(solution)/shard_map/ppermute | solution.py:307
  211.8 3.4 %collective-permute-start.13 = (f32[128,2048]{1,0:T(8,128)S(1)}, f32[128,2048]{1,0:T(8,128)S(1)}, u32[]{:S(2)}, u32[]{:S(2)}) collective-permute-start(f32[128,2048]{1,0:T(8,128)S(1)} %copy-done.13), channel_id=1, source_target_pairs={{0,1},{1,0},{2,3},{3,2},{4,5},{5,4},{6,7},{7,6}} | collective-permute-start | bytes 3145736 | tf_op jit(solution)/shard_map/ppermute | solution.py:303
  211.8 76.2 %copy-start.14 = (f32[128,2048]{1,0:T(8,128)S(1)}, f32[128,2048]{1,0:T(8,128)}, u32[]{:S(2)}) copy-start(f32[128,2048]{1,0:T(8,128)} %get-tuple-element.36) | copy-start | bytes 3145732
  211.8 76.2 %copy-start.11 = (f32[128,2048]{1,0:T(8,128)S(1)}, f32[128,2048]{1,0:T(8,128)}, u32[]{:S(2)}) copy-start(f32[128,2048]{1,0:T(8,128)} %get-tuple-element.49) | copy-start | bytes 3145732
  213.3 74.7 %collective-permute-start.15 = (f32[128,2048]{1,0:T(8,128)S(1)}, f32[128,2048]{1,0:T(8,128)S(1)}, u32[]{:S(2)}, u32[]{:S(2)}) collective-permute-start(f32[128,2048]{1,0:T(8,128)S(1)} %add.30), channel_id=1, source_target_pairs={{0,2},{1,5},{2,0},{3,7},{4,6},{5,1},{6,4},{7,3}} | collective-permute-start | bytes 3145736 | tf_op jit(solution)/shard_map/ppermute | solution.py:307
  215.1 84.1 %collective-permute-start.4 = (f32[128,2048]{1,0:T(8,128)S(1)}, f32[128,2048]{1,0:T(8,128)S(1)}, u32[]{:S(2)}, u32[]{:S(2)}) collective-permute-start(f32[128,2048]{1,0:T(8,128)S(1)} %add.24), channel_id=1, source_target_pairs={{0,2},{1,5},{2,0},{3,7},{4,6},{5,1},{6,4},{7,3}} | collective-permute-start | bytes 3145736 | tf_op jit(solution)/shard_map/ppermute | solution.py:307
  288.0 11.2 %collective-permute-start.2 = (f32[128,2048]{1,0:T(8,128)S(1)}, f32[128,2048]{1,0:T(8,128)S(1)}, u32[]{:S(2)}, u32[]{:S(2)}) collective-permute-start(f32[128,2048]{1,0:T(8,128)S(1)} %copy-done.14), channel_id=1, source_target_pairs={{0,1},{1,0},{2,3},{3,2},{4,5},{5,4},{6,7},{7,6}} | collective-permute-start | bytes 3145736 | tf_op jit(solution)/shard_map/ppermute | solution.py:303
  299.2 3.9 %copy-start.9 = (f32[128,2048]{1,0:T(8,128)}, f32[128,2048]{1,0:T(8,128)S(1)}, u32[]{:S(2)}) copy-start(f32[128,2048]{1,0:T(8,128)S(1)} %collective-permute-done.4.n0_ref) | copy-start | bytes 3145732
  299.2 15.1 %collective-permute-start.16 = (f32[128,2048]{1,0:T(8,128)}, f32[128,2048]{1,0:T(8,128)}, u32[]{:S(2)}, u32[]{:S(2)}) collective-permute-start(f32[128,2048]{1,0:T(8,128)} %add_add_fusion.1), channel_id=1, source_target_pairs={{0,4},{1,3},{2,6},{3,1},{4,0},{5,7},{6,2},{7,5}} | collective-permute-start | bytes 3145736 | tf_op jit(solution)/shard_map/ppermute | solution.py:307
  299.2 4.2 %copy-start.10 = (f32[128,2048]{1,0:T(8,128)}, f32[128,2048]{1,0:T(8,128)S(1)}, u32[]{:S(2)}) copy-start(f32[128,2048]{1,0:T(8,128)S(1)} %collective-permute-done.2.o1_ref) | copy-start | bytes 3145732
  299.3 1.7 copy-start.4
  299.3 2.7 copy-start.5
  301.0 2.1 copy-start.6

commit v11 on v10

--- a/solution.py
+++ b/solution.py
@@ -118,10 +118,10 @@
 
 
 def _expert_kernel(
-    turns, rows0, sizes, cuts, table_ref, pos_ref, xm_hbm, xo_hbm, w1_hbm, w3_hbm, w2_hbm, *refs
+    turns, rows0, sizes, cuts, inits, table_ref, pos_ref, xm_hbm, xo_hbm, w1_hbm, w3_hbm, w2_hbm, *refs
 ):
-    outs = refs[:4]
-    acc, xbuf, *ws, w2s, wsem, osem, xsem = refs[4:]
+    init_hbm, outs = refs[:inits], refs[inits : inits + 4]
+    acc, xbuf, *ws, w2s, wsem, osem, xsem = refs[inits + 4 :]
     w1s, w3s = ws[: len(ws) // 2], ws[len(ws) // 2 :]
     e_loc, d, _ = w1_hbm.shape
     _, rows, _ = acc.shape
@@ -187,7 +187,13 @@
     for chunk in chunks:
         for c in chunk(0):
             c.start()
-    acc[...] = jnp.zeros_like(acc)
+    row = 0
+    for i, ref in enumerate(init_hbm):
+        tokens.append(pltpu.make_async_copy(ref, acc.at[0, pl.ds(row, ref.shape[0])], xsem.at[2 + i]))
+        tokens[-1].start()
+        row += ref.shape[0]
+    for s in range(1 if inits else 0, 2):
+        acc[s] = jnp.zeros(acc.shape[1:], F32)
     for c in tokens:
         c.wait()
 
@@ -268,12 +274,11 @@
     return total
 
 
-def _combine_kernel(hit_ref, gate_ref, k0_ref, k1_ref, o0_ref, o1_ref, n0_ref, n1_ref, f0_ref, total_ref, sum_ref):
+def _combine_kernel(hit_ref, gate_ref, k0_ref, k1_ref, o0_ref, o1_ref, f0_ref, total_ref, sum_ref):
     most = f0_ref.shape[0]
-    near = jnp.concatenate([n0_ref[...], n1_ref[...]], axis=0)
-    y = (k0_ref[...] + o0_ref[...] + near[:most] + f0_ref[...]).astype(BF16)
+    y = (k0_ref[...] + o0_ref[...] + f0_ref[...]).astype(BF16)
     total_ref[...] = _weigh([hit_ref[j, :, :most] for j in range(hit_ref.shape[0])], gate_ref, y)
-    sum_ref[...] = k1_ref[...] + o1_ref[...] + near[most:]
+    sum_ref[...] = k1_ref[...] + o1_ref[...]
 
 
 def _close_kernel(hit_ref, gate_ref, total_ref, sum_ref, f1_ref, out_ref):
@@ -336,11 +341,11 @@
 
         sizes = (64, 152)
 
-        def stage(turns, mine, other, split, rows0=(0, 0)):
+        def stage(turns, mine, other, split, rows0=(0, 0), init=()):
             return pl.pallas_call(
-                functools.partial(_expert_kernel, turns, rows0, sizes, cuts),
+                functools.partial(_expert_kernel, turns, rows0, sizes, cuts, len(init)),
                 out_shape=[jax.ShapeDtypeStruct((n, d), F32) for n in split * 2],
-                in_specs=[smem, vmem] + [anym] * 5,
+                in_specs=[smem, vmem] + [anym] * (5 + len(init)),
                 out_specs=[anym] * 4,
                 scratch_shapes=[
                     pltpu.VMEM((2, rows, d), F32),
@@ -349,13 +354,13 @@
                     pltpu.VMEM((2, 2, ff, d // 2), BF16),
                     pltpu.SemaphoreType.DMA((2, 2 * len(widths) + 2)),
                     pltpu.SemaphoreType.DMA((2, 4)),
-                    pltpu.SemaphoreType.DMA((2,)),
+                    pltpu.SemaphoreType.DMA((2 + len(init),)),
                 ],
                 compiler_params=pltpu.CompilerParams(vmem_limit_bytes=VMEM_BYTES),
                 cost_estimate=pl.CostEstimate(
                     flops=6 * rows * d * ff, bytes_accessed=6 * e_loc * d * ff + 8 * rows * d, transcendentals=0
                 ),
-            )(groups, pos, mine, other, w1, w3, w2)
+            )(groups, pos, mine, other, w1, w3, w2, *init)
 
         def merge(parts, *more):
             sums = []
@@ -374,7 +379,7 @@
         via = [shift(a, out) for a in diag]
         far = merge(stage(back, rest, rest_other, late, (t_loc, t_loc)), via)
         far = [shift(a, back) for a in far]
-        own = stage((0, 0), x, own_x, late)
+        own = stage((0, 0), x, own_x, late, init=near)
         other = [swap(own[q]) for q in range(2)]
 
         def by_columns(steps):
@@ -387,12 +392,12 @@
         total, last = pl.pallas_call(
             _combine_kernel,
             out_shape=[jax.ShapeDtypeStruct((t_loc, d), F32), jax.ShapeDtypeStruct((late[1], d), F32)],
-            in_specs=[vmem, vmem] + [part(n) for n in late * 2 + early + late[:1]],
+            in_specs=[vmem, vmem] + [part(n) for n in late * 2 + late[:1]],
             out_specs=[part(t_loc), part(late[1])],
             compiler_params=pltpu.CompilerParams(vmem_limit_bytes=VMEM_BYTES),
             name="combine",
             **grid,
-        )(hit, gate, *own[2:], *other, *near, far[0])
+        )(hit, gate, *own[2:], *other, far[0])
         grid, part = by_columns(2)
         return pl.pallas_call(
             _close_kernel,

time: 318 us -> 315 us (level)
  local copies, waits for them, and re-layouts: 8.05 us -> 1 us
    unnamed x30 -> x18, local copies, waits for them, and re-layouts: 8.05 us -> 1 us
  transfers between devices with their start and end apart: 17 -> 17, of which waited for: 6 -> 8; matrix products, arithmetic and copies ran while one was open for 5% -> 6% of each run, Pallas kernels for 32% -> 41%
where the time goes in v11:
time: 315 us; the launch traced here: 314 us
  Pallas kernels  153 us (49%)
  waiting for transfers between devices  115 us (37%)
  starting transfers between devices  27.2 us (9%)
  other arithmetic  18 us (6%)
    pallas_call x4, Pallas kernels, stage(): pl.pallas_call(functools.partial(_expert_kernel, turns, rows0, sizes, cut...  121 us
    ppermute x7, waiting for transfers between devices, shift(): return lax.ppermute(a, ('tp', 'ep'), pairs)  111 us
    pallas_call x1, Pallas kernels, layer(): pl.pallas_call(functools.partial(_route_kernel, chips, out), out_shape=[j...  21.3 us
    ppermute x10, starting transfers between devices, swap(): return lax.ppermute(a, 'ep', [(0, 1), (1, 0)])  14.7 us
    ppermute x7, starting transfers between devices, shift(): return lax.ppermute(a, ('tp', 'ep'), pairs)  12.5 us
    add x4, other arithmetic, merge(): parts[2 + q] + other  12.1 us
    pallas_call x1, Pallas kernels, layer(): pl.pallas_call(_combine_kernel, out_shape=[jax.ShapeDtypeStruct((t_loc, d...  7.32 us
  transfers between devices with their start and end apart: 17, of which 8 were waited for; matrix products, arithmetic and copies ran while one was open for 6% of the time, Pallas kernels for 41%

profile of v11, /device:TPU:0, one launch (start us, length us, event | category | flops | bytes accessed | tf_op | source)
XLA Modules:
  0.0 314.2 jit_solution(5210890518264538979)
XLA Ops:
  0.0 21.3 %route.1 = (s32[8,8,256]{2,1,0:T(8,128)}, s32[8,128]{1,0:T(8,128)}, bf16[2,256,512]{2,1,0:T(8,128)(2,1)}, f32[256,8]{1,0:T(8,128)}, bf16[512,2048]{1,0:T(8,128)(2,1)}, /*index=5*/bf16[256,2048]{1,0:T(8,128)(2,1)}) custom-call(s32[2,256]{1,0:T(2,128)} %bitcast.2, f32[2,256]{1,0:T(2,128)} %bitcast.3, s32[8]{0:T(128)} %cap_ref.1, bf16[256,2048]{1,0:T(8,128)(2,1)} %xm_hbm.1), custom_call_target="tpu_custom_call" | custom-call | tf_op jit(solution)/shard_map/route/pallas_call | solution.py:316
  21.3 1.2 collective-permute-start.7
  22.6 25.1 %collective-permute-done.7.xm_hbm = bf16[512,2048]{1,0:T(8,128)(2,1)} collective-permute-done((bf16[512,2048]{1,0:T(8,128)(2,1)}, bf16[512,2048]{1,0:T(8,128)(2,1)}, u32[]{:S(2)}, u32[]{:S(2)}) %collective-permute-start.7) | collective-permute-done | bytes 2097184 | tf_op jit(solution)/shard_map/ppermute | solution.py:312
  47.7 0.0 collective-permute-start.8
  47.7 31.2 %shard_map.73 = (f32[128,2048]{1,0:T(8,128)}, f32[384,2048]{1,0:T(8,128)}, f32[128,2048]{1,0:T(8,128)}, f32[384,2048]{1,0:T(8,128)}) custom-call(s32[8,128]{1,0:T(8,128)} %get-tuple-element.31.table_ref, s32[8,8,256]{2,1,0:T(8,128)} %get-tuple-element.32.pos_ref, bf16[512,2048]{1,0:T(8,128)(2,1)} %get-tuple-element.33.xm_hbm, ...), custom_call_target="tpu_custom_call" | custom-call | flops 8858370048 | bytes 77594624 | tf_op jit(solution)/shard_map/pallas_call | solution.py:345
  78.9 0.5 collective-permute-start.3
  79.4 0.0 collective-permute-done.8.xo_hbm
  79.4 27.7 %shard_map.76 = (f32[384,2048]{1,0:T(8,128)}, f32[128,2048]{1,0:T(8,128)}, f32[384,2048]{1,0:T(8,128)}, f32[128,2048]{1,0:T(8,128)}) custom-call(s32[8,128]{1,0:T(8,128)} %get-tuple-element.31.table_ref, s32[8,8,256]{2,1,0:T(8,128)} %get-tuple-element.32.pos_ref, bf16[512,2048]{1,0:T(8,128)(2,1)} %collective-permute-done.7.xm_hbm, ...), custom_call_target="tpu_custom_call" | custom-call | flops 8858370048 | bytes 77594624 | tf_op jit(solution)/shard_map/pallas_call | solution.py:345
  107.1 6.2 %collective-permute-start.10 = (f32[384,2048]{1,0:T(8,128)}, f32[384,2048]{1,0:T(8,128)}, u32[]{:S(2)}, u32[]{:S(2)}) collective-permute-start(f32[384,2048]{1,0:T(8,128)} %get-tuple-element.46), channel_id=1, source_target_pairs={{0,1},{1,0},{2,3},{3,2},{4,5},{5,4},{6,7},{7,6}} | collective-permute-start | bytes 9437192 | tf_op jit(solution)/shard_map/ppermute | solution.py:308
  113.3 0.0 collective-permute-done.3
  113.3 5.2 %add.25 = f32[384,2048]{1,0:T(8,128)} add(f32[384,2048]{1,0:T(8,128)} %get-tuple-element.37, f32[384,2048]{1,0:T(8,128)} %collective-permute-done.3) | non-fusion elementwise | flops 786432 | bytes 9437184 | tf_op jit(solution)/shard_map/add | solution.py:369
  118.6 4.8 %collective-permute-start.4 = (f32[384,2048]{1,0:T(8,128)}, f32[384,2048]{1,0:T(8,128)}, u32[]{:S(2)}, u32[]{:S(2)}) collective-permute-start(f32[384,2048]{1,0:T(8,128)} %add.25), channel_id=1, source_target_pairs={{0,2},{1,5},{2,0},{3,7},{4,6},{5,1},{6,4},{7,3}} | collective-permute-start | bytes 9437192 | tf_op jit(solution)/shard_map/ppermute | solution.py:312
  123.3 26.9 %shard_map.75 = (f32[384,2048]{1,0:T(8,128)}, f32[128,2048]{1,0:T(8,128)}, f32[384,2048]{1,0:T(8,128)}, f32[128,2048]{1,0:T(8,128)}) custom-call(s32[8,128]{1,0:T(8,128)} %get-tuple-element.31.table_ref, s32[8,8,256]{2,1,0:T(8,128)} %get-tuple-element.32.pos_ref, bf16[512,2048]{1,0:T(8,128)(2,1)} %collective-permute-done.7.xm_hbm, ...), custom_call_target="tpu_custom_call" | custom-call | flops 8858370048 | bytes 77594624 | tf_op jit(solution)/shard_map/pallas_call | solution.py:345
  150.2 4.7 %collective-permute-start.9 = (f32[384,2048]{1,0:T(8,128)}, f32[384,2048]{1,0:T(8,128)}, u32[]{:S(2)}, u32[]{:S(2)}) collective-permute-start(f32[384,2048]{1,0:T(8,128)} %get-tuple-element.44), channel_id=1, source_target_pairs={{0,1},{1,0},{2,3},{3,2},{4,5},{5,4},{6,7},{7,6}} | collective-permute-start | bytes 9437192 | tf_op jit(solution)/shard_map/ppermute | solution.py:308
  154.9 0.0 collective-permute-done.10
  154.9 5.4 %add.27 = f32[384,2048]{1,0:T(8,128)} add(f32[384,2048]{1,0:T(8,128)} %get-tuple-element.45, f32[384,2048]{1,0:T(8,128)} %collective-permute-done.10) | non-fusion elementwise | flops 786432 | bytes 9437184 | tf_op jit(solution)/shard_map/add | solution.py:369
  160.3 3.6 %collective-permute-start.11 = (f32[384,2048]{1,0:T(8,128)}, f32[384,2048]{1,0:T(8,128)}, u32[]{:S(2)}, u32[]{:S(2)}) collective-permute-start(f32[384,2048]{1,0:T(8,128)} %add.27), channel_id=1, source_target_pairs={{0,2},{1,5},{2,0},{3,7},{4,6},{5,1},{6,4},{7,3}} | collective-permute-start | bytes 9437192 | tf_op jit(solution)/shard_map/ppermute | solution.py:312
  163.9 2.8 collective-permute-start.1
  166.7 0.0 collective-permute-start
  166.8 2.3 collective-permute-done.1
  169.0 0.1 add.24
  169.1 0.0 collective-permute-start.2
  169.2 1.3 collective-permute-done.xo_hbm
  170.5 1.0 copy-done.1
  171.5 0.4 collective-permute-start.14
  171.9 38.8 %collective-permute-done.2.refs_0_ = f32[128,2048]{1,0:T(8,128)} collective-permute-done((f32[128,2048]{1,0:T(8,128)S(1)}, f32[128,2048]{1,0:T(8,128)}, u32[]{:S(2)}, u32[]{:S(2)}) %collective-permute-start.2) | collective-permute-done | bytes 1048608 | tf_op jit(solution)/shard_map/ppermute | solution.py:312
  210.7 0.0 collective-permute-done.4.refs_1_
  210.7 35.1 %shard_map.74 = (f32[384,2048]{1,0:T(8,128)}, f32[128,2048]{1,0:T(8,128)}, f32[384,2048]{1,0:T(8,128)}, f32[128,2048]{1,0:T(8,128)}) custom-call(s32[8,128]{1,0:T(8,128)} %get-tuple-element.31.table_ref, s32[8,8,256]{2,1,0:T(8,128)} %get-tuple-element.32.pos_ref, bf16[256,2048]{1,0:T(8,128)(2,1)} %xm_hbm.1, bf16[256,2048]{1,0:T(8,128)(2,1)} %copy-done.1, ...), custom_call_target="tpu_custom_call" | custom-call | flops 8858370048 | bytes 77594624 | tf_op jit(solution)/shard_map/pallas_call | solution.py:345
  245.8 0.0 collective-permute-start.5
  245.9 0.0 collective-permute-done.9
  245.9 0.0 collective-permute-done.11
  245.9 4.8 %add_add_fusion = f32[384,2048]{1,0:T(8,128)S(1)} fusion(f32[384,2048]{1,0:T(8,128)} %collective-permute-done.11, f32[384,2048]{1,0:T(8,128)} %get-tuple-element.43, f32[384,2048]{1,0:T(8,128)} %collective-permute-done.9), kind=kLoop, calls=%fused_computation | loop fusion | flops 1572864 | bytes 12582912 | tf_op jit(solution)/shard_map/add | solution.py:369
  250.7 1.4 collective-permute-start.12
  252.2 0.0 collective-permute-start.13
  252.2 0.0 collective-permute-done.14
  252.2 1.4 add.30
  253.6 0.8 collective-permute-start.15
  254.4 0.0 collective-permute-start.6
  254.4 0.4 collective-permute-done.13
  254.9 24.8 %collective-permute-done.15 = f32[128,2048]{1,0:T(8,128)S(1)} collective-permute-done((f32[128,2048]{1,0:T(8,128)S(1)}, f32[128,2048]{1,0:T(8,128)S(1)}, u32[]{:S(2)}, u32[]{:S(2)}) %collective-permute-start.15) | collective-permute-done | bytes 1048608 | tf_op jit(solution)/shard_map/ppermute | solution.py:312
  279.6 1.2 add_add_fusion.1
  280.8 0.6 collective-permute-start.16
  281.4 0.0 collective-permute-done.6.o1_ref
  281.4 0.0 collective-permute-done.5.o0_ref
  281.4 18.0 %collective-permute-done.12.f0_ref = f32[384,2048]{1,0:T(8,128)} collective-permute-done((f32[384,2048]{1,0:T(8,128)S(1)}, f32[384,2048]{1,0:T(8,128)}, u32[]{:S(2)}, u32[]{:S(2)}) %collective-permute-start.12) | collective-permute-done | bytes 3145760 | tf_op jit(solution)/shard_map/ppermute | solution.py:312
  299.4 7.3 %combine.1 = (f32[256,2048]{1,0:T(8,128)}, f32[128,2048]{1,0:T(8,128)}) custom-call(bf16[2,256,512]{2,1,0:T(8,128)(2,1)} %get-tuple-element.29.hit_ref, f32[256,8]{1,0:T(8,128)} %get-tuple-element.30.gate_ref, f32[384,2048]{1,0:T(8,128)} %get-tuple-element.39.k0_ref, f32[128,2048]{1,0:T(8,128)} %get-tuple-element.40.k1_ref, ...), custom_call_target="tpu_custom_call" | custom-call | tf_op jit(solution)/shard_map/combine/pallas_call | solution.py:392
  306.7 3.9 %collective-permute-done.16.f1_ref = f32[128,2048]{1,0:T(8,128)} collective-permute-done((f32[128,2048]{1,0:T(8,128)}, f32[128,2048]{1,0:T(8,128)}, u32[]{:S(2)}, u32[]{:S(2)}) %collective-permute-start.16) | collective-permute-done | bytes 1048608 | tf_op jit(solution)/shard_map/ppermute | solution.py:312
  310.6 3.6 %close.1 = bf16[256,2048]{1,0:T(8,128)(2,1)} custom-call(bf16[2,256,512]{2,1,0:T(8,128)(2,1)} %get-tuple-element.29.hit_ref, f32[256,8]{1,0:T(8,128)} %get-tuple-element.30.gate_ref, f32[256,2048]{1,0:T(8,128)} %get-tuple-element.47.total_ref, f32[128,2048]{1,0:T(8,128)} %get-tuple-element.48.sum_ref, f32[128,2048]{1,0:T(8,128)} %collective-permute-done.16.f1_ref), custom_call_target="tpu_custom_call" | custom-call | tf_op jit(solution)/shard_map/close/pallas_call | solution.py:402
  (17 shorter events, 0.0 us)
Async XLA Ops:
  21.3 26.4 %collective-permute-start.7 = (bf16[512,2048]{1,0:T(8,128)(2,1)}, bf16[512,2048]{1,0:T(8,128)(2,1)}, u32[]{:S(2)}, u32[]{:S(2)}) collective-permute-start(bf16[512,2048]{1,0:T(8,128)(2,1)} %get-tuple-element.33.xm_hbm), channel_id=1, source_target_pairs={{0,4},{1,3},{2,6},{3,1},{4,0},{5,7},{6,2},{7,5}} | collective-permute-start | bytes 6291464 | tf_op jit(solution)/shard_map/ppermute | solution.py:312
  47.7 31.7 %collective-permute-start.8 = (bf16[512,2048]{1,0:T(8,128)(2,1)}, bf16[512,2048]{1,0:T(8,128)(2,1)}, u32[]{:S(2)}, u32[]{:S(2)}) collective-permute-start(bf16[512,2048]{1,0:T(8,128)(2,1)} %collective-permute-done.7.xm_hbm), channel_id=1, source_target_pairs={{0,1},{1,0},{2,3},{3,2},{4,5},{5,4},{6,7},{7,6}} | collective-permute-start | bytes 6291464 | tf_op jit(solution)/shard_map/ppermute | solution.py:308
  78.9 34.4 %collective-permute-start.3 = (f32[384,2048]{1,0:T(8,128)}, f32[384,2048]{1,0:T(8,128)}, u32[]{:S(2)}, u32[]{:S(2)}) collective-permute-start(f32[384,2048]{1,0:T(8,128)} %get-tuple-element.38), channel_id=1, source_target_pairs={{0,1},{1,0},{2,3},{3,2},{4,5},{5,4},{6,7},{7,6}} | collective-permute-start | bytes 9437192 | tf_op jit(solution)/shard_map/ppermute | solution.py:308
  107.1 47.8 %collective-permute-start.10 = (f32[384,2048]{1,0:T(8,128)}, f32[384,2048]{1,0:T(8,128)}, u32[]{:S(2)}, u32[]{:S(2)}) collective-permute-start(f32[384,2048]{1,0:T(8,128)} %get-tuple-element.46), channel_id=1, source_target_pairs={{0,1},{1,0},{2,3},{3,2},{4,5},{5,4},{6,7},{7,6}} | collective-permute-start | bytes 9437192 | tf_op jit(solution)/shard_map/ppermute | solution.py:308
  118.6 92.1 %collective-permute-start.4 = (f32[384,2048]{1,0:T(8,128)}, f32[384,2048]{1,0:T(8,128)}, u32[]{:S(2)}, u32[]{:S(2)}) collective-permute-start(f32[384,2048]{1,0:T(8,128)} %add.25), channel_id=1, source_target_pairs={{0,2},{1,5},{2,0},{3,7},{4,6},{5,1},{6,4},{7,3}} | collective-permute-start | bytes 9437192 | tf_op jit(solution)/shard_map/ppermute | solution.py:312
  150.2 95.6 %collective-permute-start.9 = (f32[384,2048]{1,0:T(8,128)}, f32[384,2048]{1,0:T(8,128)}, u32[]{:S(2)}, u32[]{:S(2)}) collective-permute-start(f32[384,2048]{1,0:T(8,128)} %get-tuple-element.44), channel_id=1, source_target_pairs={{0,1},{1,0},{2,3},{3,2},{4,5},{5,4},{6,7},{7,6}} | collective-permute-start | bytes 9437192 | tf_op jit(solution)/shard_map/ppermute | solution.py:308
  154.9 9.0 %copy-start.8 = (f32[128,2048]{1,0:T(8,128)S(1)}, f32[128,2048]{1,0:T(8,128)}, u32[]{:S(2)}) copy-start(f32[128,2048]{1,0:T(8,128)} %get-tuple-element.36) | copy-start | bytes 3145732
  154.9 11.8 %copy-start = (bf16[256,2048]{1,0:T(8,128)(2,1)S(1)}, bf16[256,2048]{1,0:T(8,128)(2,1)}, u32[]{:S(2)}) copy-start(bf16[256,2048]{1,0:T(8,128)(2,1)} %xm_hbm.1) | copy-start | bytes 3145732
  154.9 14.1 %copy-start.3 = (f32[128,2048]{1,0:T(8,128)S(1)}, f32[128,2048]{1,0:T(8,128)}, u32[]{:S(2)}) copy-start(f32[128,2048]{1,0:T(8,128)} %get-tuple-element.35) | copy-start | bytes 3145732
  160.3 85.6 %collective-permute-start.11 = (f32[384,2048]{1,0:T(8,128)}, f32[384,2048]{1,0:T(8,128)}, u32[]{:S(2)}, u32[]{:S(2)}) collective-permute-start(f32[384,2048]{1,0:T(8,128)} %add.27), channel_id=1, source_target_pairs={{0,2},{1,5},{2,0},{3,7},{4,6},{5,1},{6,4},{7,3}} | collective-permute-start | bytes 9437192 | tf_op jit(solution)/shard_map/ppermute | solution.py:312
  163.9 5.1 %collective-permute-start.1 = (f32[128,2048]{1,0:T(8,128)S(1)}, f32[128,2048]{1,0:T(8,128)S(1)}, u32[]{:S(2)}, u32[]{:S(2)}) collective-permute-start(f32[128,2048]{1,0:T(8,128)S(1)} %copy-done.8), channel_id=1, source_target_pairs={{0,1},{1,0},{2,3},{3,2},{4,5},{5,4},{6,7},{7,6}} | collective-permute-start | bytes 3145736 | tf_op jit(solution)/shard_map/ppermute | solution.py:308
  166.7 3.8 %collective-permute-start = (bf16[256,2048]{1,0:T(8,128)(2,1)S(1)}, bf16[256,2048]{1,0:T(8,128)(2,1)S(1)}, u32[]{:S(2)}, u32[]{:S(2)}) collective-permute-start(bf16[256,2048]{1,0:T(8,128)(2,1)S(1)} %copy-done), channel_id=1, source_target_pairs={{0,1},{1,0},{2,3},{3,2},{4,5},{5,4},{6,7},{7,6}} | collective-permute-start | bytes 3145736 | tf_op jit(solution)/shard_map/ppermute | solution.py:308
  169.1 41.6 %collective-permute-start.2 = (f32[128,2048]{1,0:T(8,128)S(1)}, f32[128,2048]{1,0:T(8,128)}, u32[]{:S(2)}, u32[]{:S(2)}) collective-permute-start(f32[128,2048]{1,0:T(8,128)S(1)} %add.24), channel_id=1, source_target_pairs={{0,2},{1,5},{2,0},{3,7},{4,6},{5,1},{6,4},{7,3}} | collective-permute-start | bytes 3145736 | tf_op jit(solution)/shard_map/ppermute | solution.py:312
  170.5 1.0 copy-start.1
  171.5 80.7 %collective-permute-start.14 = (f32[128,2048]{1,0:T(8,128)}, f32[128,2048]{1,0:T(8,128)}, u32[]{:S(2)}, u32[]{:S(2)}) collective-permute-start(f32[128,2048]{1,0:T(8,128)} %get-tuple-element.52), channel_id=1, source_target_pairs={{0,1},{1,0},{2,3},{3,2},{4,5},{5,4},{6,7},{7,6}} | collective-permute-start | bytes 3145736 | tf_op jit(solution)/shard_map/ppermute | solution.py:308
  245.8 35.6 %collective-permute-start.5 = (f32[384,2048]{1,0:T(8,128)}, f32[384,2048]{1,0:T(8,128)}, u32[]{:S(2)}, u32[]{:S(2)}) collective-permute-start(f32[384,2048]{1,0:T(8,128)} %get-tuple-element.41), channel_id=1, source_target_pairs={{0,1},{1,0},{2,3},{3,2},{4,5},{5,4},{6,7},{7,6}} | collective-permute-start | bytes 9437192 | tf_op jit(solution)/shard_map/ppermute | solution.py:308
  245.9 6.3 %copy-start.6 = (f32[128,2048]{1,0:T(8,128)S(1)}, f32[128,2048]{1,0:T(8,128)}, u32[]{:S(2)}) copy-start(f32[128,2048]{1,0:T(8,128)} %get-tuple-element.50) | copy-start | bytes 3145732
  245.9 6.3 %copy-start.2 = (f32[128,2048]{1,0:T(8,128)S(1)}, f32[128,2048]{1,0:T(8,128)}, u32[]{:S(2)}) copy-start(f32[128,2048]{1,0:T(8,128)} %get-tuple-element.51) | copy-start | bytes 3145732
  250.7 3.7 %copy-start.7 = (f32[128,2048]{1,0:T(8,128)S(1)}, f32[128,2048]{1,0:T(8,128)}, u32[]{:S(2)}) copy-start(f32[128,2048]{1,0:T(8,128)} %get-tuple-element.42) | copy-start | bytes 3145732
  250.7 28.9 %copy-start.5 = (f32[128,2048]{1,0:T(8,128)S(1)}, f32[128,2048]{1,0:T(8,128)}, u32[]{:S(2)}) copy-start(f32[128,2048]{1,0:T(8,128)} %get-tuple-element.49) | copy-start | bytes 3145732
  250.7 48.6 %collective-permute-start.12 = (f32[384,2048]{1,0:T(8,128)S(1)}, f32[384,2048]{1,0:T(8,128)}, u32[]{:S(2)}, u32[]{:S(2)}) collective-permute-start(f32[384,2048]{1,0:T(8,128)S(1)} %add_add_fusion), channel_id=1, source_target_pairs={{0,4},{1,3},{2,6},{3,1},{4,0},{5,7},{6,2},{7,5}} | collective-permute-start | bytes 9437192 | tf_op jit(solution)/shard_map/ppermute | solution.py:312
  252.2 2.7 collective-permute-start.13
  253.6 26.1 %collective-permute-start.15 = (f32[128,2048]{1,0:T(8,128)S(1)}, f32[128,2048]{1,0:T(8,128)S(1)}, u32[]{:S(2)}, u32[]{:S(2)}) collective-permute-start(f32[128,2048]{1,0:T(8,128)S(1)} %add.30), channel_id=1, source_target_pairs={{0,2},{1,5},{2,0},{3,7},{4,6},{5,1},{6,4},{7,3}} | collective-permute-start | bytes 3145736 | tf_op jit(solution)/shard_map/ppermute | solution.py:312
  254.4 27.0 %collective-permute-start.6 = (f32[128,2048]{1,0:T(8,128)S(1)}, f32[128,2048]{1,0:T(8,128)S(1)}, u32[]{:S(2)}, u32[]{:S(2)}) collective-permute-start(f32[128,2048]{1,0:T(8,128)S(1)} %copy-done.7), channel_id=1, source_target_pairs={{0,1},{1,0},{2,3},{3,2},{4,5},{5,4},{6,7},{7,6}} | collective-permute-start | bytes 3145736 | tf_op jit(solution)/shard_map/ppermute | solution.py:308
  280.8 29.8 %collective-permute-start.16 = (f32[128,2048]{1,0:T(8,128)}, f32[128,2048]{1,0:T(8,128)}, u32[]{:S(2)}, u32[]{:S(2)}) collective-permute-start(f32[128,2048]{1,0:T(8,128)} %add_add_fusion.1), channel_id=1, source_target_pairs={{0,4},{1,3},{2,6},{3,1},{4,0},{5,7},{6,2},{7,5}} | collective-permute-start | bytes 3145736 | tf_op jit(solution)/shard_map/ppermute | solution.py:312
  281.4 18.0 %copy-start.4 = (f32[128,2048]{1,0:T(8,128)}, f32[128,2048]{1,0:T(8,128)S(1)}, u32[]{:S(2)}) copy-start(f32[128,2048]{1,0:T(8,128)S(1)} %collective-permute-done.6.o1_ref) | copy-start | bytes 3145732

commit v12 on v11

--- a/solution.py
+++ b/solution.py
@@ -65,10 +65,9 @@
     ]
     own = pltpu.make_async_copy(held, pair_ref.at[pl.ds(t, t)], lsem.at[1])
     load.wait()
-    arrive[0].start()
     for c in copies:
         c.start()
-    for c in arrive[1:]:
+    for c in arrive:
         c.start()
     own.start()
     ids_all[pl.ds(here, 1)] = idx_ref[...][None]
@@ -158,6 +157,14 @@
             c.wait()
         if i == 0:
 
+            @pl.when(e == 0)
+            def _():
+                for later in chunks[len(w1s) :]:
+                    for c in later(0):
+                        c.start()
+
+        if i == 1:
+
             @pl.when((e == 0) & (e_loc > 1))
             def _():
                 for later in chunks:
@@ -184,9 +191,8 @@
     ]
     for c in tokens:
         c.start()
-    for chunk in chunks:
-        for c in chunk(0):
-            c.start()
+    for c in chunks[0](0):
+        c.start()
     row = 0
     for i, ref in enumerate(init_hbm):
         tokens.append(pltpu.make_async_copy(ref, acc.at[0, pl.ds(row, ref.shape[0])], xsem.at[2 + i]))
@@ -194,7 +200,12 @@
         row += ref.shape[0]
     for s in range(1 if inits else 0, 2):
         acc[s] = jnp.zeros(acc.shape[1:], F32)
-    for c in tokens:
+    for c in tokens[:2]:
+        c.wait()
+    for chunk in chunks[1 : len(w1s)]:
+        for c in chunk(0):
+            c.start()
+    for c in tokens[2:]:
         c.wait()
 
     def step(e, carry):
@@ -209,12 +220,10 @@
                 for c in out_copies(0):
                     c.start()
 
-        def run(m):
-            tiles = (need + m - 1) // m
-
+        def run(m, tiles, skip, opening, closing):
             def once(i, carry):
-                opens, closes = i == 0, i == tiles - 1
-                starts = [o // 8 * 8 + i * m for o in offs]
+                opens, closes = opening & (i == 0), closing & (i == tiles - 1)
+                starts = [o // 8 * 8 + skip + i * m for o in offs]
                 bases = [pl.multiple_of(jnp.minimum(b, rows - m), 8) for b in starts]
                 parts = []
                 for s in range(2):
@@ -255,8 +264,16 @@
             last(0)
 
         small, large = sizes
-        pl.when((need > 0) & (need <= small))(functools.partial(run, small))
-        pl.when(need > small)(functools.partial(run, large))
+
+        @pl.when(need > small)
+        def _():
+            run(large, 1, 0, need > 0, need <= large)
+
+        @pl.when((need > 0) & ((need <= small) | (need > large)))
+        def _():
+            skip = jnp.where(need <= small, 0, large)
+            run(small, (need - skip + small - 1) // small, skip, need <= small, need > 0)
+
         return carry
 
     lax.fori_loop(0, e_loc, step, 0)
@@ -282,9 +299,8 @@
 
 
 def _close_kernel(hit_ref, gate_ref, total_ref, sum_ref, f1_ref, out_ref):
-    most = hit_ref.shape[2] - f1_ref.shape[0]
     y = (sum_ref[...] + f1_ref[...]).astype(BF16)
-    hit = [hit_ref[j, :, most:] for j in range(hit_ref.shape[0])]
+    hit = [hit_ref[j] for j in range(hit_ref.shape[0])]
     out_ref[...] = _weigh(hit, gate_ref, y, total_ref[...]).astype(out_ref.dtype)
 
 
@@ -312,7 +328,7 @@
             return lax.ppermute(a, ("tp", "ep"), pairs)
 
         out, back = (1, 2), (2, 1)
-        pieces = 2
+        pieces = 4
         pos, groups, hit, gate, pair, x_near = pl.pallas_call(
             functools.partial(_route_kernel, chips, out),
             out_shape=[
@@ -402,7 +418,8 @@
         return pl.pallas_call(
             _close_kernel,
             out_shape=jax.ShapeDtypeStruct((t_loc, d), BF16),
-            in_specs=[vmem, vmem] + [part(n) for n in (t_loc, late[1], late[1])],
+            in_specs=[pl.BlockSpec((top, t_loc, late[1]), lambda i: (0, 0, late[0] // late[1])), vmem]
+            + [part(n) for n in (t_loc, late[1], late[1])],
             out_specs=part(t_loc),
             name="close",
             **grid,

time: 315 us -> 310 us (0.984)
    ppermute x7, starting transfers between devices: 12.5 us -> 7.45 us  [shift(): return lax.ppermute(a, ('tp', 'ep'), pairs)]
  transfers between devices with their start and end apart: 17 -> 17, of which waited for: 8 -> 7; matrix products, arithmetic and copies ran while one was open for 6% -> 6% of each run, Pallas kernels for 41% -> 41%
where the time goes in v12:
time: 310 us; the launch traced here: 309 us
  Pallas kernels  151 us (49%)
  waiting for transfers between devices  114 us (37%)
  starting transfers between devices  24.8 us (8%)
  other arithmetic  18.1 us (6%)
    pallas_call x4, Pallas kernels, stage(): pl.pallas_call(functools.partial(_expert_kernel, turns, rows0, sizes, cut...  120 us
    ppermute x7, waiting for transfers between devices, shift(): return lax.ppermute(a, ('tp', 'ep'), pairs)  110 us
    pallas_call x1, Pallas kernels, layer(): pl.pallas_call(functools.partial(_route_kernel, chips, out), out_shape=[j...  21 us
    ppermute x10, starting transfers between devices, swap(): return lax.ppermute(a, 'ep', [(0, 1), (1, 0)])  17.3 us
    add x4, other arithmetic, merge(): parts[2 + q] + other  12.1 us
    ppermute x7, starting transfers between devices, shift(): return lax.ppermute(a, ('tp', 'ep'), pairs)  7.45 us
    pallas_call x1, Pallas kernels, layer(): pl.pallas_call(_combine_kernel, out_shape=[jax.ShapeDtypeStruct((t_loc, d...  7.32 us
  transfers between devices with their start and end apart: 17, of which 7 were waited for; matrix products, arithmetic and copies ran while one was open for 6% of the time, Pallas kernels for 41%

profile of v12, /device:TPU:0, one launch (start us, length us, event | category | flops | bytes accessed | tf_op | source)
XLA Modules:
  0.0 309.4 jit_solution(6129112359340870653)
XLA Ops:
  0.0 21.0 %route.1 = (s32[8,8,256]{2,1,0:T(8,128)}, s32[8,128]{1,0:T(8,128)}, bf16[2,256,512]{2,1,0:T(8,128)(2,1)}, f32[256,8]{1,0:T(8,128)}, bf16[512,2048]{1,0:T(8,128)(2,1)}, /*index=5*/bf16[256,2048]{1,0:T(8,128)(2,1)}) custom-call(s32[2,256]{1,0:T(2,128)} %bitcast.2, f32[2,256]{1,0:T(2,128)} %bitcast.3, s32[8]{0:T(128)} %cap_ref.1, bf16[256,2048]{1,0:T(8,128)(2,1)} %xm_hbm.1), custom_call_target="tpu_custom_call" | custom-call | tf_op jit(solution)/shard_map/route/pallas_call | solution.py:332
  21.0 1.2 collective-permute-start.7
  22.3 25.1 %collective-permute-done.7.xm_hbm = bf16[512,2048]{1,0:T(8,128)(2,1)} collective-permute-done((bf16[512,2048]{1,0:T(8,128)(2,1)}, bf16[512,2048]{1,0:T(8,128)(2,1)}, u32[]{:S(2)}, u32[]{:S(2)}) %collective-permute-start.7) | collective-permute-done | bytes 2097184 | tf_op jit(solution)/shard_map/ppermute | solution.py:328
  47.4 0.0 collective-permute-start.8
  47.4 31.3 %shard_map.73 = (f32[128,2048]{1,0:T(8,128)}, f32[384,2048]{1,0:T(8,128)}, f32[128,2048]{1,0:T(8,128)}, f32[384,2048]{1,0:T(8,128)}) custom-call(s32[8,128]{1,0:T(8,128)} %get-tuple-element.31.table_ref, s32[8,8,256]{2,1,0:T(8,128)} %get-tuple-element.32.pos_ref, bf16[512,2048]{1,0:T(8,128)(2,1)} %get-tuple-element.33.xm_hbm, ...), custom_call_target="tpu_custom_call" | custom-call | flops 8858370048 | bytes 77594624 | tf_op jit(solution)/shard_map/pallas_call | solution.py:361
  78.8 0.0 collective-permute-start.3
  78.8 0.0 collective-permute-done.8.xo_hbm
  78.8 26.6 %shard_map.76 = (f32[384,2048]{1,0:T(8,128)}, f32[128,2048]{1,0:T(8,128)}, f32[384,2048]{1,0:T(8,128)}, f32[128,2048]{1,0:T(8,128)}) custom-call(s32[8,128]{1,0:T(8,128)} %get-tuple-element.31.table_ref, s32[8,8,256]{2,1,0:T(8,128)} %get-tuple-element.32.pos_ref, bf16[512,2048]{1,0:T(8,128)(2,1)} %collective-permute-done.7.xm_hbm, ...), custom_call_target="tpu_custom_call" | custom-call | flops 8858370048 | bytes 77594624 | tf_op jit(solution)/shard_map/pallas_call | solution.py:361
  105.5 8.0 %collective-permute-start.10 = (f32[384,2048]{1,0:T(8,128)}, f32[384,2048]{1,0:T(8,128)}, u32[]{:S(2)}, u32[]{:S(2)}) collective-permute-start(f32[384,2048]{1,0:T(8,128)} %get-tuple-element.46), channel_id=1, source_target_pairs={{0,1},{1,0},{2,3},{3,2},{4,5},{5,4},{6,7},{7,6}} | collective-permute-start | bytes 9437192 | tf_op jit(solution)/shard_map/ppermute | solution.py:324
  113.4 0.0 collective-permute-done.3
  113.4 5.2 %add.25 = f32[384,2048]{1,0:T(8,128)} add(f32[384,2048]{1,0:T(8,128)} %get-tuple-element.37, f32[384,2048]{1,0:T(8,128)} %collective-permute-done.3) | non-fusion elementwise | flops 786432 | bytes 9437184 | tf_op jit(solution)/shard_map/add | solution.py:385
  118.7 0.0 collective-permute-start.4
  118.7 26.6 %shard_map.75 = (f32[384,2048]{1,0:T(8,128)}, f32[128,2048]{1,0:T(8,128)}, f32[384,2048]{1,0:T(8,128)}, f32[128,2048]{1,0:T(8,128)}) custom-call(s32[8,128]{1,0:T(8,128)} %get-tuple-element.31.table_ref, s32[8,8,256]{2,1,0:T(8,128)} %get-tuple-element.32.pos_ref, bf16[512,2048]{1,0:T(8,128)(2,1)} %collective-permute-done.7.xm_hbm, ...), custom_call_target="tpu_custom_call" | custom-call | flops 8858370048 | bytes 77594624 | tf_op jit(solution)/shard_map/pallas_call | solution.py:361
  145.3 5.6 %collective-permute-start.9 = (f32[384,2048]{1,0:T(8,128)}, f32[384,2048]{1,0:T(8,128)}, u32[]{:S(2)}, u32[]{:S(2)}) collective-permute-start(f32[384,2048]{1,0:T(8,128)} %get-tuple-element.44), channel_id=1, source_target_pairs={{0,1},{1,0},{2,3},{3,2},{4,5},{5,4},{6,7},{7,6}} | collective-permute-start | bytes 9437192 | tf_op jit(solution)/shard_map/ppermute | solution.py:324
  150.9 0.0 collective-permute-done.10
  150.9 5.4 %add.27 = f32[384,2048]{1,0:T(8,128)} add(f32[384,2048]{1,0:T(8,128)} %get-tuple-element.45, f32[384,2048]{1,0:T(8,128)} %collective-permute-done.10) | non-fusion elementwise | flops 786432 | bytes 9437184 | tf_op jit(solution)/shard_map/add | solution.py:385
  156.2 3.0 collective-permute-start.11
  159.3 2.8 collective-permute-start.1
  162.1 0.0 collective-permute-start
  162.1 2.3 collective-permute-done.1
  164.4 0.1 add.24
  164.5 0.0 collective-permute-start.2
  164.5 1.3 collective-permute-done.xo_hbm
  165.9 1.0 copy-done.1
  166.9 0.4 collective-permute-start.14
  167.2 38.9 %collective-permute-done.2.refs_0_ = f32[128,2048]{1,0:T(8,128)} collective-permute-done((f32[128,2048]{1,0:T(8,128)S(1)}, f32[128,2048]{1,0:T(8,128)}, u32[]{:S(2)}, u32[]{:S(2)}) %collective-permute-start.2) | collective-permute-done | bytes 1048608 | tf_op jit(solution)/shard_map/ppermute | solution.py:328
  206.1 0.0 collective-permute-done.4.refs_1_
  206.1 35.0 %shard_map.74 = (f32[384,2048]{1,0:T(8,128)}, f32[128,2048]{1,0:T(8,128)}, f32[384,2048]{1,0:T(8,128)}, f32[128,2048]{1,0:T(8,128)}) custom-call(s32[8,128]{1,0:T(8,128)} %get-tuple-element.31.table_ref, s32[8,8,256]{2,1,0:T(8,128)} %get-tuple-element.32.pos_ref, bf16[256,2048]{1,0:T(8,128)(2,1)} %xm_hbm.1, bf16[256,2048]{1,0:T(8,128)(2,1)} %copy-done.1, ...), custom_call_target="tpu_custom_call" | custom-call | flops 8858370048 | bytes 77594624 | tf_op jit(solution)/shard_map/pallas_call | solution.py:361
  241.1 0.0 collective-permute-start.5
  241.1 0.0 collective-permute-done.9
  241.1 0.0 collective-permute-done.11
  241.2 4.8 %add_add_fusion = f32[384,2048]{1,0:T(8,128)S(1)} fusion(f32[384,2048]{1,0:T(8,128)} %collective-permute-done.11, f32[384,2048]{1,0:T(8,128)} %get-tuple-element.43, f32[384,2048]{1,0:T(8,128)} %collective-permute-done.9), kind=kLoop, calls=%fused_computation | loop fusion | flops 1572864 | bytes 12582912 | tf_op jit(solution)/shard_map/add | solution.py:385
  246.0 0.0 collective-permute-start.12
  246.1 0.5 collective-permute-start.13
  246.6 0.0 collective-permute-done.14
  246.6 1.4 add.30
  248.0 1.7 collective-permute-start.15
  249.7 0.0 collective-permute-start.6
  249.7 0.0 collective-permute-done.13
  249.7 24.3 %collective-permute-done.15 = f32[128,2048]{1,0:T(8,128)S(1)} collective-permute-done((f32[128,2048]{1,0:T(8,128)S(1)}, f32[128,2048]{1,0:T(8,128)S(1)}, u32[]{:S(2)}, u32[]{:S(2)}) %collective-permute-start.15) | collective-permute-done | bytes 1048608 | tf_op jit(solution)/shard_map/ppermute | solution.py:328
  274.0 1.2 add_add_fusion.1
  275.2 1.5 collective-permute-start.16
  276.7 0.0 collective-permute-done.6.o1_ref
  276.7 0.0 collective-permute-done.5.o0_ref
  276.7 18.0 %collective-permute-done.12.f0_ref = f32[384,2048]{1,0:T(8,128)} collective-permute-done((f32[384,2048]{1,0:T(8,128)S(1)}, f32[384,2048]{1,0:T(8,128)}, u32[]{:S(2)}, u32[]{:S(2)}) %collective-permute-start.12) | collective-permute-done | bytes 3145760 | tf_op jit(solution)/shard_map/ppermute | solution.py:328
  294.6 7.3 %combine.1 = (f32[256,2048]{1,0:T(8,128)}, f32[128,2048]{1,0:T(8,128)}) custom-call(bf16[2,256,512]{2,1,0:T(8,128)(2,1)} %get-tuple-element.29.hit_ref, f32[256,8]{1,0:T(8,128)} %get-tuple-element.30.gate_ref, f32[384,2048]{1,0:T(8,128)} %get-tuple-element.39.k0_ref, f32[128,2048]{1,0:T(8,128)} %get-tuple-element.40.k1_ref, ...), custom_call_target="tpu_custom_call" | custom-call | tf_op jit(solution)/shard_map/combine/pallas_call | solution.py:408
  302.0 3.9 %collective-permute-done.16.f1_ref = f32[128,2048]{1,0:T(8,128)} collective-permute-done((f32[128,2048]{1,0:T(8,128)}, f32[128,2048]{1,0:T(8,128)}, u32[]{:S(2)}, u32[]{:S(2)}) %collective-permute-start.16) | collective-permute-done | bytes 1048608 | tf_op jit(solution)/shard_map/ppermute | solution.py:328
  305.9 3.5 %close.1 = bf16[256,2048]{1,0:T(8,128)(2,1)} custom-call(bf16[2,256,512]{2,1,0:T(8,128)(2,1)} %get-tuple-element.29.hit_ref, f32[256,8]{1,0:T(8,128)} %get-tuple-element.30.gate_ref, f32[256,2048]{1,0:T(8,128)} %get-tuple-element.47.total_ref, f32[128,2048]{1,0:T(8,128)} %get-tuple-element.48.sum_ref, f32[128,2048]{1,0:T(8,128)} %collective-permute-done.16.f1_ref), custom_call_target="tpu_custom_call" | custom-call | tf_op jit(solution)/shard_map/close/pallas_call | solution.py:418
  (17 shorter events, 0.0 us)
Async XLA Ops:
  21.0 26.4 %collective-permute-start.7 = (bf16[512,2048]{1,0:T(8,128)(2,1)}, bf16[512,2048]{1,0:T(8,128)(2,1)}, u32[]{:S(2)}, u32[]{:S(2)}) collective-permute-start(bf16[512,2048]{1,0:T(8,128)(2,1)} %get-tuple-element.33.xm_hbm), channel_id=1, source_target_pairs={{0,4},{1,3},{2,6},{3,1},{4,0},{5,7},{6,2},{7,5}} | collective-permute-start | bytes 6291464 | tf_op jit(solution)/shard_map/ppermute | solution.py:328
  47.4 31.4 %collective-permute-start.8 = (bf16[512,2048]{1,0:T(8,128)(2,1)}, bf16[512,2048]{1,0:T(8,128)(2,1)}, u32[]{:S(2)}, u32[]{:S(2)}) collective-permute-start(bf16[512,2048]{1,0:T(8,128)(2,1)} %collective-permute-done.7.xm_hbm), channel_id=1, source_target_pairs={{0,1},{1,0},{2,3},{3,2},{4,5},{5,4},{6,7},{7,6}} | collective-permute-start | bytes 6291464 | tf_op jit(solution)/shard_map/ppermute | solution.py:324
  78.8 34.7 %collective-permute-start.3 = (f32[384,2048]{1,0:T(8,128)}, f32[384,2048]{1,0:T(8,128)}, u32[]{:S(2)}, u32[]{:S(2)}) collective-permute-start(f32[384,2048]{1,0:T(8,128)} %get-tuple-element.38), channel_id=1, source_target_pairs={{0,1},{1,0},{2,3},{3,2},{4,5},{5,4},{6,7},{7,6}} | collective-permute-start | bytes 9437192 | tf_op jit(solution)/shard_map/ppermute | solution.py:324
  105.5 45.4 %collective-permute-start.10 = (f32[384,2048]{1,0:T(8,128)}, f32[384,2048]{1,0:T(8,128)}, u32[]{:S(2)}, u32[]{:S(2)}) collective-permute-start(f32[384,2048]{1,0:T(8,128)} %get-tuple-element.46), channel_id=1, source_target_pairs={{0,1},{1,0},{2,3},{3,2},{4,5},{5,4},{6,7},{7,6}} | collective-permute-start | bytes 9437192 | tf_op jit(solution)/shard_map/ppermute | solution.py:324
  118.7 87.4 %collective-permute-start.4 = (f32[384,2048]{1,0:T(8,128)}, f32[384,2048]{1,0:T(8,128)}, u32[]{:S(2)}, u32[]{:S(2)}) collective-permute-start(f32[384,2048]{1,0:T(8,128)} %add.25), channel_id=1, source_target_pairs={{0,2},{1,5},{2,0},{3,7},{4,6},{5,1},{6,4},{7,3}} | collective-permute-start | bytes 9437192 | tf_op jit(solution)/shard_map/ppermute | solution.py:328
  145.3 95.8 %collective-permute-start.9 = (f32[384,2048]{1,0:T(8,128)}, f32[384,2048]{1,0:T(8,128)}, u32[]{:S(2)}, u32[]{:S(2)}) collective-permute-start(f32[384,2048]{1,0:T(8,128)} %get-tuple-element.44), channel_id=1, source_target_pairs={{0,1},{1,0},{2,3},{3,2},{4,5},{5,4},{6,7},{7,6}} | collective-permute-start | bytes 9437192 | tf_op jit(solution)/shard_map/ppermute | solution.py:324
  150.9 8.4 %copy-start.8 = (f32[128,2048]{1,0:T(8,128)S(1)}, f32[128,2048]{1,0:T(8,128)}, u32[]{:S(2)}) copy-start(f32[128,2048]{1,0:T(8,128)} %get-tuple-element.36) | copy-start | bytes 3145732
  150.9 11.2 %copy-start = (bf16[256,2048]{1,0:T(8,128)(2,1)S(1)}, bf16[256,2048]{1,0:T(8,128)(2,1)}, u32[]{:S(2)}) copy-start(bf16[256,2048]{1,0:T(8,128)(2,1)} %xm_hbm.1) | copy-start | bytes 3145732
  150.9 13.5 %copy-start.3 = (f32[128,2048]{1,0:T(8,128)S(1)}, f32[128,2048]{1,0:T(8,128)}, u32[]{:S(2)}) copy-start(f32[128,2048]{1,0:T(8,128)} %get-tuple-element.35) | copy-start | bytes 3145732
  156.2 84.9 %collective-permute-start.11 = (f32[384,2048]{1,0:T(8,128)}, f32[384,2048]{1,0:T(8,128)}, u32[]{:S(2)}, u32[]{:S(2)}) collective-permute-start(f32[384,2048]{1,0:T(8,128)} %add.27), channel_id=1, source_target_pairs={{0,2},{1,5},{2,0},{3,7},{4,6},{5,1},{6,4},{7,3}} | collective-permute-start | bytes 9437192 | tf_op jit(solution)/shard_map/ppermute | solution.py:328
  159.3 5.1 %collective-permute-start.1 = (f32[128,2048]{1,0:T(8,128)S(1)}, f32[128,2048]{1,0:T(8,128)S(1)}, u32[]{:S(2)}, u32[]{:S(2)}) collective-permute-start(f32[128,2048]{1,0:T(8,128)S(1)} %copy-done.8), channel_id=1, source_target_pairs={{0,1},{1,0},{2,3},{3,2},{4,5},{5,4},{6,7},{7,6}} | collective-permute-start | bytes 3145736 | tf_op jit(solution)/shard_map/ppermute | solution.py:324
  162.1 3.8 %collective-permute-start = (bf16[256,2048]{1,0:T(8,128)(2,1)S(1)}, bf16[256,2048]{1,0:T(8,128)(2,1)S(1)}, u32[]{:S(2)}, u32[]{:S(2)}) collective-permute-start(bf16[256,2048]{1,0:T(8,128)(2,1)S(1)} %copy-done), channel_id=1, source_target_pairs={{0,1},{1,0},{2,3},{3,2},{4,5},{5,4},{6,7},{7,6}} | collective-permute-start | bytes 3145736 | tf_op jit(solution)/shard_map/ppermute | solution.py:324
  164.5 41.6 %collective-permute-start.2 = (f32[128,2048]{1,0:T(8,128)S(1)}, f32[128,2048]{1,0:T(8,128)}, u32[]{:S(2)}, u32[]{:S(2)}) collective-permute-start(f32[128,2048]{1,0:T(8,128)S(1)} %add.24), channel_id=1, source_target_pairs={{0,2},{1,5},{2,0},{3,7},{4,6},{5,1},{6,4},{7,3}} | collective-permute-start | bytes 3145736 | tf_op jit(solution)/shard_map/ppermute | solution.py:328
  165.9 1.0 copy-start.1
  166.9 79.7 %collective-permute-start.14 = (f32[128,2048]{1,0:T(8,128)}, f32[128,2048]{1,0:T(8,128)}, u32[]{:S(2)}, u32[]{:S(2)}) collective-permute-start(f32[128,2048]{1,0:T(8,128)} %get-tuple-element.52), channel_id=1, source_target_pairs={{0,1},{1,0},{2,3},{3,2},{4,5},{5,4},{6,7},{7,6}} | collective-permute-start | bytes 3145736 | tf_op jit(solution)/shard_map/ppermute | solution.py:324
  241.1 35.6 %collective-permute-start.5 = (f32[384,2048]{1,0:T(8,128)}, f32[384,2048]{1,0:T(8,128)}, u32[]{:S(2)}, u32[]{:S(2)}) collective-permute-start(f32[384,2048]{1,0:T(8,128)} %get-tuple-element.41), channel_id=1, source_target_pairs={{0,1},{1,0},{2,3},{3,2},{4,5},{5,4},{6,7},{7,6}} | collective-permute-start | bytes 9437192 | tf_op jit(solution)/shard_map/ppermute | solution.py:324
  241.2 4.9 %copy-start.6 = (f32[128,2048]{1,0:T(8,128)S(1)}, f32[128,2048]{1,0:T(8,128)}, u32[]{:S(2)}) copy-start(f32[128,2048]{1,0:T(8,128)} %get-tuple-element.50) | copy-start | bytes 3145732
  241.2 5.4 %copy-start.2 = (f32[128,2048]{1,0:T(8,128)S(1)}, f32[128,2048]{1,0:T(8,128)}, u32[]{:S(2)}) copy-start(f32[128,2048]{1,0:T(8,128)} %get-tuple-element.51) | copy-start | bytes 3145732
  246.0 3.7 %copy-start.7 = (f32[128,2048]{1,0:T(8,128)S(1)}, f32[128,2048]{1,0:T(8,128)}, u32[]{:S(2)}) copy-start(f32[128,2048]{1,0:T(8,128)} %get-tuple-element.42) | copy-start | bytes 3145732
  246.0 28.0 %copy-start.5 = (f32[128,2048]{1,0:T(8,128)S(1)}, f32[128,2048]{1,0:T(8,128)}, u32[]{:S(2)}) copy-start(f32[128,2048]{1,0:T(8,128)} %get-tuple-element.49) | copy-start | bytes 3145732
  246.0 48.6 %collective-permute-start.12 = (f32[384,2048]{1,0:T(8,128)S(1)}, f32[384,2048]{1,0:T(8,128)}, u32[]{:S(2)}, u32[]{:S(2)}) collective-permute-start(f32[384,2048]{1,0:T(8,128)S(1)} %add_add_fusion), channel_id=1, source_target_pairs={{0,4},{1,3},{2,6},{3,1},{4,0},{5,7},{6,2},{7,5}} | collective-permute-start | bytes 9437192 | tf_op jit(solution)/shard_map/ppermute | solution.py:328
  246.1 3.6 %collective-permute-start.13 = (f32[128,2048]{1,0:T(8,128)S(1)}, f32[128,2048]{1,0:T(8,128)S(1)}, u32[]{:S(2)}, u32[]{:S(2)}) collective-permute-start(f32[128,2048]{1,0:T(8,128)S(1)} %copy-done.6), channel_id=1, source_target_pairs={{0,1},{1,0},{2,3},{3,2},{4,5},{5,4},{6,7},{7,6}} | collective-permute-start | bytes 3145736 | tf_op jit(solution)/shard_map/ppermute | solution.py:324
  248.0 26.1 %collective-permute-start.15 = (f32[128,2048]{1,0:T(8,128)S(1)}, f32[128,2048]{1,0:T(8,128)S(1)}, u32[]{:S(2)}, u32[]{:S(2)}) collective-permute-start(f32[128,2048]{1,0:T(8,128)S(1)} %add.30), channel_id=1, source_target_pairs={{0,2},{1,5},{2,0},{3,7},{4,6},{5,1},{6,4},{7,3}} | collective-permute-start | bytes 3145736 | tf_op jit(solution)/shard_map/ppermute | solution.py:328
  249.7 27.0 %collective-permute-start.6 = (f32[128,2048]{1,0:T(8,128)S(1)}, f32[128,2048]{1,0:T(8,128)S(1)}, u32[]{:S(2)}, u32[]{:S(2)}) collective-permute-start(f32[128,2048]{1,0:T(8,128)S(1)} %copy-done.7), channel_id=1, source_target_pairs={{0,1},{1,0},{2,3},{3,2},{4,5},{5,4},{6,7},{7,6}} | collective-permute-start | bytes 3145736 | tf_op jit(solution)/shard_map/ppermute | solution.py:324
  275.2 30.7 %collective-permute-start.16 = (f32[128,2048]{1,0:T(8,128)}, f32[128,2048]{1,0:T(8,128)}, u32[]{:S(2)}, u32[]{:S(2)}) collective-permute-start(f32[128,2048]{1,0:T(8,128)} %add_add_fusion.1), channel_id=1, source_target_pairs={{0,4},{1,3},{2,6},{3,1},{4,0},{5,7},{6,2},{7,5}} | collective-permute-start | bytes 3145736 | tf_op jit(solution)/shard_map/ppermute | solution.py:328
  276.7 18.0 %copy-start.4 = (f32[128,2048]{1,0:T(8,128)}, f32[128,2048]{1,0:T(8,128)S(1)}, u32[]{:S(2)}) copy-start(f32[128,2048]{1,0:T(8,128)S(1)} %collective-permute-done.6.o1_ref) | copy-start | bytes 3145732

commit v13 on v12

--- a/solution.py
+++ b/solution.py
@@ -191,8 +191,9 @@
     ]
     for c in tokens:
         c.start()
-    for c in chunks[0](0):
-        c.start()
+    for chunk in chunks[: len(w1s)]:
+        for c in chunk(0):
+            c.start()
     row = 0
     for i, ref in enumerate(init_hbm):
         tokens.append(pltpu.make_async_copy(ref, acc.at[0, pl.ds(row, ref.shape[0])], xsem.at[2 + i]))
@@ -200,12 +201,7 @@
         row += ref.shape[0]
     for s in range(1 if inits else 0, 2):
         acc[s] = jnp.zeros(acc.shape[1:], F32)
-    for c in tokens[:2]:
-        c.wait()
-    for chunk in chunks[1 : len(w1s)]:
-        for c in chunk(0):
-            c.start()
-    for c in tokens[2:]:
+    for c in tokens:
         c.wait()
 
     def step(e, carry):
@@ -299,8 +295,9 @@
 
 
 def _close_kernel(hit_ref, gate_ref, total_ref, sum_ref, f1_ref, out_ref):
+    most = hit_ref.shape[2] - f1_ref.shape[0]
     y = (sum_ref[...] + f1_ref[...]).astype(BF16)
-    hit = [hit_ref[j] for j in range(hit_ref.shape[0])]
+    hit = [hit_ref[j, :, most:] for j in range(hit_ref.shape[0])]
     out_ref[...] = _weigh(hit, gate_ref, y, total_ref[...]).astype(out_ref.dtype)
 
 
@@ -355,7 +352,7 @@
             name="route",
         )(idx.T, g.T, cap, x)
 
-        sizes = (64, 152)
+        sizes = (64, 160)
 
         def stage(turns, mine, other, split, rows0=(0, 0), init=()):
             return pl.pallas_call(
@@ -418,8 +415,7 @@
         return pl.pallas_call(
             _close_kernel,
             out_shape=jax.ShapeDtypeStruct((t_loc, d), BF16),
-            in_specs=[pl.BlockSpec((top, t_loc, late[1]), lambda i: (0, 0, late[0] // late[1])), vmem]
-            + [part(n) for n in (t_loc, late[1], late[1])],
+            in_specs=[vmem, vmem] + [part(n) for n in (t_loc, late[1], late[1])],
             out_specs=part(t_loc),
             name="close",
             **grid,

time: 310 us -> 314 us (1.013)
  no operation moved by 1% of the time
where the time goes in v13:
time: 314 us
  Pallas kernels  153 us (49%)
  waiting for transfers between devices  114 us (36%)
  starting transfers between devices  27.7 us (9%)
  other arithmetic  18.1 us (6%)
    pallas_call x4, Pallas kernels, stage(): pl.pallas_call(functools.partial(_expert_kernel, turns, rows0, sizes, cut...  121 us
    ppermute x7, waiting for transfers between devices, shift(): return lax.ppermute(a, ('tp', 'ep'), pairs)  110 us
    pallas_call x1, Pallas kernels, layer(): pl.pallas_call(functools.partial(_route_kernel, chips, out), out_shape=[j...  21 us
    ppermute x10, starting transfers between devices, swap(): return lax.ppermute(a, 'ep', [(0, 1), (1, 0)])  18.5 us
    add x4, other arithmetic, merge(): parts[2 + q] + other  12.1 us
    ppermute x7, starting transfers between devices, shift(): return lax.ppermute(a, ('tp', 'ep'), pairs)  9.26 us
    pallas_call x1, Pallas kernels, layer(): pl.pallas_call(_combine_kernel, out_shape=[jax.ShapeDtypeStruct((t_loc, d...  7.32 us
  transfers between devices with their start and end apart: 17, of which 7 were waited for; matrix products, arithmetic and copies ran while one was open for 6% of the time, Pallas kernels for 41%

profile of v13, /device:TPU:0, one launch (start us, length us, event | category | flops | bytes accessed | tf_op | source)
XLA Modules:
  0.0 314.0 jit_solution(8301979308694524164)
XLA Ops:
  0.0 21.0 %route.1 = (s32[8,8,256]{2,1,0:T(8,128)}, s32[8,128]{1,0:T(8,128)}, bf16[2,256,512]{2,1,0:T(8,128)(2,1)}, f32[256,8]{1,0:T(8,128)}, bf16[512,2048]{1,0:T(8,128)(2,1)}, /*index=5*/bf16[256,2048]{1,0:T(8,128)(2,1)}) custom-call(s32[2,256]{1,0:T(2,128)} %bitcast.2, f32[2,256]{1,0:T(2,128)} %bitcast.3, s32[8]{0:T(128)} %cap_ref.1, bf16[256,2048]{1,0:T(8,128)(2,1)} %xm_hbm.1), custom_call_target="tpu_custom_call" | custom-call | tf_op jit(solution)/shard_map/route/pallas_call | solution.py:329
  21.0 1.2 collective-permute-start.7
  22.3 25.1 %collective-permute-done.7.xm_hbm = bf16[512,2048]{1,0:T(8,128)(2,1)} collective-permute-done((bf16[512,2048]{1,0:T(8,128)(2,1)}, bf16[512,2048]{1,0:T(8,128)(2,1)}, u32[]{:S(2)}, u32[]{:S(2)}) %collective-permute-start.7) | collective-permute-done | bytes 2097184 | tf_op jit(solution)/shard_map/ppermute | solution.py:325
  47.4 0.0 collective-permute-start.8
  47.4 31.9 %shard_map.73 = (f32[128,2048]{1,0:T(8,128)}, f32[384,2048]{1,0:T(8,128)}, f32[128,2048]{1,0:T(8,128)}, f32[384,2048]{1,0:T(8,128)}) custom-call(s32[8,128]{1,0:T(8,128)} %get-tuple-element.31.table_ref, s32[8,8,256]{2,1,0:T(8,128)} %get-tuple-element.32.pos_ref, bf16[512,2048]{1,0:T(8,128)(2,1)} %get-tuple-element.33.xm_hbm, ...), custom_call_target="tpu_custom_call" | custom-call | flops 8858370048 | bytes 77594624 | tf_op jit(solution)/shard_map/pallas_call | solution.py:358
  79.3 0.0 collective-permute-start.3
  79.3 0.0 collective-permute-done.8.xo_hbm
  79.3 26.7 %shard_map.76 = (f32[384,2048]{1,0:T(8,128)}, f32[128,2048]{1,0:T(8,128)}, f32[384,2048]{1,0:T(8,128)}, f32[128,2048]{1,0:T(8,128)}) custom-call(s32[8,128]{1,0:T(8,128)} %get-tuple-element.31.table_ref, s32[8,8,256]{2,1,0:T(8,128)} %get-tuple-element.32.pos_ref, bf16[512,2048]{1,0:T(8,128)(2,1)} %collective-permute-done.7.xm_hbm, ...), custom_call_target="tpu_custom_call" | custom-call | flops 8858370048 | bytes 77594624 | tf_op jit(solution)/shard_map/pallas_call | solution.py:358
  106.1 8.6 %collective-permute-start.10 = (f32[384,2048]{1,0:T(8,128)}, f32[384,2048]{1,0:T(8,128)}, u32[]{:S(2)}, u32[]{:S(2)}) collective-permute-start(f32[384,2048]{1,0:T(8,128)} %get-tuple-element.46), channel_id=1, source_target_pairs={{0,1},{1,0},{2,3},{3,2},{4,5},{5,4},{6,7},{7,6}} | collective-permute-start | bytes 9437192 | tf_op jit(solution)/shard_map/ppermute | solution.py:321
  114.7 0.0 collective-permute-done.3
  114.7 5.2 %add.25 = f32[384,2048]{1,0:T(8,128)} add(f32[384,2048]{1,0:T(8,128)} %get-tuple-element.37, f32[384,2048]{1,0:T(8,128)} %collective-permute-done.3) | non-fusion elementwise | flops 786432 | bytes 9437184 | tf_op jit(solution)/shard_map/add | solution.py:382
  120.0 1.0 collective-permute-start.4
  121.0 26.7 %shard_map.75 = (f32[384,2048]{1,0:T(8,128)}, f32[128,2048]{1,0:T(8,128)}, f32[384,2048]{1,0:T(8,128)}, f32[128,2048]{1,0:T(8,128)}) custom-call(s32[8,128]{1,0:T(8,128)} %get-tuple-element.31.table_ref, s32[8,8,256]{2,1,0:T(8,128)} %get-tuple-element.32.pos_ref, bf16[512,2048]{1,0:T(8,128)(2,1)} %collective-permute-done.7.xm_hbm, ...), custom_call_target="tpu_custom_call" | custom-call | flops 8858370048 | bytes 77594624 | tf_op jit(solution)/shard_map/pallas_call | solution.py:358
  147.7 5.8 %collective-permute-start.9 = (f32[384,2048]{1,0:T(8,128)}, f32[384,2048]{1,0:T(8,128)}, u32[]{:S(2)}, u32[]{:S(2)}) collective-permute-start(f32[384,2048]{1,0:T(8,128)} %get-tuple-element.44), channel_id=1, source_target_pairs={{0,1},{1,0},{2,3},{3,2},{4,5},{5,4},{6,7},{7,6}} | collective-permute-start | bytes 9437192 | tf_op jit(solution)/shard_map/ppermute | solution.py:321
  153.4 0.0 collective-permute-done.10
  153.5 5.4 %add.27 = f32[384,2048]{1,0:T(8,128)} add(f32[384,2048]{1,0:T(8,128)} %get-tuple-element.45, f32[384,2048]{1,0:T(8,128)} %collective-permute-done.10) | non-fusion elementwise | flops 786432 | bytes 9437184 | tf_op jit(solution)/shard_map/add | solution.py:382
  158.8 3.8 %collective-permute-start.11 = (f32[384,2048]{1,0:T(8,128)}, f32[384,2048]{1,0:T(8,128)}, u32[]{:S(2)}, u32[]{:S(2)}) collective-permute-start(f32[384,2048]{1,0:T(8,128)} %add.27), channel_id=1, source_target_pairs={{0,2},{1,5},{2,0},{3,7},{4,6},{5,1},{6,4},{7,3}} | collective-permute-start | bytes 9437192 | tf_op jit(solution)/shard_map/ppermute | solution.py:325
  162.7 3.0 collective-permute-start.1
  165.7 0.0 collective-permute-start
  165.7 2.3 collective-permute-done.1
  168.0 0.1 add.24
  168.1 0.0 collective-permute-start.2
  168.1 1.3 collective-permute-done.xo_hbm
  169.5 1.0 copy-done.1
  170.5 0.4 collective-permute-start.14
  170.8 38.6 %collective-permute-done.2.refs_0_ = f32[128,2048]{1,0:T(8,128)} collective-permute-done((f32[128,2048]{1,0:T(8,128)S(1)}, f32[128,2048]{1,0:T(8,128)}, u32[]{:S(2)}, u32[]{:S(2)}) %collective-permute-start.2) | collective-permute-done | bytes 1048608 | tf_op jit(solution)/shard_map/ppermute | solution.py:325
  209.4 0.0 collective-permute-done.4.refs_1_
  209.4 36.2 %shard_map.74 = (f32[384,2048]{1,0:T(8,128)}, f32[128,2048]{1,0:T(8,128)}, f32[384,2048]{1,0:T(8,128)}, f32[128,2048]{1,0:T(8,128)}) custom-call(s32[8,128]{1,0:T(8,128)} %get-tuple-element.31.table_ref, s32[8,8,256]{2,1,0:T(8,128)} %get-tuple-element.32.pos_ref, bf16[256,2048]{1,0:T(8,128)(2,1)} %xm_hbm.1, bf16[256,2048]{1,0:T(8,128)(2,1)} %copy-done.1, ...), custom_call_target="tpu_custom_call" | custom-call | flops 8858370048 | bytes 77594624 | tf_op jit(solution)/shard_map/pallas_call | solution.py:358
  245.6 0.0 collective-permute-start.5
  245.7 0.0 collective-permute-done.9
  245.7 0.0 collective-permute-done.11
  245.7 4.8 %add_add_fusion = f32[384,2048]{1,0:T(8,128)S(1)} fusion(f32[384,2048]{1,0:T(8,128)} %collective-permute-done.11, f32[384,2048]{1,0:T(8,128)} %get-tuple-element.43, f32[384,2048]{1,0:T(8,128)} %collective-permute-done.9), kind=kLoop, calls=%fused_computation | loop fusion | flops 1572864 | bytes 12582912 | tf_op jit(solution)/shard_map/add | solution.py:382
  250.5 0.0 collective-permute-start.12
  250.6 0.5 collective-permute-start.13
  251.1 0.0 collective-permute-done.14
  251.1 1.4 add.30
  252.5 1.7 collective-permute-start.15
  254.2 0.0 collective-permute-start.6
  254.2 0.0 collective-permute-done.13
  254.2 24.3 %collective-permute-done.15 = f32[128,2048]{1,0:T(8,128)S(1)} collective-permute-done((f32[128,2048]{1,0:T(8,128)S(1)}, f32[128,2048]{1,0:T(8,128)S(1)}, u32[]{:S(2)}, u32[]{:S(2)}) %collective-permute-start.15) | collective-permute-done | bytes 1048608 | tf_op jit(solution)/shard_map/ppermute | solution.py:325
  278.6 1.2 add_add_fusion.1
  279.7 1.5 collective-permute-start.16
  281.2 0.0 collective-permute-done.6.o1_ref
  281.2 0.0 collective-permute-done.5.o0_ref
  281.2 18.0 %collective-permute-done.12.f0_ref = f32[384,2048]{1,0:T(8,128)} collective-permute-done((f32[384,2048]{1,0:T(8,128)S(1)}, f32[384,2048]{1,0:T(8,128)}, u32[]{:S(2)}, u32[]{:S(2)}) %collective-permute-start.12) | collective-permute-done | bytes 3145760 | tf_op jit(solution)/shard_map/ppermute | solution.py:325
  299.2 7.3 %combine.1 = (f32[256,2048]{1,0:T(8,128)}, f32[128,2048]{1,0:T(8,128)}) custom-call(bf16[2,256,512]{2,1,0:T(8,128)(2,1)} %get-tuple-element.29.hit_ref, f32[256,8]{1,0:T(8,128)} %get-tuple-element.30.gate_ref, f32[384,2048]{1,0:T(8,128)} %get-tuple-element.39.k0_ref, f32[128,2048]{1,0:T(8,128)} %get-tuple-element.40.k1_ref, ...), custom_call_target="tpu_custom_call" | custom-call | tf_op jit(solution)/shard_map/combine/pallas_call | solution.py:405
  306.5 3.9 %collective-permute-done.16.f1_ref = f32[128,2048]{1,0:T(8,128)} collective-permute-done((f32[128,2048]{1,0:T(8,128)}, f32[128,2048]{1,0:T(8,128)}, u32[]{:S(2)}, u32[]{:S(2)}) %collective-permute-start.16) | collective-permute-done | bytes 1048608 | tf_op jit(solution)/shard_map/ppermute | solution.py:325
  310.4 3.6 %close.1 = bf16[256,2048]{1,0:T(8,128)(2,1)} custom-call(bf16[2,256,512]{2,1,0:T(8,128)(2,1)} %get-tuple-element.29.hit_ref, f32[256,8]{1,0:T(8,128)} %get-tuple-element.30.gate_ref, f32[256,2048]{1,0:T(8,128)} %get-tuple-element.47.total_ref, f32[128,2048]{1,0:T(8,128)} %get-tuple-element.48.sum_ref, f32[128,2048]{1,0:T(8,128)} %collective-permute-done.16.f1_ref), custom_call_target="tpu_custom_call" | custom-call | tf_op jit(solution)/shard_map/close/pallas_call | solution.py:415
  (17 shorter events, 0.0 us)
Async XLA Ops:
  21.0 26.4 %collective-permute-start.7 = (bf16[512,2048]{1,0:T(8,128)(2,1)}, bf16[512,2048]{1,0:T(8,128)(2,1)}, u32[]{:S(2)}, u32[]{:S(2)}) collective-permute-start(bf16[512,2048]{1,0:T(8,128)(2,1)} %get-tuple-element.33.xm_hbm), channel_id=1, source_target_pairs={{0,4},{1,3},{2,6},{3,1},{4,0},{5,7},{6,2},{7,5}} | collective-permute-start | bytes 6291464 | tf_op jit(solution)/shard_map/ppermute | solution.py:325
  47.4 31.9 %collective-permute-start.8 = (bf16[512,2048]{1,0:T(8,128)(2,1)}, bf16[512,2048]{1,0:T(8,128)(2,1)}, u32[]{:S(2)}, u32[]{:S(2)}) collective-permute-start(bf16[512,2048]{1,0:T(8,128)(2,1)} %collective-permute-done.7.xm_hbm), channel_id=1, source_target_pairs={{0,1},{1,0},{2,3},{3,2},{4,5},{5,4},{6,7},{7,6}} | collective-permute-start | bytes 6291464 | tf_op jit(solution)/shard_map/ppermute | solution.py:321
  79.3 35.4 %collective-permute-start.3 = (f32[384,2048]{1,0:T(8,128)}, f32[384,2048]{1,0:T(8,128)}, u32[]{:S(2)}, u32[]{:S(2)}) collective-permute-start(f32[384,2048]{1,0:T(8,128)} %get-tuple-element.38), channel_id=1, source_target_pairs={{0,1},{1,0},{2,3},{3,2},{4,5},{5,4},{6,7},{7,6}} | collective-permute-start | bytes 9437192 | tf_op jit(solution)/shard_map/ppermute | solution.py:321
  106.1 47.4 %collective-permute-start.10 = (f32[384,2048]{1,0:T(8,128)}, f32[384,2048]{1,0:T(8,128)}, u32[]{:S(2)}, u32[]{:S(2)}) collective-permute-start(f32[384,2048]{1,0:T(8,128)} %get-tuple-element.46), channel_id=1, source_target_pairs={{0,1},{1,0},{2,3},{3,2},{4,5},{5,4},{6,7},{7,6}} | collective-permute-start | bytes 9437192 | tf_op jit(solution)/shard_map/ppermute | solution.py:321
  120.0 89.5 %collective-permute-start.4 = (f32[384,2048]{1,0:T(8,128)}, f32[384,2048]{1,0:T(8,128)}, u32[]{:S(2)}, u32[]{:S(2)}) collective-permute-start(f32[384,2048]{1,0:T(8,128)} %add.25), channel_id=1, source_target_pairs={{0,2},{1,5},{2,0},{3,7},{4,6},{5,1},{6,4},{7,3}} | collective-permute-start | bytes 9437192 | tf_op jit(solution)/shard_map/ppermute | solution.py:325
  147.7 98.0 %collective-permute-start.9 = (f32[384,2048]{1,0:T(8,128)}, f32[384,2048]{1,0:T(8,128)}, u32[]{:S(2)}, u32[]{:S(2)}) collective-permute-start(f32[384,2048]{1,0:T(8,128)} %get-tuple-element.44), channel_id=1, source_target_pairs={{0,1},{1,0},{2,3},{3,2},{4,5},{5,4},{6,7},{7,6}} | collective-permute-start | bytes 9437192 | tf_op jit(solution)/shard_map/ppermute | solution.py:321
  153.4 9.2 %copy-start.8 = (f32[128,2048]{1,0:T(8,128)S(1)}, f32[128,2048]{1,0:T(8,128)}, u32[]{:S(2)}) copy-start(f32[128,2048]{1,0:T(8,128)} %get-tuple-element.36) | copy-start | bytes 3145732
  153.4 12.2 %copy-start = (bf16[256,2048]{1,0:T(8,128)(2,1)S(1)}, bf16[256,2048]{1,0:T(8,128)(2,1)}, u32[]{:S(2)}) copy-start(bf16[256,2048]{1,0:T(8,128)(2,1)} %xm_hbm.1) | copy-start | bytes 3145732
  153.5 14.5 %copy-start.3 = (f32[128,2048]{1,0:T(8,128)S(1)}, f32[128,2048]{1,0:T(8,128)}, u32[]{:S(2)}) copy-start(f32[128,2048]{1,0:T(8,128)} %get-tuple-element.35) | copy-start | bytes 3145732
  158.8 86.8 %collective-permute-start.11 = (f32[384,2048]{1,0:T(8,128)}, f32[384,2048]{1,0:T(8,128)}, u32[]{:S(2)}, u32[]{:S(2)}) collective-permute-start(f32[384,2048]{1,0:T(8,128)} %add.27), channel_id=1, source_target_pairs={{0,2},{1,5},{2,0},{3,7},{4,6},{5,1},{6,4},{7,3}} | collective-permute-start | bytes 9437192 | tf_op jit(solution)/shard_map/ppermute | solution.py:325
  162.7 5.3 %collective-permute-start.1 = (f32[128,2048]{1,0:T(8,128)S(1)}, f32[128,2048]{1,0:T(8,128)S(1)}, u32[]{:S(2)}, u32[]{:S(2)}) collective-permute-start(f32[128,2048]{1,0:T(8,128)S(1)} %copy-done.8), channel_id=1, source_target_pairs={{0,1},{1,0},{2,3},{3,2},{4,5},{5,4},{6,7},{7,6}} | collective-permute-start | bytes 3145736 | tf_op jit(solution)/shard_map/ppermute | solution.py:321
  165.7 3.8 %collective-permute-start = (bf16[256,2048]{1,0:T(8,128)(2,1)S(1)}, bf16[256,2048]{1,0:T(8,128)(2,1)S(1)}, u32[]{:S(2)}, u32[]{:S(2)}) collective-permute-start(bf16[256,2048]{1,0:T(8,128)(2,1)S(1)} %copy-done), channel_id=1, source_target_pairs={{0,1},{1,0},{2,3},{3,2},{4,5},{5,4},{6,7},{7,6}} | collective-permute-start | bytes 3145736 | tf_op jit(solution)/shard_map/ppermute | solution.py:321
  168.1 41.3 %collective-permute-start.2 = (f32[128,2048]{1,0:T(8,128)S(1)}, f32[128,2048]{1,0:T(8,128)}, u32[]{:S(2)}, u32[]{:S(2)}) collective-permute-start(f32[128,2048]{1,0:T(8,128)S(1)} %add.24), channel_id=1, source_target_pairs={{0,2},{1,5},{2,0},{3,7},{4,6},{5,1},{6,4},{7,3}} | collective-permute-start | bytes 3145736 | tf_op jit(solution)/shard_map/ppermute | solution.py:325
  169.5 1.0 copy-start.1
  170.5 80.6 %collective-permute-start.14 = (f32[128,2048]{1,0:T(8,128)}, f32[128,2048]{1,0:T(8,128)}, u32[]{:S(2)}, u32[]{:S(2)}) collective-permute-start(f32[128,2048]{1,0:T(8,128)} %get-tuple-element.52), channel_id=1, source_target_pairs={{0,1},{1,0},{2,3},{3,2},{4,5},{5,4},{6,7},{7,6}} | collective-permute-start | bytes 3145736 | tf_op jit(solution)/shard_map/ppermute | solution.py:321
  245.6 35.6 %collective-permute-start.5 = (f32[384,2048]{1,0:T(8,128)}, f32[384,2048]{1,0:T(8,128)}, u32[]{:S(2)}, u32[]{:S(2)}) collective-permute-start(f32[384,2048]{1,0:T(8,128)} %get-tuple-element.41), channel_id=1, source_target_pairs={{0,1},{1,0},{2,3},{3,2},{4,5},{5,4},{6,7},{7,6}} | collective-permute-start | bytes 9437192 | tf_op jit(solution)/shard_map/ppermute | solution.py:321
  245.7 4.9 %copy-start.6 = (f32[128,2048]{1,0:T(8,128)S(1)}, f32[128,2048]{1,0:T(8,128)}, u32[]{:S(2)}) copy-start(f32[128,2048]{1,0:T(8,128)} %get-tuple-element.50) | copy-start | bytes 3145732
  245.7 5.4 %copy-start.2 = (f32[128,2048]{1,0:T(8,128)S(1)}, f32[128,2048]{1,0:T(8,128)}, u32[]{:S(2)}) copy-start(f32[128,2048]{1,0:T(8,128)} %get-tuple-element.51) | copy-start | bytes 3145732
  250.5 3.7 %copy-start.7 = (f32[128,2048]{1,0:T(8,128)S(1)}, f32[128,2048]{1,0:T(8,128)}, u32[]{:S(2)}) copy-start(f32[128,2048]{1,0:T(8,128)} %get-tuple-element.42) | copy-start | bytes 3145732
  250.5 28.0 %copy-start.5 = (f32[128,2048]{1,0:T(8,128)S(1)}, f32[128,2048]{1,0:T(8,128)}, u32[]{:S(2)}) copy-start(f32[128,2048]{1,0:T(8,128)} %get-tuple-element.49) | copy-start | bytes 3145732
  250.5 48.6 %collective-permute-start.12 = (f32[384,2048]{1,0:T(8,128)S(1)}, f32[384,2048]{1,0:T(8,128)}, u32[]{:S(2)}, u32[]{:S(2)}) collective-permute-start(f32[384,2048]{1,0:T(8,128)S(1)} %add_add_fusion), channel_id=1, source_target_pairs={{0,4},{1,3},{2,6},{3,1},{4,0},{5,7},{6,2},{7,5}} | collective-permute-start | bytes 9437192 | tf_op jit(solution)/shard_map/ppermute | solution.py:325
  250.6 3.6 %collective-permute-start.13 = (f32[128,2048]{1,0:T(8,128)S(1)}, f32[128,2048]{1,0:T(8,128)S(1)}, u32[]{:S(2)}, u32[]{:S(2)}) collective-permute-start(f32[128,2048]{1,0:T(8,128)S(1)} %copy-done.6), channel_id=1, source_target_pairs={{0,1},{1,0},{2,3},{3,2},{4,5},{5,4},{6,7},{7,6}} | collective-permute-start | bytes 3145736 | tf_op jit(solution)/shard_map/ppermute | solution.py:321
  252.5 26.1 %collective-permute-start.15 = (f32[128,2048]{1,0:T(8,128)S(1)}, f32[128,2048]{1,0:T(8,128)S(1)}, u32[]{:S(2)}, u32[]{:S(2)}) collective-permute-start(f32[128,2048]{1,0:T(8,128)S(1)} %add.30), channel_id=1, source_target_pairs={{0,2},{1,5},{2,0},{3,7},{4,6},{5,1},{6,4},{7,3}} | collective-permute-start | bytes 3145736 | tf_op jit(solution)/shard_map/ppermute | solution.py:325
  254.2 27.0 %collective-permute-start.6 = (f32[128,2048]{1,0:T(8,128)S(1)}, f32[128,2048]{1,0:T(8,128)S(1)}, u32[]{:S(2)}, u32[]{:S(2)}) collective-permute-start(f32[128,2048]{1,0:T(8,128)S(1)} %copy-done.7), channel_id=1, source_target_pairs={{0,1},{1,0},{2,3},{3,2},{4,5},{5,4},{6,7},{7,6}} | collective-permute-start | bytes 3145736 | tf_op jit(solution)/shard_map/ppermute | solution.py:321
  279.7 30.7 %collective-permute-start.16 = (f32[128,2048]{1,0:T(8,128)}, f32[128,2048]{1,0:T(8,128)}, u32[]{:S(2)}, u32[]{:S(2)}) collective-permute-start(f32[128,2048]{1,0:T(8,128)} %add_add_fusion.1), channel_id=1, source_target_pairs={{0,4},{1,3},{2,6},{3,1},{4,0},{5,7},{6,2},{7,5}} | collective-permute-start | bytes 3145736 | tf_op jit(solution)/shard_map/ppermute | solution.py:325
  281.2 18.0 %copy-start.4 = (f32[128,2048]{1,0:T(8,128)}, f32[128,2048]{1,0:T(8,128)S(1)}, u32[]{:S(2)}) copy-start(f32[128,2048]{1,0:T(8,128)S(1)} %collective-permute-done.6.o1_ref) | copy-start | bytes 3145732
